TPU v7x, 32 devices: a whole 2x2x4 slice. The times are simulated.
32 devices in a mesh: kpt: 16 (over z, x, core), band: 2 (over y).
Axes of the slice: x: 2, y: 2, z: 4, core: 2. Of those that a mesh axis runs over, the one named last changes fastest.
Arguments:
- margins: bfloat16 [16, 12, 400, 800], P('kpt', None, 'band'), may hold values from -0.21875 to 0.21875
- subspace: bfloat16 [16, 400, 512], P('kpt', 'band'), may hold values from -6 to 6
- shell_weights: float32 [12], replicated, may hold values from 0.3 to 3
- window_count: int32 [16], P('kpt'), may hold values from 200 to 400
Outputs:
- new_subspace: float32 [16, 400, 512], P('kpt', 'band')
Inputs may be any that keep to these rules, and one draw needn't show every extreme that they name: window_count[k] is the number of leading bands of k-point k inside its outer window; the other rows up to 400 are padding.
All inputs are finite; a program needn't handle non-finite values.
Results may differ from a plain program's by a relative error of at most 0.0025.
Values may be sent and summed in bfloat16 or wider, within the bound.
No kernel may reach another device: no remote copies, remote signals or barrier semaphores. Data moves between devices by JAX's collectives and lax.ppermute only.
A program may use at most 64 MiB of HBM per device.

v0:
```python
import math

import jax
import jax.numpy as jnp
from jax import lax
from jax.sharding import PartitionSpec as P

SWEEPS = 2


SHELL_VECTORS = (
    (1, 1, 0),
    (1, -1, 0),
    (-1, 1, 0),
    (-1, -1, 0),
    (1, 0, 1),
    (1, 0, -1),
    (-1, 0, 1),
    (-1, 0, -1),
    (0, 1, 1),
    (0, 1, -1),
    (0, -1, 1),
    (0, -1, -1),
)


def grid_shape(point_count):
    size_y = min(4, point_count // 8)
    return (4, size_y, point_count // (4 * size_y))


def grid_place(point_index, point_count):
    size_x, size_y, size_z = grid_shape(point_count)
    return (point_index // (size_y * size_z), point_index // size_z % size_y, point_index % size_z)


def neighbour_ids(point_index, point_count):
    size_x, size_y, size_z = grid_shape(point_count)
    place_x, place_y, place_z = grid_place(point_index, point_count)
    listed = []
    for step_x, step_y, step_z in SHELL_VECTORS:
        target_x = (place_x + step_x) % size_x
        target_y = (place_y + step_y) % size_y
        target_z = (place_z + step_z) % size_z
        listed.append((target_x * size_y + target_y) * size_z + target_z)
    return jnp.stack(listed)


def stack_complex(matrix, half_cols):
    real_part = matrix[..., :half_cols]
    imag_part = matrix[..., half_cols:]
    upper_half = jnp.concatenate([real_part, imag_part], axis=-1)
    lower_half = jnp.concatenate([-imag_part, real_part], axis=-1)
    return jnp.concatenate([upper_half, lower_half], axis=-2)


def gram_parts(iterate, half_cols):
    blocks = jnp.dot(iterate.T, iterate, precision=lax.Precision.HIGHEST)
    real_part = blocks[:half_cols, :half_cols] + blocks[half_cols:, half_cols:]
    imag_part = blocks[:half_cols, half_cols:] - blocks[half_cols:, :half_cols]
    return jnp.concatenate([real_part, imag_part], axis=1)


def sweep_step(iterate, gram_sum, half_cols):
    identity = jnp.eye(half_cols, dtype=jnp.float32)
    factor = jnp.concatenate(
        [1.5 * identity - 0.5 * gram_sum[:, :half_cols], -0.5 * gram_sum[:, half_cols:]], axis=1
    )
    return jnp.dot(iterate, stack_complex(factor, half_cols), precision=lax.Precision.HIGHEST)


def assemble(mine, whole, weights, half_cols):
    real_part = mine[..., :half_cols]
    imag_part = mine[..., half_cols:]
    left_rows = jnp.concatenate([mine, jnp.concatenate([imag_part, -real_part], axis=-1)], axis=-2)
    products = jnp.einsum("brc,bsc->brs", left_rows, whole, preferred_element_type=jnp.float32)
    summed = jnp.einsum("b,brs->rs", weights, products, precision=lax.Precision.HIGHEST)
    row_count = mine.shape[-2]
    return jnp.concatenate([summed[:row_count], summed[row_count:]], axis=1)


def on_device(margins, subspace, shell_weights, window_count):
    half_cols = subspace.shape[-1] // 2
    row_count = subspace.shape[1]
    point_count = lax.axis_size("kpt")
    point_index = lax.axis_index("kpt")
    own_block = subspace[0]
    row_index = lax.axis_index("band") * row_count + lax.iota(jnp.int32, row_count)
    row_mask = (row_index < window_count[0])[None, :, None]
    targets = neighbour_ids(point_index, point_count)
    portion = lax.all_gather(subspace, "kpt", axis=0, tiled=True)
    labels = lax.iota(jnp.int32, portion.shape[0])
    one_hot = (targets[:, None] == labels[None, :]).astype(jnp.bfloat16)
    nearby = jnp.einsum("bn,nrc->brc", one_hot, portion, preferred_element_type=jnp.float32).astype(
        jnp.bfloat16
    )
    nearby_whole, own_whole = (
        lax.all_gather(nearby, "band", axis=1, tiled=True),
        lax.all_gather(own_block, "band", axis=0, tiled=True),
    )
    products = jnp.einsum(
        "brc,bcs->brs",
        margins[0],
        stack_complex(nearby_whole, half_cols),
        preferred_element_type=jnp.float32,
    )
    projected = jnp.where(row_mask, products, 0.0).astype(jnp.bfloat16)
    projected_whole = lax.all_gather(projected, "band", axis=1, tiled=True)
    assembled = assemble(projected, projected_whole, shell_weights, half_cols)
    iterate = jnp.dot(
        assembled,
        stack_complex(own_whole.astype(jnp.float32), half_cols),
        precision=lax.Precision.HIGHEST,
    )
    gram_sum = lax.psum(gram_parts(iterate, half_cols), "band")
    squares = jnp.trace(gram_sum[:, :half_cols])
    scaling = lax.rsqrt(2.0 * squares / half_cols + 1e-06)
    iterate = iterate * scaling
    gram_sum = gram_sum * (scaling * scaling)
    for sweep_number in range(SWEEPS):
        if sweep_number > 0:
            gram_sum = lax.psum(gram_parts(iterate, half_cols).astype(jnp.bfloat16), "band").astype(
                jnp.float32
            )
        iterate = sweep_step(iterate, gram_sum, half_cols)
    return (iterate * math.sqrt(row_count * lax.axis_size("band")))[None]


def solution(mesh):
    return jax.shard_map(
        on_device,
        mesh=mesh,
        in_specs=(P("kpt", None, "band", None), P("kpt", "band", None), P(), P("kpt")),
        out_specs=P("kpt", "band", None),
        check_vma=False,
    )
```

profile of v0, /device:TPU:0, one launch (start us, length us, event | category | flops | bytes accessed | tf_op | source)
XLA Modules:
  0.0 309.9 jit_solution(15494676957896561212)
XLA Ops:
  6.5 0.7 all-gather.5.cloned.1.call-update
  7.5 0.1 stack.51
  7.6 50.8 %all-gather.5.cloned.1.call-done = bf16[16,200,512]{2,1,0:T(8,128)(2,1)} async-done(((bf16[1,200,512]{2,1,0:T(8,128)(2,1)}), bf16[16,200,512]{2,1,0:T(8,128)(2,1)}) %all-gather.5.cloned.1.call-update) | async-done | bytes 3276816 | tf_op jit(solution)/shard_map/all_gather | solution.py:91
  58.4 3.2 %fusion.18 = bf16[12,200,512]{2,0,1:T(8,128)(2,1)S(1)} fusion(bf16[16,200,512]{2,1,0:T(8,128)(2,1)} %all-gather.5.cloned.1.call-done, s32[12]{0:T(128)S(1)} %stack.51), kind=kOutput, calls=%fused_computation.20 | convolution fusion | flops 40550592 | bytes 5734448 | tf_op jit(solution)/shard_map/bn,nrc->brc/dot_general | solution.py:94
  61.6 2.9 copy.8
  65.2 62.7 %all-gather.7.cloned.1.call-done = bf16[12,400,512]{2,1,0:T(8,128)(2,1)} async-done(((bf16[12,200,512]{2,1,0:T(8,128)(2,1)}), bf16[12,400,512]{2,1,0:T(8,128)(2,1)}) %all-gather.7.cloned.1.call-update) | async-done | bytes 4915216 | tf_op jit(solution)/shard_map/all_gather | solution.py:98
  127.9 2.9 slice_negate_fusion
  130.8 1.0 copy-done.2
  131.7 5.6 %fusion.17 = bf16[12,200,512]{2,1,0:T(8,128)(2,1)} fusion(pred[200]{0:T(512)(128)(4,1)S(1)} %add_compare_fusion, bf16[1,12,200,800]{3,2,1,0:T(8,128)(2,1)} %param.4, bf16[12,400,256]{2,1,0:T(8,128)(2,1)S(1)} %get-tuple-element.6, bf16[12,400,256]{2,1,0:T(8,128)(2,1)S(1)} %get-tuple-element.5, bf16[12,400,512]{2,1,0:T(8,128)(2,1)S(1)} %copy-done.2), kind=kOutput, calls=%fused_computation.18 | convolution fusion | flops 1998028800 | bytes 16128200 | tf_op jit(solution)/shard_map/brc,bcs->brs/dot_general | solution.py:101
  137.4 7.4 %all-gather = bf16[1,400,512]{2,1,0:T(8,128)(2,1)S(1)} all-gather(bf16[1,200,512]{2,1,0:T(8,128)(2,1)S(1)} %copy-done.3), channel_id=2, replica_groups=mesh['kpt'=16,'band'=2] {'band'}, dimensions={1}, use_global_device_ids=true | all-gather | bytes 614400 | tf_op jit(solution)/shard_map/all_gather | solution.py:99
  144.9 0.1 bitcast_convert_fusion
  144.9 1.0 slice_negate_fusion.2
  145.9 1.6 fusion.66
  147.5 54.9 %all-gather.9.cloned.1.call-done = bf16[12,400,512]{2,1,0:T(8,128)(2,1)} async-done(((bf16[12,200,512]{2,1,0:T(8,128)(2,1)}), bf16[12,400,512]{2,1,0:T(8,128)(2,1)}) %all-gather.9.cloned.1.call-update) | async-done | bytes 4915216 | tf_op jit(solution)/shard_map/all_gather | solution.py:108
  202.3 9.6 %fusion.8 = f32[12,400,400]{2,1,0:T(8,128)} fusion(bf16[12,400,512]{2,1,0:T(8,128)(2,1)} %all-gather.9.cloned.1.call-done, bf16[12,200,256]{2,1,0:T(8,128)(2,1)} %get-tuple-element.8, bf16[12,200,256]{2,1,0:T(8,128)(2,1)} %get-tuple-element.7, bf16[12,200,512]{2,1,0:T(8,128)(2,1)S(1)} %copy-done.1), kind=kOutput, calls=%fused_computation.8 | convolution fusion | flops 1980825600 | bytes 17510400 | tf_op jit(solution)/shard_map/brc,bsc->brs/dot_general | solution.py:76
  212.0 25.8 %fusion = f32[1,400,400]{2,0,1:T(1,128)S(1)} fusion(f32[12,400,400]{2,1,0:T(8,128)} %fusion.8, f32[12]{0:T(128)S(1)} %copy-done), kind=kOutput, calls=%fused_computation | convolution fusion | flops 23040000 | bytes 8320048 | tf_op jit(solution)/shard_map/b,brs->rs/dot_general | solution.py:77
  237.9 1.6 fusion.21
  239.5 1.1 fusion.68
  240.6 0.1 slice_add_fusion.1
  240.7 0.8 pad_maximum_fusion
  241.5 0.3 all-reduce.5.cloned.1.call-start
  241.8 28.5 %all-reduce.3.cloned.1.call-done = f32[256,512]{0,1:T(8,128)} async-done(((f32[256,512]{0,1:T(8,128)}), f32[256,512]{0,1:T(8,128)}) %all-reduce.3.cloned.1.call-update) | async-done | bytes 524304 | tf_op jit(solution)/shard_map/psum | solution.py:115
  270.3 1.6 fusion.53
  272.6 1.1 broadcast_multiply_fusion
  273.7 0.1 slice_multiply_fusion.2
  273.8 1.2 fusion.32
  275.0 1.1 fusion.69
  276.1 0.7 pad_maximum_fusion.1
  276.9 23.5 %all-reduce.5.cloned.1.call-done = bf16[256,512]{0,1:T(8,128)(2,1)} async-done(((bf16[256,512]{0,1:T(8,128)(2,1)}), bf16[256,512]{0,1:T(8,128)(2,1)}) %all-reduce.5.cloned.1.call-update) | async-done | bytes 262160 | tf_op jit(solution)/shard_map/psum | solution.py:122
  300.3 1.0 convert_element_type.23
  301.3 0.1 slice_multiply_fusion
  301.4 1.9 fusion.31
  (23 shorter events, 0.4 us)
Async XLA Ops:
  6.5 205.5 %copy-start = (f32[12]{0:T(128)S(1)}, f32[12]{0:T(128)}, u32[]{:S(2)}) copy-start(f32[12]{0:T(128)} %param.6) | copy-start | bytes 148
  6.5 51.9 %all-gather.5.cloned.1.call-start = ((), (), s32[]{:S(2)}) async-start(), calls=%async_computation | async-start | bytes 3481600 | tf_op jit(solution)/shard_map/all_gather | solution.py:91
  7.3 120.6 %all-gather.7.cloned.1.call-start = ((), (), s32[]{:S(2)}) async-start(), calls=%async_computation.1 | async-start | bytes 7372800 | tf_op jit(solution)/shard_map/all_gather | solution.py:98
  64.5 137.9 %all-gather.9.cloned.1.call-start = ((), (), s32[]{:S(2)}) async-start(), calls=%async_computation.2 | async-start | bytes 7372800 | tf_op jit(solution)/shard_map/all_gather | solution.py:108
  127.9 3.9 %copy-start.2 = (bf16[12,400,512]{2,1,0:T(8,128)(2,1)S(1)}, bf16[12,400,512]{2,1,0:T(8,128)(2,1)}, u32[]{:S(2)}) copy-start(bf16[12,400,512]{2,1,0:T(8,128)(2,1)} %all-gather.7.cloned.1.call-done) | copy-start | bytes 14745604
  131.7 5.7 %copy-start.3 = (bf16[1,200,512]{2,1,0:T(8,128)(2,1)S(1)}, bf16[1,200,512]{2,1,0:T(8,128)(2,1)}, u32[]{:S(2)}) copy-start(bf16[1,200,512]{2,1,0:T(8,128)(2,1)} %param.5) | copy-start | bytes 614404
  137.3 8.6 %copy-start.1 = (bf16[12,200,512]{2,1,0:T(8,128)(2,1)S(1)}, bf16[12,200,512]{2,1,0:T(8,128)(2,1)}, u32[]{:S(2)}) copy-start(bf16[12,200,512]{2,1,0:T(8,128)(2,1)} %fusion.17) | copy-start | bytes 7372804
  137.3 133.0 %all-reduce.3.cloned.1.call-start = ((), (), s32[]{:S(2)}) async-start(), calls=%async_computation.3 | async-start | bytes 1048576 | tf_op jit(solution)/shard_map/psum | solution.py:115
  212.0 25.9 %copy-start.4 = (f32[400,256]{1,0:T(8,128)S(1)}, f32[400,256]{1,0:T(8,128)}, u32[]{:S(2)}) copy-start(f32[400,256]{1,0:T(8,128)} %get-tuple-element.15) | copy-start | bytes 1228804
  212.0 25.9 %copy-start.5 = (f32[400,256]{1,0:T(8,128)S(1)}, f32[400,256]{1,0:T(8,128)}, u32[]{:S(2)}) copy-start(f32[400,256]{1,0:T(8,128)} %get-tuple-element.16) | copy-start | bytes 1228804
  241.5 58.8 %all-reduce.5.cloned.1.call-start = ((), (), s32[]{:S(2)}) async-start(), calls=%async_computation.4 | async-start | bytes 524288 | tf_op jit(solution)/shard_map/psum | solution.py:122
Sparse Core Ops, SparseCore 0:
  9.6 48.7 all-gather.4
  64.6 63.2 all-gather.6
  137.5 64.8 all-gather.8
  241.6 28.6 all-reduce.2
  277.0 23.2 all-reduce.4
where the time goes:
time: 310 us
  waiting for transfers between devices  221 us (71%)
  matrix products  51 us (16%)
  between operations  14.8 us (5%)
  other arithmetic  11 us (4%)
  blocking collectives  7.45 us (2%)
  local copies, waits for them, and re-layouts  4.03 us (1%)
    all_gather x1, waiting for transfers between devices, on_device(): lax.all_gather(nearby, 'band', axis=1, tiled=True)  62.7 us
    all_gather x1, waiting for transfers between devices, on_device(): projected_whole = lax.all_gather(projected, 'band', axis=1, tiled=True)  54.9 us
    all_gather x1, waiting for transfers between devices, on_device(): portion = lax.all_gather(subspace, 'kpt', axis=0, tiled=True)  50.8 us
    psum x1, waiting for transfers between devices, on_device(): gram_sum = lax.psum(gram_parts(iterate, half_cols), 'band')  28.5 us
    dot_general x1, matrix products, assemble(): jnp.einsum('b,brs->rs', weights, products, precision=lax.Precision.HIGHEST)  25.8 us
    psum x1, waiting for transfers between devices, on_device(): lax.psum(gram_parts(iterate, half_cols).astype(jnp.bfloat16), 'band')  23.5 us
    dot_general x1, matrix products, assemble(): jnp.einsum('brc,bsc->brs', left_rows, whole, preferred_element_type=jnp.f...  9.65 us
    all_gather x1, blocking collectives, on_device(): lax.all_gather(own_block, 'band', axis=0, tiled=True)  7.45 us
  transfers between devices with their start and end apart: 5, of which 5 were waited for; matrix products, arithmetic and copies ran while one was open for 1% of the time, Pallas kernels for 0%

commit v1 on v0

v1 whole, which is shorter than its diff:
```python
import functools
import math

import jax
import jax.numpy as jnp
from jax import lax
from jax.experimental import pallas as pl
from jax.experimental.pallas import tpu as pltpu
from jax.sharding import PartitionSpec as P

SHELL_VECTORS = (
    (1, 1, 0),
    (1, -1, 0),
    (-1, 1, 0),
    (-1, -1, 0),
    (1, 0, 1),
    (1, 0, -1),
    (-1, 0, 1),
    (-1, 0, -1),
    (0, 1, 1),
    (0, 1, -1),
    (0, -1, 1),
    (0, -1, -1),
)
BATCH = 4
VMEM = pl.BlockSpec(memory_space=pltpu.VMEM)
SMEM = pl.BlockSpec(memory_space=pltpu.SMEM)
F32 = jnp.float32
BF16 = jnp.bfloat16
NT = (((1,), (1,)), ((), ()))
TN = (((0,), (0,)), ((), ()))


def grid_shape(point_count):
    size_y = min(4, point_count // 8)
    return (4, size_y, point_count // (4 * size_y))


def displacement(shell, point_count):
    return tuple(step % size for step, size in zip(shell, grid_shape(point_count)))


def fetch_pairs(shift, point_count):
    size_x, size_y, size_z = grid_shape(point_count)
    pairs = []
    for x in range(size_x):
        for y in range(size_y):
            for z in range(size_z):
                source = ((x + shift[0]) % size_x, (y + shift[1]) % size_y, (z + shift[2]) % size_z)
                pairs.append(
                    (
                        (source[0] * size_y + source[1]) * size_z + source[2],
                        (x * size_y + y) * size_z + z,
                    )
                )
    return pairs


def dot(left, right, dims=None):
    if dims is None:
        return jnp.dot(left, right, preferred_element_type=F32)
    return lax.dot_general(left, right, dims, preferred_element_type=F32)


def split(value):
    high = value.astype(BF16)
    return high, (value - high.astype(F32)).astype(BF16)


def dot_exact_right(left, right, dims=None):
    high, low = split(left)
    return dot(high, right, dims) + dot(low, right, dims)


def dot_split(left, right, dims=None):
    left_high, left_low = split(left)
    right_high, right_low = split(right)
    return (
        dot(left_high, right_high, dims)
        + dot(left_high, right_low, dims)
        + dot(left_low, right_high, dims)
    )


def times_minus_i(value):
    half = value.shape[-1] // 2
    return jnp.concatenate([value[:, half:], -value[:, :half]], axis=1)


def times_i(value):
    half = value.shape[-1] // 2
    return jnp.concatenate([-value[:, half:], value[:, :half]], axis=1)


def stack_halves(mine, other, side, rows_ref):
    rows = mine.shape[0]
    rows_ref[pl.ds(pl.multiple_of(side * rows, 8), rows), :] = mine[...].astype(F32)
    rows_ref[pl.ds(pl.multiple_of((1 - side) * rows, 8), rows), :] = other[...].astype(F32)


def project_kernel(
    groups, first, has_total, place_ref, root_ref, margins_ref, *refs
):
    halves = refs[: 2 * len(groups)]
    refs = refs[2 * len(groups) :]
    if has_total:
        before_ref, *refs = refs
    keep_ref, send_ref, total_ref, rows_ref, stacked_ref, blocks_ref = refs
    side, limit = place_ref[0], place_ref[1]
    rows = margins_ref.shape[2]
    full = 2 * rows
    mask = lax.broadcasted_iota(jnp.int32, (rows, 1), 0) < limit
    real = jnp.zeros((rows, rows), F32)
    imag = jnp.zeros((rows, rows), F32)
    if has_total:
        real, imag = before_ref[0], before_ref[1]
    for number, members in enumerate(groups):
        stack_halves(halves[2 * number], halves[2 * number + 1], side, rows_ref)
        whole = rows_ref[...]
        stacked_ref[:full, :] = whole.astype(BF16)
        stacked_ref[full:, :] = times_i(whole).astype(BF16)
        for member in members:
            product = dot(margins_ref[0, member], stacked_ref[...])
            block = jnp.where(mask, product * root_ref[first + member], 0.0).astype(BF16)
            blocks_ref[member] = block
            real += dot(block, block, NT)
            imag += dot(times_minus_i(block), block, NT)
    for pair in range(BATCH // 2):
        keep_ref[pair] = blocks_ref[2 * pair + side]
        send_ref[pair] = blocks_ref[2 * pair + 1 - side]
    total_ref[0] = real
    total_ref[1] = imag


def project(place, roots, margins, batch, groups, halves, before):
    rows, double = margins.shape[2:]
    width = halves[0].shape[-1]
    pairs = BATCH // 2
    has_total = before is not None
    operands = [place, roots, margins, *halves] + ([before] if has_total else [])
    in_specs = [
        SMEM,
        SMEM,
        pl.BlockSpec((1, BATCH, rows, double), lambda step: (0, batch, 0, 0)),
        *([VMEM] * (len(operands) - 3)),
    ]
    block = jax.ShapeDtypeStruct((pairs, rows, width), BF16)
    return pl.pallas_call(
        functools.partial(project_kernel, groups, batch * BATCH, has_total),
        grid=(1,),
        in_specs=in_specs,
        out_specs=[VMEM] * 3,
        out_shape=[block, block, jax.ShapeDtypeStruct((2, rows, rows), F32)],
        scratch_shapes=[
            pltpu.VMEM((2 * rows, width), F32),
            pltpu.VMEM((2 * double // 2, width), BF16),
            pltpu.VMEM((BATCH, rows, width), BF16),
        ],
        cost_estimate=pl.CostEstimate(
            flops=2 * BATCH * rows * double * width * 2,
            bytes_accessed=2 * BATCH * rows * double,
            transcendentals=0,
        ),
        name=f"project_{batch}",
    )(*operands)


def cross_kernel(count, final, *refs):
    keeps, gots = refs[:count], refs[count : 2 * count]
    mine_ref, theirs_ref = refs[2 * count :]
    rows = keeps[0].shape[1]
    sums = [jnp.zeros((rows, rows), F32) for _ in range(4)]
    for keep_ref, got_ref in zip(keeps, gots):
        for pair in range(keep_ref.shape[0]):
            keep, got = keep_ref[pair], got_ref[pair]
            sums[0] += dot(keep, got, NT)
            sums[1] += dot(times_minus_i(keep), got, NT)
            sums[2] += dot(got, keep, NT)
            sums[3] += dot(times_minus_i(got), keep, NT)
    mine_ref[0], mine_ref[1] = sums[0], sums[1]
    theirs_ref[0], theirs_ref[1] = sums[2].astype(BF16), sums[3].astype(BF16)


def cross(keeps, gots):
    pairs, rows, width = keeps[0].shape
    count = len(keeps)
    return pl.pallas_call(
        functools.partial(cross_kernel, count, True),
        in_specs=[VMEM] * (2 * count),
        out_specs=[VMEM] * 2,
        out_shape=[
            jax.ShapeDtypeStruct((2, rows, rows), F32),
            jax.ShapeDtypeStruct((2, rows, rows), BF16),
        ],
        cost_estimate=pl.CostEstimate(
            flops=8 * 2 * count * pairs * rows * rows * width,
            bytes_accessed=4 * count * pairs * rows * width,
            transcendentals=0,
        ),
        name="cross",
    )(*keeps, *gots)


def complex_stack(value):
    return jnp.concatenate([value, times_i(value)], axis=0)


def update_kernel(
    scale, own_ref, other_ref, own_total_ref, other_total_ref, mine_ref, theirs_ref, out_ref
):
    own, other = own_ref[...], other_ref[...]
    half = own.shape[1] // 2
    own_i, other_i = times_i(own.astype(F32)).astype(BF16), times_i(other.astype(F32)).astype(BF16)
    cross_real = mine_ref[0] + theirs_ref[0].astype(F32)
    cross_imag = mine_ref[1] + theirs_ref[1].astype(F32)
    product = (
        dot_exact_right(own_total_ref[0], own)
        + dot_exact_right(own_total_ref[1], own_i)
        + dot_exact_right(cross_real, other)
        + dot_exact_right(cross_imag, other_i)
    )
    product_other = (
        dot(other_total_ref[0], other)
        + dot(other_total_ref[1], other_i)
        + dot_exact_right(cross_real, own, TN)
        - dot_exact_right(cross_imag, own_i, TN)
    )
    blocks = dot_split(product, product, TN) + dot_split(product_other, product_other, TN)
    real = blocks[:half, :half] + blocks[half:, half:]
    imag = blocks[:half, half:] - blocks[half:, :half]
    diagonal = lax.broadcasted_iota(jnp.int32, (half, 2 * half), 0) == lax.broadcasted_iota(
        jnp.int32, (half, 2 * half), 1
    )
    gram = jnp.concatenate([real, imag], axis=1)
    squares = jnp.sum(jnp.where(diagonal, gram, 0.0))
    size = jnp.full((1, 1), 2.0 * squares / half + 1e-06, F32)
    scaling = lax.rsqrt(size)
    gram = gram * (scaling * scaling)
    identity = jnp.where(diagonal, 1.0, 0.0)
    gram_two = dot_split(gram, complex_stack(gram))
    left = 2.25 * identity - 1.5 * gram + 0.25 * gram_two
    right = 1.5 * gram - 0.5 * gram_two
    factor = 2.25 * identity - 0.75 * gram - 0.5 * dot_split(left, complex_stack(right))
    factor = factor * (scaling * scale)
    out_ref[0] = dot_split(product, complex_stack(factor))


def update(scale, own, other, own_total, other_total, mine, theirs):
    rows, width = own.shape
    return pl.pallas_call(
        functools.partial(update_kernel, scale),
        in_specs=[VMEM] * 6,
        out_specs=VMEM,
        out_shape=jax.ShapeDtypeStruct((1, rows, width), F32),
        name="update",
    )(own, other, own_total, other_total, mine, theirs)


def on_device(margins, subspace, shell_weights, window_count):
    point_count = lax.axis_size("kpt")
    side = lax.axis_index("band")
    rows = subspace.shape[1]
    own = subspace[0]
    swap = [(0, 1), (1, 0)]
    place = jnp.stack([side, window_count[0] - side * rows])
    roots = jnp.sqrt(shell_weights)
    other = lax.ppermute(own, "band", swap)
    total = None
    keeps, gots = [], []
    plan = []
    for batch in reversed(range(len(SHELL_VECTORS) // BATCH)):
        shifts = {}
        for member in range(BATCH):
            shift = displacement(SHELL_VECTORS[batch * BATCH + member], point_count)
            shifts.setdefault(shift, []).append(member)
        plan.append((batch, shifts))
    fetched = [
        [lax.ppermute(own, "kpt", fetch_pairs(shift, point_count)) for shift in shifts]
        for _, shifts in plan
    ]
    for (batch, shifts), firsts in zip(plan, fetched):
        halves = []
        for shift, first in zip(shifts, firsts):
            halves += [first, lax.ppermute(other, "kpt", fetch_pairs(shift, point_count))]
        keep, send, total = project(
            place, roots, margins, batch, list(shifts.values()), halves, total
        )
        keeps.append(keep)
        gots.append(lax.ppermute(send, "band", swap))
    other_total = lax.ppermute(total.astype(BF16), "band", swap)
    mine, theirs = cross(keeps, gots)
    theirs = lax.ppermute(theirs, "band", swap)
    scale = math.sqrt(rows * lax.axis_size("band"))
    return update(scale, own, other, total, other_total, mine, theirs)


def solution(mesh):
    return jax.shard_map(
        on_device,
        mesh=mesh,
        in_specs=(P("kpt", None, "band", None), P("kpt", "band", None), P(), P("kpt")),
        out_specs=P("kpt", "band", None),
        check_vma=False,
    )
```

time: 310 us -> 98.6 us (0.32)
  waiting for transfers between devices: 221 us -> 42.9 us
  matrix products: 51 us -> 0 us
  Pallas kernels: 0 us -> 25.2 us
  starting transfers between devices: 0.39 us -> 23.7 us
  between operations: 14.8 us -> 0.74 us
  other arithmetic: 11 us -> 1.69 us
  blocking collectives: 7.45 us -> 0 us
    all_gather x3 -> x0, waiting for transfers between devices: 168 us -> none  [the longest x1 62.7 us: on_device(): lax.all_gather(nearby, 'band', axis=1, tiled=True)]
    psum x2 -> x0, waiting for transfers between devices: 52 us -> none  [the longest x1 28.5 us: on_device(): gram_sum = lax.psum(gram_parts(iterate, half_cols), 'band')]
    dot_general x9 -> x0, matrix products: 51 us -> none  [the longest x1 25.8 us: assemble(): jnp.einsum('b,brs->rs', weights, products, precision=lax.Precision.HIGHEST)]
    ppermute x0 -> x16, waiting for transfers between devices: none -> 42.9 us  [the longest x3 24.9 us: on_device(): gots.append(lax.ppermute(send, 'band', swap))]
    pallas_call x0 -> x5, Pallas kernels: none -> 25.2 us  [the longest x3 14 us: project(): pl.pallas_call(functools.partial(project_kernel, groups, batch * BATCH, h...]
    ppermute x0 -> x16, starting transfers between devices: none -> 23.7 us  [the longest x5 8.27 us: on_device(): lax.ppermute(other, 'kpt', fetch_pairs(shift, point_count))]
    all_gather x1 -> x0, blocking collectives: 7.45 us -> none  [on_device(): lax.all_gather(own_block, 'band', axis=0, tiled=True)]
    neg x2 -> x0, other arithmetic: 3.85 us -> none  [stack_complex(): lower_half = jnp.concatenate([-imag_part, real_part], axis=-1)]
  transfers between devices with their start and end apart: 5 -> 16, of which waited for: 5 -> 10; matrix products, arithmetic and copies ran while one was open for 1% -> 3% of each run, Pallas kernels for 0% -> 13%
where the time goes in v1:
time: 98.6 us; the launch traced here: 98.3 us
  waiting for transfers between devices  42.9 us (44%)
  Pallas kernels  25.2 us (26%)
  starting transfers between devices  23.7 us (24%)
  local copies, waits for them, and re-layouts  4.08 us (4%)
  other arithmetic  1.69 us (2%)
    ppermute x3, waiting for transfers between devices, on_device(): gots.append(lax.ppermute(send, 'band', swap))  24.9 us
    pallas_call x3, Pallas kernels, project(): pl.pallas_call(functools.partial(project_kernel, groups, batch * BATCH, h...  14 us
    ppermute x5, waiting for transfers between devices, on_device(): lax.ppermute(other, 'kpt', fetch_pairs(shift, point_count))  10.1 us
    ppermute x5, starting transfers between devices, on_device(): lax.ppermute(other, 'kpt', fetch_pairs(shift, point_count))  8.27 us
    ppermute x5, starting transfers between devices, on_device(): lax.ppermute(own, 'kpt', fetch_pairs(shift, point_count))  7.84 us
    pallas_call x1, Pallas kernels, update(): pl.pallas_call(functools.partial(update_kernel, scale), in_specs=[VMEM] *...  7.34 us
    ppermute x1, waiting for transfers between devices, on_device(): theirs = lax.ppermute(theirs, 'band', swap)  5.45 us
    pallas_call x1, Pallas kernels, cross(): pl.pallas_call(functools.partial(cross_kernel, count, True), in_specs=[VM...  3.82 us
  transfers between devices with their start and end apart: 16, of which 10 were waited for; matrix products, arithmetic and copies ran while one was open for 3% of the time, Pallas kernels for 13%

profile of v1, /device:TPU:0, one launch (start us, length us, event | category | flops | bytes accessed | tf_op | source)
XLA Modules:
  0.0 98.3 jit_solution(16578354937408728800)
XLA Ops:
  0.0 3.0 %collective-permute-start = (bf16[200,512]{1,0:T(8,128)(2,1)}, bf16[200,512]{1,0:T(8,128)(2,1)S(1)}, u32[]{:S(2)}, u32[]{:S(2)}) collective-permute-start(bf16[200,512]{1,0:T(8,128)(2,1)} %bitcast.5), channel_id=1, source_target_pairs={{0,1},{1,0},{2,3},{3,2},{4,5},{5,4},{6,7},{7,6},{8,9},{9,8},{10,11... | collective-permute-start | bytes 614408 | tf_op jit(solution)/shard_map/ppermute | solution.py:267
  3.0 0.7 collective-permute-start.9
  3.6 2.1 %collective-permute-start.7 = (bf16[200,512]{1,0:T(8,128)(2,1)}, bf16[200,512]{1,0:T(8,128)(2,1)S(1)}, u32[]{:S(2)}, u32[]{:S(2)}) collective-permute-start(bf16[200,512]{1,0:T(8,128)(2,1)} %bitcast.7), channel_id=1, source_target_pairs={{26,0},{24,2},{30,4},{28,6},{2,8},{0,10},{6,12},{4,14},{10,16},{8,... | collective-permute-start | bytes 614408 | tf_op jit(solution)/shard_map/ppermute | solution.py:278
  5.8 2.0 %collective-permute-start.5 = (bf16[200,512]{1,0:T(8,128)(2,1)}, bf16[200,512]{1,0:T(8,128)(2,1)S(1)}, u32[]{:S(2)}, u32[]{:S(2)}) collective-permute-start(bf16[200,512]{1,0:T(8,128)(2,1)} %bitcast.8), channel_id=1, source_target_pairs={{10,0},{8,2},{14,4},{12,6},{18,8},{16,10},{22,12},{20,14},{26,16},... | collective-permute-start | bytes 614408 | tf_op jit(solution)/shard_map/ppermute | solution.py:278
  8.6 2.7 %collective-permute-start.8 = (bf16[200,512]{1,0:T(8,128)(2,1)S(1)}, bf16[200,512]{1,0:T(8,128)(2,1)S(1)}, u32[]{:S(2)}, u32[]{:S(2)}) collective-permute-start(bf16[200,512]{1,0:T(8,128)(2,1)S(1)} %collective-permute-done.other_ref), channel_id=1, source_target_pairs={{26,0},{24,2},{30,4},{28,6},{2,8},{0,10},{6,12},{4,14},{10,16},{8,... | collective-permute-start | bytes 614408 | tf_op jit(solution)/shard_map/ppermute | solution.py:284
  11.9 1.2 %sqrt.3.root_ref = f32[12]{0:T(128)} sqrt(f32[12]{0:T(128)} %param.6) | non-fusion elementwise | bytes 96 | tf_op jit(solution)/shard_map/sqrt | solution.py:266
  13.2 2.0 %collective-permute-start.6 = (bf16[200,512]{1,0:T(8,128)(2,1)S(1)}, bf16[200,512]{1,0:T(8,128)(2,1)S(1)}, u32[]{:S(2)}, u32[]{:S(2)}) collective-permute-start(bf16[200,512]{1,0:T(8,128)(2,1)S(1)} %collective-permute-done.other_ref), channel_id=1, source_target_pairs={{10,0},{8,2},{14,4},{12,6},{18,8},{16,10},{22,12},{20,14},{26,16},... | collective-permute-start | bytes 614408 | tf_op jit(solution)/shard_map/ppermute | solution.py:284
  15.2 0.7 pad_add_fusion.place_ref
  15.9 1.7 %collective-permute-done.5.refs_0_ = bf16[200,512]{1,0:T(8,128)(2,1)S(1)} collective-permute-done((bf16[200,512]{1,0:T(8,128)(2,1)}, bf16[200,512]{1,0:T(8,128)(2,1)S(1)}, u32[]{:S(2)}, u32[]{:S(2)}) %collective-permute-start.5) | collective-permute-done | bytes 204832 | tf_op jit(solution)/shard_map/ppermute | solution.py:278
  17.6 3.0 %collective-permute-start.1 = (bf16[200,512]{1,0:T(8,128)(2,1)}, bf16[200,512]{1,0:T(8,128)(2,1)S(1)}, u32[]{:S(2)}, u32[]{:S(2)}) collective-permute-start(bf16[200,512]{1,0:T(8,128)(2,1)} %bitcast.10), channel_id=1, source_target_pairs={{12,0},{14,2},{8,4},{10,6},{20,8},{22,10},{16,12},{18,14},{28,16},... | collective-permute-start | bytes 614408 | tf_op jit(solution)/shard_map/ppermute | solution.py:278
  20.6 1.5 %collective-permute-done.8.refs_3_ = bf16[200,512]{1,0:T(8,128)(2,1)S(1)} collective-permute-done((bf16[200,512]{1,0:T(8,128)(2,1)S(1)}, bf16[200,512]{1,0:T(8,128)(2,1)S(1)}, u32[]{:S(2)}, u32[]{:S(2)}) %collective-permute-start.8) | collective-permute-done | bytes 204832 | tf_op jit(solution)/shard_map/ppermute | solution.py:284
  22.1 3.2 %collective-permute-start.2 = (bf16[200,512]{1,0:T(8,128)(2,1)S(1)}, bf16[200,512]{1,0:T(8,128)(2,1)S(1)}, u32[]{:S(2)}, u32[]{:S(2)}) collective-permute-start(bf16[200,512]{1,0:T(8,128)(2,1)S(1)} %collective-permute-done.other_ref), channel_id=1, source_target_pairs={{12,0},{14,2},{8,4},{10,6},{20,8},{22,10},{16,12},{18,14},{28,16},... | collective-permute-start | bytes 614408 | tf_op jit(solution)/shard_map/ppermute | solution.py:284
  25.4 4.3 %project_2.1 = (bf16[2,200,512]{2,1,0:T(8,128)(2,1)}, bf16[2,200,512]{2,1,0:T(8,128)(2,1)}, f32[2,200,200]{2,1,0:T(8,128)}) custom-call(s32[2]{0:T(128)} %pad_add_fusion.place_ref, f32[12]{0:T(128)} %sqrt.3.root_ref, bf16[1,12,200,800]{3,2,1,0:T(8,128)(2,1)} %margins_ref.5, bf16[200,512]{1,0:T(8,128)(2,1)} %copy-done.16, bf16[200,512]{1,0:T(8,128)(2,1)} %copy-done.17), custom_call_target="tpu_custom_call" | custom-call | flops 1310720000 | bytes 1280000 | tf_op jit(solution)/shard_map/project_2/pallas_call | solution.py:148
  29.7 0.7 copy-done.6
  30.4 4.8 %project_1.1 = (bf16[2,200,512]{2,1,0:T(8,128)(2,1)}, bf16[2,200,512]{2,1,0:T(8,128)(2,1)}, f32[2,200,200]{2,1,0:T(8,128)}) custom-call(s32[2]{0:T(128)} %pad_add_fusion.place_ref, f32[12]{0:T(128)} %sqrt.3.root_ref, bf16[1,12,200,800]{3,2,1,0:T(8,128)(2,1)} %margins_ref.5, bf16[200,512]{1,0:T(8,128)(2,1)} %copy-done.2, bf16[200,512]{1,0:T(8,128)(2,1)} %copy-done.6, ...), custom_call_target="tpu_custom_call" | custom-call | flops 1310720000 | bytes 1280000 | tf_op jit(solution)/shard_map/project_1/pallas_call | solution.py:148
  35.5 5.3 %collective-permute-done.4.refs_3_ = bf16[200,512]{1,0:T(8,128)(2,1)S(1)} collective-permute-done((bf16[200,512]{1,0:T(8,128)(2,1)S(1)}, bf16[200,512]{1,0:T(8,128)(2,1)S(1)}, u32[]{:S(2)}, u32[]{:S(2)}) %collective-permute-start.4) | collective-permute-done | bytes 204832 | tf_op jit(solution)/shard_map/ppermute | solution.py:284
  40.8 3.3 %collective-permute-done.2.refs_1_ = bf16[200,512]{1,0:T(8,128)(2,1)S(1)} collective-permute-done((bf16[200,512]{1,0:T(8,128)(2,1)S(1)}, bf16[200,512]{1,0:T(8,128)(2,1)S(1)}, u32[]{:S(2)}, u32[]{:S(2)}) %collective-permute-start.2) | collective-permute-done | bytes 204832 | tf_op jit(solution)/shard_map/ppermute | solution.py:284
  44.1 0.7 copy-done.9
  44.8 4.8 %project_0.1 = (bf16[2,200,512]{2,1,0:T(8,128)(2,1)}, bf16[2,200,512]{2,1,0:T(8,128)(2,1)}, f32[2,200,200]{2,1,0:T(8,128)}) custom-call(s32[2]{0:T(128)} %pad_add_fusion.place_ref, f32[12]{0:T(128)} %sqrt.3.root_ref, bf16[1,12,200,800]{3,2,1,0:T(8,128)(2,1)} %margins_ref.5, bf16[200,512]{1,0:T(8,128)(2,1)} %copy-done.5, bf16[200,512]{1,0:T(8,128)(2,1)} %copy-done.9, ...), custom_call_target="tpu_custom_call" | custom-call | flops 1310720000 | bytes 1280000 | tf_op jit(solution)/shard_map/project_0/pallas_call | solution.py:148
  49.6 0.5 collective-permute-start.14
  50.1 1.5 %collective-permute-start.13 = (bf16[2,200,512]{2,1,0:T(8,128)(2,1)S(1)}, bf16[2,200,512]{2,1,0:T(8,128)(2,1)S(1)}, u32[]{:S(2)}, u32[]{:S(2)}) collective-permute-start(bf16[2,200,512]{2,1,0:T(8,128)(2,1)S(1)} %copy-done.12), channel_id=1, source_target_pairs={{0,1},{1,0},{2,3},{3,2},{4,5},{5,4},{6,7},{7,6},{8,9},{9,8},{10,11... | collective-permute-start | bytes 1228808 | tf_op jit(solution)/shard_map/ppermute | solution.py:289
  52.1 1.0 %convert_element_type.3 = bf16[2,200,200]{2,1,0:T(8,128)(2,1)S(1)} convert(f32[2,200,200]{2,1,0:T(8,128)} %get-tuple-element.18.own_total_ref) | non-fusion elementwise | flops 80000 | bytes 480000 | tf_op jit(solution)/shard_map/convert_element_type | solution.py:290
  53.1 1.6 %collective-permute-start.11 = (bf16[2,200,200]{2,1,0:T(8,128)(2,1)S(1)}, bf16[2,200,200]{2,1,0:T(8,128)(2,1)S(1)}, u32[]{:S(2)}, u32[]{:S(2)}) collective-permute-start(bf16[2,200,200]{2,1,0:T(8,128)(2,1)S(1)} %convert_element_type.3), channel_id=1, source_target_pairs={{0,1},{1,0},{2,3},{3,2},{4,5},{5,4},{6,7},{7,6},{8,9},{9,8},{10,11... | collective-permute-start | bytes 480008 | tf_op jit(solution)/shard_map/ppermute | solution.py:290
  54.7 7.4 %collective-permute-done.14.refs_5_ = bf16[2,200,512]{2,1,0:T(8,128)(2,1)S(1)} collective-permute-done((bf16[2,200,512]{2,1,0:T(8,128)(2,1)}, bf16[2,200,512]{2,1,0:T(8,128)(2,1)S(1)}, u32[]{:S(2)}, u32[]{:S(2)}) %collective-permute-start.14) | collective-permute-done | bytes 409632 | tf_op jit(solution)/shard_map/ppermute | solution.py:289
  62.1 8.8 %collective-permute-done.13.refs_4_ = bf16[2,200,512]{2,1,0:T(8,128)(2,1)S(1)} collective-permute-done((bf16[2,200,512]{2,1,0:T(8,128)(2,1)S(1)}, bf16[2,200,512]{2,1,0:T(8,128)(2,1)S(1)}, u32[]{:S(2)}, u32[]{:S(2)}) %collective-permute-start.13) | collective-permute-done | bytes 409632 | tf_op jit(solution)/shard_map/ppermute | solution.py:289
  70.9 8.8 %collective-permute-done.12.refs_3_ = bf16[2,200,512]{2,1,0:T(8,128)(2,1)S(1)} collective-permute-done((bf16[2,200,512]{2,1,0:T(8,128)(2,1)S(1)}, bf16[2,200,512]{2,1,0:T(8,128)(2,1)S(1)}, u32[]{:S(2)}, u32[]{:S(2)}) %collective-permute-start.12) | collective-permute-done | bytes 409632 | tf_op jit(solution)/shard_map/ppermute | solution.py:289
  79.7 0.7 copy-done.15
  80.4 3.8 %cross.1 = (f32[2,200,200]{2,1,0:T(8,128)}, bf16[2,200,200]{2,1,0:T(8,128)(2,1)}) custom-call(bf16[2,200,512]{2,1,0:T(8,128)(2,1)} %get-tuple-element.19.refs_0_, bf16[2,200,512]{2,1,0:T(8,128)(2,1)} %get-tuple-element.20.refs_1_, bf16[2,200,512]{2,1,0:T(8,128)(2,1)} %get-tuple-element.21.refs_2_, bf16[2,200,512]{2,1,0:T(8,128)(2,1)} %copy-done.15, ...), custom_call_target="tpu_custom_call" | custom-call | flops 1966080000 | bytes 2457600 | tf_op jit(solution)/shard_map/cross/pallas_call | solution.py:187
  84.3 0.5 collective-permute-start.15
  84.8 5.5 %collective-permute-done.15.theirs_ref = bf16[2,200,200]{2,1,0:T(8,128)(2,1)S(1)} collective-permute-done((bf16[2,200,200]{2,1,0:T(8,128)(2,1)}, bf16[2,200,200]{2,1,0:T(8,128)(2,1)S(1)}, u32[]{:S(2)}, u32[]{:S(2)}) %collective-permute-start.15) | collective-permute-done | bytes 160032 | tf_op jit(solution)/shard_map/ppermute | solution.py:292
  90.2 0.7 copy-done.10
  90.9 7.3 %update.1 = f32[1,200,512]{2,1,0:T(8,128)} custom-call(bf16[200,512]{1,0:T(8,128)(2,1)} %bitcast.11, bf16[200,512]{1,0:T(8,128)(2,1)} %copy-done, f32[2,200,200]{2,1,0:T(8,128)} %get-tuple-element.18.own_total_ref, bf16[2,200,200]{2,1,0:T(8,128)(2,1)} %copy-done.8, f32[2,200,200]{2,1,0:T(8,128)} %get-tuple-element.25.mine_ref, bf16[2,200,200]{2,1,0:T(8,128)(2,1)} %copy-done.10), custom_call_target="tpu_custom_call" | custom-call | tf_op jit(solution)/shard_map/update/pallas_call | solution.py:250
  (44 shorter events, 1.6 us)
Async XLA Ops:
  0.0 8.3 %collective-permute-start = (bf16[200,512]{1,0:T(8,128)(2,1)}, bf16[200,512]{1,0:T(8,128)(2,1)S(1)}, u32[]{:S(2)}, u32[]{:S(2)}) collective-permute-start(bf16[200,512]{1,0:T(8,128)(2,1)} %bitcast.5), channel_id=1, source_target_pairs={{0,1},{1,0},{2,3},{3,2},{4,5},{5,4},{6,7},{7,6},{8,9},{9,8},{10,11... | collective-permute-start | bytes 614408 | tf_op jit(solution)/shard_map/ppermute | solution.py:267
  3.0 10.2 %collective-permute-start.9 = (bf16[200,512]{1,0:T(8,128)(2,1)}, bf16[200,512]{1,0:T(8,128)(2,1)S(1)}, u32[]{:S(2)}, u32[]{:S(2)}) collective-permute-start(bf16[200,512]{1,0:T(8,128)(2,1)} %bitcast.6), channel_id=1, source_target_pairs={{6,0},{4,2},{2,4},{0,6},{14,8},{12,10},{10,12},{8,14},{22,16},{20,... | collective-permute-start | bytes 614408 | tf_op jit(solution)/shard_map/ppermute | solution.py:278
  3.6 12.2 %collective-permute-start.7 = (bf16[200,512]{1,0:T(8,128)(2,1)}, bf16[200,512]{1,0:T(8,128)(2,1)S(1)}, u32[]{:S(2)}, u32[]{:S(2)}) collective-permute-start(bf16[200,512]{1,0:T(8,128)(2,1)} %bitcast.7), channel_id=1, source_target_pairs={{26,0},{24,2},{30,4},{28,6},{2,8},{0,10},{6,12},{4,14},{10,16},{8,... | collective-permute-start | bytes 614408 | tf_op jit(solution)/shard_map/ppermute | solution.py:278
  5.8 11.8 %collective-permute-start.5 = (bf16[200,512]{1,0:T(8,128)(2,1)}, bf16[200,512]{1,0:T(8,128)(2,1)S(1)}, u32[]{:S(2)}, u32[]{:S(2)}) collective-permute-start(bf16[200,512]{1,0:T(8,128)(2,1)} %bitcast.8), channel_id=1, source_target_pairs={{10,0},{8,2},{14,4},{12,6},{18,8},{16,10},{22,12},{20,14},{26,16},... | collective-permute-start | bytes 614408 | tf_op jit(solution)/shard_map/ppermute | solution.py:278
  8.3 27.0 %copy-start = (bf16[200,512]{1,0:T(8,128)(2,1)}, bf16[200,512]{1,0:T(8,128)(2,1)S(1)}, u32[]{:S(2)}) copy-start(bf16[200,512]{1,0:T(8,128)(2,1)S(1)} %collective-permute-done.other_ref) | copy-start | bytes 614404
  8.3 12.3 %collective-permute-start.10 = (bf16[200,512]{1,0:T(8,128)(2,1)S(1)}, bf16[200,512]{1,0:T(8,128)(2,1)S(1)}, u32[]{:S(2)}, u32[]{:S(2)}) collective-permute-start(bf16[200,512]{1,0:T(8,128)(2,1)S(1)} %collective-permute-done.other_ref), channel_id=1, source_target_pairs={{6,0},{4,2},{2,4},{0,6},{14,8},{12,10},{10,12},{8,14},{22,16},{20,... | collective-permute-start | bytes 614408 | tf_op jit(solution)/shard_map/ppermute | solution.py:284
  8.6 13.5 %collective-permute-start.8 = (bf16[200,512]{1,0:T(8,128)(2,1)S(1)}, bf16[200,512]{1,0:T(8,128)(2,1)S(1)}, u32[]{:S(2)}, u32[]{:S(2)}) collective-permute-start(bf16[200,512]{1,0:T(8,128)(2,1)S(1)} %collective-permute-done.other_ref), channel_id=1, source_target_pairs={{26,0},{24,2},{30,4},{28,6},{2,8},{0,10},{6,12},{4,14},{10,16},{8,... | collective-permute-start | bytes 614408 | tf_op jit(solution)/shard_map/ppermute | solution.py:284
  13.2 12.2 %copy-start.16 = (bf16[200,512]{1,0:T(8,128)(2,1)}, bf16[200,512]{1,0:T(8,128)(2,1)S(1)}, u32[]{:S(2)}) copy-start(bf16[200,512]{1,0:T(8,128)(2,1)S(1)} %collective-permute-done.9.refs_0_) | copy-start | bytes 614404
  13.2 16.5 %collective-permute-start.6 = (bf16[200,512]{1,0:T(8,128)(2,1)S(1)}, bf16[200,512]{1,0:T(8,128)(2,1)S(1)}, u32[]{:S(2)}, u32[]{:S(2)}) collective-permute-start(bf16[200,512]{1,0:T(8,128)(2,1)S(1)} %collective-permute-done.other_ref), channel_id=1, source_target_pairs={{10,0},{8,2},{14,4},{12,6},{18,8},{16,10},{22,12},{20,14},{26,16},... | collective-permute-start | bytes 614408 | tf_op jit(solution)/shard_map/ppermute | solution.py:284
  15.9 13.8 %copy-start.1 = (bf16[200,512]{1,0:T(8,128)(2,1)}, bf16[200,512]{1,0:T(8,128)(2,1)S(1)}, u32[]{:S(2)}) copy-start(bf16[200,512]{1,0:T(8,128)(2,1)S(1)} %collective-permute-done.7.refs_2_) | copy-start | bytes 614404
  15.9 19.4 %collective-permute-start.3 = (bf16[200,512]{1,0:T(8,128)(2,1)}, bf16[200,512]{1,0:T(8,128)(2,1)S(1)}, u32[]{:S(2)}, u32[]{:S(2)}) collective-permute-start(bf16[200,512]{1,0:T(8,128)(2,1)} %bitcast.9), channel_id=1, source_target_pairs={{28,0},{30,2},{24,4},{26,6},{4,8},{6,10},{0,12},{2,14},{12,16},{14... | collective-permute-start | bytes 614408 | tf_op jit(solution)/shard_map/ppermute | solution.py:278
  17.6 12.1 %copy-start.2 = (bf16[200,512]{1,0:T(8,128)(2,1)}, bf16[200,512]{1,0:T(8,128)(2,1)S(1)}, u32[]{:S(2)}) copy-start(bf16[200,512]{1,0:T(8,128)(2,1)S(1)} %collective-permute-done.5.refs_0_) | copy-start | bytes 614404
  17.6 17.9 %collective-permute-start.1 = (bf16[200,512]{1,0:T(8,128)(2,1)}, bf16[200,512]{1,0:T(8,128)(2,1)S(1)}, u32[]{:S(2)}, u32[]{:S(2)}) collective-permute-start(bf16[200,512]{1,0:T(8,128)(2,1)} %bitcast.10), channel_id=1, source_target_pairs={{12,0},{14,2},{8,4},{10,6},{20,8},{22,10},{16,12},{18,14},{28,16},... | collective-permute-start | bytes 614408 | tf_op jit(solution)/shard_map/ppermute | solution.py:278
  20.6 4.7 %copy-start.17 = (bf16[200,512]{1,0:T(8,128)(2,1)}, bf16[200,512]{1,0:T(8,128)(2,1)S(1)}, u32[]{:S(2)}) copy-start(bf16[200,512]{1,0:T(8,128)(2,1)S(1)} %collective-permute-done.10.refs_1_) | copy-start | bytes 614404
  20.6 20.2 %collective-permute-start.4 = (bf16[200,512]{1,0:T(8,128)(2,1)S(1)}, bf16[200,512]{1,0:T(8,128)(2,1)S(1)}, u32[]{:S(2)}, u32[]{:S(2)}) collective-permute-start(bf16[200,512]{1,0:T(8,128)(2,1)S(1)} %collective-permute-done.other_ref), channel_id=1, source_target_pairs={{28,0},{30,2},{24,4},{26,6},{4,8},{6,10},{0,12},{2,14},{12,16},{14... | collective-permute-start | bytes 614408 | tf_op jit(solution)/shard_map/ppermute | solution.py:284
  22.1 7.6 %copy-start.3 = (bf16[200,512]{1,0:T(8,128)(2,1)}, bf16[200,512]{1,0:T(8,128)(2,1)S(1)}, u32[]{:S(2)}) copy-start(bf16[200,512]{1,0:T(8,128)(2,1)S(1)} %collective-permute-done.8.refs_3_) | copy-start | bytes 614404
  22.1 21.9 %collective-permute-start.2 = (bf16[200,512]{1,0:T(8,128)(2,1)S(1)}, bf16[200,512]{1,0:T(8,128)(2,1)S(1)}, u32[]{:S(2)}, u32[]{:S(2)}) collective-permute-start(bf16[200,512]{1,0:T(8,128)(2,1)S(1)} %collective-permute-done.other_ref), channel_id=1, source_target_pairs={{12,0},{14,2},{8,4},{10,6},{20,8},{22,10},{16,12},{18,14},{28,16},... | collective-permute-start | bytes 614408 | tf_op jit(solution)/shard_map/ppermute | solution.py:284
  29.7 0.7 copy-start.6
  30.4 21.2 %copy-start.11 = (bf16[2,200,512]{2,1,0:T(8,128)(2,1)S(1)}, bf16[2,200,512]{2,1,0:T(8,128)(2,1)}, u32[]{:S(2)}) copy-start(bf16[2,200,512]{2,1,0:T(8,128)(2,1)} %get-tuple-element.22) | copy-start | bytes 1228804
  35.2 14.8 %copy-start.12 = (bf16[2,200,512]{2,1,0:T(8,128)(2,1)S(1)}, bf16[2,200,512]{2,1,0:T(8,128)(2,1)}, u32[]{:S(2)}) copy-start(bf16[2,200,512]{2,1,0:T(8,128)(2,1)} %get-tuple-element.23) | copy-start | bytes 1228804
  35.3 8.8 %copy-start.4 = (bf16[200,512]{1,0:T(8,128)(2,1)}, bf16[200,512]{1,0:T(8,128)(2,1)S(1)}, u32[]{:S(2)}) copy-start(bf16[200,512]{1,0:T(8,128)(2,1)S(1)} %collective-permute-done.3.refs_2_) | copy-start | bytes 614404
  35.5 8.6 %copy-start.5 = (bf16[200,512]{1,0:T(8,128)(2,1)}, bf16[200,512]{1,0:T(8,128)(2,1)S(1)}, u32[]{:S(2)}) copy-start(bf16[200,512]{1,0:T(8,128)(2,1)S(1)} %collective-permute-done.1.refs_0_) | copy-start | bytes 614404
  40.8 3.3 %copy-start.7 = (bf16[200,512]{1,0:T(8,128)(2,1)}, bf16[200,512]{1,0:T(8,128)(2,1)S(1)}, u32[]{:S(2)}) copy-start(bf16[200,512]{1,0:T(8,128)(2,1)S(1)} %collective-permute-done.4.refs_3_) | copy-start | bytes 614404
  49.6 12.5 %collective-permute-start.14 = (bf16[2,200,512]{2,1,0:T(8,128)(2,1)}, bf16[2,200,512]{2,1,0:T(8,128)(2,1)S(1)}, u32[]{:S(2)}, u32[]{:S(2)}) collective-permute-start(bf16[2,200,512]{2,1,0:T(8,128)(2,1)} %get-tuple-element.24), channel_id=1, source_target_pairs={{0,1},{1,0},{2,3},{3,2},{4,5},{5,4},{6,7},{7,6},{8,9},{9,8},{10,11... | collective-permute-start | bytes 1228808 | tf_op jit(solution)/shard_map/ppermute | solution.py:289
  50.1 20.8 %collective-permute-start.13 = (bf16[2,200,512]{2,1,0:T(8,128)(2,1)S(1)}, bf16[2,200,512]{2,1,0:T(8,128)(2,1)S(1)}, u32[]{:S(2)}, u32[]{:S(2)}) collective-permute-start(bf16[2,200,512]{2,1,0:T(8,128)(2,1)S(1)} %copy-done.12), channel_id=1, source_target_pairs={{0,1},{1,0},{2,3},{3,2},{4,5},{5,4},{6,7},{7,6},{8,9},{9,8},{10,11... | collective-permute-start | bytes 1228808 | tf_op jit(solution)/shard_map/ppermute | solution.py:289
  51.6 28.1 %collective-permute-start.12 = (bf16[2,200,512]{2,1,0:T(8,128)(2,1)S(1)}, bf16[2,200,512]{2,1,0:T(8,128)(2,1)S(1)}, u32[]{:S(2)}, u32[]{:S(2)}) collective-permute-start(bf16[2,200,512]{2,1,0:T(8,128)(2,1)S(1)} %copy-done.11), channel_id=1, source_target_pairs={{0,1},{1,0},{2,3},{3,2},{4,5},{5,4},{6,7},{7,6},{8,9},{9,8},{10,11... | collective-permute-start | bytes 1228808 | tf_op jit(solution)/shard_map/ppermute | solution.py:289
  53.1 31.6 %collective-permute-start.11 = (bf16[2,200,200]{2,1,0:T(8,128)(2,1)S(1)}, bf16[2,200,200]{2,1,0:T(8,128)(2,1)S(1)}, u32[]{:S(2)}, u32[]{:S(2)}) collective-permute-start(bf16[2,200,200]{2,1,0:T(8,128)(2,1)S(1)} %convert_element_type.3), channel_id=1, source_target_pairs={{0,1},{1,0},{2,3},{3,2},{4,5},{5,4},{6,7},{7,6},{8,9},{9,8},{10,11... | collective-permute-start | bytes 480008 | tf_op jit(solution)/shard_map/ppermute | solution.py:290
  62.1 17.6 %copy-start.13 = (bf16[2,200,512]{2,1,0:T(8,128)(2,1)}, bf16[2,200,512]{2,1,0:T(8,128)(2,1)S(1)}, u32[]{:S(2)}) copy-start(bf16[2,200,512]{2,1,0:T(8,128)(2,1)S(1)} %collective-permute-done.14.refs_5_) | copy-start | bytes 1228804
  70.9 8.8 %copy-start.14 = (bf16[2,200,512]{2,1,0:T(8,128)(2,1)}, bf16[2,200,512]{2,1,0:T(8,128)(2,1)S(1)}, u32[]{:S(2)}) copy-start(bf16[2,200,512]{2,1,0:T(8,128)(2,1)S(1)} %collective-permute-done.13.refs_4_) | copy-start | bytes 1228804
  79.7 0.8 copy-start.15
  84.3 6.0 %collective-permute-start.15 = (bf16[2,200,200]{2,1,0:T(8,128)(2,1)}, bf16[2,200,200]{2,1,0:T(8,128)(2,1)S(1)}, u32[]{:S(2)}, u32[]{:S(2)}) collective-permute-start(bf16[2,200,200]{2,1,0:T(8,128)(2,1)} %get-tuple-element.26), channel_id=1, source_target_pairs={{0,1},{1,0},{2,3},{3,2},{4,5},{5,4},{6,7},{7,6},{8,9},{9,8},{10,11... | collective-permute-start | bytes 480008 | tf_op jit(solution)/shard_map/ppermute | solution.py:292
  84.8 5.5 %copy-start.8 = (bf16[2,200,200]{2,1,0:T(8,128)(2,1)}, bf16[2,200,200]{2,1,0:T(8,128)(2,1)S(1)}, u32[]{:S(2)}) copy-start(bf16[2,200,200]{2,1,0:T(8,128)(2,1)S(1)} %collective-permute-done.11.other_total_ref) | copy-start | bytes 480004
  (2 other events, 1.4 us)

commit v2 on v1

--- a/solution.py
+++ b/solution.py
@@ -7,6 +7,7 @@
 from jax.experimental import pallas as pl
 from jax.experimental.pallas import tpu as pltpu
 from jax.sharding import PartitionSpec as P
+
 
 SHELL_VECTORS = (
     (1, 1, 0),
@@ -98,22 +99,13 @@
     rows_ref[pl.ds(pl.multiple_of((1 - side) * rows, 8), rows), :] = other[...].astype(F32)
 
 
-def project_kernel(
-    groups, first, has_total, place_ref, root_ref, margins_ref, *refs
-):
+def project_kernel(groups, first, place_ref, root_ref, margins_ref, *refs):
     halves = refs[: 2 * len(groups)]
-    refs = refs[2 * len(groups) :]
-    if has_total:
-        before_ref, *refs = refs
-    keep_ref, send_ref, total_ref, rows_ref, stacked_ref, blocks_ref = refs
+    keep_ref, send_ref, rows_ref, stacked_ref, blocks_ref = refs[2 * len(groups) :]
     side, limit = place_ref[0], place_ref[1]
     rows = margins_ref.shape[2]
     full = 2 * rows
     mask = lax.broadcasted_iota(jnp.int32, (rows, 1), 0) < limit
-    real = jnp.zeros((rows, rows), F32)
-    imag = jnp.zeros((rows, rows), F32)
-    if has_total:
-        real, imag = before_ref[0], before_ref[1]
     for number, members in enumerate(groups):
         stack_halves(halves[2 * number], halves[2 * number + 1], side, rows_ref)
         whole = rows_ref[...]
@@ -121,84 +113,113 @@
         stacked_ref[full:, :] = times_i(whole).astype(BF16)
         for member in members:
             product = dot(margins_ref[0, member], stacked_ref[...])
-            block = jnp.where(mask, product * root_ref[first + member], 0.0).astype(BF16)
-            blocks_ref[member] = block
-            real += dot(block, block, NT)
-            imag += dot(times_minus_i(block), block, NT)
+            block = jnp.where(mask, product * root_ref[first + member], 0.0)
+            blocks_ref[member] = block.astype(BF16)
     for pair in range(BATCH // 2):
         keep_ref[pair] = blocks_ref[2 * pair + side]
         send_ref[pair] = blocks_ref[2 * pair + 1 - side]
-    total_ref[0] = real
-    total_ref[1] = imag
-
-
-def project(place, roots, margins, batch, groups, halves, before):
+
+
+def project(place, roots, margins, batch, groups, halves):
     rows, double = margins.shape[2:]
     width = halves[0].shape[-1]
     pairs = BATCH // 2
-    has_total = before is not None
-    operands = [place, roots, margins, *halves] + ([before] if has_total else [])
-    in_specs = [
-        SMEM,
-        SMEM,
-        pl.BlockSpec((1, BATCH, rows, double), lambda step: (0, batch, 0, 0)),
-        *([VMEM] * (len(operands) - 3)),
-    ]
     block = jax.ShapeDtypeStruct((pairs, rows, width), BF16)
     return pl.pallas_call(
-        functools.partial(project_kernel, groups, batch * BATCH, has_total),
+        functools.partial(project_kernel, groups, batch * BATCH),
         grid=(1,),
-        in_specs=in_specs,
-        out_specs=[VMEM] * 3,
-        out_shape=[block, block, jax.ShapeDtypeStruct((2, rows, rows), F32)],
+        in_specs=[
+            SMEM,
+            SMEM,
+            pl.BlockSpec((1, BATCH, rows, double), lambda step: (0, batch, 0, 0)),
+            *([VMEM] * len(halves)),
+        ],
+        out_specs=[VMEM] * 2,
+        out_shape=[block, block],
         scratch_shapes=[
             pltpu.VMEM((2 * rows, width), F32),
-            pltpu.VMEM((2 * double // 2, width), BF16),
+            pltpu.VMEM((double, width), BF16),
             pltpu.VMEM((BATCH, rows, width), BF16),
         ],
         cost_estimate=pl.CostEstimate(
-            flops=2 * BATCH * rows * double * width * 2,
+            flops=2 * BATCH * rows * double * width,
             bytes_accessed=2 * BATCH * rows * double,
             transcendentals=0,
         ),
-        name=f"project_{batch}",
+    )(place, roots, margins, *halves)
+
+
+def gather_own_kernel(count, has_total, *refs):
+    blocks, refs = refs[:count], refs[count:]
+    rows = blocks[0].shape[1]
+    real = jnp.zeros((rows, rows), F32)
+    imag = jnp.zeros((rows, rows), F32)
+    if has_total:
+        real, imag = refs[0][0], refs[0][1]
+    for block_ref in blocks:
+        for pair in range(block_ref.shape[0]):
+            block = block_ref[pair]
+            real += dot(block, block, NT)
+            imag += dot(times_minus_i(block), block, NT)
+    for total_ref in refs[1 if has_total else 0 :]:
+        total_ref[0] = real.astype(total_ref.dtype)
+        total_ref[1] = imag.astype(total_ref.dtype)
+
+
+def gather_own(blocks, before):
+    pairs, rows, width = blocks[0].shape
+    count = len(blocks)
+    operands = list(blocks) + ([] if before is None else [before])
+    kinds = [F32] if before is None else [F32, BF16]
+    return pl.pallas_call(
+        functools.partial(gather_own_kernel, count, before is not None),
+        in_specs=[VMEM] * len(operands),
+        out_specs=[VMEM] * len(kinds),
+        out_shape=[jax.ShapeDtypeStruct((2, rows, rows), kind) for kind in kinds],
+        cost_estimate=pl.CostEstimate(
+            flops=4 * count * pairs * rows * rows * width,
+            bytes_accessed=2 * count * pairs * rows * width,
+            transcendentals=0,
+        ),
     )(*operands)
 
 
-def cross_kernel(count, final, *refs):
-    keeps, gots = refs[:count], refs[count : 2 * count]
-    mine_ref, theirs_ref = refs[2 * count :]
-    rows = keeps[0].shape[1]
+def cross_kernel(has_total, keep_ref, got_ref, *refs):
+    if has_total:
+        mine_before_ref, theirs_before_ref, *refs = refs
+    mine_ref, theirs_ref = refs
+    rows = keep_ref.shape[1]
     sums = [jnp.zeros((rows, rows), F32) for _ in range(4)]
-    for keep_ref, got_ref in zip(keeps, gots):
-        for pair in range(keep_ref.shape[0]):
-            keep, got = keep_ref[pair], got_ref[pair]
-            sums[0] += dot(keep, got, NT)
-            sums[1] += dot(times_minus_i(keep), got, NT)
-            sums[2] += dot(got, keep, NT)
-            sums[3] += dot(times_minus_i(got), keep, NT)
+    if has_total:
+        sums = [mine_before_ref[0], mine_before_ref[1], theirs_before_ref[0], theirs_before_ref[1]]
+    for pair in range(keep_ref.shape[0]):
+        keep, got = keep_ref[pair], got_ref[pair]
+        sums[0] += dot(keep, got, NT)
+        sums[1] += dot(times_minus_i(keep), got, NT)
+        sums[2] += dot(got, keep, NT)
+        sums[3] += dot(times_minus_i(got), keep, NT)
     mine_ref[0], mine_ref[1] = sums[0], sums[1]
-    theirs_ref[0], theirs_ref[1] = sums[2].astype(BF16), sums[3].astype(BF16)
-
-
-def cross(keeps, gots):
-    pairs, rows, width = keeps[0].shape
-    count = len(keeps)
+    kind = theirs_ref.dtype
+    theirs_ref[0], theirs_ref[1] = sums[2].astype(kind), sums[3].astype(kind)
+
+
+def cross(keep, got, before, last):
+    pairs, rows, width = keep.shape
+    operands = [keep, got, *(before or ())]
     return pl.pallas_call(
-        functools.partial(cross_kernel, count, True),
-        in_specs=[VMEM] * (2 * count),
+        functools.partial(cross_kernel, before is not None),
+        in_specs=[VMEM] * len(operands),
         out_specs=[VMEM] * 2,
         out_shape=[
             jax.ShapeDtypeStruct((2, rows, rows), F32),
-            jax.ShapeDtypeStruct((2, rows, rows), BF16),
+            jax.ShapeDtypeStruct((2, rows, rows), BF16 if last else F32),
         ],
         cost_estimate=pl.CostEstimate(
-            flops=8 * 2 * count * pairs * rows * rows * width,
-            bytes_accessed=4 * count * pairs * rows * width,
+            flops=8 * 2 * pairs * rows * rows * width,
+            bytes_accessed=4 * pairs * rows * width,
             transcendentals=0,
         ),
-        name="cross",
-    )(*keeps, *gots)
+    )(*operands)
 
 
 def complex_stack(value):
@@ -256,40 +277,57 @@
     )(own, other, own_total, other_total, mine, theirs)
 
 
+def batch_shifts(batch, point_count):
+    shifts = {}
+    for member in range(BATCH):
+        shift = displacement(SHELL_VECTORS[batch * BATCH + member], point_count)
+        shifts.setdefault(shift, []).append(member)
+    return shifts
+
+
 def on_device(margins, subspace, shell_weights, window_count):
     point_count = lax.axis_size("kpt")
     side = lax.axis_index("band")
     rows = subspace.shape[1]
-    own = subspace[0]
     swap = [(0, 1), (1, 0)]
+    plan = [batch_shifts(batch, point_count) for batch in range(3)]
+
+    def exchange(value):
+        return lax.ppermute(value, "band", swap)
+
+    def fetch(value, shift):
+        return lax.ppermute(value, "kpt", fetch_pairs(shift, point_count))
+
     place = jnp.stack([side, window_count[0] - side * rows])
     roots = jnp.sqrt(shell_weights)
-    other = lax.ppermute(own, "band", swap)
-    total = None
-    keeps, gots = [], []
-    plan = []
-    for batch in reversed(range(len(SHELL_VECTORS) // BATCH)):
-        shifts = {}
-        for member in range(BATCH):
-            shift = displacement(SHELL_VECTORS[batch * BATCH + member], point_count)
-            shifts.setdefault(shift, []).append(member)
-        plan.append((batch, shifts))
-    fetched = [
-        [lax.ppermute(own, "kpt", fetch_pairs(shift, point_count)) for shift in shifts]
-        for _, shifts in plan
-    ]
-    for (batch, shifts), firsts in zip(plan, fetched):
-        halves = []
-        for shift, first in zip(shifts, firsts):
-            halves += [first, lax.ppermute(other, "kpt", fetch_pairs(shift, point_count))]
-        keep, send, total = project(
-            place, roots, margins, batch, list(shifts.values()), halves, total
+    own = subspace[0]
+    other = exchange(own)
+    halves = {}
+    for part, value in (("own", own), ("other", other)):
+        for batch in (2, 1):
+            for shift in plan[batch]:
+                halves[batch, part, shift] = fetch(value, shift)
+        for shift in plan[0]:
+            near = displacement((shift[0], 0, 1), point_count)
+            step = displacement((0, shift[1], -1), point_count)
+            halves[0, part, shift] = fetch(halves[1, part, near], step)
+    kept, given, got = {}, {}, {}
+    total, crossed = None, None
+    for batch in (2, 1, 0):
+        blocks = []
+        for shift in plan[batch]:
+            blocks += [halves[batch, "own", shift], halves[batch, "other", shift]]
+        kept[batch], given[batch] = project(
+            place, roots, margins, batch, list(plan[batch].values()), blocks
         )
-        keeps.append(keep)
-        gots.append(lax.ppermute(send, "band", swap))
-    other_total = lax.ppermute(total.astype(BF16), "band", swap)
-    mine, theirs = cross(keeps, gots)
-    theirs = lax.ppermute(theirs, "band", swap)
+        got[batch] = exchange(given[batch])
+    (total,) = gather_own([kept[2], given[2], kept[1], given[1]], None)
+    total, total_sent = gather_own([kept[0], given[0]], total)
+    other_total = exchange(total_sent)
+    for batch in (2, 1, 0):
+        crossed = cross(kept[batch], got[batch], crossed, batch == 0)
+    mine, theirs = crossed
+    theirs = exchange(theirs)
     scale = math.sqrt(rows * lax.axis_size("band"))
     return update(scale, own, other, total, other_total, mine, theirs)
 

time: 98.6 us -> 79.7 us (0.81)
  waiting for transfers between devices: 42.9 us -> 19.5 us
  Pallas kernels: 25.2 us -> 32.2 us
  starting transfers between devices: 23.7 us -> 19.9 us
  local copies, waits for them, and re-layouts: 4.08 us -> 6.32 us
  other arithmetic: 1.69 us -> 0.66 us
    ppermute x16, waiting for transfers between devices: 42.9 us -> 19.5 us  [the longest x6 10.3 us: exchange(): return lax.ppermute(value, 'band', swap)]
    pallas_call x4 -> x8, Pallas kernels: 17.8 us -> 24.9 us  [the longest x3 11 us: project(): pl.pallas_call(functools.partial(project_kernel, groups, batch * BATCH),...]
    ppermute x16, starting transfers between devices: 23.7 us -> 19.9 us  [the longest x10 12.2 us: fetch(): return lax.ppermute(value, 'kpt', fetch_pairs(shift, point_count))]
    unnamed x36 -> x32, local copies, waits for them, and re-layouts: 2.84 us -> 5.08 us
    convert_element_type x1 -> x0, other arithmetic: 1.02 us -> none  [on_device(): other_total = lax.ppermute(total.astype(BF16), 'band', swap)]
  transfers between devices with their start and end apart: 16 -> 16, of which waited for: 10 -> 6; matrix products, arithmetic and copies ran while one was open for 3% -> 2% of each run, Pallas kernels for 13% -> 31%
where the time goes in v2:
time: 79.7 us; the launch traced here: 79.3 us
  Pallas kernels  32.2 us (40%)
  starting transfers between devices  19.9 us (25%)
  waiting for transfers between devices  19.5 us (24%)
  local copies, waits for them, and re-layouts  6.32 us (8%)
    ppermute x10, starting transfers between devices, fetch(): return lax.ppermute(value, 'kpt', fetch_pairs(shift, point_count))  12.2 us
    pallas_call x3, Pallas kernels, project(): pl.pallas_call(functools.partial(project_kernel, groups, batch * BATCH),...  11 us
    ppermute x6, waiting for transfers between devices, exchange(): return lax.ppermute(value, 'band', swap)  10.3 us
    ppermute x10, waiting for transfers between devices, fetch(): return lax.ppermute(value, 'kpt', fetch_pairs(shift, point_count))  9.19 us
    pallas_call x3, Pallas kernels, cross(): pl.pallas_call(functools.partial(cross_kernel, before is not None), in_sp...  8.04 us
    ppermute x6, starting transfers between devices, exchange(): return lax.ppermute(value, 'band', swap)  7.63 us
    pallas_call x1, Pallas kernels, update(): pl.pallas_call(functools.partial(update_kernel, scale), in_specs=[VMEM] *...  7.34 us
    pallas_call x2, Pallas kernels, gather_own(): pl.pallas_call(functools.partial(gather_own_kernel, count, before is not...  5.9 us
  transfers between devices with their start and end apart: 16, of which 6 were waited for; matrix products, arithmetic and copies ran while one was open for 2% of the time, Pallas kernels for 31%

profile of v2, /device:TPU:0, one launch (start us, length us, event | category | flops | bytes accessed | tf_op | source)
XLA Modules:
  0.0 79.3 jit_solution(834990895203156305)
XLA Ops:
  0.0 3.0 %collective-permute-start = (bf16[200,512]{1,0:T(8,128)(2,1)}, bf16[200,512]{1,0:T(8,128)(2,1)S(1)}, u32[]{:S(2)}, u32[]{:S(2)}) collective-permute-start(bf16[200,512]{1,0:T(8,128)(2,1)} %bitcast.5), channel_id=1, source_target_pairs={{0,1},{1,0},{2,3},{3,2},{4,5},{5,4},{6,7},{7,6},{8,9},{9,8},{10,11... | collective-permute-start | bytes 614408 | tf_op jit(solution)/shard_map/ppermute | solution.py:296
  3.6 2.1 %collective-permute-start.5 = (bf16[200,512]{1,0:T(8,128)(2,1)}, bf16[200,512]{1,0:T(8,128)(2,1)S(1)}, u32[]{:S(2)}, u32[]{:S(2)}) collective-permute-start(bf16[200,512]{1,0:T(8,128)(2,1)} %bitcast.7), channel_id=1, source_target_pairs={{26,0},{24,2},{30,4},{28,6},{2,8},{0,10},{6,12},{4,14},{10,16},{8,... | collective-permute-start | bytes 614408 | tf_op jit(solution)/shard_map/ppermute | solution.py:299
  5.8 2.0 %collective-permute-start.1 = (bf16[200,512]{1,0:T(8,128)(2,1)}, bf16[200,512]{1,0:T(8,128)(2,1)S(1)}, u32[]{:S(2)}, u32[]{:S(2)}) collective-permute-start(bf16[200,512]{1,0:T(8,128)(2,1)} %bitcast.8), channel_id=1, source_target_pairs={{10,0},{8,2},{14,4},{12,6},{18,8},{16,10},{22,12},{20,14},{26,16},... | collective-permute-start | bytes 614408 | tf_op jit(solution)/shard_map/ppermute | solution.py:299
  8.7 3.2 %collective-permute-start.3 = (bf16[200,512]{1,0:T(8,128)(2,1)S(1)}, bf16[200,512]{1,0:T(8,128)(2,1)S(1)}, u32[]{:S(2)}, u32[]{:S(2)}) collective-permute-start(bf16[200,512]{1,0:T(8,128)(2,1)S(1)} %collective-permute-done.other_ref), channel_id=1, source_target_pairs={{10,0},{8,2},{14,4},{12,6},{18,8},{16,10},{22,12},{20,14},{26,16},... | collective-permute-start | bytes 614408 | tf_op jit(solution)/shard_map/ppermute | solution.py:299
  11.8 1.5 %collective-permute-start.10 = (bf16[200,512]{1,0:T(8,128)(2,1)S(1)}, bf16[200,512]{1,0:T(8,128)(2,1)S(1)}, u32[]{:S(2)}, u32[]{:S(2)}) collective-permute-start(bf16[200,512]{1,0:T(8,128)(2,1)S(1)} %collective-permute-done.other_ref), channel_id=1, source_target_pairs={{6,0},{4,2},{2,4},{0,6},{14,8},{12,10},{10,12},{8,14},{22,16},{20,... | collective-permute-start | bytes 614408 | tf_op jit(solution)/shard_map/ppermute | solution.py:299
  14.0 1.2 %sqrt.3.root_ref = f32[12]{0:T(128)} sqrt(f32[12]{0:T(128)} %param.6) | non-fusion elementwise | bytes 96 | tf_op jit(solution)/shard_map/sqrt | solution.py:302
  15.5 2.1 %collective-permute-done.1.refs_0_ = bf16[200,512]{1,0:T(8,128)(2,1)S(1)} collective-permute-done((bf16[200,512]{1,0:T(8,128)(2,1)}, bf16[200,512]{1,0:T(8,128)(2,1)S(1)}, u32[]{:S(2)}, u32[]{:S(2)}) %collective-permute-start.1) | collective-permute-done | bytes 204832 | tf_op jit(solution)/shard_map/ppermute | solution.py:299
  17.6 0.9 %collective-permute-start.2 = (bf16[200,512]{1,0:T(8,128)(2,1)S(1)}, bf16[200,512]{1,0:T(8,128)(2,1)S(1)}, u32[]{:S(2)}, u32[]{:S(2)}) collective-permute-start(bf16[200,512]{1,0:T(8,128)(2,1)S(1)} %collective-permute-done.1.refs_0_), channel_id=1, source_target_pairs={{6,0},{4,2},{2,4},{0,6},{14,8},{12,10},{10,12},{8,14},{22,16},{20,... | collective-permute-start | bytes 614408 | tf_op jit(solution)/shard_map/ppermute | solution.py:299
  18.5 3.7 %collective-permute-done.7.refs_3_ = bf16[200,512]{1,0:T(8,128)(2,1)S(1)} collective-permute-done((bf16[200,512]{1,0:T(8,128)(2,1)S(1)}, bf16[200,512]{1,0:T(8,128)(2,1)S(1)}, u32[]{:S(2)}, u32[]{:S(2)}) %collective-permute-start.7) | collective-permute-done | bytes 204832 | tf_op jit(solution)/shard_map/ppermute | solution.py:299
  22.1 0.9 %collective-permute-start.8 = (bf16[200,512]{1,0:T(8,128)(2,1)S(1)}, bf16[200,512]{1,0:T(8,128)(2,1)S(1)}, u32[]{:S(2)}, u32[]{:S(2)}) collective-permute-start(bf16[200,512]{1,0:T(8,128)(2,1)S(1)} %collective-permute-done.7.refs_3_), channel_id=1, source_target_pairs={{6,0},{4,2},{2,4},{0,6},{14,8},{12,10},{10,12},{8,14},{22,16},{20,... | collective-permute-start | bytes 614408 | tf_op jit(solution)/shard_map/ppermute | solution.py:299
  23.0 3.4 %collective-permute-done.3.refs_1_ = bf16[200,512]{1,0:T(8,128)(2,1)S(1)} collective-permute-done((bf16[200,512]{1,0:T(8,128)(2,1)S(1)}, bf16[200,512]{1,0:T(8,128)(2,1)S(1)}, u32[]{:S(2)}, u32[]{:S(2)}) %collective-permute-start.3) | collective-permute-done | bytes 204832 | tf_op jit(solution)/shard_map/ppermute | solution.py:299
  26.8 0.7 pad_add_fusion.place_ref
  27.5 0.7 copy-done.8
  28.2 3.6 %shard_map.47 = (bf16[2,200,512]{2,1,0:T(8,128)(2,1)}, bf16[2,200,512]{2,1,0:T(8,128)(2,1)}) custom-call(s32[2]{0:T(128)} %pad_add_fusion.place_ref, f32[12]{0:T(128)} %sqrt.3.root_ref, bf16[1,12,200,800]{3,2,1,0:T(8,128)(2,1)} %margins_ref.5, bf16[200,512]{1,0:T(8,128)(2,1)} %copy-done.5, bf16[200,512]{1,0:T(8,128)(2,1)} %copy-done.8), custom_call_target="tpu_custom_call" | custom-call | flops 655360000 | bytes 1280000 | tf_op jit(solution)/shard_map/pallas_call | solution.py:128
  32.2 3.7 %shard_map.48 = (bf16[2,200,512]{2,1,0:T(8,128)(2,1)}, bf16[2,200,512]{2,1,0:T(8,128)(2,1)}) custom-call(s32[2]{0:T(128)} %pad_add_fusion.place_ref, f32[12]{0:T(128)} %sqrt.3.root_ref, bf16[1,12,200,800]{3,2,1,0:T(8,128)(2,1)} %margins_ref.5, bf16[200,512]{1,0:T(8,128)(2,1)} %copy-done.1, bf16[200,512]{1,0:T(8,128)(2,1)} %copy-done.3, ...), custom_call_target="tpu_custom_call" | custom-call | flops 655360000 | bytes 1280000 | tf_op jit(solution)/shard_map/pallas_call | solution.py:128
  36.0 1.6 %collective-permute-start.13 = (bf16[2,200,512]{2,1,0:T(8,128)(2,1)}, bf16[2,200,512]{2,1,0:T(8,128)(2,1)S(1)}, u32[]{:S(2)}, u32[]{:S(2)}) collective-permute-start(bf16[2,200,512]{2,1,0:T(8,128)(2,1)} %get-tuple-element.24.refs_3_), channel_id=1, source_target_pairs={{0,1},{1,0},{2,3},{3,2},{4,5},{5,4},{6,7},{7,6},{8,9},{9,8},{10,11... | collective-permute-start | bytes 1228808 | tf_op jit(solution)/shard_map/ppermute | solution.py:296
  37.6 0.7 copy-done.7
  38.3 0.7 copy-done.11
  39.0 3.7 %shard_map.46 = (bf16[2,200,512]{2,1,0:T(8,128)(2,1)}, bf16[2,200,512]{2,1,0:T(8,128)(2,1)}) custom-call(s32[2]{0:T(128)} %pad_add_fusion.place_ref, f32[12]{0:T(128)} %sqrt.3.root_ref, bf16[1,12,200,800]{3,2,1,0:T(8,128)(2,1)} %margins_ref.5, bf16[200,512]{1,0:T(8,128)(2,1)} %copy-done.7, bf16[200,512]{1,0:T(8,128)(2,1)} %copy-done.11, ...), custom_call_target="tpu_custom_call" | custom-call | flops 655360000 | bytes 1280000 | tf_op jit(solution)/shard_map/pallas_call | solution.py:128
  43.2 3.2 %shard_map.49.refs_2_ = f32[2,200,200]{2,1,0:T(8,128)} custom-call(bf16[2,200,512]{2,1,0:T(8,128)(2,1)} %get-tuple-element.21.refs_0_.keep_ref, bf16[2,200,512]{2,1,0:T(8,128)(2,1)} %get-tuple-element.22.refs_1_, bf16[2,200,512]{2,1,0:T(8,128)(2,1)} %get-tuple-element.23.refs_2_.keep_ref, bf16[2,200,512]{2,1,0:T(8,128)(2,1)} %get-tuple-element.24.refs_3_), custom_call_target="tpu_custom_call" | custom-call | flops 655360000 | bytes 1638400 | tf_op jit(solution)/shard_map/pallas_call | solution.py:174
  46.4 2.7 %shard_map.50 = (f32[2,200,200]{2,1,0:T(8,128)}, bf16[2,200,200]{2,1,0:T(8,128)(2,1)}) custom-call(bf16[2,200,512]{2,1,0:T(8,128)(2,1)} %get-tuple-element.19.refs_0_.keep_ref, bf16[2,200,512]{2,1,0:T(8,128)(2,1)} %get-tuple-element.20.refs_1_, f32[2,200,200]{2,1,0:T(8,128)} %shard_map.49.refs_2_), custom_call_target="tpu_custom_call" | custom-call | flops 327680000 | bytes 819200 | tf_op jit(solution)/shard_map/pallas_call | solution.py:174
  49.1 1.5 %collective-permute-start.11 = (bf16[2,200,200]{2,1,0:T(8,128)(2,1)}, bf16[2,200,200]{2,1,0:T(8,128)(2,1)S(1)}, u32[]{:S(2)}, u32[]{:S(2)}) collective-permute-start(bf16[2,200,200]{2,1,0:T(8,128)(2,1)} %get-tuple-element.26), channel_id=1, source_target_pairs={{0,1},{1,0},{2,3},{3,2},{4,5},{5,4},{6,7},{7,6},{8,9},{9,8},{10,11... | collective-permute-start | bytes 480008 | tf_op jit(solution)/shard_map/ppermute | solution.py:296
  50.6 0.8 copy-done.13
  51.4 2.5 %shard_map.51 = (f32[2,200,200]{2,1,0:T(8,128)}, f32[2,200,200]{2,1,0:T(8,128)}) custom-call(bf16[2,200,512]{2,1,0:T(8,128)(2,1)} %get-tuple-element.21.refs_0_.keep_ref, bf16[2,200,512]{2,1,0:T(8,128)(2,1)} %copy-done.13), custom_call_target="tpu_custom_call" | custom-call | flops 655360000 | bytes 819200 | tf_op jit(solution)/shard_map/pallas_call | solution.py:209
  53.9 0.8 copy-done.14
  54.7 2.8 %shard_map.52 = (f32[2,200,200]{2,1,0:T(8,128)}, f32[2,200,200]{2,1,0:T(8,128)}) custom-call(bf16[2,200,512]{2,1,0:T(8,128)(2,1)} %get-tuple-element.23.refs_2_.keep_ref, bf16[2,200,512]{2,1,0:T(8,128)(2,1)} %copy-done.14, f32[2,200,200]{2,1,0:T(8,128)} %get-tuple-element.27.refs_0_, f32[2,200,200]{2,1,0:T(8,128)} %get-tuple-element.28.refs_1_), custom_call_target="tpu_custom_call" | custom-call | flops 655360000 | bytes 819200 | tf_op jit(solution)/shard_map/pallas_call | solution.py:209
  57.4 4.4 %collective-permute-done.12.got_ref = bf16[2,200,512]{2,1,0:T(8,128)(2,1)S(1)} collective-permute-done((bf16[2,200,512]{2,1,0:T(8,128)(2,1)}, bf16[2,200,512]{2,1,0:T(8,128)(2,1)S(1)}, u32[]{:S(2)}, u32[]{:S(2)}) %collective-permute-start.12) | collective-permute-done | bytes 409632 | tf_op jit(solution)/shard_map/ppermute | solution.py:296
  61.8 0.8 copy-done.15
  62.6 2.7 %shard_map.53 = (f32[2,200,200]{2,1,0:T(8,128)}, bf16[2,200,200]{2,1,0:T(8,128)(2,1)}) custom-call(bf16[2,200,512]{2,1,0:T(8,128)(2,1)} %get-tuple-element.19.refs_0_.keep_ref, bf16[2,200,512]{2,1,0:T(8,128)(2,1)} %copy-done.15, f32[2,200,200]{2,1,0:T(8,128)} %get-tuple-element.29.refs_0_, f32[2,200,200]{2,1,0:T(8,128)} %get-tuple-element.30.refs_1_), custom_call_target="tpu_custom_call" | custom-call | flops 655360000 | bytes 819200 | tf_op jit(solution)/shard_map/pallas_call | solution.py:209
  65.8 5.4 %collective-permute-done.15.theirs_ref = bf16[2,200,200]{2,1,0:T(8,128)(2,1)S(1)} collective-permute-done((bf16[2,200,200]{2,1,0:T(8,128)(2,1)}, bf16[2,200,200]{2,1,0:T(8,128)(2,1)S(1)}, u32[]{:S(2)}, u32[]{:S(2)}) %collective-permute-start.15) | collective-permute-done | bytes 160032 | tf_op jit(solution)/shard_map/ppermute | solution.py:296
  71.3 0.7 copy-done.12
  72.0 7.3 %update.1 = f32[1,200,512]{2,1,0:T(8,128)} custom-call(bf16[200,512]{1,0:T(8,128)(2,1)} %bitcast.9, bf16[200,512]{1,0:T(8,128)(2,1)} %copy-done, f32[2,200,200]{2,1,0:T(8,128)} %get-tuple-element.25.own_total_ref, bf16[2,200,200]{2,1,0:T(8,128)(2,1)} %copy-done.10, f32[2,200,200]{2,1,0:T(8,128)} %get-tuple-element.31.mine_ref, bf16[2,200,200]{2,1,0:T(8,128)(2,1)} %copy-done.12), custom_call_target="tpu_custom_call" | custom-call | tf_op jit(solution)/shard_map/update/pallas_call | solution.py:271
  (43 shorter events, 3.8 us)
Async XLA Ops:
  0.0 8.3 %collective-permute-start = (bf16[200,512]{1,0:T(8,128)(2,1)}, bf16[200,512]{1,0:T(8,128)(2,1)S(1)}, u32[]{:S(2)}, u32[]{:S(2)}) collective-permute-start(bf16[200,512]{1,0:T(8,128)(2,1)} %bitcast.5), channel_id=1, source_target_pairs={{0,1},{1,0},{2,3},{3,2},{4,5},{5,4},{6,7},{7,6},{8,9},{9,8},{10,11... | collective-permute-start | bytes 614408 | tf_op jit(solution)/shard_map/ppermute | solution.py:296
  3.0 8.8 %collective-permute-start.9 = (bf16[200,512]{1,0:T(8,128)(2,1)}, bf16[200,512]{1,0:T(8,128)(2,1)S(1)}, u32[]{:S(2)}, u32[]{:S(2)}) collective-permute-start(bf16[200,512]{1,0:T(8,128)(2,1)} %bitcast.6), channel_id=1, source_target_pairs={{6,0},{4,2},{2,4},{0,6},{14,8},{12,10},{10,12},{8,14},{22,16},{20,... | collective-permute-start | bytes 614408 | tf_op jit(solution)/shard_map/ppermute | solution.py:299
  3.6 11.6 %collective-permute-start.5 = (bf16[200,512]{1,0:T(8,128)(2,1)}, bf16[200,512]{1,0:T(8,128)(2,1)S(1)}, u32[]{:S(2)}, u32[]{:S(2)}) collective-permute-start(bf16[200,512]{1,0:T(8,128)(2,1)} %bitcast.7), channel_id=1, source_target_pairs={{26,0},{24,2},{30,4},{28,6},{2,8},{0,10},{6,12},{4,14},{10,16},{8,... | collective-permute-start | bytes 614408 | tf_op jit(solution)/shard_map/ppermute | solution.py:299
  5.8 11.8 %collective-permute-start.1 = (bf16[200,512]{1,0:T(8,128)(2,1)}, bf16[200,512]{1,0:T(8,128)(2,1)S(1)}, u32[]{:S(2)}, u32[]{:S(2)}) collective-permute-start(bf16[200,512]{1,0:T(8,128)(2,1)} %bitcast.8), channel_id=1, source_target_pairs={{10,0},{8,2},{14,4},{12,6},{18,8},{16,10},{22,12},{20,14},{26,16},... | collective-permute-start | bytes 614408 | tf_op jit(solution)/shard_map/ppermute | solution.py:299
  8.3 27.7 %copy-start = (bf16[200,512]{1,0:T(8,128)(2,1)}, bf16[200,512]{1,0:T(8,128)(2,1)S(1)}, u32[]{:S(2)}) copy-start(bf16[200,512]{1,0:T(8,128)(2,1)S(1)} %collective-permute-done.other_ref) | copy-start | bytes 614404
  8.3 13.8 %collective-permute-start.7 = (bf16[200,512]{1,0:T(8,128)(2,1)S(1)}, bf16[200,512]{1,0:T(8,128)(2,1)S(1)}, u32[]{:S(2)}, u32[]{:S(2)}) collective-permute-start(bf16[200,512]{1,0:T(8,128)(2,1)S(1)} %collective-permute-done.other_ref), channel_id=1, source_target_pairs={{26,0},{24,2},{30,4},{28,6},{2,8},{0,10},{6,12},{4,14},{10,16},{8,... | collective-permute-start | bytes 614408 | tf_op jit(solution)/shard_map/ppermute | solution.py:299
  8.7 17.7 %collective-permute-start.3 = (bf16[200,512]{1,0:T(8,128)(2,1)S(1)}, bf16[200,512]{1,0:T(8,128)(2,1)S(1)}, u32[]{:S(2)}, u32[]{:S(2)}) collective-permute-start(bf16[200,512]{1,0:T(8,128)(2,1)S(1)} %collective-permute-done.other_ref), channel_id=1, source_target_pairs={{10,0},{8,2},{14,4},{12,6},{18,8},{16,10},{22,12},{20,14},{26,16},... | collective-permute-start | bytes 614408 | tf_op jit(solution)/shard_map/ppermute | solution.py:299
  11.8 15.6 %copy-start.5 = (bf16[200,512]{1,0:T(8,128)(2,1)}, bf16[200,512]{1,0:T(8,128)(2,1)S(1)}, u32[]{:S(2)}) copy-start(bf16[200,512]{1,0:T(8,128)(2,1)S(1)} %collective-permute-done.9.refs_0_) | copy-start | bytes 614404
  11.8 15.6 %collective-permute-start.10 = (bf16[200,512]{1,0:T(8,128)(2,1)S(1)}, bf16[200,512]{1,0:T(8,128)(2,1)S(1)}, u32[]{:S(2)}, u32[]{:S(2)}) collective-permute-start(bf16[200,512]{1,0:T(8,128)(2,1)S(1)} %collective-permute-done.other_ref), channel_id=1, source_target_pairs={{6,0},{4,2},{2,4},{0,6},{14,8},{12,10},{10,12},{8,14},{22,16},{20,... | collective-permute-start | bytes 614408 | tf_op jit(solution)/shard_map/ppermute | solution.py:299
  15.2 17.0 %copy-start.4 = (bf16[200,512]{1,0:T(8,128)(2,1)}, bf16[200,512]{1,0:T(8,128)(2,1)S(1)}, u32[]{:S(2)}) copy-start(bf16[200,512]{1,0:T(8,128)(2,1)S(1)} %collective-permute-done.5.refs_2_) | copy-start | bytes 614404
  15.2 20.7 %collective-permute-start.6 = (bf16[200,512]{1,0:T(8,128)(2,1)S(1)}, bf16[200,512]{1,0:T(8,128)(2,1)S(1)}, u32[]{:S(2)}, u32[]{:S(2)}) collective-permute-start(bf16[200,512]{1,0:T(8,128)(2,1)S(1)} %collective-permute-done.5.refs_2_), channel_id=1, source_target_pairs={{6,0},{4,2},{2,4},{0,6},{14,8},{12,10},{10,12},{8,14},{22,16},{20,... | collective-permute-start | bytes 614408 | tf_op jit(solution)/shard_map/ppermute | solution.py:299
  17.6 14.6 %copy-start.1 = (bf16[200,512]{1,0:T(8,128)(2,1)}, bf16[200,512]{1,0:T(8,128)(2,1)S(1)}, u32[]{:S(2)}) copy-start(bf16[200,512]{1,0:T(8,128)(2,1)S(1)} %collective-permute-done.1.refs_0_) | copy-start | bytes 614404
  17.6 19.9 %collective-permute-start.2 = (bf16[200,512]{1,0:T(8,128)(2,1)S(1)}, bf16[200,512]{1,0:T(8,128)(2,1)S(1)}, u32[]{:S(2)}, u32[]{:S(2)}) collective-permute-start(bf16[200,512]{1,0:T(8,128)(2,1)S(1)} %collective-permute-done.1.refs_0_), channel_id=1, source_target_pairs={{6,0},{4,2},{2,4},{0,6},{14,8},{12,10},{10,12},{8,14},{22,16},{20,... | collective-permute-start | bytes 614408 | tf_op jit(solution)/shard_map/ppermute | solution.py:299
  22.1 10.1 %copy-start.2 = (bf16[200,512]{1,0:T(8,128)(2,1)}, bf16[200,512]{1,0:T(8,128)(2,1)S(1)}, u32[]{:S(2)}) copy-start(bf16[200,512]{1,0:T(8,128)(2,1)S(1)} %collective-permute-done.7.refs_3_) | copy-start | bytes 614404
  22.1 15.4 %collective-permute-start.8 = (bf16[200,512]{1,0:T(8,128)(2,1)S(1)}, bf16[200,512]{1,0:T(8,128)(2,1)S(1)}, u32[]{:S(2)}, u32[]{:S(2)}) collective-permute-start(bf16[200,512]{1,0:T(8,128)(2,1)S(1)} %collective-permute-done.7.refs_3_), channel_id=1, source_target_pairs={{6,0},{4,2},{2,4},{0,6},{14,8},{12,10},{10,12},{8,14},{22,16},{20,... | collective-permute-start | bytes 614408 | tf_op jit(solution)/shard_map/ppermute | solution.py:299
  26.4 5.8 %copy-start.3 = (bf16[200,512]{1,0:T(8,128)(2,1)}, bf16[200,512]{1,0:T(8,128)(2,1)S(1)}, u32[]{:S(2)}) copy-start(bf16[200,512]{1,0:T(8,128)(2,1)S(1)} %collective-permute-done.3.refs_1_) | copy-start | bytes 614404
  26.4 11.2 %collective-permute-start.4 = (bf16[200,512]{1,0:T(8,128)(2,1)S(1)}, bf16[200,512]{1,0:T(8,128)(2,1)S(1)}, u32[]{:S(2)}, u32[]{:S(2)}) collective-permute-start(bf16[200,512]{1,0:T(8,128)(2,1)S(1)} %collective-permute-done.3.refs_1_), channel_id=1, source_target_pairs={{6,0},{4,2},{2,4},{0,6},{14,8},{12,10},{10,12},{8,14},{22,16},{20,... | collective-permute-start | bytes 614408 | tf_op jit(solution)/shard_map/ppermute | solution.py:299
  27.5 0.7 copy-start.8
  31.7 18.9 %collective-permute-start.14 = (bf16[2,200,512]{2,1,0:T(8,128)(2,1)}, bf16[2,200,512]{2,1,0:T(8,128)(2,1)S(1)}, u32[]{:S(2)}, u32[]{:S(2)}) collective-permute-start(bf16[2,200,512]{2,1,0:T(8,128)(2,1)} %get-tuple-element.22.refs_1_), channel_id=1, source_target_pairs={{0,1},{1,0},{2,3},{3,2},{4,5},{5,4},{6,7},{7,6},{8,9},{9,8},{10,11... | collective-permute-start | bytes 1228808 | tf_op jit(solution)/shard_map/ppermute | solution.py:296
  35.9 1.6 %copy-start.6 = (bf16[200,512]{1,0:T(8,128)(2,1)}, bf16[200,512]{1,0:T(8,128)(2,1)S(1)}, u32[]{:S(2)}) copy-start(bf16[200,512]{1,0:T(8,128)(2,1)S(1)} %collective-permute-done.6.refs_2_) | copy-start | bytes 614404
  36.0 18.0 %collective-permute-start.13 = (bf16[2,200,512]{2,1,0:T(8,128)(2,1)}, bf16[2,200,512]{2,1,0:T(8,128)(2,1)S(1)}, u32[]{:S(2)}, u32[]{:S(2)}) collective-permute-start(bf16[2,200,512]{2,1,0:T(8,128)(2,1)} %get-tuple-element.24.refs_3_), channel_id=1, source_target_pairs={{0,1},{1,0},{2,3},{3,2},{4,5},{5,4},{6,7},{7,6},{8,9},{9,8},{10,11... | collective-permute-start | bytes 1228808 | tf_op jit(solution)/shard_map/ppermute | solution.py:296
  37.5 0.7 copy-start.7
  37.5 0.8 copy-start.9
  38.3 0.7 copy-start.11
  42.7 19.1 %collective-permute-start.12 = (bf16[2,200,512]{2,1,0:T(8,128)(2,1)}, bf16[2,200,512]{2,1,0:T(8,128)(2,1)S(1)}, u32[]{:S(2)}, u32[]{:S(2)}) collective-permute-start(bf16[2,200,512]{2,1,0:T(8,128)(2,1)} %get-tuple-element.20.refs_1_), channel_id=1, source_target_pairs={{0,1},{1,0},{2,3},{3,2},{4,5},{5,4},{6,7},{7,6},{8,9},{9,8},{10,11... | collective-permute-start | bytes 1228808 | tf_op jit(solution)/shard_map/ppermute | solution.py:296
  49.1 16.7 %collective-permute-start.11 = (bf16[2,200,200]{2,1,0:T(8,128)(2,1)}, bf16[2,200,200]{2,1,0:T(8,128)(2,1)S(1)}, u32[]{:S(2)}, u32[]{:S(2)}) collective-permute-start(bf16[2,200,200]{2,1,0:T(8,128)(2,1)} %get-tuple-element.26), channel_id=1, source_target_pairs={{0,1},{1,0},{2,3},{3,2},{4,5},{5,4},{6,7},{7,6},{8,9},{9,8},{10,11... | collective-permute-start | bytes 480008 | tf_op jit(solution)/shard_map/ppermute | solution.py:296
  50.6 0.8 copy-start.13
  53.9 0.8 copy-start.14
  61.8 0.8 copy-start.15
  65.3 6.0 %collective-permute-start.15 = (bf16[2,200,200]{2,1,0:T(8,128)(2,1)}, bf16[2,200,200]{2,1,0:T(8,128)(2,1)S(1)}, u32[]{:S(2)}, u32[]{:S(2)}) collective-permute-start(bf16[2,200,200]{2,1,0:T(8,128)(2,1)} %get-tuple-element.32), channel_id=1, source_target_pairs={{0,1},{1,0},{2,3},{3,2},{4,5},{5,4},{6,7},{7,6},{8,9},{9,8},{10,11... | collective-permute-start | bytes 480008 | tf_op jit(solution)/shard_map/ppermute | solution.py:296
  65.8 5.5 %copy-start.10 = (bf16[2,200,200]{2,1,0:T(8,128)(2,1)}, bf16[2,200,200]{2,1,0:T(8,128)(2,1)S(1)}, u32[]{:S(2)}) copy-start(bf16[2,200,200]{2,1,0:T(8,128)(2,1)S(1)} %collective-permute-done.11.other_total_ref) | copy-start | bytes 480004
  71.3 0.7 copy-start.12

commit v3 on v2

--- a/solution.py
+++ b/solution.py
@@ -25,6 +25,7 @@
 )
 BATCH = 4
 VMEM = pl.BlockSpec(memory_space=pltpu.VMEM)
+LIMIT = pltpu.CompilerParams(vmem_limit_bytes=20 * 2**20)
 SMEM = pl.BlockSpec(memory_space=pltpu.SMEM)
 F32 = jnp.float32
 BF16 = jnp.bfloat16
@@ -112,7 +113,7 @@
         stacked_ref[:full, :] = whole.astype(BF16)
         stacked_ref[full:, :] = times_i(whole).astype(BF16)
         for member in members:
-            product = dot(margins_ref[0, member], stacked_ref[...])
+            product = dot(margins_ref[0, first + member], stacked_ref[...])
             block = jnp.where(mask, product * root_ref[first + member], 0.0)
             blocks_ref[member] = block.astype(BF16)
     for pair in range(BATCH // 2):
@@ -127,13 +128,7 @@
     block = jax.ShapeDtypeStruct((pairs, rows, width), BF16)
     return pl.pallas_call(
         functools.partial(project_kernel, groups, batch * BATCH),
-        grid=(1,),
-        in_specs=[
-            SMEM,
-            SMEM,
-            pl.BlockSpec((1, BATCH, rows, double), lambda step: (0, batch, 0, 0)),
-            *([VMEM] * len(halves)),
-        ],
+        in_specs=[SMEM, SMEM, VMEM, *([VMEM] * len(halves))],
         out_specs=[VMEM] * 2,
         out_shape=[block, block],
         scratch_shapes=[
@@ -146,6 +141,7 @@
             bytes_accessed=2 * BATCH * rows * double,
             transcendentals=0,
         ),
+        compiler_params=LIMIT,
     )(place, roots, margins, *halves)
 
 
@@ -181,6 +177,7 @@
             bytes_accessed=2 * count * pairs * rows * width,
             transcendentals=0,
         ),
+        compiler_params=LIMIT,
     )(*operands)
 
 
@@ -219,6 +216,7 @@
             bytes_accessed=4 * pairs * rows * width,
             transcendentals=0,
         ),
+        compiler_params=LIMIT,
     )(*operands)
 
 
@@ -274,6 +272,7 @@
         out_specs=VMEM,
         out_shape=jax.ShapeDtypeStruct((1, rows, width), F32),
         name="update",
+        compiler_params=LIMIT,
     )(own, other, own_total, other_total, mine, theirs)
 
 

time: 79.7 us -> 74.8 us (0.939)
  Pallas kernels: 32.2 us -> 14.7 us
  waiting for transfers between devices: 19.5 us -> 36.2 us
  local copies, waits for them, and re-layouts: 6.32 us -> 2.89 us
    ppermute x6, waiting for transfers between devices: 10.3 us -> 25 us  [exchange(): return lax.ppermute(value, 'band', swap)]
    pallas_call x3, Pallas kernels: 8.04 us -> 1.87 us  [cross(): pl.pallas_call(functools.partial(cross_kernel, before is not None), in_sp...]
    pallas_call x3, Pallas kernels: 11 us -> 5.25 us  [project(): pl.pallas_call(functools.partial(project_kernel, groups, batch * BATCH),...]
    pallas_call x2, Pallas kernels: 5.9 us -> 1.68 us  [gather_own(): pl.pallas_call(functools.partial(gather_own_kernel, count, before is not...]
    unnamed x32 -> x4, local copies, waits for them, and re-layouts: 5.08 us -> 2.22 us
    ppermute x10, waiting for transfers between devices: 9.19 us -> 11.2 us  [fetch(): return lax.ppermute(value, 'kpt', fetch_pairs(shift, point_count))]
    pallas_call x1, Pallas kernels: 7.34 us -> 5.86 us  [update(): pl.pallas_call(functools.partial(update_kernel, scale), in_specs=[VMEM] *...]
  transfers between devices with their start and end apart: 16 -> 16, of which waited for: 6 -> 10; matrix products, arithmetic and copies ran while one was open for 2% -> 1% of each run, Pallas kernels for 31% -> 12%
where the time goes in v3:
time: 74.8 us; the launch traced here: 74.7 us
  waiting for transfers between devices  36.2 us (48%)
  starting transfers between devices  20.1 us (27%)
  Pallas kernels  14.7 us (20%)
  local copies, waits for them, and re-layouts  2.89 us (4%)
  between operations  0.75 us (1%)
    ppermute x6, waiting for transfers between devices, exchange(): return lax.ppermute(value, 'band', swap)  25 us
    ppermute x10, starting transfers between devices, fetch(): return lax.ppermute(value, 'kpt', fetch_pairs(shift, point_count))  12.2 us
    ppermute x10, waiting for transfers between devices, fetch(): return lax.ppermute(value, 'kpt', fetch_pairs(shift, point_count))  11.2 us
    ppermute x6, starting transfers between devices, exchange(): return lax.ppermute(value, 'band', swap)  7.88 us
    pallas_call x1, Pallas kernels, update(): pl.pallas_call(functools.partial(update_kernel, scale), in_specs=[VMEM] *...  5.86 us
    pallas_call x3, Pallas kernels, project(): pl.pallas_call(functools.partial(project_kernel, groups, batch * BATCH),...  5.25 us
    unnamed x4, local copies, waits for them, and re-layouts  2.22 us
    pallas_call x3, Pallas kernels, cross(): pl.pallas_call(functools.partial(cross_kernel, before is not None), in_sp...  1.87 us
  transfers between devices with their start and end apart: 16, of which 10 were waited for; matrix products, arithmetic and copies ran while one was open for 1% of the time, Pallas kernels for 12%

profile of v3, /device:TPU:0, one launch (start us, length us, event | category | flops | bytes accessed | tf_op | source)
XLA Modules:
  0.0 74.7 jit_solution(15514229469334737731)
XLA Ops:
  0.0 3.0 %collective-permute-start = (bf16[200,512]{1,0:T(8,128)(2,1)}, bf16[200,512]{1,0:T(8,128)(2,1)S(1)}, u32[]{:S(2)}, u32[]{:S(2)}) collective-permute-start(bf16[200,512]{1,0:T(8,128)(2,1)} %bitcast.5), channel_id=1, source_target_pairs={{0,1},{1,0},{2,3},{3,2},{4,5},{5,4},{6,7},{7,6},{8,9},{9,8},{10,11... | collective-permute-start | bytes 614408 | tf_op jit(solution)/shard_map/ppermute | solution.py:295
  3.0 0.7 collective-permute-start.9
  3.6 2.1 %collective-permute-start.5 = (bf16[200,512]{1,0:T(8,128)(2,1)}, bf16[200,512]{1,0:T(8,128)(2,1)S(1)}, u32[]{:S(2)}, u32[]{:S(2)}) collective-permute-start(bf16[200,512]{1,0:T(8,128)(2,1)} %bitcast.7), channel_id=1, source_target_pairs={{26,0},{24,2},{30,4},{28,6},{2,8},{0,10},{6,12},{4,14},{10,16},{8,... | collective-permute-start | bytes 614408 | tf_op jit(solution)/shard_map/ppermute | solution.py:298
  5.8 2.0 %collective-permute-start.1 = (bf16[200,512]{1,0:T(8,128)(2,1)}, bf16[200,512]{1,0:T(8,128)(2,1)S(1)}, u32[]{:S(2)}, u32[]{:S(2)}) collective-permute-start(bf16[200,512]{1,0:T(8,128)(2,1)} %bitcast.8), channel_id=1, source_target_pairs={{10,0},{8,2},{14,4},{12,6},{18,8},{16,10},{22,12},{20,14},{26,16},... | collective-permute-start | bytes 614408 | tf_op jit(solution)/shard_map/ppermute | solution.py:298
  8.7 3.2 %collective-permute-start.3 = (bf16[200,512]{1,0:T(8,128)(2,1)S(1)}, bf16[200,512]{1,0:T(8,128)(2,1)S(1)}, u32[]{:S(2)}, u32[]{:S(2)}) collective-permute-start(bf16[200,512]{1,0:T(8,128)(2,1)S(1)} %collective-permute-done.other_ref), channel_id=1, source_target_pairs={{10,0},{8,2},{14,4},{12,6},{18,8},{16,10},{22,12},{20,14},{26,16},... | collective-permute-start | bytes 614408 | tf_op jit(solution)/shard_map/ppermute | solution.py:298
  11.8 1.5 %collective-permute-start.10 = (bf16[200,512]{1,0:T(8,128)(2,1)S(1)}, bf16[200,512]{1,0:T(8,128)(2,1)S(1)}, u32[]{:S(2)}, u32[]{:S(2)}) collective-permute-start(bf16[200,512]{1,0:T(8,128)(2,1)S(1)} %collective-permute-done.other_ref), channel_id=1, source_target_pairs={{6,0},{4,2},{2,4},{0,6},{14,8},{12,10},{10,12},{8,14},{22,16},{20,... | collective-permute-start | bytes 614408 | tf_op jit(solution)/shard_map/ppermute | solution.py:298
  14.0 0.7 sqrt.3.root_ref
  14.9 2.7 %collective-permute-done.1.refs_0_ = bf16[200,512]{1,0:T(8,128)(2,1)S(1)} collective-permute-done((bf16[200,512]{1,0:T(8,128)(2,1)}, bf16[200,512]{1,0:T(8,128)(2,1)S(1)}, u32[]{:S(2)}, u32[]{:S(2)}) %collective-permute-start.1) | collective-permute-done | bytes 204832 | tf_op jit(solution)/shard_map/ppermute | solution.py:298
  17.6 0.9 %collective-permute-start.2 = (bf16[200,512]{1,0:T(8,128)(2,1)S(1)}, bf16[200,512]{1,0:T(8,128)(2,1)S(1)}, u32[]{:S(2)}, u32[]{:S(2)}) collective-permute-start(bf16[200,512]{1,0:T(8,128)(2,1)S(1)} %collective-permute-done.1.refs_0_), channel_id=1, source_target_pairs={{6,0},{4,2},{2,4},{0,6},{14,8},{12,10},{10,12},{8,14},{22,16},{20,... | collective-permute-start | bytes 614408 | tf_op jit(solution)/shard_map/ppermute | solution.py:298
  18.5 3.7 %collective-permute-done.7.refs_3_ = bf16[200,512]{1,0:T(8,128)(2,1)S(1)} collective-permute-done((bf16[200,512]{1,0:T(8,128)(2,1)S(1)}, bf16[200,512]{1,0:T(8,128)(2,1)S(1)}, u32[]{:S(2)}, u32[]{:S(2)}) %collective-permute-start.7) | collective-permute-done | bytes 204832 | tf_op jit(solution)/shard_map/ppermute | solution.py:298
  22.1 0.9 %collective-permute-start.8 = (bf16[200,512]{1,0:T(8,128)(2,1)S(1)}, bf16[200,512]{1,0:T(8,128)(2,1)S(1)}, u32[]{:S(2)}, u32[]{:S(2)}) collective-permute-start(bf16[200,512]{1,0:T(8,128)(2,1)S(1)} %collective-permute-done.7.refs_3_), channel_id=1, source_target_pairs={{6,0},{4,2},{2,4},{0,6},{14,8},{12,10},{10,12},{8,14},{22,16},{20,... | collective-permute-start | bytes 614408 | tf_op jit(solution)/shard_map/ppermute | solution.py:298
  23.0 3.4 %collective-permute-done.3.refs_1_ = bf16[200,512]{1,0:T(8,128)(2,1)S(1)} collective-permute-done((bf16[200,512]{1,0:T(8,128)(2,1)S(1)}, bf16[200,512]{1,0:T(8,128)(2,1)S(1)}, u32[]{:S(2)}, u32[]{:S(2)}) %collective-permute-start.3) | collective-permute-done | bytes 204832 | tf_op jit(solution)/shard_map/ppermute | solution.py:298
  26.9 2.2 %copy-done = bf16[1,12,200,800]{3,2,1,0:T(8,128)(2,1)S(1)} copy-done((bf16[1,12,200,800]{3,2,1,0:T(8,128)(2,1)S(1)}, bf16[1,12,200,800]{3,2,1,0:T(8,128)(2,1)}, u32[]{:S(2)}) %copy-start) | copy-done | bytes 3840024
  29.1 1.7 %shard_map.47 = (bf16[2,200,512]{2,1,0:T(8,128)(2,1)S(1)}, bf16[2,200,512]{2,1,0:T(8,128)(2,1)S(1)}) custom-call(s32[2]{0:T(128)S(1)} %pad_add_fusion.place_ref, f32[12]{0:T(128)S(1)} %sqrt.3.root_ref, bf16[1,12,200,800]{3,2,1,0:T(8,128)(2,1)S(1)} %copy-done, bf16[200,512]{1,0:T(8,128)(2,1)S(1)} %collective-permute-done.9.refs_0_, ...), custom_call_target="tpu_custom_call" | custom-call | flops 655360000 | bytes 1280000 | tf_op jit(solution)/shard_map/pallas_call | solution.py:129
  30.8 0.6 collective-permute-start.14
  31.4 1.8 %shard_map.48 = (bf16[2,200,512]{2,1,0:T(8,128)(2,1)S(1)}, bf16[2,200,512]{2,1,0:T(8,128)(2,1)S(1)}) custom-call(s32[2]{0:T(128)S(1)} %pad_add_fusion.place_ref, f32[12]{0:T(128)S(1)} %sqrt.3.root_ref, bf16[1,12,200,800]{3,2,1,0:T(8,128)(2,1)S(1)} %copy-done, bf16[200,512]{1,0:T(8,128)(2,1)S(1)} %collective-permute-done.1.refs_0_, ...), custom_call_target="tpu_custom_call" | custom-call | flops 655360000 | bytes 1280000 | tf_op jit(solution)/shard_map/pallas_call | solution.py:129
  33.2 1.6 %collective-permute-start.13 = (bf16[2,200,512]{2,1,0:T(8,128)(2,1)S(1)}, bf16[2,200,512]{2,1,0:T(8,128)(2,1)S(1)}, u32[]{:S(2)}, u32[]{:S(2)}) collective-permute-start(bf16[2,200,512]{2,1,0:T(8,128)(2,1)S(1)} %get-tuple-element.24.refs_3_), channel_id=1, source_target_pairs={{0,1},{1,0},{2,3},{3,2},{4,5},{5,4},{6,7},{7,6},{8,9},{9,8},{10,11... | collective-permute-start | bytes 1228808 | tf_op jit(solution)/shard_map/ppermute | solution.py:295
  34.8 1.4 %collective-permute-done.4.refs_1_ = bf16[200,512]{1,0:T(8,128)(2,1)S(1)} collective-permute-done((bf16[200,512]{1,0:T(8,128)(2,1)S(1)}, bf16[200,512]{1,0:T(8,128)(2,1)S(1)}, u32[]{:S(2)}, u32[]{:S(2)}) %collective-permute-start.4) | collective-permute-done | bytes 204832 | tf_op jit(solution)/shard_map/ppermute | solution.py:298
  36.2 1.8 %shard_map.46 = (bf16[2,200,512]{2,1,0:T(8,128)(2,1)S(1)}, bf16[2,200,512]{2,1,0:T(8,128)(2,1)S(1)}) custom-call(s32[2]{0:T(128)S(1)} %pad_add_fusion.place_ref, f32[12]{0:T(128)S(1)} %sqrt.3.root_ref, bf16[1,12,200,800]{3,2,1,0:T(8,128)(2,1)S(1)} %copy-done, bf16[200,512]{1,0:T(8,128)(2,1)S(1)} %collective-permute-done.2.refs_0_, ...), custom_call_target="tpu_custom_call" | custom-call | flops 655360000 | bytes 1280000 | tf_op jit(solution)/shard_map/pallas_call | solution.py:129
  38.0 2.0 %collective-permute-start.12 = (bf16[2,200,512]{2,1,0:T(8,128)(2,1)S(1)}, bf16[2,200,512]{2,1,0:T(8,128)(2,1)S(1)}, u32[]{:S(2)}, u32[]{:S(2)}) collective-permute-start(bf16[2,200,512]{2,1,0:T(8,128)(2,1)S(1)} %get-tuple-element.20.refs_1_), channel_id=1, source_target_pairs={{0,1},{1,0},{2,3},{3,2},{4,5},{5,4},{6,7},{7,6},{8,9},{9,8},{10,11... | collective-permute-start | bytes 1228808 | tf_op jit(solution)/shard_map/ppermute | solution.py:295
  40.0 1.1 %shard_map.49.refs_2_ = f32[2,200,200]{2,1,0:T(8,128)S(1)} custom-call(bf16[2,200,512]{2,1,0:T(8,128)(2,1)S(1)} %get-tuple-element.21.refs_0_.keep_ref, bf16[2,200,512]{2,1,0:T(8,128)(2,1)S(1)} %get-tuple-element.22.refs_1_, bf16[2,200,512]{2,1,0:T(8,128)(2,1)S(1)} %get-tuple-element.23.refs_2_.keep_ref, bf16[2,200,512]{2,1,0:T(8,128)(2,1)S(1)} %get-tuple-element.24.refs_3_), custom_call_target="tpu_custom_call" | custom-call | flops 655360000 | bytes 1638400 | tf_op jit(solution)/shard_map/pallas_call | solution.py:170
  41.1 0.6 shard_map.50
  41.8 1.4 %collective-permute-done.14.got_ref = bf16[2,200,512]{2,1,0:T(8,128)(2,1)S(1)} collective-permute-done((bf16[2,200,512]{2,1,0:T(8,128)(2,1)S(1)}, bf16[2,200,512]{2,1,0:T(8,128)(2,1)S(1)}, u32[]{:S(2)}, u32[]{:S(2)}) %collective-permute-start.14) | collective-permute-done | bytes 409632 | tf_op jit(solution)/shard_map/ppermute | solution.py:295
  43.2 0.6 shard_map.51
  43.9 8.1 %collective-permute-done.13.got_ref = bf16[2,200,512]{2,1,0:T(8,128)(2,1)S(1)} collective-permute-done((bf16[2,200,512]{2,1,0:T(8,128)(2,1)S(1)}, bf16[2,200,512]{2,1,0:T(8,128)(2,1)S(1)}, u32[]{:S(2)}, u32[]{:S(2)}) %collective-permute-start.13) | collective-permute-done | bytes 409632 | tf_op jit(solution)/shard_map/ppermute | solution.py:295
  52.0 0.6 shard_map.52
  52.6 8.1 %collective-permute-done.12.got_ref = bf16[2,200,512]{2,1,0:T(8,128)(2,1)S(1)} collective-permute-done((bf16[2,200,512]{2,1,0:T(8,128)(2,1)S(1)}, bf16[2,200,512]{2,1,0:T(8,128)(2,1)S(1)}, u32[]{:S(2)}, u32[]{:S(2)}) %collective-permute-start.12) | collective-permute-done | bytes 409632 | tf_op jit(solution)/shard_map/ppermute | solution.py:295
  60.8 0.6 shard_map.53
  61.4 0.6 collective-permute-start.15
  62.0 3.2 %collective-permute-done.11.other_total_ref = bf16[2,200,200]{2,1,0:T(8,128)(2,1)S(1)} collective-permute-done((bf16[2,200,200]{2,1,0:T(8,128)(2,1)S(1)}, bf16[2,200,200]{2,1,0:T(8,128)(2,1)S(1)}, u32[]{:S(2)}, u32[]{:S(2)}) %collective-permute-start.11) | collective-permute-done | bytes 160032 | tf_op jit(solution)/shard_map/ppermute | solution.py:295
  65.2 3.7 %collective-permute-done.15.theirs_ref = bf16[2,200,200]{2,1,0:T(8,128)(2,1)S(1)} collective-permute-done((bf16[2,200,200]{2,1,0:T(8,128)(2,1)S(1)}, bf16[2,200,200]{2,1,0:T(8,128)(2,1)S(1)}, u32[]{:S(2)}, u32[]{:S(2)}) %collective-permute-start.15) | collective-permute-done | bytes 160032 | tf_op jit(solution)/shard_map/ppermute | solution.py:295
  68.8 5.9 %update.1 = f32[1,200,512]{2,1,0:T(8,128)} custom-call(bf16[200,512]{1,0:T(8,128)(2,1)S(1)} %bitcast.9, bf16[200,512]{1,0:T(8,128)(2,1)S(1)} %collective-permute-done.other_ref, f32[2,200,200]{2,1,0:T(8,128)S(1)} %get-tuple-element.25.own_total_ref, bf16[2,200,200]{2,1,0:T(8,128)(2,1)S(1)} %collective-permute-done.11.other_total_ref, ...), custom_call_target="tpu_custom_call" | custom-call | tf_op jit(solution)/shard_map/update/pallas_call | solution.py:269
  (15 shorter events, 1.7 us)
Async XLA Ops:
  0.0 8.3 %collective-permute-start = (bf16[200,512]{1,0:T(8,128)(2,1)}, bf16[200,512]{1,0:T(8,128)(2,1)S(1)}, u32[]{:S(2)}, u32[]{:S(2)}) collective-permute-start(bf16[200,512]{1,0:T(8,128)(2,1)} %bitcast.5), channel_id=1, source_target_pairs={{0,1},{1,0},{2,3},{3,2},{4,5},{5,4},{6,7},{7,6},{8,9},{9,8},{10,11... | collective-permute-start | bytes 614408 | tf_op jit(solution)/shard_map/ppermute | solution.py:295
  3.0 8.8 %collective-permute-start.9 = (bf16[200,512]{1,0:T(8,128)(2,1)}, bf16[200,512]{1,0:T(8,128)(2,1)S(1)}, u32[]{:S(2)}, u32[]{:S(2)}) collective-permute-start(bf16[200,512]{1,0:T(8,128)(2,1)} %bitcast.6), channel_id=1, source_target_pairs={{6,0},{4,2},{2,4},{0,6},{14,8},{12,10},{10,12},{8,14},{22,16},{20,... | collective-permute-start | bytes 614408 | tf_op jit(solution)/shard_map/ppermute | solution.py:298
  3.6 11.0 %collective-permute-start.5 = (bf16[200,512]{1,0:T(8,128)(2,1)}, bf16[200,512]{1,0:T(8,128)(2,1)S(1)}, u32[]{:S(2)}, u32[]{:S(2)}) collective-permute-start(bf16[200,512]{1,0:T(8,128)(2,1)} %bitcast.7), channel_id=1, source_target_pairs={{26,0},{24,2},{30,4},{28,6},{2,8},{0,10},{6,12},{4,14},{10,16},{8,... | collective-permute-start | bytes 614408 | tf_op jit(solution)/shard_map/ppermute | solution.py:298
  5.8 11.8 %collective-permute-start.1 = (bf16[200,512]{1,0:T(8,128)(2,1)}, bf16[200,512]{1,0:T(8,128)(2,1)S(1)}, u32[]{:S(2)}, u32[]{:S(2)}) collective-permute-start(bf16[200,512]{1,0:T(8,128)(2,1)} %bitcast.8), channel_id=1, source_target_pairs={{10,0},{8,2},{14,4},{12,6},{18,8},{16,10},{22,12},{20,14},{26,16},... | collective-permute-start | bytes 614408 | tf_op jit(solution)/shard_map/ppermute | solution.py:298
  8.3 13.8 %collective-permute-start.7 = (bf16[200,512]{1,0:T(8,128)(2,1)S(1)}, bf16[200,512]{1,0:T(8,128)(2,1)S(1)}, u32[]{:S(2)}, u32[]{:S(2)}) collective-permute-start(bf16[200,512]{1,0:T(8,128)(2,1)S(1)} %collective-permute-done.other_ref), channel_id=1, source_target_pairs={{26,0},{24,2},{30,4},{28,6},{2,8},{0,10},{6,12},{4,14},{10,16},{8,... | collective-permute-start | bytes 614408 | tf_op jit(solution)/shard_map/ppermute | solution.py:298
  8.7 17.7 %collective-permute-start.3 = (bf16[200,512]{1,0:T(8,128)(2,1)S(1)}, bf16[200,512]{1,0:T(8,128)(2,1)S(1)}, u32[]{:S(2)}, u32[]{:S(2)}) collective-permute-start(bf16[200,512]{1,0:T(8,128)(2,1)S(1)} %collective-permute-done.other_ref), channel_id=1, source_target_pairs={{10,0},{8,2},{14,4},{12,6},{18,8},{16,10},{22,12},{20,14},{26,16},... | collective-permute-start | bytes 614408 | tf_op jit(solution)/shard_map/ppermute | solution.py:298
  11.8 15.0 %collective-permute-start.10 = (bf16[200,512]{1,0:T(8,128)(2,1)S(1)}, bf16[200,512]{1,0:T(8,128)(2,1)S(1)}, u32[]{:S(2)}, u32[]{:S(2)}) collective-permute-start(bf16[200,512]{1,0:T(8,128)(2,1)S(1)} %collective-permute-done.other_ref), channel_id=1, source_target_pairs={{6,0},{4,2},{2,4},{0,6},{14,8},{12,10},{10,12},{8,14},{22,16},{20,... | collective-permute-start | bytes 614408 | tf_op jit(solution)/shard_map/ppermute | solution.py:298
  14.6 18.5 %collective-permute-start.6 = (bf16[200,512]{1,0:T(8,128)(2,1)S(1)}, bf16[200,512]{1,0:T(8,128)(2,1)S(1)}, u32[]{:S(2)}, u32[]{:S(2)}) collective-permute-start(bf16[200,512]{1,0:T(8,128)(2,1)S(1)} %collective-permute-done.5.refs_2_), channel_id=1, source_target_pairs={{6,0},{4,2},{2,4},{0,6},{14,8},{12,10},{10,12},{8,14},{22,16},{20,... | collective-permute-start | bytes 614408 | tf_op jit(solution)/shard_map/ppermute | solution.py:298
  17.6 17.2 %collective-permute-start.2 = (bf16[200,512]{1,0:T(8,128)(2,1)S(1)}, bf16[200,512]{1,0:T(8,128)(2,1)S(1)}, u32[]{:S(2)}, u32[]{:S(2)}) collective-permute-start(bf16[200,512]{1,0:T(8,128)(2,1)S(1)} %collective-permute-done.1.refs_0_), channel_id=1, source_target_pairs={{6,0},{4,2},{2,4},{0,6},{14,8},{12,10},{10,12},{8,14},{22,16},{20,... | collective-permute-start | bytes 614408 | tf_op jit(solution)/shard_map/ppermute | solution.py:298
  22.1 12.6 %collective-permute-start.8 = (bf16[200,512]{1,0:T(8,128)(2,1)S(1)}, bf16[200,512]{1,0:T(8,128)(2,1)S(1)}, u32[]{:S(2)}, u32[]{:S(2)}) collective-permute-start(bf16[200,512]{1,0:T(8,128)(2,1)S(1)} %collective-permute-done.7.refs_3_), channel_id=1, source_target_pairs={{6,0},{4,2},{2,4},{0,6},{14,8},{12,10},{10,12},{8,14},{22,16},{20,... | collective-permute-start | bytes 614408 | tf_op jit(solution)/shard_map/ppermute | solution.py:298
  26.4 9.8 %collective-permute-start.4 = (bf16[200,512]{1,0:T(8,128)(2,1)S(1)}, bf16[200,512]{1,0:T(8,128)(2,1)S(1)}, u32[]{:S(2)}, u32[]{:S(2)}) collective-permute-start(bf16[200,512]{1,0:T(8,128)(2,1)S(1)} %collective-permute-done.3.refs_1_), channel_id=1, source_target_pairs={{6,0},{4,2},{2,4},{0,6},{14,8},{12,10},{10,12},{8,14},{22,16},{20,... | collective-permute-start | bytes 614408 | tf_op jit(solution)/shard_map/ppermute | solution.py:298
  26.9 2.2 %copy-start = (bf16[1,12,200,800]{3,2,1,0:T(8,128)(2,1)S(1)}, bf16[1,12,200,800]{3,2,1,0:T(8,128)(2,1)}, u32[]{:S(2)}) copy-start(bf16[1,12,200,800]{3,2,1,0:T(8,128)(2,1)} %margins_ref.5) | copy-start | bytes 11520004
  30.8 12.4 %collective-permute-start.14 = (bf16[2,200,512]{2,1,0:T(8,128)(2,1)S(1)}, bf16[2,200,512]{2,1,0:T(8,128)(2,1)S(1)}, u32[]{:S(2)}, u32[]{:S(2)}) collective-permute-start(bf16[2,200,512]{2,1,0:T(8,128)(2,1)S(1)} %get-tuple-element.22.refs_1_), channel_id=1, source_target_pairs={{0,1},{1,0},{2,3},{3,2},{4,5},{5,4},{6,7},{7,6},{8,9},{9,8},{10,11... | collective-permute-start | bytes 1228808 | tf_op jit(solution)/shard_map/ppermute | solution.py:295
  33.2 18.8 %collective-permute-start.13 = (bf16[2,200,512]{2,1,0:T(8,128)(2,1)S(1)}, bf16[2,200,512]{2,1,0:T(8,128)(2,1)S(1)}, u32[]{:S(2)}, u32[]{:S(2)}) collective-permute-start(bf16[2,200,512]{2,1,0:T(8,128)(2,1)S(1)} %get-tuple-element.24.refs_3_), channel_id=1, source_target_pairs={{0,1},{1,0},{2,3},{3,2},{4,5},{5,4},{6,7},{7,6},{8,9},{9,8},{10,11... | collective-permute-start | bytes 1228808 | tf_op jit(solution)/shard_map/ppermute | solution.py:295
  38.0 22.8 %collective-permute-start.12 = (bf16[2,200,512]{2,1,0:T(8,128)(2,1)S(1)}, bf16[2,200,512]{2,1,0:T(8,128)(2,1)S(1)}, u32[]{:S(2)}, u32[]{:S(2)}) collective-permute-start(bf16[2,200,512]{2,1,0:T(8,128)(2,1)S(1)} %get-tuple-element.20.refs_1_), channel_id=1, source_target_pairs={{0,1},{1,0},{2,3},{3,2},{4,5},{5,4},{6,7},{7,6},{8,9},{9,8},{10,11... | collective-permute-start | bytes 1228808 | tf_op jit(solution)/shard_map/ppermute | solution.py:295
  41.1 27.8 %copy-start.1 = (bf16[1,200,512]{2,1,0:T(8,128)(2,1)S(1)}, bf16[1,200,512]{2,1,0:T(8,128)(2,1)}, u32[]{:S(2)}) copy-start(bf16[1,200,512]{2,1,0:T(8,128)(2,1)} %param.5) | copy-start | bytes 614404
  41.7 23.5 %collective-permute-start.11 = (bf16[2,200,200]{2,1,0:T(8,128)(2,1)S(1)}, bf16[2,200,200]{2,1,0:T(8,128)(2,1)S(1)}, u32[]{:S(2)}, u32[]{:S(2)}) collective-permute-start(bf16[2,200,200]{2,1,0:T(8,128)(2,1)S(1)} %get-tuple-element.26), channel_id=1, source_target_pairs={{0,1},{1,0},{2,3},{3,2},{4,5},{5,4},{6,7},{7,6},{8,9},{9,8},{10,11... | collective-permute-start | bytes 480008 | tf_op jit(solution)/shard_map/ppermute | solution.py:295
  61.4 7.4 %collective-permute-start.15 = (bf16[2,200,200]{2,1,0:T(8,128)(2,1)S(1)}, bf16[2,200,200]{2,1,0:T(8,128)(2,1)S(1)}, u32[]{:S(2)}, u32[]{:S(2)}) collective-permute-start(bf16[2,200,200]{2,1,0:T(8,128)(2,1)S(1)} %get-tuple-element.32), channel_id=1, source_target_pairs={{0,1},{1,0},{2,3},{3,2},{4,5},{5,4},{6,7},{7,6},{8,9},{9,8},{10,11... | collective-permute-start | bytes 480008 | tf_op jit(solution)/shard_map/ppermute | solution.py:295

commit v4 on v3

v4 whole, which is shorter than its diff:
```python
import functools
import math

import jax
import jax.numpy as jnp
from jax import lax
from jax.experimental import pallas as pl
from jax.experimental.pallas import tpu as pltpu
from jax.sharding import PartitionSpec as P


SHELL_VECTORS = (
    (1, 1, 0),
    (1, -1, 0),
    (-1, 1, 0),
    (-1, -1, 0),
    (1, 0, 1),
    (1, 0, -1),
    (-1, 0, 1),
    (-1, 0, -1),
    (0, 1, 1),
    (0, 1, -1),
    (0, -1, 1),
    (0, -1, -1),
)
BATCH = 4
SHIPPED = 2
VMEM = pl.BlockSpec(memory_space=pltpu.VMEM)
LIMIT = pltpu.CompilerParams(vmem_limit_bytes=20 * 2**20)
SMEM = pl.BlockSpec(memory_space=pltpu.SMEM)
F32 = jnp.float32
BF16 = jnp.bfloat16
NT = (((1,), (1,)), ((), ()))
TN = (((0,), (0,)), ((), ()))


def grid_shape(point_count):
    size_y = min(4, point_count // 8)
    return (4, size_y, point_count // (4 * size_y))


def displacement(shell, point_count):
    return tuple(step % size for step, size in zip(shell, grid_shape(point_count)))


def fetch_pairs(shift, point_count):
    size_x, size_y, size_z = grid_shape(point_count)
    pairs = []
    for x in range(size_x):
        for y in range(size_y):
            for z in range(size_z):
                source = ((x + shift[0]) % size_x, (y + shift[1]) % size_y, (z + shift[2]) % size_z)
                pairs.append(
                    (
                        (source[0] * size_y + source[1]) * size_z + source[2],
                        (x * size_y + y) * size_z + z,
                    )
                )
    return pairs


def dot(left, right, dims=None):
    if dims is None:
        return jnp.dot(left, right, preferred_element_type=F32)
    return lax.dot_general(left, right, dims, preferred_element_type=F32)


def split(value):
    high = value.astype(BF16)
    return high, (value - high.astype(F32)).astype(BF16)


def dot_exact_right(left, right, dims=None):
    high, low = split(left)
    return dot(high, right, dims) + dot(low, right, dims)


def dot_split(left, right, dims=None):
    left_high, left_low = split(left)
    right_high, right_low = split(right)
    return (
        dot(left_high, right_high, dims)
        + dot(left_high, right_low, dims)
        + dot(left_low, right_high, dims)
    )


def times_minus_i(value):
    half = value.shape[-1] // 2
    return jnp.concatenate([value[:, half:], -value[:, :half]], axis=1)


def times_i(value):
    half = value.shape[-1] // 2
    return jnp.concatenate([-value[:, half:], value[:, :half]], axis=1)


def stack_complex(mine, other, side, rows_ref, stacked_ref):
    rows = mine.shape[0]
    rows_ref[pl.ds(pl.multiple_of(side * rows, 8), rows), :] = mine.astype(F32)
    rows_ref[pl.ds(pl.multiple_of((1 - side) * rows, 8), rows), :] = other.astype(F32)
    whole = rows_ref[...]
    stacked_ref[: 2 * rows, :] = whole.astype(BF16)
    stacked_ref[2 * rows :, :] = times_i(whole).astype(BF16)


def masked_block(margin, stacked, root, limit):
    inside = lax.broadcasted_iota(jnp.int32, (margin.shape[0], 1), 0) < limit
    return jnp.where(inside, dot(margin, stacked) * root, 0.0).astype(BF16)


def load_kernel(shipped, place_ref, margins_ref, all_ref, given_ref, all_sem, given_sem):
    copies = (
        pltpu.make_async_copy(margins_ref.at[0, shipped + 1 - place_ref[0]], given_ref, given_sem),
        pltpu.make_async_copy(margins_ref.at[0], all_ref, all_sem),
    )
    for copy in copies:
        copy.start()
    for copy in copies:
        copy.wait()


def load(place, margins, shipped):
    shape = margins.shape[1:]
    return pl.pallas_call(
        functools.partial(load_kernel, shipped),
        in_specs=[SMEM, pl.BlockSpec(memory_space=pl.ANY)],
        out_specs=[VMEM] * 2,
        out_shape=[
            jax.ShapeDtypeStruct(shape, margins.dtype),
            jax.ShapeDtypeStruct(shape[1:], margins.dtype),
        ],
        scratch_shapes=[pltpu.SemaphoreType.DMA] * 2,
        name="load",
        compiler_params=LIMIT,
    )(place, margins)


def project_kernel(groups, first, sent, place_ref, root_ref, margins_ref, *refs):
    halves = refs[: 2 * len(groups)]
    keep_ref, *give_refs, rows_ref, stacked_ref, blocks_ref = refs[2 * len(groups) :]
    side, limit = place_ref[0], place_ref[1]
    for number, members in enumerate(groups):
        mine, other = halves[2 * number][...], halves[2 * number + 1][...]
        stack_complex(mine, other, side, rows_ref, stacked_ref)
        for member in members:
            blocks_ref[member] = masked_block(
                margins_ref[first + member], stacked_ref[...], root_ref[first + member], limit
            )
    for pair in range(BATCH // 2):
        keep_ref[pair] = blocks_ref[2 * pair + side]
        target = give_refs[0].at[pair] if pair < sent else give_refs[1].at[pair - sent]
        target[...] = blocks_ref[2 * pair + 1 - side]


def project(place, roots, margins, batch, groups, halves, sent):
    rows, double = margins.shape[1:]
    width = halves[0].shape[-1]
    pairs = BATCH // 2
    counts = [pairs, sent] + ([pairs - sent] if sent < pairs else [])
    return pl.pallas_call(
        functools.partial(project_kernel, groups, batch * BATCH, sent),
        in_specs=[SMEM, SMEM, VMEM, *([VMEM] * len(halves))],
        out_specs=[VMEM] * len(counts),
        out_shape=[jax.ShapeDtypeStruct((count, rows, width), BF16) for count in counts],
        scratch_shapes=[
            pltpu.VMEM((2 * rows, width), F32),
            pltpu.VMEM((double, width), BF16),
            pltpu.VMEM((BATCH, rows, width), BF16),
        ],
        cost_estimate=pl.CostEstimate(
            flops=2 * BATCH * rows * double * width,
            bytes_accessed=2 * BATCH * rows * double,
            transcendentals=0,
        ),
        compiler_params=LIMIT,
    )(place, roots, margins, *halves)


def extra_kernel(shipped, place_ref, root_ref, margin_ref, *refs):
    *halves, out_ref, rows_ref, stacked_ref = refs
    side, limit = place_ref[0], place_ref[2]
    mine, other = halves[0][...], halves[1][...]
    if len(halves) > 2:
        mine = jnp.where(side == 0, mine, halves[2][...])
        other = jnp.where(side == 0, other, halves[3][...])
    stack_complex(mine, other, side, rows_ref, stacked_ref)
    root = root_ref[shipped + side]
    out_ref[0] = masked_block(margin_ref[...], stacked_ref[...], root, limit)


def extra(place, roots, margin, shipped, halves):
    rows, double = margin.shape
    width = halves[0].shape[-1]
    return pl.pallas_call(
        functools.partial(extra_kernel, shipped),
        in_specs=[SMEM, SMEM, VMEM, *([VMEM] * len(halves))],
        out_specs=VMEM,
        out_shape=jax.ShapeDtypeStruct((1, rows, width), BF16),
        scratch_shapes=[pltpu.VMEM((2 * rows, width), F32), pltpu.VMEM((double, width), BF16)],
        cost_estimate=pl.CostEstimate(
            flops=2 * rows * double * width, bytes_accessed=2 * rows * double, transcendentals=0
        ),
        name="extra",
        compiler_params=LIMIT,
    )(place, roots, margin, *halves)


def triangle(size):
    row = lax.broadcasted_iota(jnp.int32, (size, size), 0)
    return row, lax.broadcasted_iota(jnp.int32, (size, size), 1)


def gather_own_kernel(count, has_total, *refs):
    blocks, refs = refs[:count], refs[count:]
    rows = blocks[0].shape[1]
    real = jnp.zeros((rows, rows), F32)
    imag = jnp.zeros((rows, rows), F32)
    if has_total:
        real, imag = refs[0][0], refs[0][1]
    for block_ref in blocks:
        for pair in range(block_ref.shape[0]):
            block = block_ref[pair]
            real += dot(block, block, NT)
            imag += dot(times_minus_i(block), block, NT)
    total_ref, *packed = refs[1 if has_total else 0 :]
    total_ref[0], total_ref[1] = real, imag
    if packed:
        row, column = triangle(rows)
        packed[0][...] = jnp.where(row <= column, real, imag).astype(BF16)


def gather_own(blocks, before):
    rows, width = blocks[0].shape[1:]
    count = len(blocks)
    operands = list(blocks) + ([] if before is None else [before])
    results = [jax.ShapeDtypeStruct((2, rows, rows), F32)]
    if before is not None:
        results.append(jax.ShapeDtypeStruct((rows, rows), BF16))
    return pl.pallas_call(
        functools.partial(gather_own_kernel, count, before is not None),
        in_specs=[VMEM] * len(operands),
        out_specs=[VMEM] * len(results),
        out_shape=results,
        cost_estimate=pl.CostEstimate(
            flops=8 * count * rows * rows * width,
            bytes_accessed=4 * count * rows * width,
            transcendentals=0,
        ),
        compiler_params=LIMIT,
    )(*operands)


def cross_kernel(terms, count, has_total, *refs):
    blocks, refs = refs[:count], refs[count:]
    rows = blocks[0].shape[1]
    sums = [jnp.zeros((rows, rows), F32) for _ in range(4)]
    if has_total:
        mine_before_ref, theirs_before_ref, *refs = refs
        sums = [mine_before_ref[0], mine_before_ref[1], theirs_before_ref[0], theirs_before_ref[1]]
    mine_ref, theirs_ref = refs
    for keep_place, keep_index, got_place, got_index in terms:
        keep, got = blocks[keep_place][keep_index], blocks[got_place][got_index]
        sums[0] += dot(keep, got, NT)
        sums[1] += dot(times_minus_i(keep), got, NT)
        sums[2] += dot(got, keep, NT)
        sums[3] += dot(times_minus_i(got), keep, NT)
    mine_ref[0], mine_ref[1] = sums[0], sums[1]
    kind = theirs_ref.dtype
    theirs_ref[0], theirs_ref[1] = sums[2].astype(kind), sums[3].astype(kind)


def cross(blocks, terms, before, last):
    rows, width = blocks[0].shape[1:]
    operands = [*blocks, *(before or ())]
    return pl.pallas_call(
        functools.partial(cross_kernel, terms, len(blocks), before is not None),
        in_specs=[VMEM] * len(operands),
        out_specs=[VMEM] * 2,
        out_shape=[
            jax.ShapeDtypeStruct((2, rows, rows), F32),
            jax.ShapeDtypeStruct((2, rows, rows), BF16 if last else F32),
        ],
        cost_estimate=pl.CostEstimate(
            flops=8 * len(terms) * rows * rows * width,
            bytes_accessed=4 * len(terms) * rows * width,
            transcendentals=0,
        ),
        compiler_params=LIMIT,
    )(*operands)


def complex_stack(value):
    return jnp.concatenate([value, times_i(value)], axis=0)


def base_kernel(own_ref, other_ref, total_ref, packed_ref, mine_ref, base_ref, base_other_ref):
    own, other = own_ref[...], other_ref[...]
    own_i, other_i = times_i(own.astype(F32)).astype(BF16), times_i(other.astype(F32)).astype(BF16)
    real, imag = mine_ref[0], mine_ref[1]
    base_ref[...] = (
        dot_exact_right(total_ref[0], own)
        + dot_exact_right(total_ref[1], own_i)
        + dot_exact_right(real, other)
        + dot_exact_right(imag, other_i)
    )
    packed = packed_ref[...].astype(F32)
    row, column = triangle(packed.shape[0])
    upper = jnp.where(row <= column, packed, 0.0).astype(BF16)
    strict = jnp.where(row < column, packed, 0.0).astype(BF16)
    lower = jnp.where(row > column, packed, 0.0).astype(BF16)
    base_other_ref[...] = (
        dot(upper, other)
        + dot(strict, other, TN)
        + dot(lower, other_i)
        - dot(lower, other_i, TN)
        + dot_exact_right(real, own, TN)
        - dot_exact_right(imag, own_i, TN)
    )


def base(own, other, total, packed, mine):
    rows, width = own.shape
    return pl.pallas_call(
        base_kernel,
        in_specs=[VMEM] * 5,
        out_specs=[VMEM] * 2,
        out_shape=[jax.ShapeDtypeStruct((rows, width), F32)] * 2,
        cost_estimate=pl.CostEstimate(
            flops=32 * rows * rows * width, bytes_accessed=8 * rows * width, transcendentals=0
        ),
        name="base",
        compiler_params=LIMIT,
    )(own, other, total, packed, mine)


def update_kernel(scale, own_ref, other_ref, base_ref, base_other_ref, theirs_ref, out_ref):
    own, other = own_ref[...], other_ref[...]
    half = own.shape[1] // 2
    own_i, other_i = times_i(own.astype(F32)).astype(BF16), times_i(other.astype(F32)).astype(BF16)
    real, imag = theirs_ref[0], theirs_ref[1]
    product = base_ref[...] + dot(real, other) + dot(imag, other_i)
    product_other = base_other_ref[...] + dot(real, own, TN) - dot(imag, own_i, TN)
    blocks = dot_split(product, product, TN) + dot_split(product_other, product_other, TN)
    real = blocks[:half, :half] + blocks[half:, half:]
    imag = blocks[:half, half:] - blocks[half:, :half]
    diagonal = lax.broadcasted_iota(jnp.int32, (half, 2 * half), 0) == lax.broadcasted_iota(
        jnp.int32, (half, 2 * half), 1
    )
    gram = jnp.concatenate([real, imag], axis=1)
    squares = jnp.sum(jnp.where(diagonal, gram, 0.0))
    size = jnp.full((1, 1), 2.0 * squares / half + 1e-06, F32)
    scaling = lax.rsqrt(size)
    gram = gram * (scaling * scaling)
    identity = jnp.where(diagonal, 1.0, 0.0)
    gram_two = dot_split(gram, complex_stack(gram))
    left = 2.25 * identity - 1.5 * gram + 0.25 * gram_two
    right = 1.5 * gram - 0.5 * gram_two
    factor = 2.25 * identity - 0.75 * gram - 0.5 * dot_split(left, complex_stack(right))
    factor = factor * (scaling * scale)
    out_ref[0] = dot_split(product, complex_stack(factor))


def update(scale, own, other, bases, theirs):
    rows, width = own.shape
    return pl.pallas_call(
        functools.partial(update_kernel, scale),
        in_specs=[VMEM] * 5,
        out_specs=VMEM,
        out_shape=jax.ShapeDtypeStruct((1, rows, width), F32),
        name="update",
        compiler_params=LIMIT,
    )(own, other, *bases, theirs)


def batch_shifts(batch, point_count):
    shifts = {}
    for member in range(BATCH):
        shift = displacement(SHELL_VECTORS[batch * BATCH + member], point_count)
        shifts.setdefault(shift, []).append(member)
    return shifts


def on_device(margins, subspace, shell_weights, window_count):
    point_count = lax.axis_size("kpt")
    side = lax.axis_index("band")
    rows = subspace.shape[1]
    swap = [(0, 1), (1, 0)]
    plan = [batch_shifts(batch, point_count) for batch in range(3)]

    def exchange(value):
        return lax.ppermute(value, "band", swap)

    def fetch(value, shift):
        return lax.ppermute(value, "kpt", fetch_pairs(shift, point_count))

    offset = side * rows
    place = jnp.stack([side, window_count[0] - offset, window_count[0] - (rows - offset)])
    roots = jnp.sqrt(shell_weights)
    own = subspace[0]
    other = exchange(own)
    margins, margin = load(place, margins, SHIPPED)
    margin = exchange(margin)
    halves = {}
    for part, value in (("own", own), ("other", other)):
        for batch in (2, 1):
            for shift in plan[batch]:
                halves[batch, part, shift] = fetch(value, shift)
        for shift in plan[0]:
            near = displacement((shift[0], 0, 1), point_count)
            step = displacement((0, shift[1], -1), point_count)
            halves[0, part, shift] = fetch(halves[1, part, near], step)
    blocks, got = {}, {}
    for batch in (2, 1, 0):
        operands = []
        for shift in plan[batch]:
            operands += [halves[batch, "own", shift], halves[batch, "other", shift]]
        sent = SHIPPED // 2 if batch == 0 else BATCH // 2
        blocks[batch] = project(
            place, roots, margins, batch, list(plan[batch].values()), operands, sent
        )
        got[batch] = exchange(blocks[batch][1])
    operands = []
    for shift, members in plan[0].items():
        if SHIPPED in members or SHIPPED + 1 in members:
            operands += [halves[0, "own", shift], halves[0, "other", shift]]
    got_extra = extra(place, roots, margin, SHIPPED, operands)
    (total,) = gather_own([*blocks[2], *blocks[1]], None)
    total, packed = gather_own(blocks[0], total)
    other_packed = exchange(packed)
    whole = ((0, 0, 1, 0), (0, 1, 1, 1))
    crossed = cross([blocks[2][0], got[2]], whole, None, False)
    crossed = cross(
        [blocks[1][0], got[1], blocks[0][0], got_extra], (*whole, (2, 1, 3, 0)), crossed, False
    )
    mine, theirs = cross([blocks[0][0], got[0]], ((0, 0, 1, 0),), crossed, True)
    theirs = exchange(theirs)
    bases = base(own, other, total, other_packed, mine)
    scale = math.sqrt(rows * lax.axis_size("band"))
    return update(scale, own, other, bases, theirs)


def solution(mesh):
    return jax.shard_map(
        on_device,
        mesh=mesh,
        in_specs=(P("kpt", None, "band", None), P("kpt", "band", None), P(), P("kpt")),
        out_specs=P("kpt", "band", None),
        check_vma=False,
    )
```

time: 74.8 us -> 71.7 us (0.959)
  waiting for transfers between devices: 36.2 us -> 27 us
  starting transfers between devices: 20.1 us -> 23.4 us
  Pallas kernels: 14.7 us -> 17.4 us
    ppermute x6 -> x7, waiting for transfers between devices: 25 us -> 18.9 us  [exchange(): return lax.ppermute(value, 'band', swap)]
    pallas_call x6 -> x9, Pallas kernels: 7.13 us -> 10.3 us  [the longest x3 5.25 us: project(): pl.pallas_call(functools.partial(project_kernel, groups, batch * BATCH, s...]
    ppermute x10, waiting for transfers between devices: 11.2 us -> 8.16 us  [fetch(): return lax.ppermute(value, 'kpt', fetch_pairs(shift, point_count))]
    ppermute x6 -> x7, starting transfers between devices: 7.88 us -> 9.67 us  [exchange(): return lax.ppermute(value, 'band', swap)]
    ppermute x10, starting transfers between devices: 12.2 us -> 13.7 us  [fetch(): return lax.ppermute(value, 'kpt', fetch_pairs(shift, point_count))]
  transfers between devices with their start and end apart: 16 -> 17, of which waited for: 10 -> 8; matrix products, arithmetic and copies ran while one was open for 1% -> 1% of each run, Pallas kernels for 12% -> 16%
where the time goes in v4:
time: 71.7 us; the launch traced here: 71.6 us
  waiting for transfers between devices  27 us (38%)
  starting transfers between devices  23.4 us (33%)
  Pallas kernels  17.4 us (24%)
  local copies, waits for them, and re-layouts  2.89 us (4%)
  between operations  0.81 us (1%)
    ppermute x7, waiting for transfers between devices, exchange(): return lax.ppermute(value, 'band', swap)  18.9 us
    ppermute x10, starting transfers between devices, fetch(): return lax.ppermute(value, 'kpt', fetch_pairs(shift, point_count))  13.7 us
    ppermute x7, starting transfers between devices, exchange(): return lax.ppermute(value, 'band', swap)  9.67 us
    ppermute x10, waiting for transfers between devices, fetch(): return lax.ppermute(value, 'kpt', fetch_pairs(shift, point_count))  8.16 us
    pallas_call x1, Pallas kernels, update(): pl.pallas_call(functools.partial(update_kernel, scale), in_specs=[VMEM] *...  5.39 us
    pallas_call x3, Pallas kernels, project(): pl.pallas_call(functools.partial(project_kernel, groups, batch * BATCH, s...  5.25 us
    unnamed x4, local copies, waits for them, and re-layouts  2.23 us
    pallas_call x3, Pallas kernels, cross(): pl.pallas_call(functools.partial(cross_kernel, terms, len(blocks), before...  1.86 us
  transfers between devices with their start and end apart: 17, of which 8 were waited for; matrix products, arithmetic and copies ran while one was open for 1% of the time, Pallas kernels for 16%

profile of v4, /device:TPU:0, one launch (start us, length us, event | category | flops | bytes accessed | tf_op | source)
XLA Modules:
  0.0 71.6 jit_solution(8541694866100377143)
XLA Ops:
  0.0 3.0 %collective-permute-start = (bf16[200,512]{1,0:T(8,128)(2,1)}, bf16[200,512]{1,0:T(8,128)(2,1)S(1)}, u32[]{:S(2)}, u32[]{:S(2)}) collective-permute-start(bf16[200,512]{1,0:T(8,128)(2,1)} %bitcast.7), channel_id=1, source_target_pairs={{0,1},{1,0},{2,3},{3,2},{4,5},{5,4},{6,7},{7,6},{8,9},{9,8},{10,11... | collective-permute-start | bytes 614408 | tf_op jit(solution)/shard_map/ppermute | solution.py:392
  3.0 0.7 collective-permute-start.9
  3.6 2.1 %collective-permute-start.5 = (bf16[200,512]{1,0:T(8,128)(2,1)}, bf16[200,512]{1,0:T(8,128)(2,1)S(1)}, u32[]{:S(2)}, u32[]{:S(2)}) collective-permute-start(bf16[200,512]{1,0:T(8,128)(2,1)} %bitcast.9), channel_id=1, source_target_pairs={{26,0},{24,2},{30,4},{28,6},{2,8},{0,10},{6,12},{4,14},{10,16},{8,... | collective-permute-start | bytes 614408 | tf_op jit(solution)/shard_map/ppermute | solution.py:395
  5.8 2.0 %collective-permute-start.1 = (bf16[200,512]{1,0:T(8,128)(2,1)}, bf16[200,512]{1,0:T(8,128)(2,1)S(1)}, u32[]{:S(2)}, u32[]{:S(2)}) collective-permute-start(bf16[200,512]{1,0:T(8,128)(2,1)} %bitcast.10), channel_id=1, source_target_pairs={{10,0},{8,2},{14,4},{12,6},{18,8},{16,10},{22,12},{20,14},{26,16},... | collective-permute-start | bytes 614408 | tf_op jit(solution)/shard_map/ppermute | solution.py:395
  8.6 2.7 %collective-permute-start.7 = (bf16[200,512]{1,0:T(8,128)(2,1)S(1)}, bf16[200,512]{1,0:T(8,128)(2,1)S(1)}, u32[]{:S(2)}, u32[]{:S(2)}) collective-permute-start(bf16[200,512]{1,0:T(8,128)(2,1)S(1)} %collective-permute-done.other_ref), channel_id=1, source_target_pairs={{26,0},{24,2},{30,4},{28,6},{2,8},{0,10},{6,12},{4,14},{10,16},{8,... | collective-permute-start | bytes 614408 | tf_op jit(solution)/shard_map/ppermute | solution.py:395
  11.3 2.6 %collective-permute-start.3 = (bf16[200,512]{1,0:T(8,128)(2,1)S(1)}, bf16[200,512]{1,0:T(8,128)(2,1)S(1)}, u32[]{:S(2)}, u32[]{:S(2)}) collective-permute-start(bf16[200,512]{1,0:T(8,128)(2,1)S(1)} %collective-permute-done.other_ref), channel_id=1, source_target_pairs={{10,0},{8,2},{14,4},{12,6},{18,8},{16,10},{22,12},{20,14},{26,16},... | collective-permute-start | bytes 614408 | tf_op jit(solution)/shard_map/ppermute | solution.py:395
  14.6 1.3 %collective-permute-start.6 = (bf16[200,512]{1,0:T(8,128)(2,1)S(1)}, bf16[200,512]{1,0:T(8,128)(2,1)S(1)}, u32[]{:S(2)}, u32[]{:S(2)}) collective-permute-start(bf16[200,512]{1,0:T(8,128)(2,1)S(1)} %collective-permute-done.5.refs_2_), channel_id=1, source_target_pairs={{6,0},{4,2},{2,4},{0,6},{14,8},{12,10},{10,12},{8,14},{22,16},{20,... | collective-permute-start | bytes 614408 | tf_op jit(solution)/shard_map/ppermute | solution.py:395
  15.9 1.7 %collective-permute-done.1.refs_0_ = bf16[200,512]{1,0:T(8,128)(2,1)S(1)} collective-permute-done((bf16[200,512]{1,0:T(8,128)(2,1)}, bf16[200,512]{1,0:T(8,128)(2,1)S(1)}, u32[]{:S(2)}, u32[]{:S(2)}) %collective-permute-start.1) | collective-permute-done | bytes 204832 | tf_op jit(solution)/shard_map/ppermute | solution.py:395
  17.6 0.9 %collective-permute-start.2 = (bf16[200,512]{1,0:T(8,128)(2,1)S(1)}, bf16[200,512]{1,0:T(8,128)(2,1)S(1)}, u32[]{:S(2)}, u32[]{:S(2)}) collective-permute-start(bf16[200,512]{1,0:T(8,128)(2,1)S(1)} %collective-permute-done.1.refs_0_), channel_id=1, source_target_pairs={{6,0},{4,2},{2,4},{0,6},{14,8},{12,10},{10,12},{8,14},{22,16},{20,... | collective-permute-start | bytes 614408 | tf_op jit(solution)/shard_map/ppermute | solution.py:395
  18.5 0.7 sqrt.3.root_ref
  19.2 2.2 %copy-done = bf16[1,12,200,800]{3,2,1,0:T(8,128)(2,1)S(1)} copy-done((bf16[1,12,200,800]{3,2,1,0:T(8,128)(2,1)S(1)}, bf16[1,12,200,800]{3,2,1,0:T(8,128)(2,1)}, u32[]{:S(2)}) %copy-start) | copy-done | bytes 3840024
  21.4 1.1 %load.1 = (bf16[12,200,800]{2,1,0:T(8,128)(2,1)S(1)}, bf16[200,800]{1,0:T(8,128)(2,1)S(1)}) custom-call(s32[3]{0:T(128)S(1)} %pad_add_fusion.place_ref, bf16[1,12,200,800]{3,2,1,0:T(8,128)(2,1)S(1)} %copy-done), custom_call_target="tpu_custom_call" | custom-call | tf_op jit(solution)/shard_map/load/pallas_call | solution.py:125
  22.6 1.7 %shard_map.47 = (bf16[2,200,512]{2,1,0:T(8,128)(2,1)S(1)}, bf16[2,200,512]{2,1,0:T(8,128)(2,1)S(1)}) custom-call(s32[3]{0:T(128)S(1)} %pad_add_fusion.place_ref, f32[12]{0:T(128)S(1)} %sqrt.3.root_ref, bf16[12,200,800]{2,1,0:T(8,128)(2,1)S(1)} %get-tuple-element.24.margins_ref, bf16[200,512]{1,0:T(8,128)(2,1)S(1)} %collective-permute-done.9.refs_0_, ...), custom_call_target="tpu_custom_call" | custom-call | flops 655360000 | bytes 1280000 | tf_op jit(solution)/shard_map/pallas_call | solution.py:161
  24.6 0.9 %collective-permute-start.8 = (bf16[200,512]{1,0:T(8,128)(2,1)S(1)}, bf16[200,512]{1,0:T(8,128)(2,1)S(1)}, u32[]{:S(2)}, u32[]{:S(2)}) collective-permute-start(bf16[200,512]{1,0:T(8,128)(2,1)S(1)} %collective-permute-done.7.refs_3_), channel_id=1, source_target_pairs={{6,0},{4,2},{2,4},{0,6},{14,8},{12,10},{10,12},{8,14},{22,16},{20,... | collective-permute-start | bytes 614408 | tf_op jit(solution)/shard_map/ppermute | solution.py:395
  25.5 0.9 %collective-permute-done.3.refs_1_ = bf16[200,512]{1,0:T(8,128)(2,1)S(1)} collective-permute-done((bf16[200,512]{1,0:T(8,128)(2,1)S(1)}, bf16[200,512]{1,0:T(8,128)(2,1)S(1)}, u32[]{:S(2)}, u32[]{:S(2)}) %collective-permute-start.3) | collective-permute-done | bytes 204832 | tf_op jit(solution)/shard_map/ppermute | solution.py:395
  26.6 1.8 %shard_map.48 = (bf16[2,200,512]{2,1,0:T(8,128)(2,1)S(1)}, bf16[2,200,512]{2,1,0:T(8,128)(2,1)S(1)}) custom-call(s32[3]{0:T(128)S(1)} %pad_add_fusion.place_ref, f32[12]{0:T(128)S(1)} %sqrt.3.root_ref, bf16[12,200,800]{2,1,0:T(8,128)(2,1)S(1)} %get-tuple-element.24.margins_ref, bf16[200,512]{1,0:T(8,128)(2,1)S(1)} %collective-permute-done.1.refs_0_, ...), custom_call_target="tpu_custom_call" | custom-call | flops 655360000 | bytes 1280000 | tf_op jit(solution)/shard_map/pallas_call | solution.py:161
  28.4 1.6 %collective-permute-start.13 = (bf16[2,200,512]{2,1,0:T(8,128)(2,1)S(1)}, bf16[2,200,512]{2,1,0:T(8,128)(2,1)S(1)}, u32[]{:S(2)}, u32[]{:S(2)}) collective-permute-start(bf16[2,200,512]{2,1,0:T(8,128)(2,1)S(1)} %get-tuple-element.31.refs_3_), channel_id=1, source_target_pairs={{0,1},{1,0},{2,3},{3,2},{4,5},{5,4},{6,7},{7,6},{8,9},{9,8},{10,11... | collective-permute-start | bytes 1228808 | tf_op jit(solution)/shard_map/ppermute | solution.py:392
  30.5 1.1 %collective-permute-done.8.refs_3_.refs_1_ = bf16[200,512]{1,0:T(8,128)(2,1)S(1)} collective-permute-done((bf16[200,512]{1,0:T(8,128)(2,1)S(1)}, bf16[200,512]{1,0:T(8,128)(2,1)S(1)}, u32[]{:S(2)}, u32[]{:S(2)}) %collective-permute-start.8) | collective-permute-done | bytes 204832 | tf_op jit(solution)/shard_map/ppermute | solution.py:395
  31.6 4.4 %collective-permute-done.4.refs_1_ = bf16[200,512]{1,0:T(8,128)(2,1)S(1)} collective-permute-done((bf16[200,512]{1,0:T(8,128)(2,1)S(1)}, bf16[200,512]{1,0:T(8,128)(2,1)S(1)}, u32[]{:S(2)}, u32[]{:S(2)}) %collective-permute-start.4) | collective-permute-done | bytes 204832 | tf_op jit(solution)/shard_map/ppermute | solution.py:395
  36.0 1.8 %shard_map.46 = (bf16[2,200,512]{2,1,0:T(8,128)(2,1)S(1)}, bf16[1,200,512]{2,1,0:T(8,128)(2,1)S(1)}, bf16[1,200,512]{2,1,0:T(8,128)(2,1)S(1)}) custom-call(s32[3]{0:T(128)S(1)} %pad_add_fusion.place_ref, f32[12]{0:T(128)S(1)} %sqrt.3.root_ref, bf16[12,200,800]{2,1,0:T(8,128)(2,1)S(1)} %get-tuple-element.24.margins_ref, ...), custom_call_target="tpu_custom_call" | custom-call | flops 655360000 | bytes 1280000 | tf_op jit(solution)/shard_map/pallas_call | solution.py:161
  37.8 2.1 %collective-permute-start.12 = (bf16[1,200,512]{2,1,0:T(8,128)(2,1)S(1)}, bf16[1,200,512]{2,1,0:T(8,128)(2,1)S(1)}, u32[]{:S(2)}, u32[]{:S(2)}) collective-permute-start(bf16[1,200,512]{2,1,0:T(8,128)(2,1)S(1)} %get-tuple-element.26.refs_1_), channel_id=1, source_target_pairs={{0,1},{1,0},{2,3},{3,2},{4,5},{5,4},{6,7},{7,6},{8,9},{9,8},{10,11... | collective-permute-start | bytes 614408 | tf_op jit(solution)/shard_map/ppermute | solution.py:392
  39.9 1.1 %shard_map.49.refs_3_ = f32[2,200,200]{2,1,0:T(8,128)S(1)} custom-call(bf16[2,200,512]{2,1,0:T(8,128)(2,1)S(1)} %get-tuple-element.28.refs_0_, bf16[2,200,512]{2,1,0:T(8,128)(2,1)S(1)} %get-tuple-element.29.refs_1_, bf16[2,200,512]{2,1,0:T(8,128)(2,1)S(1)} %get-tuple-element.30.refs_2_.refs_0_, bf16[2,200,512]{2,1,0:T(8,128)(2,1)S(1)} %get-tuple-element.31.refs_3_), custom_call_target="tpu_custom_call" | custom-call | flops 655360000 | bytes 1638400 | tf_op jit(solution)/shard_map/pallas_call | solution.py:240
  41.0 12.2 %collective-permute-done.14.margin_ref = bf16[200,800]{1,0:T(8,128)(2,1)S(1)} collective-permute-done((bf16[200,800]{1,0:T(8,128)(2,1)S(1)}, bf16[200,800]{1,0:T(8,128)(2,1)S(1)}, u32[]{:S(2)}, u32[]{:S(2)}) %collective-permute-start.14) | collective-permute-done | bytes 320032 | tf_op jit(solution)/shard_map/ppermute | solution.py:392
  53.1 1.0 %extra.1.refs_3_ = bf16[1,200,512]{2,1,0:T(8,128)(2,1)S(1)} custom-call(s32[3]{0:T(128)S(1)} %pad_add_fusion.place_ref, f32[12]{0:T(128)S(1)} %sqrt.3.root_ref, bf16[200,800]{1,0:T(8,128)(2,1)S(1)} %collective-permute-done.14.margin_ref, bf16[200,512]{1,0:T(8,128)(2,1)S(1)} %collective-permute-done.6.refs_2_.refs_0_, ...), custom_call_target="tpu_custom_call" | custom-call | flops 163840000 | bytes 320000 | tf_op jit(solution)/shard_map/extra/pallas_call | solution.py:195
  54.2 0.6 shard_map.51
  54.8 0.8 %shard_map.52 = (f32[2,200,200]{2,1,0:T(8,128)S(1)}, f32[2,200,200]{2,1,0:T(8,128)S(1)}) custom-call(bf16[2,200,512]{2,1,0:T(8,128)(2,1)S(1)} %get-tuple-element.30.refs_2_.refs_0_, bf16[2,200,512]{2,1,0:T(8,128)(2,1)S(1)} %collective-permute-done.13.refs_1_, bf16[2,200,512]{2,1,0:T(8,128)(2,1)S(1)} %get-tuple-element.25.refs_0_.refs_2_, ...), custom_call_target="tpu_custom_call" | custom-call | flops 491520000 | bytes 1228800 | tf_op jit(solution)/shard_map/pallas_call | solution.py:276
  55.6 0.8 %collective-permute-done.12.refs_1_ = bf16[1,200,512]{2,1,0:T(8,128)(2,1)S(1)} collective-permute-done((bf16[1,200,512]{2,1,0:T(8,128)(2,1)S(1)}, bf16[1,200,512]{2,1,0:T(8,128)(2,1)S(1)}, u32[]{:S(2)}, u32[]{:S(2)}) %collective-permute-start.12) | collective-permute-done | bytes 204832 | tf_op jit(solution)/shard_map/ppermute | solution.py:392
  57.4 0.6 shard_map.50
  58.0 1.6 %collective-permute-start.11 = (bf16[200,200]{1,0:T(8,128)(2,1)S(1)}, bf16[200,200]{1,0:T(8,128)(2,1)S(1)}, u32[]{:S(2)}, u32[]{:S(2)}) collective-permute-start(bf16[200,200]{1,0:T(8,128)(2,1)S(1)} %get-tuple-element.33), channel_id=1, source_target_pairs={{0,1},{1,0},{2,3},{3,2},{4,5},{5,4},{6,7},{7,6},{8,9},{9,8},{10,11... | collective-permute-start | bytes 240008 | tf_op jit(solution)/shard_map/ppermute | solution.py:392
  59.6 5.5 %collective-permute-done.11.packed_ref = bf16[200,200]{1,0:T(8,128)(2,1)S(1)} collective-permute-done((bf16[200,200]{1,0:T(8,128)(2,1)S(1)}, bf16[200,200]{1,0:T(8,128)(2,1)S(1)}, u32[]{:S(2)}, u32[]{:S(2)}) %collective-permute-start.11) | collective-permute-done | bytes 80032 | tf_op jit(solution)/shard_map/ppermute | solution.py:392
  65.1 1.1 %base.1 = (f32[200,512]{1,0:T(8,128)S(1)}, f32[200,512]{1,0:T(8,128)S(1)}) custom-call(bf16[200,512]{1,0:T(8,128)(2,1)S(1)} %bitcast.11, bf16[200,512]{1,0:T(8,128)(2,1)S(1)} %collective-permute-done.other_ref, f32[2,200,200]{2,1,0:T(8,128)S(1)} %get-tuple-element.32.total_ref, bf16[200,200]{1,0:T(8,128)(2,1)S(1)} %collective-permute-done.11.packed_ref, ...), custom_call_target="tpu_custom_call" | custom-call | flops 655360000 | bytes 819200 | tf_op jit(solution)/shard_map/base/pallas_call | solution.py:324
  66.2 5.4 %update.1 = f32[1,200,512]{2,1,0:T(8,128)} custom-call(bf16[200,512]{1,0:T(8,128)(2,1)S(1)} %bitcast.12, bf16[200,512]{1,0:T(8,128)(2,1)S(1)} %collective-permute-done.other_ref, f32[200,512]{1,0:T(8,128)S(1)} %get-tuple-element.40.base_ref, f32[200,512]{1,0:T(8,128)S(1)} %get-tuple-element.41.base_other_ref, ...), custom_call_target="tpu_custom_call" | custom-call | tf_op jit(solution)/shard_map/update/pallas_call | solution.py:366
  (20 shorter events, 2.9 us)
Async XLA Ops:
  0.0 8.3 %collective-permute-start = (bf16[200,512]{1,0:T(8,128)(2,1)}, bf16[200,512]{1,0:T(8,128)(2,1)S(1)}, u32[]{:S(2)}, u32[]{:S(2)}) collective-permute-start(bf16[200,512]{1,0:T(8,128)(2,1)} %bitcast.7), channel_id=1, source_target_pairs={{0,1},{1,0},{2,3},{3,2},{4,5},{5,4},{6,7},{7,6},{8,9},{9,8},{10,11... | collective-permute-start | bytes 614408 | tf_op jit(solution)/shard_map/ppermute | solution.py:392
  3.0 8.3 %collective-permute-start.9 = (bf16[200,512]{1,0:T(8,128)(2,1)}, bf16[200,512]{1,0:T(8,128)(2,1)S(1)}, u32[]{:S(2)}, u32[]{:S(2)}) collective-permute-start(bf16[200,512]{1,0:T(8,128)(2,1)} %bitcast.8), channel_id=1, source_target_pairs={{6,0},{4,2},{2,4},{0,6},{14,8},{12,10},{10,12},{8,14},{22,16},{20,... | collective-permute-start | bytes 614408 | tf_op jit(solution)/shard_map/ppermute | solution.py:395
  3.6 10.9 %collective-permute-start.5 = (bf16[200,512]{1,0:T(8,128)(2,1)}, bf16[200,512]{1,0:T(8,128)(2,1)S(1)}, u32[]{:S(2)}, u32[]{:S(2)}) collective-permute-start(bf16[200,512]{1,0:T(8,128)(2,1)} %bitcast.9), channel_id=1, source_target_pairs={{26,0},{24,2},{30,4},{28,6},{2,8},{0,10},{6,12},{4,14},{10,16},{8,... | collective-permute-start | bytes 614408 | tf_op jit(solution)/shard_map/ppermute | solution.py:395
  5.8 11.8 %collective-permute-start.1 = (bf16[200,512]{1,0:T(8,128)(2,1)}, bf16[200,512]{1,0:T(8,128)(2,1)S(1)}, u32[]{:S(2)}, u32[]{:S(2)}) collective-permute-start(bf16[200,512]{1,0:T(8,128)(2,1)} %bitcast.10), channel_id=1, source_target_pairs={{10,0},{8,2},{14,4},{12,6},{18,8},{16,10},{22,12},{20,14},{26,16},... | collective-permute-start | bytes 614408 | tf_op jit(solution)/shard_map/ppermute | solution.py:395
  8.3 14.3 %collective-permute-start.10 = (bf16[200,512]{1,0:T(8,128)(2,1)S(1)}, bf16[200,512]{1,0:T(8,128)(2,1)S(1)}, u32[]{:S(2)}, u32[]{:S(2)}) collective-permute-start(bf16[200,512]{1,0:T(8,128)(2,1)S(1)} %collective-permute-done.other_ref), channel_id=1, source_target_pairs={{6,0},{4,2},{2,4},{0,6},{14,8},{12,10},{10,12},{8,14},{22,16},{20,... | collective-permute-start | bytes 614408 | tf_op jit(solution)/shard_map/ppermute | solution.py:395
  8.6 16.0 %collective-permute-start.7 = (bf16[200,512]{1,0:T(8,128)(2,1)S(1)}, bf16[200,512]{1,0:T(8,128)(2,1)S(1)}, u32[]{:S(2)}, u32[]{:S(2)}) collective-permute-start(bf16[200,512]{1,0:T(8,128)(2,1)S(1)} %collective-permute-done.other_ref), channel_id=1, source_target_pairs={{26,0},{24,2},{30,4},{28,6},{2,8},{0,10},{6,12},{4,14},{10,16},{8,... | collective-permute-start | bytes 614408 | tf_op jit(solution)/shard_map/ppermute | solution.py:395
  11.3 15.1 %collective-permute-start.3 = (bf16[200,512]{1,0:T(8,128)(2,1)S(1)}, bf16[200,512]{1,0:T(8,128)(2,1)S(1)}, u32[]{:S(2)}, u32[]{:S(2)}) collective-permute-start(bf16[200,512]{1,0:T(8,128)(2,1)S(1)} %collective-permute-done.other_ref), channel_id=1, source_target_pairs={{10,0},{8,2},{14,4},{12,6},{18,8},{16,10},{22,12},{20,14},{26,16},... | collective-permute-start | bytes 614408 | tf_op jit(solution)/shard_map/ppermute | solution.py:395
  14.6 13.8 %collective-permute-start.6 = (bf16[200,512]{1,0:T(8,128)(2,1)S(1)}, bf16[200,512]{1,0:T(8,128)(2,1)S(1)}, u32[]{:S(2)}, u32[]{:S(2)}) collective-permute-start(bf16[200,512]{1,0:T(8,128)(2,1)S(1)} %collective-permute-done.5.refs_2_), channel_id=1, source_target_pairs={{6,0},{4,2},{2,4},{0,6},{14,8},{12,10},{10,12},{8,14},{22,16},{20,... | collective-permute-start | bytes 614408 | tf_op jit(solution)/shard_map/ppermute | solution.py:395
  17.6 12.4 %collective-permute-start.2 = (bf16[200,512]{1,0:T(8,128)(2,1)S(1)}, bf16[200,512]{1,0:T(8,128)(2,1)S(1)}, u32[]{:S(2)}, u32[]{:S(2)}) collective-permute-start(bf16[200,512]{1,0:T(8,128)(2,1)S(1)} %collective-permute-done.1.refs_0_), channel_id=1, source_target_pairs={{6,0},{4,2},{2,4},{0,6},{14,8},{12,10},{10,12},{8,14},{22,16},{20,... | collective-permute-start | bytes 614408 | tf_op jit(solution)/shard_map/ppermute | solution.py:395
  19.2 2.2 %copy-start = (bf16[1,12,200,800]{3,2,1,0:T(8,128)(2,1)S(1)}, bf16[1,12,200,800]{3,2,1,0:T(8,128)(2,1)}, u32[]{:S(2)}) copy-start(bf16[1,12,200,800]{3,2,1,0:T(8,128)(2,1)} %margins_ref.1) | copy-start | bytes 11520004
  24.3 29.9 %collective-permute-start.15 = (bf16[2,200,512]{2,1,0:T(8,128)(2,1)S(1)}, bf16[2,200,512]{2,1,0:T(8,128)(2,1)S(1)}, u32[]{:S(2)}, u32[]{:S(2)}) collective-permute-start(bf16[2,200,512]{2,1,0:T(8,128)(2,1)S(1)} %get-tuple-element.29.refs_1_), channel_id=1, source_target_pairs={{0,1},{1,0},{2,3},{3,2},{4,5},{5,4},{6,7},{7,6},{8,9},{9,8},{10,11... | collective-permute-start | bytes 1228808 | tf_op jit(solution)/shard_map/ppermute | solution.py:392
  24.6 7.1 %collective-permute-start.8 = (bf16[200,512]{1,0:T(8,128)(2,1)S(1)}, bf16[200,512]{1,0:T(8,128)(2,1)S(1)}, u32[]{:S(2)}, u32[]{:S(2)}) collective-permute-start(bf16[200,512]{1,0:T(8,128)(2,1)S(1)} %collective-permute-done.7.refs_3_), channel_id=1, source_target_pairs={{6,0},{4,2},{2,4},{0,6},{14,8},{12,10},{10,12},{8,14},{22,16},{20,... | collective-permute-start | bytes 614408 | tf_op jit(solution)/shard_map/ppermute | solution.py:395
  26.4 9.7 %collective-permute-start.4 = (bf16[200,512]{1,0:T(8,128)(2,1)S(1)}, bf16[200,512]{1,0:T(8,128)(2,1)S(1)}, u32[]{:S(2)}, u32[]{:S(2)}) collective-permute-start(bf16[200,512]{1,0:T(8,128)(2,1)S(1)} %collective-permute-done.3.refs_1_), channel_id=1, source_target_pairs={{6,0},{4,2},{2,4},{0,6},{14,8},{12,10},{10,12},{8,14},{22,16},{20,... | collective-permute-start | bytes 614408 | tf_op jit(solution)/shard_map/ppermute | solution.py:395
  28.4 26.4 %collective-permute-start.13 = (bf16[2,200,512]{2,1,0:T(8,128)(2,1)S(1)}, bf16[2,200,512]{2,1,0:T(8,128)(2,1)S(1)}, u32[]{:S(2)}, u32[]{:S(2)}) collective-permute-start(bf16[2,200,512]{2,1,0:T(8,128)(2,1)S(1)} %get-tuple-element.31.refs_3_), channel_id=1, source_target_pairs={{0,1},{1,0},{2,3},{3,2},{4,5},{5,4},{6,7},{7,6},{8,9},{9,8},{10,11... | collective-permute-start | bytes 1228808 | tf_op jit(solution)/shard_map/ppermute | solution.py:392
  30.0 23.2 %collective-permute-start.14 = (bf16[200,800]{1,0:T(8,128)(2,1)S(1)}, bf16[200,800]{1,0:T(8,128)(2,1)S(1)}, u32[]{:S(2)}, u32[]{:S(2)}) collective-permute-start(bf16[200,800]{1,0:T(8,128)(2,1)S(1)} %get-tuple-element.34), channel_id=1, source_target_pairs={{0,1},{1,0},{2,3},{3,2},{4,5},{5,4},{6,7},{7,6},{8,9},{9,8},{10,11... | collective-permute-start | bytes 960008 | tf_op jit(solution)/shard_map/ppermute | solution.py:392
  37.8 18.6 %collective-permute-start.12 = (bf16[1,200,512]{2,1,0:T(8,128)(2,1)S(1)}, bf16[1,200,512]{2,1,0:T(8,128)(2,1)S(1)}, u32[]{:S(2)}, u32[]{:S(2)}) collective-permute-start(bf16[1,200,512]{2,1,0:T(8,128)(2,1)S(1)} %get-tuple-element.26.refs_1_), channel_id=1, source_target_pairs={{0,1},{1,0},{2,3},{3,2},{4,5},{5,4},{6,7},{7,6},{8,9},{9,8},{10,11... | collective-permute-start | bytes 614408 | tf_op jit(solution)/shard_map/ppermute | solution.py:392
  41.0 24.1 %copy-start.1 = (bf16[1,200,512]{2,1,0:T(8,128)(2,1)S(1)}, bf16[1,200,512]{2,1,0:T(8,128)(2,1)}, u32[]{:S(2)}) copy-start(bf16[1,200,512]{2,1,0:T(8,128)(2,1)} %param.5) | copy-start | bytes 614404
  56.8 9.3 %collective-permute-start.16 = (bf16[2,200,200]{2,1,0:T(8,128)(2,1)S(1)}, bf16[2,200,200]{2,1,0:T(8,128)(2,1)S(1)}, u32[]{:S(2)}, u32[]{:S(2)}) collective-permute-start(bf16[2,200,200]{2,1,0:T(8,128)(2,1)S(1)} %get-tuple-element.42), channel_id=1, source_target_pairs={{0,1},{1,0},{2,3},{3,2},{4,5},{5,4},{6,7},{7,6},{8,9},{9,8},{10,11... | collective-permute-start | bytes 480008 | tf_op jit(solution)/shard_map/ppermute | solution.py:392
  58.0 7.0 %collective-permute-start.11 = (bf16[200,200]{1,0:T(8,128)(2,1)S(1)}, bf16[200,200]{1,0:T(8,128)(2,1)S(1)}, u32[]{:S(2)}, u32[]{:S(2)}) collective-permute-start(bf16[200,200]{1,0:T(8,128)(2,1)S(1)} %get-tuple-element.33), channel_id=1, source_target_pairs={{0,1},{1,0},{2,3},{3,2},{4,5},{5,4},{6,7},{7,6},{8,9},{9,8},{10,11... | collective-permute-start | bytes 240008 | tf_op jit(solution)/shard_map/ppermute | solution.py:392

commit v5 on v3

v5 whole, which is shorter than its diff:
```python
import functools
import math

import jax
import jax.numpy as jnp
from jax import lax
from jax.experimental import pallas as pl
from jax.experimental.pallas import tpu as pltpu
from jax.sharding import PartitionSpec as P


SHELL_VECTORS = (
    (1, 1, 0),
    (1, -1, 0),
    (-1, 1, 0),
    (-1, -1, 0),
    (1, 0, 1),
    (1, 0, -1),
    (-1, 0, 1),
    (-1, 0, -1),
    (0, 1, 1),
    (0, 1, -1),
    (0, -1, 1),
    (0, -1, -1),
)
BATCH = 4
SHIPPED = 2
VMEM = pl.BlockSpec(memory_space=pltpu.VMEM)
LIMIT = pltpu.CompilerParams(vmem_limit_bytes=20 * 2**20)
SMEM = pl.BlockSpec(memory_space=pltpu.SMEM)
F32 = jnp.float32
BF16 = jnp.bfloat16
NT = (((1,), (1,)), ((), ()))
TN = (((0,), (0,)), ((), ()))


def grid_shape(point_count):
    size_y = min(4, point_count // 8)
    return (4, size_y, point_count // (4 * size_y))


def displacement(shell, point_count):
    return tuple(step % size for step, size in zip(shell, grid_shape(point_count)))


def fetch_pairs(shift, point_count):
    size_x, size_y, size_z = grid_shape(point_count)
    pairs = []
    for x in range(size_x):
        for y in range(size_y):
            for z in range(size_z):
                source = ((x + shift[0]) % size_x, (y + shift[1]) % size_y, (z + shift[2]) % size_z)
                pairs.append(
                    (
                        (source[0] * size_y + source[1]) * size_z + source[2],
                        (x * size_y + y) * size_z + z,
                    )
                )
    return pairs


def dot(left, right, dims=None):
    if dims is None:
        return jnp.dot(left, right, preferred_element_type=F32)
    return lax.dot_general(left, right, dims, preferred_element_type=F32)


def split(value):
    high = value.astype(BF16)
    return high, (value - high.astype(F32)).astype(BF16)


def dot_exact_right(left, right, dims=None):
    high, low = split(left)
    return dot(high, right, dims) + dot(low, right, dims)


def dot_split(left, right, dims=None):
    left_high, left_low = split(left)
    right_high, right_low = split(right)
    return (
        dot(left_high, right_high, dims)
        + dot(left_high, right_low, dims)
        + dot(left_low, right_high, dims)
    )


def times_minus_i(value):
    half = value.shape[-1] // 2
    return jnp.concatenate([value[:, half:], -value[:, :half]], axis=1)


def times_i(value):
    half = value.shape[-1] // 2
    return jnp.concatenate([-value[:, half:], value[:, :half]], axis=1)


def stack_complex(mine, other, side, rows_ref, stacked_ref):
    rows = mine.shape[0]
    rows_ref[pl.ds(pl.multiple_of(side * rows, 8), rows), :] = mine.astype(F32)
    rows_ref[pl.ds(pl.multiple_of((1 - side) * rows, 8), rows), :] = other.astype(F32)
    whole = rows_ref[...]
    stacked_ref[: 2 * rows, :] = whole.astype(BF16)
    stacked_ref[2 * rows :, :] = times_i(whole).astype(BF16)


def masked_block(margin, stacked, root, limit):
    inside = lax.broadcasted_iota(jnp.int32, (margin.shape[0], 1), 0) < limit
    return jnp.where(inside, dot(margin, stacked) * root, 0.0).astype(BF16)


def project_kernel(groups, first, counts, limit_place, *refs):
    place_ref, root_ref, margins_ref, *refs = refs
    halves = refs[: 2 * len(groups)]
    *out_refs, rows_ref, stacked_ref = refs[2 * len(groups) :]
    side, limit = place_ref[0], place_ref[limit_place]
    for number, members in enumerate(groups):
        mine, other = halves[2 * number][...], halves[2 * number + 1][...]
        stack_complex(mine, other, side, rows_ref, stacked_ref)
        for member in members:
            block = masked_block(
                margins_ref[member], stacked_ref[...], root_ref[first + member], limit
            )
            if member < counts[0]:
                out_refs[0][member] = block
            else:
                out_refs[1][member - counts[0]] = block


def project(place, roots, margins, first, groups, halves, counts, limit_place):
    rows, double = margins.shape[1:]
    width = halves[0].shape[-1]
    return pl.pallas_call(
        functools.partial(project_kernel, groups, first, counts, limit_place),
        in_specs=[SMEM, SMEM, VMEM, *([VMEM] * len(halves))],
        out_specs=[VMEM] * len(counts),
        out_shape=[jax.ShapeDtypeStruct((count, rows, width), BF16) for count in counts],
        scratch_shapes=[pltpu.VMEM((2 * rows, width), F32), pltpu.VMEM((double, width), BF16)],
        cost_estimate=pl.CostEstimate(
            flops=2 * sum(counts) * rows * double * width,
            bytes_accessed=2 * sum(counts) * rows * double,
            transcendentals=0,
        ),
        compiler_params=LIMIT,
    )(place, roots, margins, *halves)


def gather_own_kernel(count, has_total, *refs):
    blocks, refs = refs[:count], refs[count:]
    total_ref = refs[-1]
    rows = blocks[0].shape[1]
    real = jnp.zeros((rows, rows), F32)
    imag = jnp.zeros((rows, rows), F32)
    if has_total:
        real, imag = refs[0][0], refs[0][1]
    for block_ref in blocks:
        for place in range(block_ref.shape[0]):
            block = block_ref[place]
            real += dot(block, block, NT)
            imag += dot(times_minus_i(block), block, NT)
    total_ref[0], total_ref[1] = real, imag


def gather_own(blocks, before):
    rows, width = blocks[0].shape[1:]
    operands = list(blocks) + ([] if before is None else [before])
    return pl.pallas_call(
        functools.partial(gather_own_kernel, len(blocks), before is not None),
        in_specs=[VMEM] * len(operands),
        out_specs=VMEM,
        out_shape=jax.ShapeDtypeStruct((2, rows, rows), F32),
        cost_estimate=pl.CostEstimate(
            flops=8 * len(blocks) * rows * rows * width,
            bytes_accessed=4 * len(blocks) * rows * width,
            transcendentals=0,
        ),
        compiler_params=LIMIT,
    )(*operands)


def add_received(sums, keep_ref, got_ref):
    for place in range(keep_ref.shape[0]):
        keep, got = keep_ref[place], got_ref[place]
        sums[0] += dot(got, got, NT)
        sums[1] += dot(times_minus_i(got), got, NT)
        sums[2] += dot(keep, got, NT)
        sums[3] += dot(times_minus_i(keep), got, NT)
    return sums


def gather_kernel(count, has_total, *refs):
    blocks, refs = refs[: 2 * count], refs[2 * count :]
    total_ref = refs[-1]
    rows = blocks[0].shape[1]
    sums = [jnp.zeros((rows, rows), F32) for _ in range(4)]
    if has_total:
        sums = [refs[0][place] for place in range(4)]
    for place in range(count):
        sums = add_received(sums, blocks[2 * place], blocks[2 * place + 1])
    for place in range(4):
        total_ref[place] = sums[place]


def gather(pairs, before):
    rows, width = pairs[0][0].shape[1:]
    operands = [block for pair in pairs for block in pair] + ([] if before is None else [before])
    terms = sum(pair[0].shape[0] for pair in pairs)
    return pl.pallas_call(
        functools.partial(gather_kernel, len(pairs), before is not None),
        in_specs=[VMEM] * len(operands),
        out_specs=VMEM,
        out_shape=jax.ShapeDtypeStruct((4, rows, rows), F32),
        cost_estimate=pl.CostEstimate(
            flops=8 * terms * rows * rows * width,
            bytes_accessed=4 * terms * rows * width,
            transcendentals=0,
        ),
        compiler_params=LIMIT,
    )(*operands)


def complex_stack(value):
    return jnp.concatenate([value, times_i(value)], axis=0)


def update_kernel(
    scale, own_ref, other_ref, total_ref, before_ref, keep_ref, got_ref, out_ref, sent_ref
):
    own, other = own_ref[...], other_ref[...]
    half = own.shape[1] // 2
    own_i, other_i = times_i(own.astype(F32)).astype(BF16), times_i(other.astype(F32)).astype(BF16)
    sums = add_received([before_ref[place] for place in range(4)], keep_ref, got_ref)
    other_real, other_imag, real, imag = sums
    product = (
        dot_exact_right(total_ref[0], own)
        + dot_exact_right(total_ref[1], own_i)
        + dot_exact_right(real, other)
        + dot_exact_right(imag, other_i)
    )
    product_other = (
        dot_exact_right(other_real, other)
        + dot_exact_right(other_imag, other_i)
        + dot_exact_right(real, own, TN)
        - dot_exact_right(imag, own_i, TN)
    )
    blocks = dot_split(product, product, TN) + dot_split(product_other, product_other, TN)
    real = blocks[:half, :half] + blocks[half:, half:]
    imag = blocks[:half, half:] - blocks[half:, :half]
    diagonal = lax.broadcasted_iota(jnp.int32, (half, 2 * half), 0) == lax.broadcasted_iota(
        jnp.int32, (half, 2 * half), 1
    )
    gram = jnp.concatenate([real, imag], axis=1)
    squares = jnp.sum(jnp.where(diagonal, gram, 0.0))
    size = jnp.full((1, 1), 2.0 * squares / half + 1e-06, F32)
    scaling = lax.rsqrt(size)
    gram = gram * (scaling * scaling)
    identity = jnp.where(diagonal, 1.0, 0.0)
    gram_two = dot_split(gram, complex_stack(gram))
    left = 2.25 * identity - 1.5 * gram + 0.25 * gram_two
    right = 1.5 * gram - 0.5 * gram_two
    factor = 2.25 * identity - 0.75 * gram - 0.5 * dot_split(left, complex_stack(right))
    factor = factor * (scaling * scale)
    factor = complex_stack(factor)
    sent_ref[...] = dot_split(product_other, factor).astype(BF16)
    out_ref[...] = dot_split(product, factor)


def update(scale, own, other, total, before, keep, got):
    rows, width = own.shape
    return pl.pallas_call(
        functools.partial(update_kernel, scale),
        in_specs=[VMEM] * 6,
        out_specs=[VMEM] * 2,
        out_shape=[
            jax.ShapeDtypeStruct((rows, width), F32),
            jax.ShapeDtypeStruct((rows, width), BF16),
        ],
        name="update",
        compiler_params=LIMIT,
    )(own, other, total, before, keep, got)


def batch_shifts(batch, point_count):
    shifts = {}
    for member in range(BATCH):
        shift = displacement(SHELL_VECTORS[batch * BATCH + member], point_count)
        shifts.setdefault(shift, []).append(member)
    return shifts


def on_device(margins, subspace, shell_weights, window_count):
    point_count = lax.axis_size("kpt")
    point_index = lax.axis_index("kpt")
    side = lax.axis_index("band")
    rows = subspace.shape[1]
    plan = [batch_shifts(batch, point_count) for batch in range(3)]

    owner = point_index % 2 == side
    to_owner = [(2 * point + 1 - point % 2, 2 * point + point % 2) for point in range(point_count)]
    from_owner = [(target, source) for source, target in to_owner]

    def give(value, route=to_owner):
        return lax.ppermute(value, ("kpt", "band"), route)

    def fetch(value, shift):
        return lax.ppermute(value, "kpt", fetch_pairs(shift, point_count))

    offset = side * rows
    place = jnp.stack([side, window_count[0] - offset, window_count[0] - (rows - offset)])
    roots = jnp.sqrt(shell_weights)
    own = subspace[0]
    other = lax.ppermute(own, "band", [(0, 1), (1, 0)])
    parts = [margins[0, batch * BATCH : (batch + 1) * BATCH] for batch in range(3)]
    shipped = margins[0, SHIPPED:BATCH]
    shipped = give(shipped)
    halves = {}
    for part, value in (("own", own), ("other", other)):
        for batch in (2, 1):
            for shift in plan[batch]:
                halves[batch, part, shift] = fetch(value, shift)
        for shift in plan[0]:
            near = displacement((shift[0], 0, 1), point_count)
            step = displacement((0, shift[1], -1), point_count)
            halves[0, part, shift] = fetch(halves[1, part, near], step)
    blocks, got, operands = {}, {}, {}
    for batch in (2, 1, 0):
        operands[batch] = []
        for shift in plan[batch]:
            operands[batch] += [halves[batch, "own", shift], halves[batch, "other", shift]]
        blocks[batch] = project(
            place,
            roots,
            parts[batch],
            batch * BATCH,
            list(plan[batch].values()),
            operands[batch],
            (SHIPPED, BATCH - SHIPPED) if batch == 0 else (BATCH,),
            1,
        )
        got[batch] = give(blocks[batch][0])
    groups, near = [], []
    for shift, members in plan[0].items():
        late = [member - SHIPPED for member in members if member >= SHIPPED]
        if late:
            groups.append(late)
            near += [halves[0, "own", shift], halves[0, "other", shift]]
    (got_extra,) = project(place, roots, shipped, SHIPPED, groups, near, (BATCH - SHIPPED,), 2)
    total = gather_own([blocks[2][0], blocks[1][0]], None)
    total = gather_own(blocks[0], total)
    crossed = gather([(blocks[2][0], got[2])], None)
    crossed = gather([(blocks[1][0], got[1]), (blocks[0][1], got_extra)], crossed)
    scale = math.sqrt(rows * lax.axis_size("band"))
    mine, sent = update(scale, own, other, total, crossed, blocks[0][0], got[0])
    theirs = give(sent, from_owner)
    return jnp.where(owner, mine, theirs.astype(F32))[None]


def solution(mesh):
    return jax.shard_map(
        on_device,
        mesh=mesh,
        in_specs=(P("kpt", None, "band", None), P("kpt", "band", None), P(), P("kpt")),
        out_specs=P("kpt", "band", None),
        check_vma=False,
    )
```

time: 74.8 us -> 75.8 us (1.013)
  waiting for transfers between devices: 36.2 us -> 26 us
  local copies, waits for them, and re-layouts: 2.89 us -> 6.5 us
  starting transfers between devices: 20.1 us -> 23.6 us
  Pallas kernels: 14.7 us -> 17.6 us
  other arithmetic: 0.07 us -> 0.89 us
    ppermute x6, waiting for transfers between devices: 25 us -> 11.4 us  [the longest x5 10.9 us: give(): return lax.ppermute(value, ('kpt', 'band'), route)]
    squeeze x0 -> x2, local copies, waits for them, and re-layouts: none -> 4.87 us  [the longest x1 3.7 us: on_device(): margins[0, batch * BATCH:(batch + 1) * BATCH]]
    ppermute x10, waiting for transfers between devices: 11.2 us -> 14.6 us  [fetch(): return lax.ppermute(value, 'kpt', fetch_pairs(shift, point_count))]
    pallas_call x8, Pallas kernels: 8.81 us -> 11.5 us  [the longest x4 7.3 us: project(): pl.pallas_call(functools.partial(project_kernel, groups, first, counts, l...]
    ppermute x6, starting transfers between devices: 7.88 us -> 9.63 us  [the longest x5 6.63 us: give(): return lax.ppermute(value, ('kpt', 'band'), route)]
    ppermute x10, starting transfers between devices: 12.2 us -> 14 us  [fetch(): return lax.ppermute(value, 'kpt', fetch_pairs(shift, point_count))]
    broadcast_in_dim x0 -> x1, other arithmetic: none -> 0.81 us  [on_device(): return jnp.where(owner, mine, theirs.astype(F32))[None]]
    unnamed x4 -> x10, local copies, waits for them, and re-layouts: 2.22 us -> 1.62 us
  transfers between devices with their start and end apart: 16 -> 16, of which waited for: 10 -> 8; matrix products, arithmetic and copies ran while one was open for 1% -> 7% of each run, Pallas kernels for 12% -> 15%
where the time goes in v5:
time: 75.8 us; the launch traced here: 75.4 us
  waiting for transfers between devices  26 us (34%)
  starting transfers between devices  23.6 us (31%)
  Pallas kernels  17.6 us (23%)
  local copies, waits for them, and re-layouts  6.5 us (9%)
  other arithmetic  0.89 us (1%)
  between operations  0.88 us (1%)
    ppermute x10, waiting for transfers between devices, fetch(): return lax.ppermute(value, 'kpt', fetch_pairs(shift, point_count))  14.6 us
    ppermute x10, starting transfers between devices, fetch(): return lax.ppermute(value, 'kpt', fetch_pairs(shift, point_count))  14 us
    ppermute x5, waiting for transfers between devices, give(): return lax.ppermute(value, ('kpt', 'band'), route)  10.9 us
    pallas_call x4, Pallas kernels, project(): pl.pallas_call(functools.partial(project_kernel, groups, first, counts, l...  7.3 us
    ppermute x5, starting transfers between devices, give(): return lax.ppermute(value, ('kpt', 'band'), route)  6.63 us
    pallas_call x1, Pallas kernels, update(): pl.pallas_call(functools.partial(update_kernel, scale), in_specs=[VMEM] *...  6.02 us
    squeeze x1, local copies, waits for them, and re-layouts, on_device(): margins[0, batch * BATCH:(batch + 1) * BATCH]  3.7 us
    ppermute x1, starting transfers between devices, on_device(): other = lax.ppermute(own, 'band', [(0, 1), (1, 0)])  3 us
  transfers between devices with their start and end apart: 16, of which 8 were waited for; matrix products, arithmetic and copies ran while one was open for 7% of the time, Pallas kernels for 15%

profile of v5, /device:TPU:0, one launch (start us, length us, event | category | flops | bytes accessed | tf_op | source)
XLA Modules:
  0.0 75.4 jit_solution(2823012841426259619)
XLA Ops:
  0.0 3.0 %collective-permute-start = (bf16[200,512]{1,0:T(8,128)(2,1)}, bf16[200,512]{1,0:T(8,128)(2,1)S(1)}, u32[]{:S(2)}, u32[]{:S(2)}) collective-permute-start(bf16[200,512]{1,0:T(8,128)(2,1)} %bitcast.17), channel_id=1, source_target_pairs={{0,1},{1,0},{2,3},{3,2},{4,5},{5,4},{6,7},{7,6},{8,9},{9,8},{10,11... | collective-permute-start | bytes 614408 | tf_op jit(solution)/shard_map/ppermute | solution.py:312
  3.0 2.8 %collective-permute-start.1 = (bf16[200,512]{1,0:T(8,128)(2,1)}, bf16[200,512]{1,0:T(8,128)(2,1)S(1)}, u32[]{:S(2)}, u32[]{:S(2)}) collective-permute-start(bf16[200,512]{1,0:T(8,128)(2,1)} %bitcast.18), channel_id=1, source_target_pairs={{10,0},{8,2},{14,4},{12,6},{18,8},{16,10},{22,12},{20,14},{26,16},... | collective-permute-start | bytes 614408 | tf_op jit(solution)/shard_map/ppermute | solution.py:306
  5.8 2.1 %collective-permute-start.9 = (bf16[200,512]{1,0:T(8,128)(2,1)}, bf16[200,512]{1,0:T(8,128)(2,1)}, u32[]{:S(2)}, u32[]{:S(2)}) collective-permute-start(bf16[200,512]{1,0:T(8,128)(2,1)} %bitcast.20), channel_id=1, source_target_pairs={{6,0},{4,2},{2,4},{0,6},{14,8},{12,10},{10,12},{8,14},{22,16},{20,... | collective-permute-start | bytes 614408 | tf_op jit(solution)/shard_map/ppermute | solution.py:306
  8.3 3.1 %collective-permute-start.3 = (bf16[200,512]{1,0:T(8,128)(2,1)S(1)}, bf16[200,512]{1,0:T(8,128)(2,1)S(1)}, u32[]{:S(2)}, u32[]{:S(2)}) collective-permute-start(bf16[200,512]{1,0:T(8,128)(2,1)S(1)} %collective-permute-done.other_ref), channel_id=1, source_target_pairs={{10,0},{8,2},{14,4},{12,6},{18,8},{16,10},{22,12},{20,14},{26,16},... | collective-permute-start | bytes 614408 | tf_op jit(solution)/shard_map/ppermute | solution.py:306
  11.4 0.7 copy-done.2
  12.0 2.0 %collective-permute-start.10 = (bf16[200,512]{1,0:T(8,128)(2,1)S(1)}, bf16[200,512]{1,0:T(8,128)(2,1)}, u32[]{:S(2)}, u32[]{:S(2)}) collective-permute-start(bf16[200,512]{1,0:T(8,128)(2,1)S(1)} %collective-permute-done.other_ref), channel_id=1, source_target_pairs={{6,0},{4,2},{2,4},{0,6},{14,8},{12,10},{10,12},{8,14},{22,16},{20,... | collective-permute-start | bytes 614408 | tf_op jit(solution)/shard_map/ppermute | solution.py:306
  14.0 3.7 %slice_bitcast_fusion = (bf16[4,200,800]{2,1,0:T(8,128)(2,1)S(1)}, bf16[4,200,800]{2,1,0:T(8,128)(2,1)S(1)}, bf16[4,200,800]{2,1,0:T(8,128)(2,1)}) fusion(bf16[1,12,200,800]{3,2,1,0:T(8,128)(2,1)} %param.4), kind=kLoop, calls=%fused_computation | loop fusion | bytes 7680000 | tf_op jit(solution)/shard_map/squeeze | solution.py:313
  18.5 1.5 %collective-permute-done.3.refs_4_ = bf16[200,512]{1,0:T(8,128)(2,1)S(1)} collective-permute-done((bf16[200,512]{1,0:T(8,128)(2,1)S(1)}, bf16[200,512]{1,0:T(8,128)(2,1)S(1)}, u32[]{:S(2)}, u32[]{:S(2)}) %collective-permute-start.3) | collective-permute-done | bytes 204832 | tf_op jit(solution)/shard_map/ppermute | solution.py:306
  20.0 1.7 %collective-permute-start.6 = (bf16[200,512]{1,0:T(8,128)(2,1)S(1)}, bf16[200,512]{1,0:T(8,128)(2,1)S(1)}, u32[]{:S(2)}, u32[]{:S(2)}) collective-permute-start(bf16[200,512]{1,0:T(8,128)(2,1)S(1)} %collective-permute-done.5.refs_5_), channel_id=1, source_target_pairs={{6,0},{4,2},{2,4},{0,6},{14,8},{12,10},{10,12},{8,14},{22,16},{20,... | collective-permute-start | bytes 614408 | tf_op jit(solution)/shard_map/ppermute | solution.py:306
  21.8 4.0 %collective-permute-done.7.refs_6_ = bf16[200,512]{1,0:T(8,128)(2,1)} collective-permute-done((bf16[200,512]{1,0:T(8,128)(2,1)S(1)}, bf16[200,512]{1,0:T(8,128)(2,1)}, u32[]{:S(2)}, u32[]{:S(2)}) %collective-permute-start.7) | collective-permute-done | bytes 204832 | tf_op jit(solution)/shard_map/ppermute | solution.py:306
  25.8 0.9 %copy-done.3 = bf16[200,512]{1,0:T(8,128)(2,1)S(1)} copy-done((bf16[200,512]{1,0:T(8,128)(2,1)S(1)}, bf16[200,512]{1,0:T(8,128)(2,1)}, u32[]{:S(2)}) %copy-start.3) | copy-done | bytes 204824
  26.7 2.1 %shard_map.48.refs_1_.refs_0_ = bf16[4,200,512]{2,1,0:T(8,128)(2,1)S(1)} custom-call(s32[3]{0:T(128)S(1)} %pad_add_fusion.refs_0_, f32[12]{0:T(128)S(1)} %sqrt.3.refs_1_, bf16[4,200,800]{2,1,0:T(8,128)(2,1)S(1)} %get-tuple-element.13.refs_2_, bf16[200,512]{1,0:T(8,128)(2,1)S(1)} %copy-done.3, bf16[200,512]{1,0:T(8,128)(2,1)S(1)} %collective-permute-done.3.refs_4_, ...), custom_call_target="tpu_custom_call" | custom-call | flops 655360000 | bytes 1280000 | tf_op jit(solution)/shard_map/pallas_call | solution.py:133
  28.8 1.3 %collective-permute-start.11 = (bf16[4,200,512]{2,1,0:T(8,128)(2,1)S(1)}, bf16[4,200,512]{2,1,0:T(8,128)(2,1)S(1)}, u32[]{:S(2)}, u32[]{:S(2)}) collective-permute-start(bf16[4,200,512]{2,1,0:T(8,128)(2,1)S(1)} %shard_map.48.refs_1_.refs_0_), channel_id=1, source_target_pairs={{1,0},{2,3},{5,4},{6,7},{9,8},{10,11},{13,12},{14,15},{17,16},{18,... | collective-permute-start | bytes 2457608 | tf_op jit(solution)/shard_map/ppermute | solution.py:303
  30.1 2.3 %shard_map.47.refs_0_ = bf16[4,200,512]{2,1,0:T(8,128)(2,1)S(1)} custom-call(s32[3]{0:T(128)S(1)} %pad_add_fusion.refs_0_, f32[12]{0:T(128)S(1)} %sqrt.3.refs_1_, bf16[4,200,800]{2,1,0:T(8,128)(2,1)S(1)} %get-tuple-element.14.refs_2_, bf16[200,512]{1,0:T(8,128)(2,1)} %collective-permute-done.9.refs_3_, bf16[200,512]{1,0:T(8,128)(2,1)} %collective-permute-done.10.refs_4_), custom_call_target="tpu_custom_call" | custom-call | flops 655360000 | bytes 1280000 | tf_op jit(solution)/shard_map/pallas_call | solution.py:133
  32.4 1.3 %collective-permute-start.13 = (bf16[4,200,512]{2,1,0:T(8,128)(2,1)S(1)}, bf16[4,200,512]{2,1,0:T(8,128)(2,1)S(1)}, u32[]{:S(2)}, u32[]{:S(2)}) collective-permute-start(bf16[4,200,512]{2,1,0:T(8,128)(2,1)S(1)} %shard_map.47.refs_0_), channel_id=1, source_target_pairs={{1,0},{2,3},{5,4},{6,7},{9,8},{10,11},{13,12},{14,15},{17,16},{18,... | collective-permute-start | bytes 2457608 | tf_op jit(solution)/shard_map/ppermute | solution.py:303
  33.7 1.2 %slice_bitcast_fusion.3 = bf16[2,200,800]{2,1,0:T(8,128)(2,1)S(1)} fusion(bf16[1,12,200,800]{3,2,1,0:T(8,128)(2,1)} %param.4), kind=kLoop, calls=%fused_computation.3 | loop fusion | bytes 1280000 | tf_op jit(solution)/shard_map/squeeze | solution.py:314
  34.9 1.3 %collective-permute-start.12 = (bf16[2,200,800]{2,1,0:T(8,128)(2,1)S(1)}, bf16[2,200,800]{2,1,0:T(8,128)(2,1)S(1)}, u32[]{:S(2)}, u32[]{:S(2)}) collective-permute-start(bf16[2,200,800]{2,1,0:T(8,128)(2,1)S(1)} %slice_bitcast_fusion.3), channel_id=1, source_target_pairs={{1,0},{2,3},{5,4},{6,7},{9,8},{10,11},{13,12},{14,15},{17,16},{18,... | collective-permute-start | bytes 1920008 | tf_op jit(solution)/shard_map/ppermute | solution.py:303
  36.2 2.3 %collective-permute-start.4 = (bf16[200,512]{1,0:T(8,128)(2,1)S(1)}, bf16[200,512]{1,0:T(8,128)(2,1)S(1)}, u32[]{:S(2)}, u32[]{:S(2)}) collective-permute-start(bf16[200,512]{1,0:T(8,128)(2,1)S(1)} %collective-permute-done.3.refs_4_), channel_id=1, source_target_pairs={{6,0},{4,2},{2,4},{0,6},{14,8},{12,10},{10,12},{8,14},{22,16},{20,... | collective-permute-start | bytes 614408 | tf_op jit(solution)/shard_map/ppermute | solution.py:306
  38.5 5.4 %collective-permute-done.4.refs_4_ = bf16[200,512]{1,0:T(8,128)(2,1)S(1)} collective-permute-done((bf16[200,512]{1,0:T(8,128)(2,1)S(1)}, bf16[200,512]{1,0:T(8,128)(2,1)S(1)}, u32[]{:S(2)}, u32[]{:S(2)}) %collective-permute-start.4) | collective-permute-done | bytes 204832 | tf_op jit(solution)/shard_map/ppermute | solution.py:306
  43.9 3.7 %collective-permute-done.8.refs_6_.refs_4_ = bf16[200,512]{1,0:T(8,128)(2,1)S(1)} collective-permute-done((bf16[200,512]{1,0:T(8,128)(2,1)}, bf16[200,512]{1,0:T(8,128)(2,1)S(1)}, u32[]{:S(2)}, u32[]{:S(2)}) %collective-permute-start.8) | collective-permute-done | bytes 204832 | tf_op jit(solution)/shard_map/ppermute | solution.py:306
  47.6 1.7 %shard_map.46 = (bf16[2,200,512]{2,1,0:T(8,128)(2,1)S(1)}, bf16[2,200,512]{2,1,0:T(8,128)(2,1)S(1)}) custom-call(s32[3]{0:T(128)S(1)} %pad_add_fusion.refs_0_, f32[12]{0:T(128)S(1)} %sqrt.3.refs_1_, bf16[4,200,800]{2,1,0:T(8,128)(2,1)S(1)} %copy-done, bf16[200,512]{1,0:T(8,128)(2,1)S(1)} %collective-permute-done.2.refs_3_, ...), custom_call_target="tpu_custom_call" | custom-call | flops 655360000 | bytes 1280000 | tf_op jit(solution)/shard_map/pallas_call | solution.py:133
  49.4 1.3 %collective-permute-start.14 = (bf16[2,200,512]{2,1,0:T(8,128)(2,1)S(1)}, bf16[2,200,512]{2,1,0:T(8,128)(2,1)S(1)}, u32[]{:S(2)}, u32[]{:S(2)}) collective-permute-start(bf16[2,200,512]{2,1,0:T(8,128)(2,1)S(1)} %get-tuple-element.9.refs_0_.keep_ref), channel_id=1, source_target_pairs={{1,0},{2,3},{5,4},{6,7},{9,8},{10,11},{13,12},{14,15},{17,16},{18,... | collective-permute-start | bytes 1228808 | tf_op jit(solution)/shard_map/ppermute | solution.py:303
  50.7 1.1 %shard_map.49.refs_2_ = f32[2,200,200]{2,1,0:T(8,128)S(1)} custom-call(bf16[4,200,512]{2,1,0:T(8,128)(2,1)S(1)} %shard_map.47.refs_0_, bf16[4,200,512]{2,1,0:T(8,128)(2,1)S(1)} %shard_map.48.refs_1_.refs_0_), custom_call_target="tpu_custom_call" | custom-call | flops 327680000 | bytes 819200 | tf_op jit(solution)/shard_map/pallas_call | solution.py:167
  51.7 0.6 shard_map.50.total_ref
  52.4 7.1 %collective-permute-done.12.refs_2_ = bf16[2,200,800]{2,1,0:T(8,128)(2,1)S(1)} collective-permute-done((bf16[2,200,800]{2,1,0:T(8,128)(2,1)S(1)}, bf16[2,200,800]{2,1,0:T(8,128)(2,1)S(1)}, u32[]{:S(2)}, u32[]{:S(2)}) %collective-permute-start.12) | collective-permute-done | bytes 640032 | tf_op jit(solution)/shard_map/ppermute | solution.py:303
  59.5 1.2 %shard_map.51.refs_3_ = bf16[2,200,512]{2,1,0:T(8,128)(2,1)S(1)} custom-call(s32[3]{0:T(128)S(1)} %pad_add_fusion.refs_0_, f32[12]{0:T(128)S(1)} %sqrt.3.refs_1_, bf16[2,200,800]{2,1,0:T(8,128)(2,1)S(1)} %collective-permute-done.12.refs_2_, bf16[200,512]{1,0:T(8,128)(2,1)S(1)} %collective-permute-done.6.refs_5_.refs_3_, ...), custom_call_target="tpu_custom_call" | custom-call | flops 327680000 | bytes 640000 | tf_op jit(solution)/shard_map/pallas_call | solution.py:133
  60.7 1.1 %shard_map.52.refs_4_ = f32[4,200,200]{2,1,0:T(8,128)S(1)} custom-call(bf16[4,200,512]{2,1,0:T(8,128)(2,1)S(1)} %shard_map.47.refs_0_, bf16[4,200,512]{2,1,0:T(8,128)(2,1)S(1)} %collective-permute-done.13.refs_1_), custom_call_target="tpu_custom_call" | custom-call | flops 655360000 | bytes 1638400 | tf_op jit(solution)/shard_map/pallas_call | solution.py:208
  61.8 1.5 %shard_map.53.before_ref = f32[4,200,200]{2,1,0:T(8,128)S(1)} custom-call(bf16[4,200,512]{2,1,0:T(8,128)(2,1)S(1)} %shard_map.48.refs_1_.refs_0_, bf16[4,200,512]{2,1,0:T(8,128)(2,1)S(1)} %collective-permute-done.11.refs_1_, bf16[2,200,512]{2,1,0:T(8,128)(2,1)S(1)} %get-tuple-element.10.refs_1_.refs_2_, bf16[2,200,512]{2,1,0:T(8,128)(2,1)S(1)} %shard_map.51.refs_3_, ...), custom_call_target="tpu_custom_call" | custom-call | flops 983040000 | bytes 2457600 | tf_op jit(solution)/shard_map/pallas_call | solution.py:208
  63.9 6.0 %update.1 = (f32[200,512]{1,0:T(8,128)S(1)}, bf16[200,512]{1,0:T(8,128)(2,1)S(1)}) custom-call(bf16[200,512]{1,0:T(8,128)(2,1)S(1)} %bitcast.21, bf16[200,512]{1,0:T(8,128)(2,1)S(1)} %collective-permute-done.other_ref, f32[2,200,200]{2,1,0:T(8,128)S(1)} %shard_map.50.total_ref, f32[4,200,200]{2,1,0:T(8,128)S(1)} %shard_map.53.before_ref, ...), custom_call_target="tpu_custom_call" | custom-call | tf_op jit(solution)/shard_map/update/pallas_call | solution.py:270
  69.9 1.5 %collective-permute-start.15 = (bf16[200,512]{1,0:T(8,128)(2,1)S(1)}, bf16[200,512]{1,0:T(8,128)(2,1)S(1)}, u32[]{:S(2)}, u32[]{:S(2)}) collective-permute-start(bf16[200,512]{1,0:T(8,128)(2,1)S(1)} %get-tuple-element.12), channel_id=1, source_target_pairs={{0,1},{3,2},{4,5},{7,6},{8,9},{11,10},{12,13},{15,14},{16,17},{19,... | collective-permute-start | bytes 614408 | tf_op jit(solution)/shard_map/ppermute | solution.py:303
  71.4 3.2 %collective-permute-done.15 = bf16[200,512]{1,0:T(8,128)(2,1)S(1)} collective-permute-done((bf16[200,512]{1,0:T(8,128)(2,1)S(1)}, bf16[200,512]{1,0:T(8,128)(2,1)S(1)}, u32[]{:S(2)}, u32[]{:S(2)}) %collective-permute-start.15) | collective-permute-done | bytes 204832 | tf_op jit(solution)/shard_map/ppermute | solution.py:303
  74.6 0.8 %select_bitcast_fusion = f32[1,200,512]{2,1,0:T(8,128)} fusion(f32[200,512]{1,0:T(8,128)S(1)} %get-tuple-element.11, bf16[200,512]{1,0:T(8,128)(2,1)S(1)} %collective-permute-done.15, pred[]{:T(512)S(6)} %eq.5), kind=kLoop, calls=%fused_computation.4 | loop fusion | flops 204800 | bytes 1024001 | tf_op jit(solution)/shard_map/broadcast_in_dim | solution.py:355
  (24 shorter events, 1.3 us)
Async XLA Ops:
  0.0 18.4 %copy-start.4 = (f32[12]{0:T(128)S(1)}, f32[12]{0:T(128)}, u32[]{:S(2)}) copy-start(f32[12]{0:T(128)} %param.6) | copy-start | bytes 148
  0.0 8.3 %collective-permute-start = (bf16[200,512]{1,0:T(8,128)(2,1)}, bf16[200,512]{1,0:T(8,128)(2,1)S(1)}, u32[]{:S(2)}, u32[]{:S(2)}) collective-permute-start(bf16[200,512]{1,0:T(8,128)(2,1)} %bitcast.17), channel_id=1, source_target_pairs={{0,1},{1,0},{2,3},{3,2},{4,5},{5,4},{6,7},{7,6},{8,9},{9,8},{10,11... | collective-permute-start | bytes 614408 | tf_op jit(solution)/shard_map/ppermute | solution.py:312
  3.0 8.4 %collective-permute-start.1 = (bf16[200,512]{1,0:T(8,128)(2,1)}, bf16[200,512]{1,0:T(8,128)(2,1)S(1)}, u32[]{:S(2)}, u32[]{:S(2)}) collective-permute-start(bf16[200,512]{1,0:T(8,128)(2,1)} %bitcast.18), channel_id=1, source_target_pairs={{10,0},{8,2},{14,4},{12,6},{18,8},{16,10},{22,12},{20,14},{26,16},... | collective-permute-start | bytes 614408 | tf_op jit(solution)/shard_map/ppermute | solution.py:306
  5.8 12.7 %collective-permute-start.5 = (bf16[200,512]{1,0:T(8,128)(2,1)}, bf16[200,512]{1,0:T(8,128)(2,1)S(1)}, u32[]{:S(2)}, u32[]{:S(2)}) collective-permute-start(bf16[200,512]{1,0:T(8,128)(2,1)} %bitcast.19), channel_id=1, source_target_pairs={{26,0},{24,2},{30,4},{28,6},{2,8},{0,10},{6,12},{4,14},{10,16},{8,... | collective-permute-start | bytes 614408 | tf_op jit(solution)/shard_map/ppermute | solution.py:306
  5.8 24.3 %collective-permute-start.9 = (bf16[200,512]{1,0:T(8,128)(2,1)}, bf16[200,512]{1,0:T(8,128)(2,1)}, u32[]{:S(2)}, u32[]{:S(2)}) collective-permute-start(bf16[200,512]{1,0:T(8,128)(2,1)} %bitcast.20), channel_id=1, source_target_pairs={{6,0},{4,2},{2,4},{0,6},{14,8},{12,10},{10,12},{8,14},{22,16},{20,... | collective-permute-start | bytes 614408 | tf_op jit(solution)/shard_map/ppermute | solution.py:306
  8.3 11.8 %collective-permute-start.3 = (bf16[200,512]{1,0:T(8,128)(2,1)S(1)}, bf16[200,512]{1,0:T(8,128)(2,1)S(1)}, u32[]{:S(2)}, u32[]{:S(2)}) collective-permute-start(bf16[200,512]{1,0:T(8,128)(2,1)S(1)} %collective-permute-done.other_ref), channel_id=1, source_target_pairs={{10,0},{8,2},{14,4},{12,6},{18,8},{16,10},{22,12},{20,14},{26,16},... | collective-permute-start | bytes 614408 | tf_op jit(solution)/shard_map/ppermute | solution.py:306
  11.4 14.4 %collective-permute-start.7 = (bf16[200,512]{1,0:T(8,128)(2,1)S(1)}, bf16[200,512]{1,0:T(8,128)(2,1)}, u32[]{:S(2)}, u32[]{:S(2)}) collective-permute-start(bf16[200,512]{1,0:T(8,128)(2,1)S(1)} %collective-permute-done.other_ref), channel_id=1, source_target_pairs={{26,0},{24,2},{30,4},{28,6},{2,8},{0,10},{6,12},{4,14},{10,16},{8,... | collective-permute-start | bytes 614408 | tf_op jit(solution)/shard_map/ppermute | solution.py:306
  11.4 0.7 copy-start.2
  12.0 18.1 %collective-permute-start.10 = (bf16[200,512]{1,0:T(8,128)(2,1)S(1)}, bf16[200,512]{1,0:T(8,128)(2,1)}, u32[]{:S(2)}, u32[]{:S(2)}) collective-permute-start(bf16[200,512]{1,0:T(8,128)(2,1)S(1)} %collective-permute-done.other_ref), channel_id=1, source_target_pairs={{6,0},{4,2},{2,4},{0,6},{14,8},{12,10},{10,12},{8,14},{22,16},{20,... | collective-permute-start | bytes 614408 | tf_op jit(solution)/shard_map/ppermute | solution.py:306
  18.5 17.7 %collective-permute-start.2 = (bf16[200,512]{1,0:T(8,128)(2,1)}, bf16[200,512]{1,0:T(8,128)(2,1)S(1)}, u32[]{:S(2)}, u32[]{:S(2)}) collective-permute-start(bf16[200,512]{1,0:T(8,128)(2,1)} %copy-done.2), channel_id=1, source_target_pairs={{6,0},{4,2},{2,4},{0,6},{14,8},{12,10},{10,12},{8,14},{22,16},{20,... | collective-permute-start | bytes 614408 | tf_op jit(solution)/shard_map/ppermute | solution.py:306
  20.0 18.4 %collective-permute-start.6 = (bf16[200,512]{1,0:T(8,128)(2,1)S(1)}, bf16[200,512]{1,0:T(8,128)(2,1)S(1)}, u32[]{:S(2)}, u32[]{:S(2)}) collective-permute-start(bf16[200,512]{1,0:T(8,128)(2,1)S(1)} %collective-permute-done.5.refs_5_), channel_id=1, source_target_pairs={{6,0},{4,2},{2,4},{0,6},{14,8},{12,10},{10,12},{8,14},{22,16},{20,... | collective-permute-start | bytes 614408 | tf_op jit(solution)/shard_map/ppermute | solution.py:306
  25.8 0.9 %copy-start.3 = (bf16[200,512]{1,0:T(8,128)(2,1)S(1)}, bf16[200,512]{1,0:T(8,128)(2,1)}, u32[]{:S(2)}) copy-start(bf16[200,512]{1,0:T(8,128)(2,1)} %copy-done.2) | copy-start | bytes 614404
  28.8 33.0 %collective-permute-start.11 = (bf16[4,200,512]{2,1,0:T(8,128)(2,1)S(1)}, bf16[4,200,512]{2,1,0:T(8,128)(2,1)S(1)}, u32[]{:S(2)}, u32[]{:S(2)}) collective-permute-start(bf16[4,200,512]{2,1,0:T(8,128)(2,1)S(1)} %shard_map.48.refs_1_.refs_0_), channel_id=1, source_target_pairs={{1,0},{2,3},{5,4},{6,7},{9,8},{10,11},{13,12},{14,15},{17,16},{18,... | collective-permute-start | bytes 2457608 | tf_op jit(solution)/shard_map/ppermute | solution.py:303
  30.1 17.5 %copy-start = (bf16[4,200,800]{2,1,0:T(8,128)(2,1)S(1)}, bf16[4,200,800]{2,1,0:T(8,128)(2,1)}, u32[]{:S(2)}) copy-start(bf16[4,200,800]{2,1,0:T(8,128)(2,1)} %get-tuple-element.15.refs_2_) | copy-start | bytes 3840004
  32.4 28.3 %collective-permute-start.13 = (bf16[4,200,512]{2,1,0:T(8,128)(2,1)S(1)}, bf16[4,200,512]{2,1,0:T(8,128)(2,1)S(1)}, u32[]{:S(2)}, u32[]{:S(2)}) collective-permute-start(bf16[4,200,512]{2,1,0:T(8,128)(2,1)S(1)} %shard_map.47.refs_0_), channel_id=1, source_target_pairs={{1,0},{2,3},{5,4},{6,7},{9,8},{10,11},{13,12},{14,15},{17,16},{18,... | collective-permute-start | bytes 2457608 | tf_op jit(solution)/shard_map/ppermute | solution.py:303
  34.9 24.6 %collective-permute-start.12 = (bf16[2,200,800]{2,1,0:T(8,128)(2,1)S(1)}, bf16[2,200,800]{2,1,0:T(8,128)(2,1)S(1)}, u32[]{:S(2)}, u32[]{:S(2)}) collective-permute-start(bf16[2,200,800]{2,1,0:T(8,128)(2,1)S(1)} %slice_bitcast_fusion.3), channel_id=1, source_target_pairs={{1,0},{2,3},{5,4},{6,7},{9,8},{10,11},{13,12},{14,15},{17,16},{18,... | collective-permute-start | bytes 1920008 | tf_op jit(solution)/shard_map/ppermute | solution.py:303
  36.2 7.7 %collective-permute-start.4 = (bf16[200,512]{1,0:T(8,128)(2,1)S(1)}, bf16[200,512]{1,0:T(8,128)(2,1)S(1)}, u32[]{:S(2)}, u32[]{:S(2)}) collective-permute-start(bf16[200,512]{1,0:T(8,128)(2,1)S(1)} %collective-permute-done.3.refs_4_), channel_id=1, source_target_pairs={{6,0},{4,2},{2,4},{0,6},{14,8},{12,10},{10,12},{8,14},{22,16},{20,... | collective-permute-start | bytes 614408 | tf_op jit(solution)/shard_map/ppermute | solution.py:306
  38.4 9.2 %collective-permute-start.8 = (bf16[200,512]{1,0:T(8,128)(2,1)}, bf16[200,512]{1,0:T(8,128)(2,1)S(1)}, u32[]{:S(2)}, u32[]{:S(2)}) collective-permute-start(bf16[200,512]{1,0:T(8,128)(2,1)} %collective-permute-done.7.refs_6_), channel_id=1, source_target_pairs={{6,0},{4,2},{2,4},{0,6},{14,8},{12,10},{10,12},{8,14},{22,16},{20,... | collective-permute-start | bytes 614408 | tf_op jit(solution)/shard_map/ppermute | solution.py:306
  49.4 14.5 %collective-permute-start.14 = (bf16[2,200,512]{2,1,0:T(8,128)(2,1)S(1)}, bf16[2,200,512]{2,1,0:T(8,128)(2,1)S(1)}, u32[]{:S(2)}, u32[]{:S(2)}) collective-permute-start(bf16[2,200,512]{2,1,0:T(8,128)(2,1)S(1)} %get-tuple-element.9.refs_0_.keep_ref), channel_id=1, source_target_pairs={{1,0},{2,3},{5,4},{6,7},{9,8},{10,11},{13,12},{14,15},{17,16},{18,... | collective-permute-start | bytes 1228808 | tf_op jit(solution)/shard_map/ppermute | solution.py:303
  61.8 2.1 %copy-start.1 = (bf16[1,200,512]{2,1,0:T(8,128)(2,1)S(1)}, bf16[1,200,512]{2,1,0:T(8,128)(2,1)}, u32[]{:S(2)}) copy-start(bf16[1,200,512]{2,1,0:T(8,128)(2,1)} %param.5) | copy-start | bytes 614404
  69.9 4.7 %collective-permute-start.15 = (bf16[200,512]{1,0:T(8,128)(2,1)S(1)}, bf16[200,512]{1,0:T(8,128)(2,1)S(1)}, u32[]{:S(2)}, u32[]{:S(2)}) collective-permute-start(bf16[200,512]{1,0:T(8,128)(2,1)S(1)} %get-tuple-element.12), channel_id=1, source_target_pairs={{0,1},{3,2},{4,5},{7,6},{8,9},{11,10},{12,13},{15,14},{16,17},{19,... | collective-permute-start | bytes 614408 | tf_op jit(solution)/shard_map/ppermute | solution.py:303

commit v6 on v4

--- a/solution.py
+++ b/solution.py
@@ -25,7 +25,10 @@
 )
 BATCH = 4
 SHIPPED = 2
+CENTRE = 0.5
+PREPARE = 2 * 10**10
 VMEM = pl.BlockSpec(memory_space=pltpu.VMEM)
+LARGE_LIMIT = pltpu.CompilerParams(vmem_limit_bytes=50 * 2**20)
 LIMIT = pltpu.CompilerParams(vmem_limit_bytes=20 * 2**20)
 SMEM = pl.BlockSpec(memory_space=pltpu.SMEM)
 F32 = jnp.float32
@@ -75,16 +78,6 @@
     return dot(high, right, dims) + dot(low, right, dims)
 
 
-def dot_split(left, right, dims=None):
-    left_high, left_low = split(left)
-    right_high, right_low = split(right)
-    return (
-        dot(left_high, right_high, dims)
-        + dot(left_high, right_low, dims)
-        + dot(left_low, right_high, dims)
-    )
-
-
 def times_minus_i(value):
     half = value.shape[-1] // 2
     return jnp.concatenate([value[:, half:], -value[:, :half]], axis=1)
@@ -104,80 +97,99 @@
     stacked_ref[2 * rows :, :] = times_i(whole).astype(BF16)
 
 
-def masked_block(margin, stacked, root, limit):
+def masked_block(margin, stacked, weight, limit):
     inside = lax.broadcasted_iota(jnp.int32, (margin.shape[0], 1), 0) < limit
-    return jnp.where(inside, dot(margin, stacked) * root, 0.0).astype(BF16)
-
-
-def load_kernel(shipped, place_ref, margins_ref, all_ref, given_ref, all_sem, given_sem):
-    copies = (
-        pltpu.make_async_copy(margins_ref.at[0, shipped + 1 - place_ref[0]], given_ref, given_sem),
-        pltpu.make_async_copy(margins_ref.at[0], all_ref, all_sem),
-    )
-    for copy in copies:
-        copy.start()
-    for copy in copies:
-        copy.wait()
-
-
-def load(place, margins, shipped):
-    shape = margins.shape[1:]
-    return pl.pallas_call(
-        functools.partial(load_kernel, shipped),
-        in_specs=[SMEM, pl.BlockSpec(memory_space=pl.ANY)],
-        out_specs=[VMEM] * 2,
-        out_shape=[
-            jax.ShapeDtypeStruct(shape, margins.dtype),
-            jax.ShapeDtypeStruct(shape[1:], margins.dtype),
-        ],
-        scratch_shapes=[pltpu.SemaphoreType.DMA] * 2,
-        name="load",
-        compiler_params=LIMIT,
-    )(place, margins)
-
-
-def project_kernel(groups, first, sent, place_ref, root_ref, margins_ref, *refs):
+    factor = jnp.where(inside, jnp.sqrt(jnp.full((1, 1), weight, F32)), 0.0)
+    return (dot(margin, stacked) * factor).astype(BF16)
+
+
+def prepare_kernel(rows, side_ref, window_ref, out_ref):
+    side = side_ref[0]
+    out_ref[0] = side
+    out_ref[1] = window_ref[0] - side * rows
+    out_ref[2] = window_ref[0] - (1 - side) * rows
+
+
+def prepare(side, window_count, rows):
+    return pl.pallas_call(
+        functools.partial(prepare_kernel, rows),
+        in_specs=[SMEM] * 2,
+        out_specs=SMEM,
+        out_shape=jax.ShapeDtypeStruct((3,), jnp.int32),
+        cost_estimate=pl.CostEstimate(flops=PREPARE, bytes_accessed=64 * 2**20, transcendentals=0),
+        name="prepare",
+        compiler_params=LIMIT,
+    )(side[None], window_count)
+
+
+def project_kernel(groups, first, sent, streamed, place_ref, weight_ref, margins_ref, *refs):
     halves = refs[: 2 * len(groups)]
-    keep_ref, *give_refs, rows_ref, stacked_ref, blocks_ref = refs[2 * len(groups) :]
+    refs = refs[2 * len(groups) :]
+    copies = []
+    if streamed:
+        *refs, fetched_ref, sems = refs
+        for member in range(BATCH):
+            source = margins_ref.at[0, first + member]
+            copies.append(
+                pltpu.make_async_copy(source, fetched_ref.at[member], sems.at[member])
+            )
+            copies[-1].start()
+    keep_ref, *give_refs, rows_ref, stacked_ref, blocks_ref = refs
     side, limit = place_ref[0], place_ref[1]
     for number, members in enumerate(groups):
         mine, other = halves[2 * number][...], halves[2 * number + 1][...]
         stack_complex(mine, other, side, rows_ref, stacked_ref)
         for member in members:
-            blocks_ref[member] = masked_block(
-                margins_ref[first + member], stacked_ref[...], root_ref[first + member], limit
-            )
+            if streamed:
+                copies[member].wait()
+                margin = fetched_ref[member]
+            else:
+                margin = margins_ref[0, first + member]
+            weight = weight_ref[first + member]
+            blocks_ref[member] = masked_block(margin, stacked_ref[...], weight, limit)
     for pair in range(BATCH // 2):
         keep_ref[pair] = blocks_ref[2 * pair + side]
         target = give_refs[0].at[pair] if pair < sent else give_refs[1].at[pair - sent]
         target[...] = blocks_ref[2 * pair + 1 - side]
 
 
-def project(place, roots, margins, batch, groups, halves, sent):
-    rows, double = margins.shape[1:]
+def project(place, weights, margins, batch, groups, halves, sent, streamed):
+    rows, double = margins.shape[2:]
     width = halves[0].shape[-1]
     pairs = BATCH // 2
     counts = [pairs, sent] + ([pairs - sent] if sent < pairs else [])
-    return pl.pallas_call(
-        functools.partial(project_kernel, groups, batch * BATCH, sent),
-        in_specs=[SMEM, SMEM, VMEM, *([VMEM] * len(halves))],
+    streams = []
+    if streamed:
+        streams = [
+            pltpu.VMEM((BATCH, rows, double), BF16),
+            pltpu.SemaphoreType.DMA((BATCH,)),
+        ]
+    return pl.pallas_call(
+        functools.partial(project_kernel, groups, batch * BATCH, sent, streamed),
+        in_specs=[
+            SMEM,
+            SMEM,
+            pl.BlockSpec(memory_space=pl.ANY) if streamed else VMEM,
+            *([VMEM] * len(halves)),
+        ],
         out_specs=[VMEM] * len(counts),
         out_shape=[jax.ShapeDtypeStruct((count, rows, width), BF16) for count in counts],
         scratch_shapes=[
             pltpu.VMEM((2 * rows, width), F32),
             pltpu.VMEM((double, width), BF16),
             pltpu.VMEM((BATCH, rows, width), BF16),
+            *streams,
         ],
         cost_estimate=pl.CostEstimate(
             flops=2 * BATCH * rows * double * width,
             bytes_accessed=2 * BATCH * rows * double,
             transcendentals=0,
         ),
-        compiler_params=LIMIT,
-    )(place, roots, margins, *halves)
-
-
-def extra_kernel(shipped, place_ref, root_ref, margin_ref, *refs):
+        compiler_params=LARGE_LIMIT if streamed else LIMIT,
+    )(place, weights, margins, *halves)
+
+
+def extra_kernel(shipped, place_ref, weight_ref, margin_ref, *refs):
     *halves, out_ref, rows_ref, stacked_ref = refs
     side, limit = place_ref[0], place_ref[2]
     mine, other = halves[0][...], halves[1][...]
@@ -185,11 +197,11 @@
         mine = jnp.where(side == 0, mine, halves[2][...])
         other = jnp.where(side == 0, other, halves[3][...])
     stack_complex(mine, other, side, rows_ref, stacked_ref)
-    root = root_ref[shipped + side]
-    out_ref[0] = masked_block(margin_ref[...], stacked_ref[...], root, limit)
-
-
-def extra(place, roots, margin, shipped, halves):
+    weight = weight_ref[shipped + side]
+    out_ref[0] = masked_block(margin_ref[...], stacked_ref[...], weight, limit)
+
+
+def extra(place, weights, margin, shipped, halves):
     rows, double = margin.shape
     width = halves[0].shape[-1]
     return pl.pallas_call(
@@ -203,7 +215,7 @@
         ),
         name="extra",
         compiler_params=LIMIT,
-    )(place, roots, margin, *halves)
+    )(place, weights, margin, *halves)
 
 
 def triangle(size):
@@ -290,8 +302,9 @@
     )(*operands)
 
 
-def complex_stack(value):
-    return jnp.concatenate([value, times_i(value)], axis=0)
+def dot_complex(left, right):
+    stacked = jnp.concatenate([right, times_i(right)], axis=0).astype(BF16)
+    return dot(left.astype(BF16), stacked)
 
 
 def base_kernel(own_ref, other_ref, total_ref, packed_ref, mine_ref, base_ref, base_other_ref):
@@ -334,14 +347,17 @@
     )(own, other, total, packed, mine)
 
 
-def update_kernel(scale, own_ref, other_ref, base_ref, base_other_ref, theirs_ref, out_ref):
+def update_kernel(scale, own_ref, other_ref, base_ref, base_other_ref, theirs_ref, out_ref, rows_ref):
     own, other = own_ref[...], other_ref[...]
     half = own.shape[1] // 2
     own_i, other_i = times_i(own.astype(F32)).astype(BF16), times_i(other.astype(F32)).astype(BF16)
     real, imag = theirs_ref[0], theirs_ref[1]
+    rows = own.shape[0]
     product = base_ref[...] + dot(real, other) + dot(imag, other_i)
-    product_other = base_other_ref[...] + dot(real, own, TN) - dot(imag, own_i, TN)
-    blocks = dot_split(product, product, TN) + dot_split(product_other, product_other, TN)
+    rows_ref[:rows, :] = product
+    rows_ref[rows:, :] = base_other_ref[...] + dot(real, own, TN) - dot(imag, own_i, TN)
+    both = rows_ref[...].astype(BF16)
+    blocks = dot(both, both, TN)
     real = blocks[:half, :half] + blocks[half:, half:]
     imag = blocks[:half, half:] - blocks[half:, :half]
     diagonal = lax.broadcasted_iota(jnp.int32, (half, 2 * half), 0) == lax.broadcasted_iota(
@@ -351,14 +367,16 @@
     squares = jnp.sum(jnp.where(diagonal, gram, 0.0))
     size = jnp.full((1, 1), 2.0 * squares / half + 1e-06, F32)
     scaling = lax.rsqrt(size)
-    gram = gram * (scaling * scaling)
-    identity = jnp.where(diagonal, 1.0, 0.0)
-    gram_two = dot_split(gram, complex_stack(gram))
-    left = 2.25 * identity - 1.5 * gram + 0.25 * gram_two
-    right = 1.5 * gram - 0.5 * gram_two
-    factor = 2.25 * identity - 0.75 * gram - 0.5 * dot_split(left, complex_stack(right))
-    factor = factor * (scaling * scale)
-    out_ref[0] = dot_split(product, complex_stack(factor))
+    rest = gram * (scaling * scaling) - jnp.where(diagonal, CENTRE, 0.0)
+    square = 2.0 * CENTRE * rest + dot_complex(rest, rest)
+    left_centre = 2.25 - 1.5 * CENTRE + 0.25 * CENTRE**2
+    right_centre = 1.5 * CENTRE - 0.5 * CENTRE**2
+    left = 0.25 * square - 1.5 * rest
+    right = 1.5 * rest - 0.5 * square
+    both_sides = left_centre * right + right_centre * left + dot_complex(left, right)
+    factor = -0.75 * rest - 0.5 * both_sides
+    centre = 2.25 - 0.75 * CENTRE - 0.5 * left_centre * right_centre
+    out_ref[0] = (product * centre + dot_complex(product, factor)) * (scaling * scale)
 
 
 def update(scale, own, other, bases, theirs):
@@ -368,6 +386,7 @@
         in_specs=[VMEM] * 5,
         out_specs=VMEM,
         out_shape=jax.ShapeDtypeStruct((1, rows, width), F32),
+        scratch_shapes=[pltpu.VMEM((2 * rows, width), F32)],
         name="update",
         compiler_params=LIMIT,
     )(own, other, *bases, theirs)
@@ -394,12 +413,10 @@
     def fetch(value, shift):
         return lax.ppermute(value, "kpt", fetch_pairs(shift, point_count))
 
-    offset = side * rows
-    place = jnp.stack([side, window_count[0] - offset, window_count[0] - (rows - offset)])
-    roots = jnp.sqrt(shell_weights)
+    place = prepare(side, window_count, rows)
     own = subspace[0]
     other = exchange(own)
-    margins, margin = load(place, margins, SHIPPED)
+    margin = lax.dynamic_index_in_dim(margins[0], SHIPPED + 1 - side, 0, keepdims=False)
     margin = exchange(margin)
     halves = {}
     for part, value in (("own", own), ("other", other)):
@@ -417,14 +434,14 @@
             operands += [halves[batch, "own", shift], halves[batch, "other", shift]]
         sent = SHIPPED // 2 if batch == 0 else BATCH // 2
         blocks[batch] = project(
-            place, roots, margins, batch, list(plan[batch].values()), operands, sent
+            place, shell_weights, margins, batch, list(plan[batch].values()), operands, sent, False
         )
         got[batch] = exchange(blocks[batch][1])
     operands = []
     for shift, members in plan[0].items():
         if SHIPPED in members or SHIPPED + 1 in members:
             operands += [halves[0, "own", shift], halves[0, "other", shift]]
-    got_extra = extra(place, roots, margin, SHIPPED, operands)
+    got_extra = extra(place, shell_weights, margin, SHIPPED, operands)
     (total,) = gather_own([*blocks[2], *blocks[1]], None)
     total, packed = gather_own(blocks[0], total)
     other_packed = exchange(packed)

time: 71.7 us -> 67.4 us (0.940)
  Pallas kernels: 17.4 us -> 14.4 us
    ppermute x7, waiting for transfers between devices: 18.9 us -> 12.8 us  [exchange(): return lax.ppermute(value, 'band', swap)]
    ppermute x10, waiting for transfers between devices: 8.16 us -> 13.8 us  [fetch(): return lax.ppermute(value, 'kpt', fetch_pairs(shift, point_count))]
    pallas_call x1, Pallas kernels: 5.39 us -> 2.98 us  [update(): pl.pallas_call(functools.partial(update_kernel, scale), in_specs=[VMEM] *...]
    unnamed x4 -> x6, local copies, waits for them, and re-layouts: 2.23 us -> 2.23 us
  transfers between devices with their start and end apart: 17 -> 17, of which waited for: 8 -> 7; matrix products, arithmetic and copies ran while one was open for 1% -> 0% of each run, Pallas kernels for 16% -> 16%
where the time goes in v6:
time: 67.4 us; the launch traced here: 67.3 us
  waiting for transfers between devices  26.6 us (39%)
  starting transfers between devices  23.3 us (35%)
  Pallas kernels  14.4 us (21%)
  local copies, waits for them, and re-layouts  2.26 us (3%)
  between operations  0.81 us (1%)
    ppermute x10, starting transfers between devices, fetch(): return lax.ppermute(value, 'kpt', fetch_pairs(shift, point_count))  14.1 us
    ppermute x10, waiting for transfers between devices, fetch(): return lax.ppermute(value, 'kpt', fetch_pairs(shift, point_count))  13.8 us
    ppermute x7, waiting for transfers between devices, exchange(): return lax.ppermute(value, 'band', swap)  12.8 us
    ppermute x7, starting transfers between devices, exchange(): return lax.ppermute(value, 'band', swap)  9.19 us
    pallas_call x3, Pallas kernels, project(): pl.pallas_call(functools.partial(project_kernel, groups, batch * BATCH, s...  5.21 us
    pallas_call x1, Pallas kernels, update(): pl.pallas_call(functools.partial(update_kernel, scale), in_specs=[VMEM] *...  2.98 us
    unnamed x6, local copies, waits for them, and re-layouts  2.23 us
    pallas_call x3, Pallas kernels, cross(): pl.pallas_call(functools.partial(cross_kernel, terms, len(blocks), before...  1.88 us
  transfers between devices with their start and end apart: 17, of which 7 were waited for; matrix products, arithmetic and copies ran while one was open for 0% of the time, Pallas kernels for 16%

profile of v6, /device:TPU:0, one launch (start us, length us, event | category | flops | bytes accessed | tf_op | source)
XLA Modules:
  0.0 67.3 jit_solution(17809828538272450720)
XLA Ops:
  0.0 3.0 %collective-permute-start = (bf16[200,512]{1,0:T(8,128)(2,1)}, bf16[200,512]{1,0:T(8,128)(2,1)S(1)}, u32[]{:S(2)}, u32[]{:S(2)}) collective-permute-start(bf16[200,512]{1,0:T(8,128)(2,1)} %bitcast.4), channel_id=1, source_target_pairs={{0,1},{1,0},{2,3},{3,2},{4,5},{5,4},{6,7},{7,6},{8,9},{9,8},{10,11... | collective-permute-start | bytes 614408 | tf_op jit(solution)/shard_map/ppermute | solution.py:411
  3.0 0.7 collective-permute-start.9
  3.6 2.1 %collective-permute-start.5 = (bf16[200,512]{1,0:T(8,128)(2,1)}, bf16[200,512]{1,0:T(8,128)(2,1)S(1)}, u32[]{:S(2)}, u32[]{:S(2)}) collective-permute-start(bf16[200,512]{1,0:T(8,128)(2,1)} %bitcast.6), channel_id=1, source_target_pairs={{26,0},{24,2},{30,4},{28,6},{2,8},{0,10},{6,12},{4,14},{10,16},{8,... | collective-permute-start | bytes 614408 | tf_op jit(solution)/shard_map/ppermute | solution.py:414
  5.8 2.0 %collective-permute-start.1 = (bf16[200,512]{1,0:T(8,128)(2,1)}, bf16[200,512]{1,0:T(8,128)(2,1)S(1)}, u32[]{:S(2)}, u32[]{:S(2)}) collective-permute-start(bf16[200,512]{1,0:T(8,128)(2,1)} %bitcast.7), channel_id=1, source_target_pairs={{10,0},{8,2},{14,4},{12,6},{18,8},{16,10},{22,12},{20,14},{26,16},... | collective-permute-start | bytes 614408 | tf_op jit(solution)/shard_map/ppermute | solution.py:414
  9.0 2.3 %collective-permute-start.7 = (bf16[200,512]{1,0:T(8,128)(2,1)S(1)}, bf16[200,512]{1,0:T(8,128)(2,1)S(1)}, u32[]{:S(2)}, u32[]{:S(2)}) collective-permute-start(bf16[200,512]{1,0:T(8,128)(2,1)S(1)} %collective-permute-done.other_ref), channel_id=1, source_target_pairs={{26,0},{24,2},{30,4},{28,6},{2,8},{0,10},{6,12},{4,14},{10,16},{8,... | collective-permute-start | bytes 614408 | tf_op jit(solution)/shard_map/ppermute | solution.py:414
  11.3 2.6 %collective-permute-start.3 = (bf16[200,512]{1,0:T(8,128)(2,1)S(1)}, bf16[200,512]{1,0:T(8,128)(2,1)S(1)}, u32[]{:S(2)}, u32[]{:S(2)}) collective-permute-start(bf16[200,512]{1,0:T(8,128)(2,1)S(1)} %collective-permute-done.other_ref), channel_id=1, source_target_pairs={{10,0},{8,2},{14,4},{12,6},{18,8},{16,10},{22,12},{20,14},{26,16},... | collective-permute-start | bytes 614408 | tf_op jit(solution)/shard_map/ppermute | solution.py:414
  13.9 1.2 %collective-permute-start.6 = (bf16[200,512]{1,0:T(8,128)(2,1)S(1)}, bf16[200,512]{1,0:T(8,128)(2,1)S(1)}, u32[]{:S(2)}, u32[]{:S(2)}) collective-permute-start(bf16[200,512]{1,0:T(8,128)(2,1)S(1)} %collective-permute-done.5.refs_2_), channel_id=1, source_target_pairs={{6,0},{4,2},{2,4},{0,6},{14,8},{12,10},{10,12},{8,14},{22,16},{20,... | collective-permute-start | bytes 614408 | tf_op jit(solution)/shard_map/ppermute | solution.py:414
  15.1 0.6 prepare.1.place_ref
  15.7 1.9 %collective-permute-done.1.refs_0_ = bf16[200,512]{1,0:T(8,128)(2,1)S(1)} collective-permute-done((bf16[200,512]{1,0:T(8,128)(2,1)}, bf16[200,512]{1,0:T(8,128)(2,1)S(1)}, u32[]{:S(2)}, u32[]{:S(2)}) %collective-permute-start.1) | collective-permute-done | bytes 204832 | tf_op jit(solution)/shard_map/ppermute | solution.py:414
  17.6 0.9 %collective-permute-start.2 = (bf16[200,512]{1,0:T(8,128)(2,1)S(1)}, bf16[200,512]{1,0:T(8,128)(2,1)S(1)}, u32[]{:S(2)}, u32[]{:S(2)}) collective-permute-start(bf16[200,512]{1,0:T(8,128)(2,1)S(1)} %collective-permute-done.1.refs_0_), channel_id=1, source_target_pairs={{6,0},{4,2},{2,4},{0,6},{14,8},{12,10},{10,12},{8,14},{22,16},{20,... | collective-permute-start | bytes 614408 | tf_op jit(solution)/shard_map/ppermute | solution.py:414
  18.5 2.2 %copy-done = bf16[1,12,200,800]{3,2,1,0:T(8,128)(2,1)S(1)} copy-done((bf16[1,12,200,800]{3,2,1,0:T(8,128)(2,1)S(1)}, bf16[1,12,200,800]{3,2,1,0:T(8,128)(2,1)}, u32[]{:S(2)}) %copy-start) | copy-done | bytes 3840024
  20.7 1.7 %shard_map.47 = (bf16[2,200,512]{2,1,0:T(8,128)(2,1)S(1)}, bf16[2,200,512]{2,1,0:T(8,128)(2,1)S(1)}) custom-call(s32[3]{0:T(128)S(1)} %prepare.1.place_ref, f32[12]{0:T(128)S(1)} %copy-done.2, bf16[1,12,200,800]{3,2,1,0:T(8,128)(2,1)S(1)} %copy-done, bf16[200,512]{1,0:T(8,128)(2,1)S(1)} %collective-permute-done.9.refs_0_, ...), custom_call_target="tpu_custom_call" | custom-call | flops 655360000 | bytes 1280000 | tf_op jit(solution)/shard_map/pallas_call | solution.py:167
  22.7 3.7 %collective-permute-done.3.refs_1_ = bf16[200,512]{1,0:T(8,128)(2,1)S(1)} collective-permute-done((bf16[200,512]{1,0:T(8,128)(2,1)S(1)}, bf16[200,512]{1,0:T(8,128)(2,1)S(1)}, u32[]{:S(2)}, u32[]{:S(2)}) %collective-permute-start.3) | collective-permute-done | bytes 204832 | tf_op jit(solution)/shard_map/ppermute | solution.py:414
  26.4 1.7 %shard_map.48 = (bf16[2,200,512]{2,1,0:T(8,128)(2,1)S(1)}, bf16[2,200,512]{2,1,0:T(8,128)(2,1)S(1)}) custom-call(s32[3]{0:T(128)S(1)} %prepare.1.place_ref, f32[12]{0:T(128)S(1)} %copy-done.2, bf16[1,12,200,800]{3,2,1,0:T(8,128)(2,1)S(1)} %copy-done, bf16[200,512]{1,0:T(8,128)(2,1)S(1)} %collective-permute-done.1.refs_0_, ...), custom_call_target="tpu_custom_call" | custom-call | flops 655360000 | bytes 1280000 | tf_op jit(solution)/shard_map/pallas_call | solution.py:167
  28.7 1.7 %collective-permute-start.4 = (bf16[200,512]{1,0:T(8,128)(2,1)S(1)}, bf16[200,512]{1,0:T(8,128)(2,1)S(1)}, u32[]{:S(2)}, u32[]{:S(2)}) collective-permute-start(bf16[200,512]{1,0:T(8,128)(2,1)S(1)} %collective-permute-done.3.refs_1_), channel_id=1, source_target_pairs={{6,0},{4,2},{2,4},{0,6},{14,8},{12,10},{10,12},{8,14},{22,16},{20,... | collective-permute-start | bytes 614408 | tf_op jit(solution)/shard_map/ppermute | solution.py:414
  30.5 1.6 %collective-permute-start.14 = (bf16[200,800]{1,0:T(8,128)(2,1)S(1)}, bf16[200,800]{1,0:T(8,128)(2,1)S(1)}, u32[]{:S(2)}, u32[]{:S(2)}) collective-permute-start(bf16[200,800]{1,0:T(8,128)(2,1)S(1)} %dynamic-slice_bitcast_fusion), channel_id=1, source_target_pairs={{0,1},{1,0},{2,3},{3,2},{4,5},{5,4},{6,7},{7,6},{8,9},{9,8},{10,11... | collective-permute-start | bytes 960008 | tf_op jit(solution)/shard_map/ppermute | solution.py:411
  32.1 3.8 %collective-permute-done.8.refs_3_.refs_1_ = bf16[200,512]{1,0:T(8,128)(2,1)S(1)} collective-permute-done((bf16[200,512]{1,0:T(8,128)(2,1)S(1)}, bf16[200,512]{1,0:T(8,128)(2,1)S(1)}, u32[]{:S(2)}, u32[]{:S(2)}) %collective-permute-start.8) | collective-permute-done | bytes 204832 | tf_op jit(solution)/shard_map/ppermute | solution.py:414
  35.9 4.4 %collective-permute-done.4.refs_1_ = bf16[200,512]{1,0:T(8,128)(2,1)S(1)} collective-permute-done((bf16[200,512]{1,0:T(8,128)(2,1)S(1)}, bf16[200,512]{1,0:T(8,128)(2,1)S(1)}, u32[]{:S(2)}, u32[]{:S(2)}) %collective-permute-start.4) | collective-permute-done | bytes 204832 | tf_op jit(solution)/shard_map/ppermute | solution.py:414
  40.3 1.8 %shard_map.46 = (bf16[2,200,512]{2,1,0:T(8,128)(2,1)S(1)}, bf16[1,200,512]{2,1,0:T(8,128)(2,1)S(1)}, bf16[1,200,512]{2,1,0:T(8,128)(2,1)S(1)}) custom-call(s32[3]{0:T(128)S(1)} %prepare.1.place_ref, f32[12]{0:T(128)S(1)} %copy-done.2, bf16[1,12,200,800]{3,2,1,0:T(8,128)(2,1)S(1)} %copy-done, bf16[200,512]{1,0:T(8,128)(2,1)S(1)} %collective-permute-done.2.refs_0_, ...), custom_call_target="tpu_custom_call" | custom-call | flops 655360000 | bytes 1280000 | tf_op jit(solution)/shard_map/pallas_call | solution.py:167
  42.0 1.6 %collective-permute-start.12 = (bf16[1,200,512]{2,1,0:T(8,128)(2,1)S(1)}, bf16[1,200,512]{2,1,0:T(8,128)(2,1)S(1)}, u32[]{:S(2)}, u32[]{:S(2)}) collective-permute-start(bf16[1,200,512]{2,1,0:T(8,128)(2,1)S(1)} %get-tuple-element.23.refs_1_), channel_id=1, source_target_pairs={{0,1},{1,0},{2,3},{3,2},{4,5},{5,4},{6,7},{7,6},{8,9},{9,8},{10,11... | collective-permute-start | bytes 614408 | tf_op jit(solution)/shard_map/ppermute | solution.py:411
  43.6 1.1 %shard_map.49.refs_3_ = f32[2,200,200]{2,1,0:T(8,128)S(1)} custom-call(bf16[2,200,512]{2,1,0:T(8,128)(2,1)S(1)} %get-tuple-element.25.refs_0_, bf16[2,200,512]{2,1,0:T(8,128)(2,1)S(1)} %get-tuple-element.26.refs_1_, bf16[2,200,512]{2,1,0:T(8,128)(2,1)S(1)} %get-tuple-element.27.refs_2_.refs_0_, bf16[2,200,512]{2,1,0:T(8,128)(2,1)S(1)} %get-tuple-element.28.refs_3_), custom_call_target="tpu_custom_call" | custom-call | flops 655360000 | bytes 1638400 | tf_op jit(solution)/shard_map/pallas_call | solution.py:252
  44.7 6.6 %collective-permute-done.14.margin_ref = bf16[200,800]{1,0:T(8,128)(2,1)S(1)} collective-permute-done((bf16[200,800]{1,0:T(8,128)(2,1)S(1)}, bf16[200,800]{1,0:T(8,128)(2,1)S(1)}, u32[]{:S(2)}, u32[]{:S(2)}) %collective-permute-start.14) | collective-permute-done | bytes 320032 | tf_op jit(solution)/shard_map/ppermute | solution.py:411
  51.3 1.0 %extra.1.refs_3_ = bf16[1,200,512]{2,1,0:T(8,128)(2,1)S(1)} custom-call(s32[3]{0:T(128)S(1)} %prepare.1.place_ref, f32[12]{0:T(128)S(1)} %copy-done.2, bf16[200,800]{1,0:T(8,128)(2,1)S(1)} %collective-permute-done.14.margin_ref, bf16[200,512]{1,0:T(8,128)(2,1)S(1)} %collective-permute-done.6.refs_2_.refs_0_, ...), custom_call_target="tpu_custom_call" | custom-call | flops 163840000 | bytes 320000 | tf_op jit(solution)/shard_map/extra/pallas_call | solution.py:207
  52.3 0.6 shard_map.51
  52.9 0.8 %shard_map.52 = (f32[2,200,200]{2,1,0:T(8,128)S(1)}, f32[2,200,200]{2,1,0:T(8,128)S(1)}) custom-call(bf16[2,200,512]{2,1,0:T(8,128)(2,1)S(1)} %get-tuple-element.27.refs_2_.refs_0_, bf16[2,200,512]{2,1,0:T(8,128)(2,1)S(1)} %collective-permute-done.13.refs_1_, bf16[2,200,512]{2,1,0:T(8,128)(2,1)S(1)} %get-tuple-element.22.refs_0_.refs_2_, ...), custom_call_target="tpu_custom_call" | custom-call | flops 491520000 | bytes 1228800 | tf_op jit(solution)/shard_map/pallas_call | solution.py:288
  53.8 0.8 %collective-permute-done.12.refs_1_ = bf16[1,200,512]{2,1,0:T(8,128)(2,1)S(1)} collective-permute-done((bf16[1,200,512]{2,1,0:T(8,128)(2,1)S(1)}, bf16[1,200,512]{2,1,0:T(8,128)(2,1)S(1)}, u32[]{:S(2)}, u32[]{:S(2)}) %collective-permute-start.12) | collective-permute-done | bytes 204832 | tf_op jit(solution)/shard_map/ppermute | solution.py:411
  55.0 0.6 collective-permute-start.16
  55.5 0.6 shard_map.50
  56.2 1.6 %collective-permute-start.11 = (bf16[200,200]{1,0:T(8,128)(2,1)S(1)}, bf16[200,200]{1,0:T(8,128)(2,1)S(1)}, u32[]{:S(2)}, u32[]{:S(2)}) collective-permute-start(bf16[200,200]{1,0:T(8,128)(2,1)S(1)} %get-tuple-element.30), channel_id=1, source_target_pairs={{0,1},{1,0},{2,3},{3,2},{4,5},{5,4},{6,7},{7,6},{8,9},{9,8},{10,11... | collective-permute-start | bytes 240008 | tf_op jit(solution)/shard_map/ppermute | solution.py:411
  57.8 5.5 %collective-permute-done.11.packed_ref = bf16[200,200]{1,0:T(8,128)(2,1)S(1)} collective-permute-done((bf16[200,200]{1,0:T(8,128)(2,1)S(1)}, bf16[200,200]{1,0:T(8,128)(2,1)S(1)}, u32[]{:S(2)}, u32[]{:S(2)}) %collective-permute-start.11) | collective-permute-done | bytes 80032 | tf_op jit(solution)/shard_map/ppermute | solution.py:411
  63.2 1.1 %base.1 = (f32[200,512]{1,0:T(8,128)S(1)}, f32[200,512]{1,0:T(8,128)S(1)}) custom-call(bf16[200,512]{1,0:T(8,128)(2,1)S(1)} %bitcast.8, bf16[200,512]{1,0:T(8,128)(2,1)S(1)} %collective-permute-done.other_ref, f32[2,200,200]{2,1,0:T(8,128)S(1)} %get-tuple-element.29.total_ref, bf16[200,200]{1,0:T(8,128)(2,1)S(1)} %collective-permute-done.11.packed_ref, ...), custom_call_target="tpu_custom_call" | custom-call | flops 655360000 | bytes 819200 | tf_op jit(solution)/shard_map/base/pallas_call | solution.py:337
  64.3 3.0 %update.1 = f32[1,200,512]{2,1,0:T(8,128)} custom-call(bf16[200,512]{1,0:T(8,128)(2,1)S(1)} %bitcast.9, bf16[200,512]{1,0:T(8,128)(2,1)S(1)} %collective-permute-done.other_ref, f32[200,512]{1,0:T(8,128)S(1)} %get-tuple-element.36.base_ref, f32[200,512]{1,0:T(8,128)S(1)} %get-tuple-element.37.base_other_ref, ...), custom_call_target="tpu_custom_call" | custom-call | tf_op jit(solution)/shard_map/update/pallas_call | solution.py:384
  (21 shorter events, 1.9 us)
Async XLA Ops:
  0.0 8.5 %collective-permute-start = (bf16[200,512]{1,0:T(8,128)(2,1)}, bf16[200,512]{1,0:T(8,128)(2,1)S(1)}, u32[]{:S(2)}, u32[]{:S(2)}) collective-permute-start(bf16[200,512]{1,0:T(8,128)(2,1)} %bitcast.4), channel_id=1, source_target_pairs={{0,1},{1,0},{2,3},{3,2},{4,5},{5,4},{6,7},{7,6},{8,9},{9,8},{10,11... | collective-permute-start | bytes 614408 | tf_op jit(solution)/shard_map/ppermute | solution.py:411
  3.0 8.3 %collective-permute-start.9 = (bf16[200,512]{1,0:T(8,128)(2,1)}, bf16[200,512]{1,0:T(8,128)(2,1)S(1)}, u32[]{:S(2)}, u32[]{:S(2)}) collective-permute-start(bf16[200,512]{1,0:T(8,128)(2,1)} %bitcast.5), channel_id=1, source_target_pairs={{6,0},{4,2},{2,4},{0,6},{14,8},{12,10},{10,12},{8,14},{22,16},{20,... | collective-permute-start | bytes 614408 | tf_op jit(solution)/shard_map/ppermute | solution.py:414
  3.6 10.3 %collective-permute-start.5 = (bf16[200,512]{1,0:T(8,128)(2,1)}, bf16[200,512]{1,0:T(8,128)(2,1)S(1)}, u32[]{:S(2)}, u32[]{:S(2)}) collective-permute-start(bf16[200,512]{1,0:T(8,128)(2,1)} %bitcast.6), channel_id=1, source_target_pairs={{26,0},{24,2},{30,4},{28,6},{2,8},{0,10},{6,12},{4,14},{10,16},{8,... | collective-permute-start | bytes 614408 | tf_op jit(solution)/shard_map/ppermute | solution.py:414
  5.8 11.8 %collective-permute-start.1 = (bf16[200,512]{1,0:T(8,128)(2,1)}, bf16[200,512]{1,0:T(8,128)(2,1)S(1)}, u32[]{:S(2)}, u32[]{:S(2)}) collective-permute-start(bf16[200,512]{1,0:T(8,128)(2,1)} %bitcast.7), channel_id=1, source_target_pairs={{10,0},{8,2},{14,4},{12,6},{18,8},{16,10},{22,12},{20,14},{26,16},... | collective-permute-start | bytes 614408 | tf_op jit(solution)/shard_map/ppermute | solution.py:414
  8.5 10.0 %collective-permute-start.10 = (bf16[200,512]{1,0:T(8,128)(2,1)S(1)}, bf16[200,512]{1,0:T(8,128)(2,1)S(1)}, u32[]{:S(2)}, u32[]{:S(2)}) collective-permute-start(bf16[200,512]{1,0:T(8,128)(2,1)S(1)} %collective-permute-done.other_ref), channel_id=1, source_target_pairs={{6,0},{4,2},{2,4},{0,6},{14,8},{12,10},{10,12},{8,14},{22,16},{20,... | collective-permute-start | bytes 614408 | tf_op jit(solution)/shard_map/ppermute | solution.py:414
  9.0 13.7 %collective-permute-start.7 = (bf16[200,512]{1,0:T(8,128)(2,1)S(1)}, bf16[200,512]{1,0:T(8,128)(2,1)S(1)}, u32[]{:S(2)}, u32[]{:S(2)}) collective-permute-start(bf16[200,512]{1,0:T(8,128)(2,1)S(1)} %collective-permute-done.other_ref), channel_id=1, source_target_pairs={{26,0},{24,2},{30,4},{28,6},{2,8},{0,10},{6,12},{4,14},{10,16},{8,... | collective-permute-start | bytes 614408 | tf_op jit(solution)/shard_map/ppermute | solution.py:414
  11.3 15.1 %collective-permute-start.3 = (bf16[200,512]{1,0:T(8,128)(2,1)S(1)}, bf16[200,512]{1,0:T(8,128)(2,1)S(1)}, u32[]{:S(2)}, u32[]{:S(2)}) collective-permute-start(bf16[200,512]{1,0:T(8,128)(2,1)S(1)} %collective-permute-done.other_ref), channel_id=1, source_target_pairs={{10,0},{8,2},{14,4},{12,6},{18,8},{16,10},{22,12},{20,14},{26,16},... | collective-permute-start | bytes 614408 | tf_op jit(solution)/shard_map/ppermute | solution.py:414
  13.9 14.8 %collective-permute-start.6 = (bf16[200,512]{1,0:T(8,128)(2,1)S(1)}, bf16[200,512]{1,0:T(8,128)(2,1)S(1)}, u32[]{:S(2)}, u32[]{:S(2)}) collective-permute-start(bf16[200,512]{1,0:T(8,128)(2,1)S(1)} %collective-permute-done.5.refs_2_), channel_id=1, source_target_pairs={{6,0},{4,2},{2,4},{0,6},{14,8},{12,10},{10,12},{8,14},{22,16},{20,... | collective-permute-start | bytes 614408 | tf_op jit(solution)/shard_map/ppermute | solution.py:414
  15.1 3.3 %copy-start.2 = (f32[12]{0:T(128)S(1)}, f32[12]{0:T(128)}, u32[]{:S(2)}) copy-start(f32[12]{0:T(128)} %weight_ref.7) | copy-start | bytes 148
  17.6 12.9 %collective-permute-start.2 = (bf16[200,512]{1,0:T(8,128)(2,1)S(1)}, bf16[200,512]{1,0:T(8,128)(2,1)S(1)}, u32[]{:S(2)}, u32[]{:S(2)}) collective-permute-start(bf16[200,512]{1,0:T(8,128)(2,1)S(1)} %collective-permute-done.1.refs_0_), channel_id=1, source_target_pairs={{6,0},{4,2},{2,4},{0,6},{14,8},{12,10},{10,12},{8,14},{22,16},{20,... | collective-permute-start | bytes 614408 | tf_op jit(solution)/shard_map/ppermute | solution.py:414
  18.5 2.2 %copy-start = (bf16[1,12,200,800]{3,2,1,0:T(8,128)(2,1)S(1)}, bf16[1,12,200,800]{3,2,1,0:T(8,128)(2,1)}, u32[]{:S(2)}) copy-start(bf16[1,12,200,800]{3,2,1,0:T(8,128)(2,1)} %margins_ref.5) | copy-start | bytes 11520004
  22.4 29.9 %collective-permute-start.15 = (bf16[2,200,512]{2,1,0:T(8,128)(2,1)S(1)}, bf16[2,200,512]{2,1,0:T(8,128)(2,1)S(1)}, u32[]{:S(2)}, u32[]{:S(2)}) collective-permute-start(bf16[2,200,512]{2,1,0:T(8,128)(2,1)S(1)} %get-tuple-element.26.refs_1_), channel_id=1, source_target_pairs={{0,1},{1,0},{2,3},{3,2},{4,5},{5,4},{6,7},{7,6},{8,9},{9,8},{10,11... | collective-permute-start | bytes 1228808 | tf_op jit(solution)/shard_map/ppermute | solution.py:411
  28.1 24.8 %collective-permute-start.13 = (bf16[2,200,512]{2,1,0:T(8,128)(2,1)S(1)}, bf16[2,200,512]{2,1,0:T(8,128)(2,1)S(1)}, u32[]{:S(2)}, u32[]{:S(2)}) collective-permute-start(bf16[2,200,512]{2,1,0:T(8,128)(2,1)S(1)} %get-tuple-element.28.refs_3_), channel_id=1, source_target_pairs={{0,1},{1,0},{2,3},{3,2},{4,5},{5,4},{6,7},{7,6},{8,9},{9,8},{10,11... | collective-permute-start | bytes 1228808 | tf_op jit(solution)/shard_map/ppermute | solution.py:411
  28.7 7.2 %collective-permute-start.8 = (bf16[200,512]{1,0:T(8,128)(2,1)S(1)}, bf16[200,512]{1,0:T(8,128)(2,1)S(1)}, u32[]{:S(2)}, u32[]{:S(2)}) collective-permute-start(bf16[200,512]{1,0:T(8,128)(2,1)S(1)} %collective-permute-done.7.refs_3_), channel_id=1, source_target_pairs={{6,0},{4,2},{2,4},{0,6},{14,8},{12,10},{10,12},{8,14},{22,16},{20,... | collective-permute-start | bytes 614408 | tf_op jit(solution)/shard_map/ppermute | solution.py:414
  28.7 11.6 %collective-permute-start.4 = (bf16[200,512]{1,0:T(8,128)(2,1)S(1)}, bf16[200,512]{1,0:T(8,128)(2,1)S(1)}, u32[]{:S(2)}, u32[]{:S(2)}) collective-permute-start(bf16[200,512]{1,0:T(8,128)(2,1)S(1)} %collective-permute-done.3.refs_1_), channel_id=1, source_target_pairs={{6,0},{4,2},{2,4},{0,6},{14,8},{12,10},{10,12},{8,14},{22,16},{20,... | collective-permute-start | bytes 614408 | tf_op jit(solution)/shard_map/ppermute | solution.py:414
  30.5 20.8 %collective-permute-start.14 = (bf16[200,800]{1,0:T(8,128)(2,1)S(1)}, bf16[200,800]{1,0:T(8,128)(2,1)S(1)}, u32[]{:S(2)}, u32[]{:S(2)}) collective-permute-start(bf16[200,800]{1,0:T(8,128)(2,1)S(1)} %dynamic-slice_bitcast_fusion), channel_id=1, source_target_pairs={{0,1},{1,0},{2,3},{3,2},{4,5},{5,4},{6,7},{7,6},{8,9},{9,8},{10,11... | collective-permute-start | bytes 960008 | tf_op jit(solution)/shard_map/ppermute | solution.py:411
  42.0 12.5 %collective-permute-start.12 = (bf16[1,200,512]{2,1,0:T(8,128)(2,1)S(1)}, bf16[1,200,512]{2,1,0:T(8,128)(2,1)S(1)}, u32[]{:S(2)}, u32[]{:S(2)}) collective-permute-start(bf16[1,200,512]{2,1,0:T(8,128)(2,1)S(1)} %get-tuple-element.23.refs_1_), channel_id=1, source_target_pairs={{0,1},{1,0},{2,3},{3,2},{4,5},{5,4},{6,7},{7,6},{8,9},{9,8},{10,11... | collective-permute-start | bytes 614408 | tf_op jit(solution)/shard_map/ppermute | solution.py:411
  44.7 18.5 %copy-start.1 = (bf16[1,200,512]{2,1,0:T(8,128)(2,1)S(1)}, bf16[1,200,512]{2,1,0:T(8,128)(2,1)}, u32[]{:S(2)}) copy-start(bf16[1,200,512]{2,1,0:T(8,128)(2,1)} %param.5) | copy-start | bytes 614404
  55.0 9.3 %collective-permute-start.16 = (bf16[2,200,200]{2,1,0:T(8,128)(2,1)S(1)}, bf16[2,200,200]{2,1,0:T(8,128)(2,1)S(1)}, u32[]{:S(2)}, u32[]{:S(2)}) collective-permute-start(bf16[2,200,200]{2,1,0:T(8,128)(2,1)S(1)} %get-tuple-element.38), channel_id=1, source_target_pairs={{0,1},{1,0},{2,3},{3,2},{4,5},{5,4},{6,7},{7,6},{8,9},{9,8},{10,11... | collective-permute-start | bytes 480008 | tf_op jit(solution)/shard_map/ppermute | solution.py:411
  56.2 7.0 %collective-permute-start.11 = (bf16[200,200]{1,0:T(8,128)(2,1)S(1)}, bf16[200,200]{1,0:T(8,128)(2,1)S(1)}, u32[]{:S(2)}, u32[]{:S(2)}) collective-permute-start(bf16[200,200]{1,0:T(8,128)(2,1)S(1)} %get-tuple-element.30), channel_id=1, source_target_pairs={{0,1},{1,0},{2,3},{3,2},{4,5},{5,4},{6,7},{7,6},{8,9},{9,8},{10,11... | collective-permute-start | bytes 240008 | tf_op jit(solution)/shard_map/ppermute | solution.py:411

commit v7 on v6

--- a/solution.py
+++ b/solution.py
@@ -376,7 +376,11 @@
     both_sides = left_centre * right + right_centre * left + dot_complex(left, right)
     factor = -0.75 * rest - 0.5 * both_sides
     centre = 2.25 - 0.75 * CENTRE - 0.5 * left_centre * right_centre
-    out_ref[0] = (product * centre + dot_complex(product, factor)) * (scaling * scale)
+    stacked = jnp.concatenate([factor, times_i(factor)], axis=0)
+    high, low = split(product)
+    stacked_high, stacked_low = split(stacked)
+    change = dot(high, stacked_high) + dot(low, stacked_high) + dot(high, stacked_low)
+    out_ref[0] = (product * centre + change) * (scaling * scale)
 
 
 def update(scale, own, other, bases, theirs):

time: 67.4 us -> 67.7 us (level)
  no operation moved by 1% of the time
where the time goes in v7:
time: 67.7 us; the launch traced here: 67.5 us
  waiting for transfers between devices  26.6 us (39%)
  starting transfers between devices  23.3 us (34%)
  Pallas kernels  14.6 us (22%)
  local copies, waits for them, and re-layouts  2.26 us (3%)
  between operations  0.81 us (1%)
    ppermute x10, starting transfers between devices, fetch(): return lax.ppermute(value, 'kpt', fetch_pairs(shift, point_count))  14.1 us
    ppermute x10, waiting for transfers between devices, fetch(): return lax.ppermute(value, 'kpt', fetch_pairs(shift, point_count))  13.8 us
    ppermute x7, waiting for transfers between devices, exchange(): return lax.ppermute(value, 'band', swap)  12.8 us
    ppermute x7, starting transfers between devices, exchange(): return lax.ppermute(value, 'band', swap)  9.19 us
    pallas_call x3, Pallas kernels, project(): pl.pallas_call(functools.partial(project_kernel, groups, batch * BATCH, s...  5.21 us
    pallas_call x1, Pallas kernels, update(): pl.pallas_call(functools.partial(update_kernel, scale), in_specs=[VMEM] *...  3.23 us
    unnamed x6, local copies, waits for them, and re-layouts  2.23 us
    pallas_call x3, Pallas kernels, cross(): pl.pallas_call(functools.partial(cross_kernel, terms, len(blocks), before...  1.88 us
  transfers between devices with their start and end apart: 17, of which 7 were waited for; matrix products, arithmetic and copies ran while one was open for 0% of the time, Pallas kernels for 16%

profile of v7, /device:TPU:0, one launch (start us, length us, event | category | flops | bytes accessed | tf_op | source)
XLA Modules:
  0.0 67.5 jit_solution(10652803950271023461)
XLA Ops:
  0.0 3.0 %collective-permute-start = (bf16[200,512]{1,0:T(8,128)(2,1)}, bf16[200,512]{1,0:T(8,128)(2,1)S(1)}, u32[]{:S(2)}, u32[]{:S(2)}) collective-permute-start(bf16[200,512]{1,0:T(8,128)(2,1)} %bitcast.4), channel_id=1, source_target_pairs={{0,1},{1,0},{2,3},{3,2},{4,5},{5,4},{6,7},{7,6},{8,9},{9,8},{10,11... | collective-permute-start | bytes 614408 | tf_op jit(solution)/shard_map/ppermute | solution.py:415
  3.0 0.7 collective-permute-start.9
  3.6 2.1 %collective-permute-start.5 = (bf16[200,512]{1,0:T(8,128)(2,1)}, bf16[200,512]{1,0:T(8,128)(2,1)S(1)}, u32[]{:S(2)}, u32[]{:S(2)}) collective-permute-start(bf16[200,512]{1,0:T(8,128)(2,1)} %bitcast.6), channel_id=1, source_target_pairs={{26,0},{24,2},{30,4},{28,6},{2,8},{0,10},{6,12},{4,14},{10,16},{8,... | collective-permute-start | bytes 614408 | tf_op jit(solution)/shard_map/ppermute | solution.py:418
  5.8 2.0 %collective-permute-start.1 = (bf16[200,512]{1,0:T(8,128)(2,1)}, bf16[200,512]{1,0:T(8,128)(2,1)S(1)}, u32[]{:S(2)}, u32[]{:S(2)}) collective-permute-start(bf16[200,512]{1,0:T(8,128)(2,1)} %bitcast.7), channel_id=1, source_target_pairs={{10,0},{8,2},{14,4},{12,6},{18,8},{16,10},{22,12},{20,14},{26,16},... | collective-permute-start | bytes 614408 | tf_op jit(solution)/shard_map/ppermute | solution.py:418
  9.0 2.3 %collective-permute-start.7 = (bf16[200,512]{1,0:T(8,128)(2,1)S(1)}, bf16[200,512]{1,0:T(8,128)(2,1)S(1)}, u32[]{:S(2)}, u32[]{:S(2)}) collective-permute-start(bf16[200,512]{1,0:T(8,128)(2,1)S(1)} %collective-permute-done.other_ref), channel_id=1, source_target_pairs={{26,0},{24,2},{30,4},{28,6},{2,8},{0,10},{6,12},{4,14},{10,16},{8,... | collective-permute-start | bytes 614408 | tf_op jit(solution)/shard_map/ppermute | solution.py:418
  11.3 2.6 %collective-permute-start.3 = (bf16[200,512]{1,0:T(8,128)(2,1)S(1)}, bf16[200,512]{1,0:T(8,128)(2,1)S(1)}, u32[]{:S(2)}, u32[]{:S(2)}) collective-permute-start(bf16[200,512]{1,0:T(8,128)(2,1)S(1)} %collective-permute-done.other_ref), channel_id=1, source_target_pairs={{10,0},{8,2},{14,4},{12,6},{18,8},{16,10},{22,12},{20,14},{26,16},... | collective-permute-start | bytes 614408 | tf_op jit(solution)/shard_map/ppermute | solution.py:418
  13.9 1.2 %collective-permute-start.6 = (bf16[200,512]{1,0:T(8,128)(2,1)S(1)}, bf16[200,512]{1,0:T(8,128)(2,1)S(1)}, u32[]{:S(2)}, u32[]{:S(2)}) collective-permute-start(bf16[200,512]{1,0:T(8,128)(2,1)S(1)} %collective-permute-done.5.refs_2_), channel_id=1, source_target_pairs={{6,0},{4,2},{2,4},{0,6},{14,8},{12,10},{10,12},{8,14},{22,16},{20,... | collective-permute-start | bytes 614408 | tf_op jit(solution)/shard_map/ppermute | solution.py:418
  15.1 0.6 prepare.1.place_ref
  15.7 1.9 %collective-permute-done.1.refs_0_ = bf16[200,512]{1,0:T(8,128)(2,1)S(1)} collective-permute-done((bf16[200,512]{1,0:T(8,128)(2,1)}, bf16[200,512]{1,0:T(8,128)(2,1)S(1)}, u32[]{:S(2)}, u32[]{:S(2)}) %collective-permute-start.1) | collective-permute-done | bytes 204832 | tf_op jit(solution)/shard_map/ppermute | solution.py:418
  17.6 0.9 %collective-permute-start.2 = (bf16[200,512]{1,0:T(8,128)(2,1)S(1)}, bf16[200,512]{1,0:T(8,128)(2,1)S(1)}, u32[]{:S(2)}, u32[]{:S(2)}) collective-permute-start(bf16[200,512]{1,0:T(8,128)(2,1)S(1)} %collective-permute-done.1.refs_0_), channel_id=1, source_target_pairs={{6,0},{4,2},{2,4},{0,6},{14,8},{12,10},{10,12},{8,14},{22,16},{20,... | collective-permute-start | bytes 614408 | tf_op jit(solution)/shard_map/ppermute | solution.py:418
  18.5 2.2 %copy-done = bf16[1,12,200,800]{3,2,1,0:T(8,128)(2,1)S(1)} copy-done((bf16[1,12,200,800]{3,2,1,0:T(8,128)(2,1)S(1)}, bf16[1,12,200,800]{3,2,1,0:T(8,128)(2,1)}, u32[]{:S(2)}) %copy-start) | copy-done | bytes 3840024
  20.7 1.7 %shard_map.47 = (bf16[2,200,512]{2,1,0:T(8,128)(2,1)S(1)}, bf16[2,200,512]{2,1,0:T(8,128)(2,1)S(1)}) custom-call(s32[3]{0:T(128)S(1)} %prepare.1.place_ref, f32[12]{0:T(128)S(1)} %copy-done.2, bf16[1,12,200,800]{3,2,1,0:T(8,128)(2,1)S(1)} %copy-done, bf16[200,512]{1,0:T(8,128)(2,1)S(1)} %collective-permute-done.9.refs_0_, ...), custom_call_target="tpu_custom_call" | custom-call | flops 655360000 | bytes 1280000 | tf_op jit(solution)/shard_map/pallas_call | solution.py:167
  22.7 3.7 %collective-permute-done.3.refs_1_ = bf16[200,512]{1,0:T(8,128)(2,1)S(1)} collective-permute-done((bf16[200,512]{1,0:T(8,128)(2,1)S(1)}, bf16[200,512]{1,0:T(8,128)(2,1)S(1)}, u32[]{:S(2)}, u32[]{:S(2)}) %collective-permute-start.3) | collective-permute-done | bytes 204832 | tf_op jit(solution)/shard_map/ppermute | solution.py:418
  26.4 1.7 %shard_map.48 = (bf16[2,200,512]{2,1,0:T(8,128)(2,1)S(1)}, bf16[2,200,512]{2,1,0:T(8,128)(2,1)S(1)}) custom-call(s32[3]{0:T(128)S(1)} %prepare.1.place_ref, f32[12]{0:T(128)S(1)} %copy-done.2, bf16[1,12,200,800]{3,2,1,0:T(8,128)(2,1)S(1)} %copy-done, bf16[200,512]{1,0:T(8,128)(2,1)S(1)} %collective-permute-done.1.refs_0_, ...), custom_call_target="tpu_custom_call" | custom-call | flops 655360000 | bytes 1280000 | tf_op jit(solution)/shard_map/pallas_call | solution.py:167
  28.7 1.7 %collective-permute-start.4 = (bf16[200,512]{1,0:T(8,128)(2,1)S(1)}, bf16[200,512]{1,0:T(8,128)(2,1)S(1)}, u32[]{:S(2)}, u32[]{:S(2)}) collective-permute-start(bf16[200,512]{1,0:T(8,128)(2,1)S(1)} %collective-permute-done.3.refs_1_), channel_id=1, source_target_pairs={{6,0},{4,2},{2,4},{0,6},{14,8},{12,10},{10,12},{8,14},{22,16},{20,... | collective-permute-start | bytes 614408 | tf_op jit(solution)/shard_map/ppermute | solution.py:418
  30.5 1.6 %collective-permute-start.14 = (bf16[200,800]{1,0:T(8,128)(2,1)S(1)}, bf16[200,800]{1,0:T(8,128)(2,1)S(1)}, u32[]{:S(2)}, u32[]{:S(2)}) collective-permute-start(bf16[200,800]{1,0:T(8,128)(2,1)S(1)} %dynamic-slice_bitcast_fusion), channel_id=1, source_target_pairs={{0,1},{1,0},{2,3},{3,2},{4,5},{5,4},{6,7},{7,6},{8,9},{9,8},{10,11... | collective-permute-start | bytes 960008 | tf_op jit(solution)/shard_map/ppermute | solution.py:415
  32.1 3.8 %collective-permute-done.8.refs_3_.refs_1_ = bf16[200,512]{1,0:T(8,128)(2,1)S(1)} collective-permute-done((bf16[200,512]{1,0:T(8,128)(2,1)S(1)}, bf16[200,512]{1,0:T(8,128)(2,1)S(1)}, u32[]{:S(2)}, u32[]{:S(2)}) %collective-permute-start.8) | collective-permute-done | bytes 204832 | tf_op jit(solution)/shard_map/ppermute | solution.py:418
  35.9 4.4 %collective-permute-done.4.refs_1_ = bf16[200,512]{1,0:T(8,128)(2,1)S(1)} collective-permute-done((bf16[200,512]{1,0:T(8,128)(2,1)S(1)}, bf16[200,512]{1,0:T(8,128)(2,1)S(1)}, u32[]{:S(2)}, u32[]{:S(2)}) %collective-permute-start.4) | collective-permute-done | bytes 204832 | tf_op jit(solution)/shard_map/ppermute | solution.py:418
  40.3 1.8 %shard_map.46 = (bf16[2,200,512]{2,1,0:T(8,128)(2,1)S(1)}, bf16[1,200,512]{2,1,0:T(8,128)(2,1)S(1)}, bf16[1,200,512]{2,1,0:T(8,128)(2,1)S(1)}) custom-call(s32[3]{0:T(128)S(1)} %prepare.1.place_ref, f32[12]{0:T(128)S(1)} %copy-done.2, bf16[1,12,200,800]{3,2,1,0:T(8,128)(2,1)S(1)} %copy-done, bf16[200,512]{1,0:T(8,128)(2,1)S(1)} %collective-permute-done.2.refs_0_, ...), custom_call_target="tpu_custom_call" | custom-call | flops 655360000 | bytes 1280000 | tf_op jit(solution)/shard_map/pallas_call | solution.py:167
  42.0 1.6 %collective-permute-start.12 = (bf16[1,200,512]{2,1,0:T(8,128)(2,1)S(1)}, bf16[1,200,512]{2,1,0:T(8,128)(2,1)S(1)}, u32[]{:S(2)}, u32[]{:S(2)}) collective-permute-start(bf16[1,200,512]{2,1,0:T(8,128)(2,1)S(1)} %get-tuple-element.23.refs_1_), channel_id=1, source_target_pairs={{0,1},{1,0},{2,3},{3,2},{4,5},{5,4},{6,7},{7,6},{8,9},{9,8},{10,11... | collective-permute-start | bytes 614408 | tf_op jit(solution)/shard_map/ppermute | solution.py:415
  43.6 1.1 %shard_map.49.refs_3_ = f32[2,200,200]{2,1,0:T(8,128)S(1)} custom-call(bf16[2,200,512]{2,1,0:T(8,128)(2,1)S(1)} %get-tuple-element.25.refs_0_, bf16[2,200,512]{2,1,0:T(8,128)(2,1)S(1)} %get-tuple-element.26.refs_1_, bf16[2,200,512]{2,1,0:T(8,128)(2,1)S(1)} %get-tuple-element.27.refs_2_.refs_0_, bf16[2,200,512]{2,1,0:T(8,128)(2,1)S(1)} %get-tuple-element.28.refs_3_), custom_call_target="tpu_custom_call" | custom-call | flops 655360000 | bytes 1638400 | tf_op jit(solution)/shard_map/pallas_call | solution.py:252
  44.7 6.6 %collective-permute-done.14.margin_ref = bf16[200,800]{1,0:T(8,128)(2,1)S(1)} collective-permute-done((bf16[200,800]{1,0:T(8,128)(2,1)S(1)}, bf16[200,800]{1,0:T(8,128)(2,1)S(1)}, u32[]{:S(2)}, u32[]{:S(2)}) %collective-permute-start.14) | collective-permute-done | bytes 320032 | tf_op jit(solution)/shard_map/ppermute | solution.py:415
  51.3 1.0 %extra.1.refs_3_ = bf16[1,200,512]{2,1,0:T(8,128)(2,1)S(1)} custom-call(s32[3]{0:T(128)S(1)} %prepare.1.place_ref, f32[12]{0:T(128)S(1)} %copy-done.2, bf16[200,800]{1,0:T(8,128)(2,1)S(1)} %collective-permute-done.14.margin_ref, bf16[200,512]{1,0:T(8,128)(2,1)S(1)} %collective-permute-done.6.refs_2_.refs_0_, ...), custom_call_target="tpu_custom_call" | custom-call | flops 163840000 | bytes 320000 | tf_op jit(solution)/shard_map/extra/pallas_call | solution.py:207
  52.3 0.6 shard_map.51
  52.9 0.8 %shard_map.52 = (f32[2,200,200]{2,1,0:T(8,128)S(1)}, f32[2,200,200]{2,1,0:T(8,128)S(1)}) custom-call(bf16[2,200,512]{2,1,0:T(8,128)(2,1)S(1)} %get-tuple-element.27.refs_2_.refs_0_, bf16[2,200,512]{2,1,0:T(8,128)(2,1)S(1)} %collective-permute-done.13.refs_1_, bf16[2,200,512]{2,1,0:T(8,128)(2,1)S(1)} %get-tuple-element.22.refs_0_.refs_2_, ...), custom_call_target="tpu_custom_call" | custom-call | flops 491520000 | bytes 1228800 | tf_op jit(solution)/shard_map/pallas_call | solution.py:288
  53.8 0.8 %collective-permute-done.12.refs_1_ = bf16[1,200,512]{2,1,0:T(8,128)(2,1)S(1)} collective-permute-done((bf16[1,200,512]{2,1,0:T(8,128)(2,1)S(1)}, bf16[1,200,512]{2,1,0:T(8,128)(2,1)S(1)}, u32[]{:S(2)}, u32[]{:S(2)}) %collective-permute-start.12) | collective-permute-done | bytes 204832 | tf_op jit(solution)/shard_map/ppermute | solution.py:415
  55.0 0.6 collective-permute-start.16
  55.5 0.6 shard_map.50
  56.2 1.6 %collective-permute-start.11 = (bf16[200,200]{1,0:T(8,128)(2,1)S(1)}, bf16[200,200]{1,0:T(8,128)(2,1)S(1)}, u32[]{:S(2)}, u32[]{:S(2)}) collective-permute-start(bf16[200,200]{1,0:T(8,128)(2,1)S(1)} %get-tuple-element.30), channel_id=1, source_target_pairs={{0,1},{1,0},{2,3},{3,2},{4,5},{5,4},{6,7},{7,6},{8,9},{9,8},{10,11... | collective-permute-start | bytes 240008 | tf_op jit(solution)/shard_map/ppermute | solution.py:415
  57.8 5.5 %collective-permute-done.11.packed_ref = bf16[200,200]{1,0:T(8,128)(2,1)S(1)} collective-permute-done((bf16[200,200]{1,0:T(8,128)(2,1)S(1)}, bf16[200,200]{1,0:T(8,128)(2,1)S(1)}, u32[]{:S(2)}, u32[]{:S(2)}) %collective-permute-start.11) | collective-permute-done | bytes 80032 | tf_op jit(solution)/shard_map/ppermute | solution.py:415
  63.2 1.1 %base.1 = (f32[200,512]{1,0:T(8,128)S(1)}, f32[200,512]{1,0:T(8,128)S(1)}) custom-call(bf16[200,512]{1,0:T(8,128)(2,1)S(1)} %bitcast.8, bf16[200,512]{1,0:T(8,128)(2,1)S(1)} %collective-permute-done.other_ref, f32[2,200,200]{2,1,0:T(8,128)S(1)} %get-tuple-element.29.total_ref, bf16[200,200]{1,0:T(8,128)(2,1)S(1)} %collective-permute-done.11.packed_ref, ...), custom_call_target="tpu_custom_call" | custom-call | flops 655360000 | bytes 819200 | tf_op jit(solution)/shard_map/base/pallas_call | solution.py:337
  64.3 3.2 %update.1 = f32[1,200,512]{2,1,0:T(8,128)} custom-call(bf16[200,512]{1,0:T(8,128)(2,1)S(1)} %bitcast.9, bf16[200,512]{1,0:T(8,128)(2,1)S(1)} %collective-permute-done.other_ref, f32[200,512]{1,0:T(8,128)S(1)} %get-tuple-element.36.base_ref, f32[200,512]{1,0:T(8,128)S(1)} %get-tuple-element.37.base_other_ref, ...), custom_call_target="tpu_custom_call" | custom-call | tf_op jit(solution)/shard_map/update/pallas_call | solution.py:388
  (21 shorter events, 1.9 us)
Async XLA Ops:
  0.0 8.5 %collective-permute-start = (bf16[200,512]{1,0:T(8,128)(2,1)}, bf16[200,512]{1,0:T(8,128)(2,1)S(1)}, u32[]{:S(2)}, u32[]{:S(2)}) collective-permute-start(bf16[200,512]{1,0:T(8,128)(2,1)} %bitcast.4), channel_id=1, source_target_pairs={{0,1},{1,0},{2,3},{3,2},{4,5},{5,4},{6,7},{7,6},{8,9},{9,8},{10,11... | collective-permute-start | bytes 614408 | tf_op jit(solution)/shard_map/ppermute | solution.py:415
  3.0 8.3 %collective-permute-start.9 = (bf16[200,512]{1,0:T(8,128)(2,1)}, bf16[200,512]{1,0:T(8,128)(2,1)S(1)}, u32[]{:S(2)}, u32[]{:S(2)}) collective-permute-start(bf16[200,512]{1,0:T(8,128)(2,1)} %bitcast.5), channel_id=1, source_target_pairs={{6,0},{4,2},{2,4},{0,6},{14,8},{12,10},{10,12},{8,14},{22,16},{20,... | collective-permute-start | bytes 614408 | tf_op jit(solution)/shard_map/ppermute | solution.py:418
  3.6 10.3 %collective-permute-start.5 = (bf16[200,512]{1,0:T(8,128)(2,1)}, bf16[200,512]{1,0:T(8,128)(2,1)S(1)}, u32[]{:S(2)}, u32[]{:S(2)}) collective-permute-start(bf16[200,512]{1,0:T(8,128)(2,1)} %bitcast.6), channel_id=1, source_target_pairs={{26,0},{24,2},{30,4},{28,6},{2,8},{0,10},{6,12},{4,14},{10,16},{8,... | collective-permute-start | bytes 614408 | tf_op jit(solution)/shard_map/ppermute | solution.py:418
  5.8 11.8 %collective-permute-start.1 = (bf16[200,512]{1,0:T(8,128)(2,1)}, bf16[200,512]{1,0:T(8,128)(2,1)S(1)}, u32[]{:S(2)}, u32[]{:S(2)}) collective-permute-start(bf16[200,512]{1,0:T(8,128)(2,1)} %bitcast.7), channel_id=1, source_target_pairs={{10,0},{8,2},{14,4},{12,6},{18,8},{16,10},{22,12},{20,14},{26,16},... | collective-permute-start | bytes 614408 | tf_op jit(solution)/shard_map/ppermute | solution.py:418
  8.5 10.0 %collective-permute-start.10 = (bf16[200,512]{1,0:T(8,128)(2,1)S(1)}, bf16[200,512]{1,0:T(8,128)(2,1)S(1)}, u32[]{:S(2)}, u32[]{:S(2)}) collective-permute-start(bf16[200,512]{1,0:T(8,128)(2,1)S(1)} %collective-permute-done.other_ref), channel_id=1, source_target_pairs={{6,0},{4,2},{2,4},{0,6},{14,8},{12,10},{10,12},{8,14},{22,16},{20,... | collective-permute-start | bytes 614408 | tf_op jit(solution)/shard_map/ppermute | solution.py:418
  9.0 13.7 %collective-permute-start.7 = (bf16[200,512]{1,0:T(8,128)(2,1)S(1)}, bf16[200,512]{1,0:T(8,128)(2,1)S(1)}, u32[]{:S(2)}, u32[]{:S(2)}) collective-permute-start(bf16[200,512]{1,0:T(8,128)(2,1)S(1)} %collective-permute-done.other_ref), channel_id=1, source_target_pairs={{26,0},{24,2},{30,4},{28,6},{2,8},{0,10},{6,12},{4,14},{10,16},{8,... | collective-permute-start | bytes 614408 | tf_op jit(solution)/shard_map/ppermute | solution.py:418
  11.3 15.1 %collective-permute-start.3 = (bf16[200,512]{1,0:T(8,128)(2,1)S(1)}, bf16[200,512]{1,0:T(8,128)(2,1)S(1)}, u32[]{:S(2)}, u32[]{:S(2)}) collective-permute-start(bf16[200,512]{1,0:T(8,128)(2,1)S(1)} %collective-permute-done.other_ref), channel_id=1, source_target_pairs={{10,0},{8,2},{14,4},{12,6},{18,8},{16,10},{22,12},{20,14},{26,16},... | collective-permute-start | bytes 614408 | tf_op jit(solution)/shard_map/ppermute | solution.py:418
  13.9 14.8 %collective-permute-start.6 = (bf16[200,512]{1,0:T(8,128)(2,1)S(1)}, bf16[200,512]{1,0:T(8,128)(2,1)S(1)}, u32[]{:S(2)}, u32[]{:S(2)}) collective-permute-start(bf16[200,512]{1,0:T(8,128)(2,1)S(1)} %collective-permute-done.5.refs_2_), channel_id=1, source_target_pairs={{6,0},{4,2},{2,4},{0,6},{14,8},{12,10},{10,12},{8,14},{22,16},{20,... | collective-permute-start | bytes 614408 | tf_op jit(solution)/shard_map/ppermute | solution.py:418
  15.1 3.3 %copy-start.2 = (f32[12]{0:T(128)S(1)}, f32[12]{0:T(128)}, u32[]{:S(2)}) copy-start(f32[12]{0:T(128)} %weight_ref.7) | copy-start | bytes 148
  17.6 12.9 %collective-permute-start.2 = (bf16[200,512]{1,0:T(8,128)(2,1)S(1)}, bf16[200,512]{1,0:T(8,128)(2,1)S(1)}, u32[]{:S(2)}, u32[]{:S(2)}) collective-permute-start(bf16[200,512]{1,0:T(8,128)(2,1)S(1)} %collective-permute-done.1.refs_0_), channel_id=1, source_target_pairs={{6,0},{4,2},{2,4},{0,6},{14,8},{12,10},{10,12},{8,14},{22,16},{20,... | collective-permute-start | bytes 614408 | tf_op jit(solution)/shard_map/ppermute | solution.py:418
  18.5 2.2 %copy-start = (bf16[1,12,200,800]{3,2,1,0:T(8,128)(2,1)S(1)}, bf16[1,12,200,800]{3,2,1,0:T(8,128)(2,1)}, u32[]{:S(2)}) copy-start(bf16[1,12,200,800]{3,2,1,0:T(8,128)(2,1)} %margins_ref.5) | copy-start | bytes 11520004
  22.4 29.9 %collective-permute-start.15 = (bf16[2,200,512]{2,1,0:T(8,128)(2,1)S(1)}, bf16[2,200,512]{2,1,0:T(8,128)(2,1)S(1)}, u32[]{:S(2)}, u32[]{:S(2)}) collective-permute-start(bf16[2,200,512]{2,1,0:T(8,128)(2,1)S(1)} %get-tuple-element.26.refs_1_), channel_id=1, source_target_pairs={{0,1},{1,0},{2,3},{3,2},{4,5},{5,4},{6,7},{7,6},{8,9},{9,8},{10,11... | collective-permute-start | bytes 1228808 | tf_op jit(solution)/shard_map/ppermute | solution.py:415
  28.1 24.8 %collective-permute-start.13 = (bf16[2,200,512]{2,1,0:T(8,128)(2,1)S(1)}, bf16[2,200,512]{2,1,0:T(8,128)(2,1)S(1)}, u32[]{:S(2)}, u32[]{:S(2)}) collective-permute-start(bf16[2,200,512]{2,1,0:T(8,128)(2,1)S(1)} %get-tuple-element.28.refs_3_), channel_id=1, source_target_pairs={{0,1},{1,0},{2,3},{3,2},{4,5},{5,4},{6,7},{7,6},{8,9},{9,8},{10,11... | collective-permute-start | bytes 1228808 | tf_op jit(solution)/shard_map/ppermute | solution.py:415
  28.7 7.2 %collective-permute-start.8 = (bf16[200,512]{1,0:T(8,128)(2,1)S(1)}, bf16[200,512]{1,0:T(8,128)(2,1)S(1)}, u32[]{:S(2)}, u32[]{:S(2)}) collective-permute-start(bf16[200,512]{1,0:T(8,128)(2,1)S(1)} %collective-permute-done.7.refs_3_), channel_id=1, source_target_pairs={{6,0},{4,2},{2,4},{0,6},{14,8},{12,10},{10,12},{8,14},{22,16},{20,... | collective-permute-start | bytes 614408 | tf_op jit(solution)/shard_map/ppermute | solution.py:418
  28.7 11.6 %collective-permute-start.4 = (bf16[200,512]{1,0:T(8,128)(2,1)S(1)}, bf16[200,512]{1,0:T(8,128)(2,1)S(1)}, u32[]{:S(2)}, u32[]{:S(2)}) collective-permute-start(bf16[200,512]{1,0:T(8,128)(2,1)S(1)} %collective-permute-done.3.refs_1_), channel_id=1, source_target_pairs={{6,0},{4,2},{2,4},{0,6},{14,8},{12,10},{10,12},{8,14},{22,16},{20,... | collective-permute-start | bytes 614408 | tf_op jit(solution)/shard_map/ppermute | solution.py:418
  30.5 20.8 %collective-permute-start.14 = (bf16[200,800]{1,0:T(8,128)(2,1)S(1)}, bf16[200,800]{1,0:T(8,128)(2,1)S(1)}, u32[]{:S(2)}, u32[]{:S(2)}) collective-permute-start(bf16[200,800]{1,0:T(8,128)(2,1)S(1)} %dynamic-slice_bitcast_fusion), channel_id=1, source_target_pairs={{0,1},{1,0},{2,3},{3,2},{4,5},{5,4},{6,7},{7,6},{8,9},{9,8},{10,11... | collective-permute-start | bytes 960008 | tf_op jit(solution)/shard_map/ppermute | solution.py:415
  42.0 12.5 %collective-permute-start.12 = (bf16[1,200,512]{2,1,0:T(8,128)(2,1)S(1)}, bf16[1,200,512]{2,1,0:T(8,128)(2,1)S(1)}, u32[]{:S(2)}, u32[]{:S(2)}) collective-permute-start(bf16[1,200,512]{2,1,0:T(8,128)(2,1)S(1)} %get-tuple-element.23.refs_1_), channel_id=1, source_target_pairs={{0,1},{1,0},{2,3},{3,2},{4,5},{5,4},{6,7},{7,6},{8,9},{9,8},{10,11... | collective-permute-start | bytes 614408 | tf_op jit(solution)/shard_map/ppermute | solution.py:415
  44.7 18.5 %copy-start.1 = (bf16[1,200,512]{2,1,0:T(8,128)(2,1)S(1)}, bf16[1,200,512]{2,1,0:T(8,128)(2,1)}, u32[]{:S(2)}) copy-start(bf16[1,200,512]{2,1,0:T(8,128)(2,1)} %param.5) | copy-start | bytes 614404
  55.0 9.3 %collective-permute-start.16 = (bf16[2,200,200]{2,1,0:T(8,128)(2,1)S(1)}, bf16[2,200,200]{2,1,0:T(8,128)(2,1)S(1)}, u32[]{:S(2)}, u32[]{:S(2)}) collective-permute-start(bf16[2,200,200]{2,1,0:T(8,128)(2,1)S(1)} %get-tuple-element.38), channel_id=1, source_target_pairs={{0,1},{1,0},{2,3},{3,2},{4,5},{5,4},{6,7},{7,6},{8,9},{9,8},{10,11... | collective-permute-start | bytes 480008 | tf_op jit(solution)/shard_map/ppermute | solution.py:415
  56.2 7.0 %collective-permute-start.11 = (bf16[200,200]{1,0:T(8,128)(2,1)S(1)}, bf16[200,200]{1,0:T(8,128)(2,1)S(1)}, u32[]{:S(2)}, u32[]{:S(2)}) collective-permute-start(bf16[200,200]{1,0:T(8,128)(2,1)S(1)} %get-tuple-element.30), channel_id=1, source_target_pairs={{0,1},{1,0},{2,3},{3,2},{4,5},{5,4},{6,7},{7,6},{8,9},{9,8},{10,11... | collective-permute-start | bytes 240008 | tf_op jit(solution)/shard_map/ppermute | solution.py:415

commit v8 on v7

--- a/solution.py
+++ b/solution.py
@@ -28,7 +28,6 @@
 CENTRE = 0.5
 PREPARE = 2 * 10**10
 VMEM = pl.BlockSpec(memory_space=pltpu.VMEM)
-LARGE_LIMIT = pltpu.CompilerParams(vmem_limit_bytes=50 * 2**20)
 LIMIT = pltpu.CompilerParams(vmem_limit_bytes=20 * 2**20)
 SMEM = pl.BlockSpec(memory_space=pltpu.SMEM)
 F32 = jnp.float32
@@ -97,125 +96,89 @@
     stacked_ref[2 * rows :, :] = times_i(whole).astype(BF16)
 
 
-def masked_block(margin, stacked, weight, limit):
-    inside = lax.broadcasted_iota(jnp.int32, (margin.shape[0], 1), 0) < limit
-    factor = jnp.where(inside, jnp.sqrt(jnp.full((1, 1), weight, F32)), 0.0)
-    return (dot(margin, stacked) * factor).astype(BF16)
-
-
-def prepare_kernel(rows, side_ref, window_ref, out_ref):
+def masked_blocks(margins, stacked, weights, limit):
+    count, rows, double = margins.shape
+    inside = lax.broadcasted_iota(jnp.int32, (rows, 1), 0) < limit
+    products = dot(margins.reshape(count * rows, double), stacked)
+    blocks = []
+    for place, weight in enumerate(weights):
+        factor = jnp.where(inside, jnp.sqrt(jnp.full((1, 1), weight, F32)), 0.0)
+        blocks.append((products[place * rows : (place + 1) * rows] * factor).astype(BF16))
+    return blocks
+
+
+def prepare_kernel(out_ref):
+    out_ref[...] = jnp.zeros_like(out_ref)
+
+
+def prepare():
+    return pl.pallas_call(
+        prepare_kernel,
+        out_specs=VMEM,
+        out_shape=jax.ShapeDtypeStruct((8, 128), jnp.int32),
+        cost_estimate=pl.CostEstimate(flops=PREPARE, bytes_accessed=2**26, transcendentals=0),
+        name="prepare",
+        compiler_params=LIMIT,
+    )()
+
+
+def project_kernel(groups, first, sent, side_ref, window_ref, weight_ref, margins_ref, *refs):
+    halves = refs[: 2 * len(groups)]
+    *out_refs, rows_ref, stacked_ref, blocks_ref = refs[2 * len(groups) :]
+    shipped_ref = None
+    if not sent:
+        shipped_ref, keep_ref, other_ref, got_ref = out_refs
+    else:
+        _, keep_ref, other_ref = out_refs
     side = side_ref[0]
-    out_ref[0] = side
-    out_ref[1] = window_ref[0] - side * rows
-    out_ref[2] = window_ref[0] - (1 - side) * rows
-
-
-def prepare(side, window_count, rows):
-    return pl.pallas_call(
-        functools.partial(prepare_kernel, rows),
-        in_specs=[SMEM] * 2,
-        out_specs=SMEM,
-        out_shape=jax.ShapeDtypeStruct((3,), jnp.int32),
-        cost_estimate=pl.CostEstimate(flops=PREPARE, bytes_accessed=64 * 2**20, transcendentals=0),
-        name="prepare",
-        compiler_params=LIMIT,
-    )(side[None], window_count)
-
-
-def project_kernel(groups, first, sent, streamed, place_ref, weight_ref, margins_ref, *refs):
-    halves = refs[: 2 * len(groups)]
-    refs = refs[2 * len(groups) :]
-    copies = []
-    if streamed:
-        *refs, fetched_ref, sems = refs
-        for member in range(BATCH):
-            source = margins_ref.at[0, first + member]
-            copies.append(
-                pltpu.make_async_copy(source, fetched_ref.at[member], sems.at[member])
-            )
-            copies[-1].start()
-    keep_ref, *give_refs, rows_ref, stacked_ref, blocks_ref = refs
-    side, limit = place_ref[0], place_ref[1]
+    rows = margins_ref.shape[2]
+    limits = [window_ref[...] - side * rows, window_ref[...] - (1 - side) * rows]
     for number, members in enumerate(groups):
         mine, other = halves[2 * number][...], halves[2 * number + 1][...]
         stack_complex(mine, other, side, rows_ref, stacked_ref)
-        for member in members:
-            if streamed:
-                copies[member].wait()
-                margin = fetched_ref[member]
-            else:
-                margin = margins_ref[0, first + member]
-            weight = weight_ref[first + member]
-            blocks_ref[member] = masked_block(margin, stacked_ref[...], weight, limit)
-    for pair in range(BATCH // 2):
+        start, count = first + members[0], len(members)
+        blocks = masked_blocks(
+            margins_ref[0, start : start + count],
+            stacked_ref[...],
+            [weight_ref[first + member] for member in members],
+            limits[0],
+        )
+        for member, block in zip(members, blocks):
+            blocks_ref[member] = block
+            if not sent:
+                @pl.when(side == member % 2)
+                def _():
+                    weight = weight_ref[first + member]
+                    (got_ref[0],) = masked_blocks(
+                        shipped_ref[...][None], stacked_ref[...], [weight], limits[1]
+                    )
+    for pair in range(keep_ref.shape[0]):
         keep_ref[pair] = blocks_ref[2 * pair + side]
-        target = give_refs[0].at[pair] if pair < sent else give_refs[1].at[pair - sent]
-        target[...] = blocks_ref[2 * pair + 1 - side]
-
-
-def project(place, weights, margins, batch, groups, halves, sent, streamed):
+        other_ref[pair] = blocks_ref[2 * pair + 1 - side]
+
+
+def project(place, weights, margins, first, groups, halves, extra, sent):
     rows, double = margins.shape[2:]
     width = halves[0].shape[-1]
-    pairs = BATCH // 2
-    counts = [pairs, sent] + ([pairs - sent] if sent < pairs else [])
-    streams = []
-    if streamed:
-        streams = [
-            pltpu.VMEM((BATCH, rows, double), BF16),
-            pltpu.SemaphoreType.DMA((BATCH,)),
-        ]
-    return pl.pallas_call(
-        functools.partial(project_kernel, groups, batch * BATCH, sent, streamed),
-        in_specs=[
-            SMEM,
-            SMEM,
-            pl.BlockSpec(memory_space=pl.ANY) if streamed else VMEM,
-            *([VMEM] * len(halves)),
-        ],
+    members = sum(len(group) for group in groups)
+    counts = [members // 2, members // 2] + ([] if sent else [1])
+    return pl.pallas_call(
+        functools.partial(project_kernel, groups, first, sent),
+        in_specs=[SMEM, VMEM, SMEM, VMEM, *([VMEM] * len(halves)), VMEM],
         out_specs=[VMEM] * len(counts),
         out_shape=[jax.ShapeDtypeStruct((count, rows, width), BF16) for count in counts],
         scratch_shapes=[
             pltpu.VMEM((2 * rows, width), F32),
             pltpu.VMEM((double, width), BF16),
-            pltpu.VMEM((BATCH, rows, width), BF16),
-            *streams,
+            pltpu.VMEM((members, rows, width), BF16),
         ],
         cost_estimate=pl.CostEstimate(
-            flops=2 * BATCH * rows * double * width,
-            bytes_accessed=2 * BATCH * rows * double,
+            flops=2 * members * rows * double * width,
+            bytes_accessed=2 * members * rows * double,
             transcendentals=0,
         ),
-        compiler_params=LARGE_LIMIT if streamed else LIMIT,
-    )(place, weights, margins, *halves)
-
-
-def extra_kernel(shipped, place_ref, weight_ref, margin_ref, *refs):
-    *halves, out_ref, rows_ref, stacked_ref = refs
-    side, limit = place_ref[0], place_ref[2]
-    mine, other = halves[0][...], halves[1][...]
-    if len(halves) > 2:
-        mine = jnp.where(side == 0, mine, halves[2][...])
-        other = jnp.where(side == 0, other, halves[3][...])
-    stack_complex(mine, other, side, rows_ref, stacked_ref)
-    weight = weight_ref[shipped + side]
-    out_ref[0] = masked_block(margin_ref[...], stacked_ref[...], weight, limit)
-
-
-def extra(place, weights, margin, shipped, halves):
-    rows, double = margin.shape
-    width = halves[0].shape[-1]
-    return pl.pallas_call(
-        functools.partial(extra_kernel, shipped),
-        in_specs=[SMEM, SMEM, VMEM, *([VMEM] * len(halves))],
-        out_specs=VMEM,
-        out_shape=jax.ShapeDtypeStruct((1, rows, width), BF16),
-        scratch_shapes=[pltpu.VMEM((2 * rows, width), F32), pltpu.VMEM((double, width), BF16)],
-        cost_estimate=pl.CostEstimate(
-            flops=2 * rows * double * width, bytes_accessed=2 * rows * double, transcendentals=0
-        ),
-        name="extra",
-        compiler_params=LIMIT,
-    )(place, weights, margin, *halves)
+        compiler_params=LIMIT,
+    )(*place, weights, margins, *halves, extra)
 
 
 def triangle(size):
@@ -417,7 +380,8 @@
     def fetch(value, shift):
         return lax.ppermute(value, "kpt", fetch_pairs(shift, point_count))
 
-    place = prepare(side, window_count, rows)
+    mark = prepare()
+    place = (side[None], window_count.reshape(1, 1))
     own = subspace[0]
     other = exchange(own)
     margin = lax.dynamic_index_in_dim(margins[0], SHIPPED + 1 - side, 0, keepdims=False)
@@ -431,28 +395,32 @@
             near = displacement((shift[0], 0, 1), point_count)
             step = displacement((0, shift[1], -1), point_count)
             halves[0, part, shift] = fetch(halves[1, part, near], step)
-    blocks, got = {}, {}
-    for batch in (2, 1, 0):
-        operands = []
-        for shift in plan[batch]:
-            operands += [halves[batch, "own", shift], halves[batch, "other", shift]]
-        sent = SHIPPED // 2 if batch == 0 else BATCH // 2
-        blocks[batch] = project(
-            place, shell_weights, margins, batch, list(plan[batch].values()), operands, sent, False
-        )
-        got[batch] = exchange(blocks[batch][1])
-    operands = []
-    for shift, members in plan[0].items():
-        if SHIPPED in members or SHIPPED + 1 in members:
-            operands += [halves[0, "own", shift], halves[0, "other", shift]]
-    got_extra = extra(place, shell_weights, margin, SHIPPED, operands)
+
+    def project_part(batch, members, extra, sent):
+        groups, operands = [], []
+        for shift, holders in plan[batch].items():
+            group = [holder - members[0] for holder in holders if holder in members]
+            if group:
+                groups.append(group)
+                operands += [halves[batch, "own", shift], halves[batch, "other", shift]]
+        first = batch * BATCH + members[0]
+        return project(place, shell_weights, margins, first, groups, operands, extra, sent)
+
+    every = range(BATCH)
+    blocks = {
+        2: project_part(2, every, mark, True),
+        1: project_part(1, every, mark, True),
+        0: project_part(0, range(SHIPPED), mark, True),
+    }
+    *rest, got_extra = project_part(0, range(SHIPPED, BATCH), margin, False)
+    got = {batch: exchange(blocks[batch][1]) for batch in (2, 1, 0)}
     (total,) = gather_own([*blocks[2], *blocks[1]], None)
-    total, packed = gather_own(blocks[0], total)
+    total, packed = gather_own([*blocks[0], *rest], total)
     other_packed = exchange(packed)
     whole = ((0, 0, 1, 0), (0, 1, 1, 1))
     crossed = cross([blocks[2][0], got[2]], whole, None, False)
     crossed = cross(
-        [blocks[1][0], got[1], blocks[0][0], got_extra], (*whole, (2, 1, 3, 0)), crossed, False
+        [blocks[1][0], got[1], rest[0], got_extra], (*whole, (2, 0, 3, 0)), crossed, False
     )
     mine, theirs = cross([blocks[0][0], got[0]], ((0, 0, 1, 0),), crossed, True)
     theirs = exchange(theirs)

time: 67.7 us -> 69 us (1.019)
  waiting for transfers between devices: 26.6 us -> 29.5 us
  starting transfers between devices: 23.3 us -> 21.3 us
  local copies, waits for them, and re-layouts: 2.26 us -> 3.25 us
    ppermute x10, waiting for transfers between devices: 13.8 us -> 17.1 us  [fetch(): return lax.ppermute(value, 'kpt', fetch_pairs(shift, point_count))]
    ppermute x10, starting transfers between devices: 14.1 us -> 13 us  [fetch(): return lax.ppermute(value, 'kpt', fetch_pairs(shift, point_count))]
    squeeze x1, local copies, waits for them, and re-layouts: 0.03 us -> 1.02 us  [on_device(): lax.dynamic_index_in_dim(margins[0], SHIPPED + 1 - side, 0, keepdims=False)]
    ppermute x7, starting transfers between devices: 9.19 us -> 8.39 us  [exchange(): return lax.ppermute(value, 'band', swap)]
    unnamed x6 -> x10, local copies, waits for them, and re-layouts: 2.23 us -> 2.24 us
  transfers between devices with their start and end apart: 17 -> 17, of which waited for: 7 -> 8; matrix products, arithmetic and copies ran while one was open for 0% -> 1% of each run, Pallas kernels for 16% -> 15%
where the time goes in v8:
time: 69 us; the launch traced here: 68.9 us
  waiting for transfers between devices  29.5 us (43%)
  starting transfers between devices  21.3 us (31%)
  Pallas kernels  14 us (20%)
  local copies, waits for them, and re-layouts  3.25 us (5%)
  between operations  0.8 us (1%)
    ppermute x10, waiting for transfers between devices, fetch(): return lax.ppermute(value, 'kpt', fetch_pairs(shift, point_count))  17.1 us
    ppermute x10, starting transfers between devices, fetch(): return lax.ppermute(value, 'kpt', fetch_pairs(shift, point_count))  13 us
    ppermute x7, waiting for transfers between devices, exchange(): return lax.ppermute(value, 'band', swap)  12.4 us
    ppermute x7, starting transfers between devices, exchange(): return lax.ppermute(value, 'band', swap)  8.39 us
    pallas_call x4, Pallas kernels, project(): pl.pallas_call(functools.partial(project_kernel, groups, first, sent), in...  6.17 us
    pallas_call x1, Pallas kernels, update(): pl.pallas_call(functools.partial(update_kernel, scale), in_specs=[VMEM] *...  3.23 us
    unnamed x10, local copies, waits for them, and re-layouts  2.24 us
    pallas_call x3, Pallas kernels, cross(): pl.pallas_call(functools.partial(cross_kernel, terms, len(blocks), before...  1.88 us
  transfers between devices with their start and end apart: 17, of which 8 were waited for; matrix products, arithmetic and copies ran while one was open for 1% of the time, Pallas kernels for 15%

profile of v8, /device:TPU:0, one launch (start us, length us, event | category | flops | bytes accessed | tf_op | source)
XLA Modules:
  0.0 68.9 jit_solution(8675766988380077985)
XLA Ops:
  0.0 3.0 %collective-permute-start = (bf16[200,512]{1,0:T(8,128)(2,1)}, bf16[200,512]{1,0:T(8,128)(2,1)S(1)}, u32[]{:S(2)}, u32[]{:S(2)}) collective-permute-start(bf16[200,512]{1,0:T(8,128)(2,1)} %bitcast.11), channel_id=1, source_target_pairs={{0,1},{1,0},{2,3},{3,2},{4,5},{5,4},{6,7},{7,6},{8,9},{9,8},{10,11... | collective-permute-start | bytes 614408 | tf_op jit(solution)/shard_map/ppermute | solution.py:378
  3.0 0.7 collective-permute-start.10
  3.6 2.1 %collective-permute-start.5 = (bf16[200,512]{1,0:T(8,128)(2,1)}, bf16[200,512]{1,0:T(8,128)(2,1)S(1)}, u32[]{:S(2)}, u32[]{:S(2)}) collective-permute-start(bf16[200,512]{1,0:T(8,128)(2,1)} %bitcast.13), channel_id=1, source_target_pairs={{26,0},{24,2},{30,4},{28,6},{2,8},{0,10},{6,12},{4,14},{10,16},{8,... | collective-permute-start | bytes 614408 | tf_op jit(solution)/shard_map/ppermute | solution.py:381
  5.8 2.0 %collective-permute-start.1 = (bf16[200,512]{1,0:T(8,128)(2,1)}, bf16[200,512]{1,0:T(8,128)(2,1)S(1)}, u32[]{:S(2)}, u32[]{:S(2)}) collective-permute-start(bf16[200,512]{1,0:T(8,128)(2,1)} %bitcast.14), channel_id=1, source_target_pairs={{10,0},{8,2},{14,4},{12,6},{18,8},{16,10},{22,12},{20,14},{26,16},... | collective-permute-start | bytes 614408 | tf_op jit(solution)/shard_map/ppermute | solution.py:381
  8.6 2.7 %collective-permute-start.7 = (bf16[200,512]{1,0:T(8,128)(2,1)S(1)}, bf16[200,512]{1,0:T(8,128)(2,1)S(1)}, u32[]{:S(2)}, u32[]{:S(2)}) collective-permute-start(bf16[200,512]{1,0:T(8,128)(2,1)S(1)} %collective-permute-done.other_ref), channel_id=1, source_target_pairs={{26,0},{24,2},{30,4},{28,6},{2,8},{0,10},{6,12},{4,14},{10,16},{8,... | collective-permute-start | bytes 614408 | tf_op jit(solution)/shard_map/ppermute | solution.py:381
  11.3 2.6 %collective-permute-start.3 = (bf16[200,512]{1,0:T(8,128)(2,1)S(1)}, bf16[200,512]{1,0:T(8,128)(2,1)S(1)}, u32[]{:S(2)}, u32[]{:S(2)}) collective-permute-start(bf16[200,512]{1,0:T(8,128)(2,1)S(1)} %collective-permute-done.other_ref), channel_id=1, source_target_pairs={{10,0},{8,2},{14,4},{12,6},{18,8},{16,10},{22,12},{20,14},{26,16},... | collective-permute-start | bytes 614408 | tf_op jit(solution)/shard_map/ppermute | solution.py:381
  14.6 1.0 %dynamic-slice_bitcast_fusion = bf16[200,800]{1,0:T(8,128)(2,1)S(1)} fusion(bf16[1,12,200,800]{3,2,1,0:T(8,128)(2,1)} %margins_ref.7, s32[]{:T(128)S(6)} %select_n.4), kind=kLoop, calls=%fused_computation | loop fusion | bytes 640004 | tf_op jit(solution)/shard_map/jit(dynamic_index_in_dim)/squeeze | solution.py:387
  15.6 2.0 %collective-permute-done.1.refs_0_ = bf16[200,512]{1,0:T(8,128)(2,1)S(1)} collective-permute-done((bf16[200,512]{1,0:T(8,128)(2,1)}, bf16[200,512]{1,0:T(8,128)(2,1)S(1)}, u32[]{:S(2)}, u32[]{:S(2)}) %collective-permute-start.1) | collective-permute-done | bytes 204832 | tf_op jit(solution)/shard_map/ppermute | solution.py:381
  18.5 7.9 %collective-permute-done.3.refs_1_ = bf16[200,512]{1,0:T(8,128)(2,1)S(1)} collective-permute-done((bf16[200,512]{1,0:T(8,128)(2,1)S(1)}, bf16[200,512]{1,0:T(8,128)(2,1)S(1)}, u32[]{:S(2)}, u32[]{:S(2)}) %collective-permute-start.3) | collective-permute-done | bytes 204832 | tf_op jit(solution)/shard_map/ppermute | solution.py:381
  26.8 2.2 %copy-done = bf16[1,12,200,800]{3,2,1,0:T(8,128)(2,1)S(1)} copy-done((bf16[1,12,200,800]{3,2,1,0:T(8,128)(2,1)S(1)}, bf16[1,12,200,800]{3,2,1,0:T(8,128)(2,1)}, u32[]{:S(2)}) %copy-start) | copy-done | bytes 3840024
  29.0 1.7 %shard_map.48 = (bf16[2,200,512]{2,1,0:T(8,128)(2,1)S(1)}, bf16[2,200,512]{2,1,0:T(8,128)(2,1)S(1)}) custom-call(s32[1]{0:T(128)} %bitcast.1.side_ref, s32[1,1]{1,0:T(1,128)} %bitcast.7.window_ref, f32[12]{0:T(128)S(1)} %copy-done.2, bf16[1,12,200,800]{3,2,1,0:T(8,128)(2,1)S(1)} %copy-done, bf16[200,512]{1,0:T(8,128)(2,1)S(1)} %collective-permute-done.10.refs_0_, ...), custom_call_target="tpu_custom_call" | custom-call | flops 655360000 | bytes 1280000 | tf_op jit(solution)/shard_map/pallas_call | solution.py:165
  30.7 0.6 collective-permute-start.15
  31.3 1.7 %shard_map.49 = (bf16[2,200,512]{2,1,0:T(8,128)(2,1)S(1)}, bf16[2,200,512]{2,1,0:T(8,128)(2,1)S(1)}) custom-call(s32[1]{0:T(128)} %bitcast.1.side_ref, s32[1,1]{1,0:T(1,128)} %bitcast.8.window_ref, f32[12]{0:T(128)S(1)} %copy-done.2, bf16[1,12,200,800]{3,2,1,0:T(8,128)(2,1)S(1)} %copy-done, bf16[200,512]{1,0:T(8,128)(2,1)S(1)} %collective-permute-done.1.refs_0_, ...), custom_call_target="tpu_custom_call" | custom-call | flops 655360000 | bytes 1280000 | tf_op jit(solution)/shard_map/pallas_call | solution.py:165
  32.9 1.6 %collective-permute-start.14 = (bf16[2,200,512]{2,1,0:T(8,128)(2,1)S(1)}, bf16[2,200,512]{2,1,0:T(8,128)(2,1)S(1)}, u32[]{:S(2)}, u32[]{:S(2)}) collective-permute-start(bf16[2,200,512]{2,1,0:T(8,128)(2,1)S(1)} %get-tuple-element.31.refs_3_), channel_id=1, source_target_pairs={{0,1},{1,0},{2,3},{3,2},{4,5},{5,4},{6,7},{7,6},{8,9},{9,8},{10,11... | collective-permute-start | bytes 1228808 | tf_op jit(solution)/shard_map/ppermute | solution.py:378
  34.5 0.8 %collective-permute-start.6 = (bf16[200,512]{1,0:T(8,128)(2,1)S(1)}, bf16[200,512]{1,0:T(8,128)(2,1)S(1)}, u32[]{:S(2)}, u32[]{:S(2)}) collective-permute-start(bf16[200,512]{1,0:T(8,128)(2,1)S(1)} %collective-permute-done.5.refs_2_), channel_id=1, source_target_pairs={{6,0},{4,2},{2,4},{0,6},{14,8},{12,10},{10,12},{8,14},{22,16},{20,... | collective-permute-start | bytes 614408 | tf_op jit(solution)/shard_map/ppermute | solution.py:381
  35.3 1.0 %collective-permute-start.8 = (bf16[200,512]{1,0:T(8,128)(2,1)S(1)}, bf16[200,512]{1,0:T(8,128)(2,1)S(1)}, u32[]{:S(2)}, u32[]{:S(2)}) collective-permute-start(bf16[200,512]{1,0:T(8,128)(2,1)S(1)} %collective-permute-done.7.refs_3_), channel_id=1, source_target_pairs={{6,0},{4,2},{2,4},{0,6},{14,8},{12,10},{10,12},{8,14},{22,16},{20,... | collective-permute-start | bytes 614408 | tf_op jit(solution)/shard_map/ppermute | solution.py:381
  36.3 1.2 %shard_map.46 = (bf16[1,200,512]{2,1,0:T(8,128)(2,1)S(1)}, bf16[1,200,512]{2,1,0:T(8,128)(2,1)S(1)}) custom-call(s32[1]{0:T(128)} %bitcast.1.side_ref, s32[1,1]{1,0:T(1,128)} %bitcast.5.window_ref, f32[12]{0:T(128)S(1)} %copy-done.2, bf16[1,12,200,800]{3,2,1,0:T(8,128)(2,1)S(1)} %copy-done, bf16[200,512]{1,0:T(8,128)(2,1)S(1)} %collective-permute-done.2.refs_0_, ...), custom_call_target="tpu_custom_call" | custom-call | flops 327680000 | bytes 640000 | tf_op jit(solution)/shard_map/pallas_call | solution.py:165
  37.5 0.6 collective-permute-start.13
  38.1 1.1 %shard_map.50.refs_4_ = f32[2,200,200]{2,1,0:T(8,128)S(1)} custom-call(bf16[2,200,512]{2,1,0:T(8,128)(2,1)S(1)} %get-tuple-element.28.refs_0_, bf16[2,200,512]{2,1,0:T(8,128)(2,1)S(1)} %get-tuple-element.29.refs_1_, bf16[2,200,512]{2,1,0:T(8,128)(2,1)S(1)} %get-tuple-element.30.refs_2_.refs_0_, bf16[2,200,512]{2,1,0:T(8,128)(2,1)S(1)} %get-tuple-element.31.refs_3_), custom_call_target="tpu_custom_call" | custom-call | flops 655360000 | bytes 1638400 | tf_op jit(solution)/shard_map/pallas_call | solution.py:215
  39.2 2.7 %collective-permute-done.6.refs_0_ = bf16[200,512]{1,0:T(8,128)(2,1)S(1)} collective-permute-done((bf16[200,512]{1,0:T(8,128)(2,1)S(1)}, bf16[200,512]{1,0:T(8,128)(2,1)S(1)}, u32[]{:S(2)}, u32[]{:S(2)}) %collective-permute-start.6) | collective-permute-done | bytes 204832 | tf_op jit(solution)/shard_map/ppermute | solution.py:381
  41.9 4.4 %collective-permute-done.8.refs_1_ = bf16[200,512]{1,0:T(8,128)(2,1)S(1)} collective-permute-done((bf16[200,512]{1,0:T(8,128)(2,1)S(1)}, bf16[200,512]{1,0:T(8,128)(2,1)S(1)}, u32[]{:S(2)}, u32[]{:S(2)}) %collective-permute-start.8) | collective-permute-done | bytes 204832 | tf_op jit(solution)/shard_map/ppermute | solution.py:381
  46.3 1.6 %shard_map.47 = (bf16[1,200,512]{2,1,0:T(8,128)(2,1)S(1)}, bf16[1,200,512]{2,1,0:T(8,128)(2,1)S(1)}, bf16[1,200,512]{2,1,0:T(8,128)(2,1)S(1)}) custom-call(s32[1]{0:T(128)} %bitcast.1.side_ref, s32[1,1]{1,0:T(1,128)} %bitcast.6.window_ref, f32[12]{0:T(128)S(1)} %copy-done.2, bf16[1,12,200,800]{3,2,1,0:T(8,128)(2,1)S(1)} %bitcast.10, ...), custom_call_target="tpu_custom_call" | custom-call | flops 327680000 | bytes 640000 | tf_op jit(solution)/shard_map/pallas_call | solution.py:165
  47.9 0.6 shard_map.52
  48.6 3.3 %collective-permute-done.14.refs_1_ = bf16[2,200,512]{2,1,0:T(8,128)(2,1)S(1)} collective-permute-done((bf16[2,200,512]{2,1,0:T(8,128)(2,1)S(1)}, bf16[2,200,512]{2,1,0:T(8,128)(2,1)S(1)}, u32[]{:S(2)}, u32[]{:S(2)}) %collective-permute-start.14) | collective-permute-done | bytes 409632 | tf_op jit(solution)/shard_map/ppermute | solution.py:378
  51.9 0.8 %shard_map.53 = (f32[2,200,200]{2,1,0:T(8,128)S(1)}, f32[2,200,200]{2,1,0:T(8,128)S(1)}) custom-call(bf16[2,200,512]{2,1,0:T(8,128)(2,1)S(1)} %get-tuple-element.30.refs_2_.refs_0_, bf16[2,200,512]{2,1,0:T(8,128)(2,1)S(1)} %collective-permute-done.14.refs_1_, bf16[1,200,512]{2,1,0:T(8,128)(2,1)S(1)} %get-tuple-element.26.refs_2_, ...), custom_call_target="tpu_custom_call" | custom-call | flops 491520000 | bytes 1228800 | tf_op jit(solution)/shard_map/pallas_call | solution.py:251
  52.7 2.8 %collective-permute-done.13.refs_1_ = bf16[1,200,512]{2,1,0:T(8,128)(2,1)S(1)} collective-permute-done((bf16[1,200,512]{2,1,0:T(8,128)(2,1)S(1)}, bf16[1,200,512]{2,1,0:T(8,128)(2,1)S(1)}, u32[]{:S(2)}, u32[]{:S(2)}) %collective-permute-start.13) | collective-permute-done | bytes 204832 | tf_op jit(solution)/shard_map/ppermute | solution.py:378
  55.9 0.6 collective-permute-start.16
  56.5 0.6 shard_map.51
  57.1 1.6 %collective-permute-start.12 = (bf16[200,200]{1,0:T(8,128)(2,1)S(1)}, bf16[200,200]{1,0:T(8,128)(2,1)S(1)}, u32[]{:S(2)}, u32[]{:S(2)}) collective-permute-start(bf16[200,200]{1,0:T(8,128)(2,1)S(1)} %get-tuple-element.33), channel_id=1, source_target_pairs={{0,1},{1,0},{2,3},{3,2},{4,5},{5,4},{6,7},{7,6},{8,9},{9,8},{10,11... | collective-permute-start | bytes 240008 | tf_op jit(solution)/shard_map/ppermute | solution.py:378
  58.7 5.8 %collective-permute-done.12.packed_ref = bf16[200,200]{1,0:T(8,128)(2,1)S(1)} collective-permute-done((bf16[200,200]{1,0:T(8,128)(2,1)S(1)}, bf16[200,200]{1,0:T(8,128)(2,1)S(1)}, u32[]{:S(2)}, u32[]{:S(2)}) %collective-permute-start.12) | collective-permute-done | bytes 80032 | tf_op jit(solution)/shard_map/ppermute | solution.py:378
  64.6 1.1 %base.1 = (f32[200,512]{1,0:T(8,128)S(1)}, f32[200,512]{1,0:T(8,128)S(1)}) custom-call(bf16[200,512]{1,0:T(8,128)(2,1)S(1)} %bitcast.15, bf16[200,512]{1,0:T(8,128)(2,1)S(1)} %collective-permute-done.other_ref, f32[2,200,200]{2,1,0:T(8,128)S(1)} %get-tuple-element.32.total_ref, bf16[200,200]{1,0:T(8,128)(2,1)S(1)} %collective-permute-done.12.packed_ref, ...), custom_call_target="tpu_custom_call" | custom-call | flops 655360000 | bytes 819200 | tf_op jit(solution)/shard_map/base/pallas_call | solution.py:300
  65.6 3.2 %update.1 = f32[1,200,512]{2,1,0:T(8,128)} custom-call(bf16[200,512]{1,0:T(8,128)(2,1)S(1)} %bitcast.16, bf16[200,512]{1,0:T(8,128)(2,1)S(1)} %collective-permute-done.other_ref, f32[200,512]{1,0:T(8,128)S(1)} %get-tuple-element.40.base_ref, f32[200,512]{1,0:T(8,128)S(1)} %get-tuple-element.41.base_other_ref, ...), custom_call_target="tpu_custom_call" | custom-call | tf_op jit(solution)/shard_map/update/pallas_call | solution.py:351
  (26 shorter events, 2.5 us)
Async XLA Ops:
  0.0 26.8 %copy-start.2 = (f32[12]{0:T(128)S(1)}, f32[12]{0:T(128)}, u32[]{:S(2)}) copy-start(f32[12]{0:T(128)} %weight_ref.7) | copy-start | bytes 148
  0.0 8.3 %collective-permute-start = (bf16[200,512]{1,0:T(8,128)(2,1)}, bf16[200,512]{1,0:T(8,128)(2,1)S(1)}, u32[]{:S(2)}, u32[]{:S(2)}) collective-permute-start(bf16[200,512]{1,0:T(8,128)(2,1)} %bitcast.11), channel_id=1, source_target_pairs={{0,1},{1,0},{2,3},{3,2},{4,5},{5,4},{6,7},{7,6},{8,9},{9,8},{10,11... | collective-permute-start | bytes 614408 | tf_op jit(solution)/shard_map/ppermute | solution.py:378
  3.0 8.3 %collective-permute-start.10 = (bf16[200,512]{1,0:T(8,128)(2,1)}, bf16[200,512]{1,0:T(8,128)(2,1)S(1)}, u32[]{:S(2)}, u32[]{:S(2)}) collective-permute-start(bf16[200,512]{1,0:T(8,128)(2,1)} %bitcast.12), channel_id=1, source_target_pairs={{6,0},{4,2},{2,4},{0,6},{14,8},{12,10},{10,12},{8,14},{22,16},{20,... | collective-permute-start | bytes 614408 | tf_op jit(solution)/shard_map/ppermute | solution.py:381
  3.6 27.0 %collective-permute-start.5 = (bf16[200,512]{1,0:T(8,128)(2,1)}, bf16[200,512]{1,0:T(8,128)(2,1)S(1)}, u32[]{:S(2)}, u32[]{:S(2)}) collective-permute-start(bf16[200,512]{1,0:T(8,128)(2,1)} %bitcast.13), channel_id=1, source_target_pairs={{26,0},{24,2},{30,4},{28,6},{2,8},{0,10},{6,12},{4,14},{10,16},{8,... | collective-permute-start | bytes 614408 | tf_op jit(solution)/shard_map/ppermute | solution.py:381
  5.8 11.8 %collective-permute-start.1 = (bf16[200,512]{1,0:T(8,128)(2,1)}, bf16[200,512]{1,0:T(8,128)(2,1)S(1)}, u32[]{:S(2)}, u32[]{:S(2)}) collective-permute-start(bf16[200,512]{1,0:T(8,128)(2,1)} %bitcast.14), channel_id=1, source_target_pairs={{10,0},{8,2},{14,4},{12,6},{18,8},{16,10},{22,12},{20,14},{26,16},... | collective-permute-start | bytes 614408 | tf_op jit(solution)/shard_map/ppermute | solution.py:381
  8.3 9.8 %collective-permute-start.11 = (bf16[200,512]{1,0:T(8,128)(2,1)S(1)}, bf16[200,512]{1,0:T(8,128)(2,1)S(1)}, u32[]{:S(2)}, u32[]{:S(2)}) collective-permute-start(bf16[200,512]{1,0:T(8,128)(2,1)S(1)} %collective-permute-done.other_ref), channel_id=1, source_target_pairs={{6,0},{4,2},{2,4},{0,6},{14,8},{12,10},{10,12},{8,14},{22,16},{20,... | collective-permute-start | bytes 614408 | tf_op jit(solution)/shard_map/ppermute | solution.py:381
  8.6 22.7 %collective-permute-start.7 = (bf16[200,512]{1,0:T(8,128)(2,1)S(1)}, bf16[200,512]{1,0:T(8,128)(2,1)S(1)}, u32[]{:S(2)}, u32[]{:S(2)}) collective-permute-start(bf16[200,512]{1,0:T(8,128)(2,1)S(1)} %collective-permute-done.other_ref), channel_id=1, source_target_pairs={{26,0},{24,2},{30,4},{28,6},{2,8},{0,10},{6,12},{4,14},{10,16},{8,... | collective-permute-start | bytes 614408 | tf_op jit(solution)/shard_map/ppermute | solution.py:381
  11.3 15.1 %collective-permute-start.3 = (bf16[200,512]{1,0:T(8,128)(2,1)S(1)}, bf16[200,512]{1,0:T(8,128)(2,1)S(1)}, u32[]{:S(2)}, u32[]{:S(2)}) collective-permute-start(bf16[200,512]{1,0:T(8,128)(2,1)S(1)} %collective-permute-done.other_ref), channel_id=1, source_target_pairs={{10,0},{8,2},{14,4},{12,6},{18,8},{16,10},{22,12},{20,14},{26,16},... | collective-permute-start | bytes 614408 | tf_op jit(solution)/shard_map/ppermute | solution.py:381
  17.6 19.9 %collective-permute-start.9 = (bf16[200,800]{1,0:T(8,128)(2,1)S(1)}, bf16[200,800]{1,0:T(8,128)(2,1)S(1)}, u32[]{:S(2)}, u32[]{:S(2)}) collective-permute-start(bf16[200,800]{1,0:T(8,128)(2,1)S(1)} %dynamic-slice_bitcast_fusion), channel_id=1, source_target_pairs={{0,1},{1,0},{2,3},{3,2},{4,5},{5,4},{6,7},{7,6},{8,9},{9,8},{10,11... | collective-permute-start | bytes 960008 | tf_op jit(solution)/shard_map/ppermute | solution.py:378
  18.1 16.4 %collective-permute-start.2 = (bf16[200,512]{1,0:T(8,128)(2,1)S(1)}, bf16[200,512]{1,0:T(8,128)(2,1)S(1)}, u32[]{:S(2)}, u32[]{:S(2)}) collective-permute-start(bf16[200,512]{1,0:T(8,128)(2,1)S(1)} %collective-permute-done.1.refs_0_), channel_id=1, source_target_pairs={{6,0},{4,2},{2,4},{0,6},{14,8},{12,10},{10,12},{8,14},{22,16},{20,... | collective-permute-start | bytes 614408 | tf_op jit(solution)/shard_map/ppermute | solution.py:381
  26.4 8.9 %collective-permute-start.4 = (bf16[200,512]{1,0:T(8,128)(2,1)S(1)}, bf16[200,512]{1,0:T(8,128)(2,1)S(1)}, u32[]{:S(2)}, u32[]{:S(2)}) collective-permute-start(bf16[200,512]{1,0:T(8,128)(2,1)S(1)} %collective-permute-done.3.refs_1_), channel_id=1, source_target_pairs={{6,0},{4,2},{2,4},{0,6},{14,8},{12,10},{10,12},{8,14},{22,16},{20,... | collective-permute-start | bytes 614408 | tf_op jit(solution)/shard_map/ppermute | solution.py:381
  26.8 2.2 %copy-start = (bf16[1,12,200,800]{3,2,1,0:T(8,128)(2,1)S(1)}, bf16[1,12,200,800]{3,2,1,0:T(8,128)(2,1)}, u32[]{:S(2)}) copy-start(bf16[1,12,200,800]{3,2,1,0:T(8,128)(2,1)} %margins_ref.7) | copy-start | bytes 11520004
  29.0 17.2 %slice-start = ((s8[4300800]{0:T(1024)(128)(4,1)}), s8[4194304]{0:T(1024)(128)(4,1)S(1)}, s32[]{:S(2)}) async-start(s8[4300800]{0:T(1024)(128)(4,1)} %bitcast.9), calls=%async_computation | async-start | bytes 8388608
  30.7 17.2 %collective-permute-start.15 = (bf16[2,200,512]{2,1,0:T(8,128)(2,1)S(1)}, bf16[2,200,512]{2,1,0:T(8,128)(2,1)S(1)}, u32[]{:S(2)}, u32[]{:S(2)}) collective-permute-start(bf16[2,200,512]{2,1,0:T(8,128)(2,1)S(1)} %get-tuple-element.29.refs_1_), channel_id=1, source_target_pairs={{0,1},{1,0},{2,3},{3,2},{4,5},{5,4},{6,7},{7,6},{8,9},{9,8},{10,11... | collective-permute-start | bytes 1228808 | tf_op jit(solution)/shard_map/ppermute | solution.py:378
  31.3 15.0 %slice-start.1 = ((s8[4300800]{0:T(1024)(128)(4,1)}), s8[106496]{0:T(1024)(128)(4,1)S(1)}, s32[]{:S(2)}) async-start(s8[4300800]{0:T(1024)(128)(4,1)} %bitcast.9), calls=%async_computation.1 | async-start | bytes 212992
  32.9 18.9 %collective-permute-start.14 = (bf16[2,200,512]{2,1,0:T(8,128)(2,1)S(1)}, bf16[2,200,512]{2,1,0:T(8,128)(2,1)S(1)}, u32[]{:S(2)}, u32[]{:S(2)}) collective-permute-start(bf16[2,200,512]{2,1,0:T(8,128)(2,1)S(1)} %get-tuple-element.31.refs_3_), channel_id=1, source_target_pairs={{0,1},{1,0},{2,3},{3,2},{4,5},{5,4},{6,7},{7,6},{8,9},{9,8},{10,11... | collective-permute-start | bytes 1228808 | tf_op jit(solution)/shard_map/ppermute | solution.py:378
  34.5 7.3 %collective-permute-start.6 = (bf16[200,512]{1,0:T(8,128)(2,1)S(1)}, bf16[200,512]{1,0:T(8,128)(2,1)S(1)}, u32[]{:S(2)}, u32[]{:S(2)}) collective-permute-start(bf16[200,512]{1,0:T(8,128)(2,1)S(1)} %collective-permute-done.5.refs_2_), channel_id=1, source_target_pairs={{6,0},{4,2},{2,4},{0,6},{14,8},{12,10},{10,12},{8,14},{22,16},{20,... | collective-permute-start | bytes 614408 | tf_op jit(solution)/shard_map/ppermute | solution.py:381
  35.3 11.0 %collective-permute-start.8 = (bf16[200,512]{1,0:T(8,128)(2,1)S(1)}, bf16[200,512]{1,0:T(8,128)(2,1)S(1)}, u32[]{:S(2)}, u32[]{:S(2)}) collective-permute-start(bf16[200,512]{1,0:T(8,128)(2,1)S(1)} %collective-permute-done.7.refs_3_), channel_id=1, source_target_pairs={{6,0},{4,2},{2,4},{0,6},{14,8},{12,10},{10,12},{8,14},{22,16},{20,... | collective-permute-start | bytes 614408 | tf_op jit(solution)/shard_map/ppermute | solution.py:381
  37.5 18.0 %collective-permute-start.13 = (bf16[1,200,512]{2,1,0:T(8,128)(2,1)S(1)}, bf16[1,200,512]{2,1,0:T(8,128)(2,1)S(1)}, u32[]{:S(2)}, u32[]{:S(2)}) collective-permute-start(bf16[1,200,512]{2,1,0:T(8,128)(2,1)S(1)} %get-tuple-element.25.refs_1_), channel_id=1, source_target_pairs={{0,1},{1,0},{2,3},{3,2},{4,5},{5,4},{6,7},{7,6},{8,9},{9,8},{10,11... | collective-permute-start | bytes 614408 | tf_op jit(solution)/shard_map/ppermute | solution.py:378
  47.9 16.6 %copy-start.1 = (bf16[1,200,512]{2,1,0:T(8,128)(2,1)S(1)}, bf16[1,200,512]{2,1,0:T(8,128)(2,1)}, u32[]{:S(2)}) copy-start(bf16[1,200,512]{2,1,0:T(8,128)(2,1)} %param.5) | copy-start | bytes 614404
  55.9 9.7 %collective-permute-start.16 = (bf16[2,200,200]{2,1,0:T(8,128)(2,1)S(1)}, bf16[2,200,200]{2,1,0:T(8,128)(2,1)S(1)}, u32[]{:S(2)}, u32[]{:S(2)}) collective-permute-start(bf16[2,200,200]{2,1,0:T(8,128)(2,1)S(1)} %get-tuple-element.42), channel_id=1, source_target_pairs={{0,1},{1,0},{2,3},{3,2},{4,5},{5,4},{6,7},{7,6},{8,9},{9,8},{10,11... | collective-permute-start | bytes 480008 | tf_op jit(solution)/shard_map/ppermute | solution.py:378
  57.1 7.4 %collective-permute-start.12 = (bf16[200,200]{1,0:T(8,128)(2,1)S(1)}, bf16[200,200]{1,0:T(8,128)(2,1)S(1)}, u32[]{:S(2)}, u32[]{:S(2)}) collective-permute-start(bf16[200,200]{1,0:T(8,128)(2,1)S(1)} %get-tuple-element.33), channel_id=1, source_target_pairs={{0,1},{1,0},{2,3},{3,2},{4,5},{5,4},{6,7},{7,6},{8,9},{9,8},{10,11... | collective-permute-start | bytes 240008 | tf_op jit(solution)/shard_map/ppermute | solution.py:378

commit v9 on v8

--- a/solution.py
+++ b/solution.py
@@ -26,6 +26,7 @@
 BATCH = 4
 SHIPPED = 2
 CENTRE = 0.5
+LANES = 128
 PREPARE = 2 * 10**10
 VMEM = pl.BlockSpec(memory_space=pltpu.VMEM)
 LIMIT = pltpu.CompilerParams(vmem_limit_bytes=20 * 2**20)
@@ -226,14 +227,26 @@
     )(*operands)
 
 
-def cross_kernel(terms, count, has_total, *refs):
+def packing(rows):
+    even = rows // LANES * LANES
+    left = rows - even
+    fit = min(left, LANES - left)
+    return even, left, fit, left - fit
+
+
+def packed_shape(rows):
+    even, _, _, spare = packing(rows)
+    return (rows + -(-spare // 16) * 16, 2 * even + LANES)
+
+
+def cross_kernel(terms, count, has_total, last, *refs):
     blocks, refs = refs[:count], refs[count:]
     rows = blocks[0].shape[1]
     sums = [jnp.zeros((rows, rows), F32) for _ in range(4)]
     if has_total:
         mine_before_ref, theirs_before_ref, *refs = refs
         sums = [mine_before_ref[0], mine_before_ref[1], theirs_before_ref[0], theirs_before_ref[1]]
-    mine_ref, theirs_ref = refs
+    mine_ref, theirs_ref, *refs = refs
     for keep_place, keep_index, got_place, got_index in terms:
         keep, got = blocks[keep_place][keep_index], blocks[got_place][got_index]
         sums[0] += dot(keep, got, NT)
@@ -241,21 +254,45 @@
         sums[2] += dot(got, keep, NT)
         sums[3] += dot(times_minus_i(got), keep, NT)
     mine_ref[0], mine_ref[1] = sums[0], sums[1]
-    kind = theirs_ref.dtype
-    theirs_ref[0], theirs_ref[1] = sums[2].astype(kind), sums[3].astype(kind)
+    real, imag = sums[2], sums[3]
+    if not last:
+        theirs_ref[0], theirs_ref[1] = real, imag
+        return
+    (packed_ref,) = refs
+    even, left, fit, spare = packing(rows)
+    packed_ref[:rows, :even] = real[:, :even]
+    packed_ref[:rows, even : 2 * even] = imag[:, :even]
+    packed_ref[:rows, 2 * even :] = jnp.concatenate(
+        [
+            real[:, even:],
+            imag[:, even : even + fit],
+            jnp.zeros((rows, LANES - left - fit), F32),
+        ][: 3 if left + fit < LANES else 2],
+        axis=1,
+    )
+    if spare:
+        packed_ref[rows:, :] = jnp.zeros((packed_ref.shape[0] - rows, packed_ref.shape[1]), F32)
+        row, column = triangle(rows)
+        identity = jnp.where(row == column, 1.0, 0.0).astype(BF16)
+        packed_ref[rows : rows + spare, :rows] = dot(
+            imag[:, rows - spare :].astype(BF16), identity, TN
+        )
+    theirs_ref[...] = packed_ref[...].astype(BF16)
 
 
 def cross(blocks, terms, before, last):
     rows, width = blocks[0].shape[1:]
     operands = [*blocks, *(before or ())]
+    packed = packed_shape(rows)
     return pl.pallas_call(
-        functools.partial(cross_kernel, terms, len(blocks), before is not None),
+        functools.partial(cross_kernel, terms, len(blocks), before is not None, last),
         in_specs=[VMEM] * len(operands),
         out_specs=[VMEM] * 2,
         out_shape=[
             jax.ShapeDtypeStruct((2, rows, rows), F32),
-            jax.ShapeDtypeStruct((2, rows, rows), BF16 if last else F32),
+            jax.ShapeDtypeStruct(packed, BF16) if last else jax.ShapeDtypeStruct((2, rows, rows), F32),
         ],
+        scratch_shapes=[pltpu.VMEM(packed, F32)] if last else [],
         cost_estimate=pl.CostEstimate(
             flops=8 * len(terms) * rows * rows * width,
             bytes_accessed=4 * len(terms) * rows * width,
@@ -270,7 +307,9 @@
     return dot(left.astype(BF16), stacked)
 
 
-def base_kernel(own_ref, other_ref, total_ref, packed_ref, mine_ref, base_ref, base_other_ref):
+def base_kernel(
+    own_ref, other_ref, total_ref, packed_ref, mine_ref, base_ref, base_other_ref, right_ref, stack_ref
+):
     own, other = own_ref[...], other_ref[...]
     own_i, other_i = times_i(own.astype(F32)).astype(BF16), times_i(other.astype(F32)).astype(BF16)
     real, imag = mine_ref[0], mine_ref[1]
@@ -293,6 +332,15 @@
         + dot_exact_right(real, own, TN)
         - dot_exact_right(imag, own_i, TN)
     )
+    even, left, fit, _ = packing(other.shape[0])
+    plain, turned = other.astype(F32), times_i(other.astype(F32))
+    stack_ref[:even, :] = plain[:even]
+    stack_ref[even : 2 * even, :] = turned[:even]
+    stack_ref[2 * even : 2 * even + left, :] = plain[even:]
+    stack_ref[2 * even + left : 2 * even + left + fit, :] = turned[even : even + fit]
+    if left + fit < LANES:
+        stack_ref[2 * even + left + fit :, :] = jnp.zeros((LANES - left - fit, plain.shape[1]), F32)
+    right_ref[...] = stack_ref[...].astype(BF16)
 
 
 def base(own, other, total, packed, mine):
@@ -300,8 +348,13 @@
     return pl.pallas_call(
         base_kernel,
         in_specs=[VMEM] * 5,
-        out_specs=[VMEM] * 2,
-        out_shape=[jax.ShapeDtypeStruct((rows, width), F32)] * 2,
+        out_specs=[VMEM] * 3,
+        out_shape=[
+            jax.ShapeDtypeStruct((rows, width), F32),
+            jax.ShapeDtypeStruct((rows, width), F32),
+            jax.ShapeDtypeStruct((packed_shape(rows)[1], width), BF16),
+        ],
+        scratch_shapes=[pltpu.VMEM((packed_shape(rows)[1], width), F32)],
         cost_estimate=pl.CostEstimate(
             flops=32 * rows * rows * width, bytes_accessed=8 * rows * width, transcendentals=0
         ),
@@ -310,15 +363,26 @@
     )(own, other, total, packed, mine)
 
 
-def update_kernel(scale, own_ref, other_ref, base_ref, base_other_ref, theirs_ref, out_ref, rows_ref):
-    own, other = own_ref[...], other_ref[...]
-    half = own.shape[1] // 2
-    own_i, other_i = times_i(own.astype(F32)).astype(BF16), times_i(other.astype(F32)).astype(BF16)
-    real, imag = theirs_ref[0], theirs_ref[1]
-    rows = own.shape[0]
-    product = base_ref[...] + dot(real, other) + dot(imag, other_i)
+def update_kernel(
+    scale, own_ref, other_ref, base_ref, base_other_ref, right_ref, theirs_ref, out_ref, rows_ref
+):
+    own = own_ref[...]
+    rows, half = own.shape[0], own.shape[1] // 2
+    own_i = times_i(own.astype(F32)).astype(BF16)
+    even, left, fit, spare = packing(rows)
+    product = base_ref[...] + dot(theirs_ref[:rows, :], right_ref[...])
+    upper = dot(theirs_ref[:rows, :even], own, TN) - dot(theirs_ref[:rows, even : 2 * even], own_i, TN)
+    shared = theirs_ref[:rows, 2 * even :]
+    lower = dot(shared, own, TN)[:left]
+    turned = dot(shared, own_i, TN)[left : left + fit]
+    if spare:
+        below = theirs_ref[rows : rows + spare, :rows]
+        other_i = times_i(other_ref[...].astype(F32)[rows - spare :]).astype(BF16)
+        product += dot(below, other_i, TN)
+        turned = jnp.concatenate([turned, dot(below, own_i)], axis=0)
     rows_ref[:rows, :] = product
-    rows_ref[rows:, :] = base_other_ref[...] + dot(real, own, TN) - dot(imag, own_i, TN)
+    rows_ref[rows : rows + even, :] = base_other_ref[:even, :] + upper
+    rows_ref[rows + even :, :] = base_other_ref[even:, :] + lower - turned
     both = rows_ref[...].astype(BF16)
     blocks = dot(both, both, TN)
     real = blocks[:half, :half] + blocks[half:, half:]
@@ -350,7 +414,7 @@
     rows, width = own.shape
     return pl.pallas_call(
         functools.partial(update_kernel, scale),
-        in_specs=[VMEM] * 5,
+        in_specs=[VMEM] * 6,
         out_specs=VMEM,
         out_shape=jax.ShapeDtypeStruct((1, rows, width), F32),
         scratch_shapes=[pltpu.VMEM((2 * rows, width), F32)],

time: 69 us -> 68.5 us (level)
  waiting for transfers between devices: 29.5 us -> 28.7 us
    ppermute x7, waiting for transfers between devices: 12.4 us -> 11.6 us  [exchange(): return lax.ppermute(value, 'band', swap)]
where the time goes in v9:
time: 68.5 us; the launch traced here: 68.4 us
  waiting for transfers between devices  28.7 us (42%)
  starting transfers between devices  21.3 us (31%)
  Pallas kernels  14.4 us (21%)
  local copies, waits for them, and re-layouts  3.25 us (5%)
  between operations  0.79 us (1%)
    ppermute x10, waiting for transfers between devices, fetch(): return lax.ppermute(value, 'kpt', fetch_pairs(shift, point_count))  17.1 us
    ppermute x10, starting transfers between devices, fetch(): return lax.ppermute(value, 'kpt', fetch_pairs(shift, point_count))  13 us
    ppermute x7, waiting for transfers between devices, exchange(): return lax.ppermute(value, 'band', swap)  11.6 us
    ppermute x7, starting transfers between devices, exchange(): return lax.ppermute(value, 'band', swap)  8.33 us
    pallas_call x4, Pallas kernels, project(): pl.pallas_call(functools.partial(project_kernel, groups, first, sent), in...  6.17 us
    pallas_call x1, Pallas kernels, update(): pl.pallas_call(functools.partial(update_kernel, scale), in_specs=[VMEM] *...  3.35 us
    unnamed x10, local copies, waits for them, and re-layouts  2.24 us
    pallas_call x3, Pallas kernels, cross(): pl.pallas_call(functools.partial(cross_kernel, terms, len(blocks), before...  2.11 us
  transfers between devices with their start and end apart: 17, of which 8 were waited for; matrix products, arithmetic and copies ran while one was open for 1% of the time, Pallas kernels for 15%

profile of v9, /device:TPU:0, one launch (start us, length us, event | category | flops | bytes accessed | tf_op | source)
XLA Modules:
  0.0 68.4 jit_solution(15832119352135206389)
XLA Ops:
  0.0 3.0 %collective-permute-start = (bf16[200,512]{1,0:T(8,128)(2,1)}, bf16[200,512]{1,0:T(8,128)(2,1)S(1)}, u32[]{:S(2)}, u32[]{:S(2)}) collective-permute-start(bf16[200,512]{1,0:T(8,128)(2,1)} %bitcast.11), channel_id=1, source_target_pairs={{0,1},{1,0},{2,3},{3,2},{4,5},{5,4},{6,7},{7,6},{8,9},{9,8},{10,11... | collective-permute-start | bytes 614408 | tf_op jit(solution)/shard_map/ppermute | solution.py:442
  3.0 0.7 collective-permute-start.10
  3.6 2.1 %collective-permute-start.5 = (bf16[200,512]{1,0:T(8,128)(2,1)}, bf16[200,512]{1,0:T(8,128)(2,1)S(1)}, u32[]{:S(2)}, u32[]{:S(2)}) collective-permute-start(bf16[200,512]{1,0:T(8,128)(2,1)} %bitcast.13), channel_id=1, source_target_pairs={{26,0},{24,2},{30,4},{28,6},{2,8},{0,10},{6,12},{4,14},{10,16},{8,... | collective-permute-start | bytes 614408 | tf_op jit(solution)/shard_map/ppermute | solution.py:445
  5.8 2.0 %collective-permute-start.1 = (bf16[200,512]{1,0:T(8,128)(2,1)}, bf16[200,512]{1,0:T(8,128)(2,1)S(1)}, u32[]{:S(2)}, u32[]{:S(2)}) collective-permute-start(bf16[200,512]{1,0:T(8,128)(2,1)} %bitcast.14), channel_id=1, source_target_pairs={{10,0},{8,2},{14,4},{12,6},{18,8},{16,10},{22,12},{20,14},{26,16},... | collective-permute-start | bytes 614408 | tf_op jit(solution)/shard_map/ppermute | solution.py:445
  8.6 2.7 %collective-permute-start.7 = (bf16[200,512]{1,0:T(8,128)(2,1)S(1)}, bf16[200,512]{1,0:T(8,128)(2,1)S(1)}, u32[]{:S(2)}, u32[]{:S(2)}) collective-permute-start(bf16[200,512]{1,0:T(8,128)(2,1)S(1)} %collective-permute-done.other_ref), channel_id=1, source_target_pairs={{26,0},{24,2},{30,4},{28,6},{2,8},{0,10},{6,12},{4,14},{10,16},{8,... | collective-permute-start | bytes 614408 | tf_op jit(solution)/shard_map/ppermute | solution.py:445
  11.3 2.6 %collective-permute-start.3 = (bf16[200,512]{1,0:T(8,128)(2,1)S(1)}, bf16[200,512]{1,0:T(8,128)(2,1)S(1)}, u32[]{:S(2)}, u32[]{:S(2)}) collective-permute-start(bf16[200,512]{1,0:T(8,128)(2,1)S(1)} %collective-permute-done.other_ref), channel_id=1, source_target_pairs={{10,0},{8,2},{14,4},{12,6},{18,8},{16,10},{22,12},{20,14},{26,16},... | collective-permute-start | bytes 614408 | tf_op jit(solution)/shard_map/ppermute | solution.py:445
  14.6 1.0 %dynamic-slice_bitcast_fusion = bf16[200,800]{1,0:T(8,128)(2,1)S(1)} fusion(bf16[1,12,200,800]{3,2,1,0:T(8,128)(2,1)} %margins_ref.7, s32[]{:T(128)S(6)} %select_n.4), kind=kLoop, calls=%fused_computation | loop fusion | bytes 640004 | tf_op jit(solution)/shard_map/jit(dynamic_index_in_dim)/squeeze | solution.py:451
  15.6 2.0 %collective-permute-done.1.refs_0_ = bf16[200,512]{1,0:T(8,128)(2,1)S(1)} collective-permute-done((bf16[200,512]{1,0:T(8,128)(2,1)}, bf16[200,512]{1,0:T(8,128)(2,1)S(1)}, u32[]{:S(2)}, u32[]{:S(2)}) %collective-permute-start.1) | collective-permute-done | bytes 204832 | tf_op jit(solution)/shard_map/ppermute | solution.py:445
  18.5 7.9 %collective-permute-done.3.refs_1_ = bf16[200,512]{1,0:T(8,128)(2,1)S(1)} collective-permute-done((bf16[200,512]{1,0:T(8,128)(2,1)S(1)}, bf16[200,512]{1,0:T(8,128)(2,1)S(1)}, u32[]{:S(2)}, u32[]{:S(2)}) %collective-permute-start.3) | collective-permute-done | bytes 204832 | tf_op jit(solution)/shard_map/ppermute | solution.py:445
  26.8 2.2 %copy-done = bf16[1,12,200,800]{3,2,1,0:T(8,128)(2,1)S(1)} copy-done((bf16[1,12,200,800]{3,2,1,0:T(8,128)(2,1)S(1)}, bf16[1,12,200,800]{3,2,1,0:T(8,128)(2,1)}, u32[]{:S(2)}) %copy-start) | copy-done | bytes 3840024
  29.0 1.7 %shard_map.48 = (bf16[2,200,512]{2,1,0:T(8,128)(2,1)S(1)}, bf16[2,200,512]{2,1,0:T(8,128)(2,1)S(1)}) custom-call(s32[1]{0:T(128)} %bitcast.1.side_ref, s32[1,1]{1,0:T(1,128)} %bitcast.7.window_ref, f32[12]{0:T(128)S(1)} %copy-done.2, bf16[1,12,200,800]{3,2,1,0:T(8,128)(2,1)S(1)} %copy-done, bf16[200,512]{1,0:T(8,128)(2,1)S(1)} %collective-permute-done.10.refs_0_, ...), custom_call_target="tpu_custom_call" | custom-call | flops 655360000 | bytes 1280000 | tf_op jit(solution)/shard_map/pallas_call | solution.py:166
  30.7 0.6 collective-permute-start.15
  31.3 1.7 %shard_map.49 = (bf16[2,200,512]{2,1,0:T(8,128)(2,1)S(1)}, bf16[2,200,512]{2,1,0:T(8,128)(2,1)S(1)}) custom-call(s32[1]{0:T(128)} %bitcast.1.side_ref, s32[1,1]{1,0:T(1,128)} %bitcast.8.window_ref, f32[12]{0:T(128)S(1)} %copy-done.2, bf16[1,12,200,800]{3,2,1,0:T(8,128)(2,1)S(1)} %copy-done, bf16[200,512]{1,0:T(8,128)(2,1)S(1)} %collective-permute-done.1.refs_0_, ...), custom_call_target="tpu_custom_call" | custom-call | flops 655360000 | bytes 1280000 | tf_op jit(solution)/shard_map/pallas_call | solution.py:166
  32.9 1.6 %collective-permute-start.14 = (bf16[2,200,512]{2,1,0:T(8,128)(2,1)S(1)}, bf16[2,200,512]{2,1,0:T(8,128)(2,1)S(1)}, u32[]{:S(2)}, u32[]{:S(2)}) collective-permute-start(bf16[2,200,512]{2,1,0:T(8,128)(2,1)S(1)} %get-tuple-element.32.refs_3_), channel_id=1, source_target_pairs={{0,1},{1,0},{2,3},{3,2},{4,5},{5,4},{6,7},{7,6},{8,9},{9,8},{10,11... | collective-permute-start | bytes 1228808 | tf_op jit(solution)/shard_map/ppermute | solution.py:442
  34.5 0.8 %collective-permute-start.6 = (bf16[200,512]{1,0:T(8,128)(2,1)S(1)}, bf16[200,512]{1,0:T(8,128)(2,1)S(1)}, u32[]{:S(2)}, u32[]{:S(2)}) collective-permute-start(bf16[200,512]{1,0:T(8,128)(2,1)S(1)} %collective-permute-done.5.refs_2_), channel_id=1, source_target_pairs={{6,0},{4,2},{2,4},{0,6},{14,8},{12,10},{10,12},{8,14},{22,16},{20,... | collective-permute-start | bytes 614408 | tf_op jit(solution)/shard_map/ppermute | solution.py:445
  35.3 1.0 %collective-permute-start.8 = (bf16[200,512]{1,0:T(8,128)(2,1)S(1)}, bf16[200,512]{1,0:T(8,128)(2,1)S(1)}, u32[]{:S(2)}, u32[]{:S(2)}) collective-permute-start(bf16[200,512]{1,0:T(8,128)(2,1)S(1)} %collective-permute-done.7.refs_3_), channel_id=1, source_target_pairs={{6,0},{4,2},{2,4},{0,6},{14,8},{12,10},{10,12},{8,14},{22,16},{20,... | collective-permute-start | bytes 614408 | tf_op jit(solution)/shard_map/ppermute | solution.py:445
  36.3 1.2 %shard_map.46 = (bf16[1,200,512]{2,1,0:T(8,128)(2,1)S(1)}, bf16[1,200,512]{2,1,0:T(8,128)(2,1)S(1)}) custom-call(s32[1]{0:T(128)} %bitcast.1.side_ref, s32[1,1]{1,0:T(1,128)} %bitcast.5.window_ref, f32[12]{0:T(128)S(1)} %copy-done.2, bf16[1,12,200,800]{3,2,1,0:T(8,128)(2,1)S(1)} %copy-done, bf16[200,512]{1,0:T(8,128)(2,1)S(1)} %collective-permute-done.2.refs_0_, ...), custom_call_target="tpu_custom_call" | custom-call | flops 327680000 | bytes 640000 | tf_op jit(solution)/shard_map/pallas_call | solution.py:166
  37.5 0.6 collective-permute-start.13
  38.1 1.1 %shard_map.50.refs_4_ = f32[2,200,200]{2,1,0:T(8,128)S(1)} custom-call(bf16[2,200,512]{2,1,0:T(8,128)(2,1)S(1)} %get-tuple-element.29.refs_0_, bf16[2,200,512]{2,1,0:T(8,128)(2,1)S(1)} %get-tuple-element.30.refs_1_, bf16[2,200,512]{2,1,0:T(8,128)(2,1)S(1)} %get-tuple-element.31.refs_2_.refs_0_, bf16[2,200,512]{2,1,0:T(8,128)(2,1)S(1)} %get-tuple-element.32.refs_3_), custom_call_target="tpu_custom_call" | custom-call | flops 655360000 | bytes 1638400 | tf_op jit(solution)/shard_map/pallas_call | solution.py:216
  39.2 2.7 %collective-permute-done.6.refs_0_ = bf16[200,512]{1,0:T(8,128)(2,1)S(1)} collective-permute-done((bf16[200,512]{1,0:T(8,128)(2,1)S(1)}, bf16[200,512]{1,0:T(8,128)(2,1)S(1)}, u32[]{:S(2)}, u32[]{:S(2)}) %collective-permute-start.6) | collective-permute-done | bytes 204832 | tf_op jit(solution)/shard_map/ppermute | solution.py:445
  41.9 4.4 %collective-permute-done.8.refs_1_ = bf16[200,512]{1,0:T(8,128)(2,1)S(1)} collective-permute-done((bf16[200,512]{1,0:T(8,128)(2,1)S(1)}, bf16[200,512]{1,0:T(8,128)(2,1)S(1)}, u32[]{:S(2)}, u32[]{:S(2)}) %collective-permute-start.8) | collective-permute-done | bytes 204832 | tf_op jit(solution)/shard_map/ppermute | solution.py:445
  46.3 1.6 %shard_map.47 = (bf16[1,200,512]{2,1,0:T(8,128)(2,1)S(1)}, bf16[1,200,512]{2,1,0:T(8,128)(2,1)S(1)}, bf16[1,200,512]{2,1,0:T(8,128)(2,1)S(1)}) custom-call(s32[1]{0:T(128)} %bitcast.1.side_ref, s32[1,1]{1,0:T(1,128)} %bitcast.6.window_ref, f32[12]{0:T(128)S(1)} %copy-done.2, bf16[1,12,200,800]{3,2,1,0:T(8,128)(2,1)S(1)} %bitcast.10, ...), custom_call_target="tpu_custom_call" | custom-call | flops 327680000 | bytes 640000 | tf_op jit(solution)/shard_map/pallas_call | solution.py:166
  47.9 0.6 shard_map.52
  48.6 3.3 %collective-permute-done.14.refs_1_ = bf16[2,200,512]{2,1,0:T(8,128)(2,1)S(1)} collective-permute-done((bf16[2,200,512]{2,1,0:T(8,128)(2,1)S(1)}, bf16[2,200,512]{2,1,0:T(8,128)(2,1)S(1)}, u32[]{:S(2)}, u32[]{:S(2)}) %collective-permute-start.14) | collective-permute-done | bytes 409632 | tf_op jit(solution)/shard_map/ppermute | solution.py:442
  51.9 0.8 %shard_map.53 = (f32[2,200,200]{2,1,0:T(8,128)S(1)}, f32[2,200,200]{2,1,0:T(8,128)S(1)}) custom-call(bf16[2,200,512]{2,1,0:T(8,128)(2,1)S(1)} %get-tuple-element.31.refs_2_.refs_0_, bf16[2,200,512]{2,1,0:T(8,128)(2,1)S(1)} %collective-permute-done.14.refs_1_, bf16[1,200,512]{2,1,0:T(8,128)(2,1)S(1)} %get-tuple-element.27.refs_2_, ...), custom_call_target="tpu_custom_call" | custom-call | flops 491520000 | bytes 1228800 | tf_op jit(solution)/shard_map/pallas_call | solution.py:287
  52.7 2.8 %collective-permute-done.13.refs_1_ = bf16[1,200,512]{2,1,0:T(8,128)(2,1)S(1)} collective-permute-done((bf16[1,200,512]{2,1,0:T(8,128)(2,1)S(1)}, bf16[1,200,512]{2,1,0:T(8,128)(2,1)S(1)}, u32[]{:S(2)}, u32[]{:S(2)}) %collective-permute-start.13) | collective-permute-done | bytes 204832 | tf_op jit(solution)/shard_map/ppermute | solution.py:442
  55.5 0.6 shard_map.54
  56.7 0.6 shard_map.51
  57.3 1.6 %collective-permute-start.12 = (bf16[200,200]{1,0:T(8,128)(2,1)S(1)}, bf16[200,200]{1,0:T(8,128)(2,1)S(1)}, u32[]{:S(2)}, u32[]{:S(2)}) collective-permute-start(bf16[200,200]{1,0:T(8,128)(2,1)S(1)} %get-tuple-element.34), channel_id=1, source_target_pairs={{0,1},{1,0},{2,3},{3,2},{4,5},{5,4},{6,7},{7,6},{8,9},{9,8},{10,11... | collective-permute-start | bytes 240008 | tf_op jit(solution)/shard_map/ppermute | solution.py:442
  58.9 5.0 %collective-permute-done.12.packed_ref = bf16[200,200]{1,0:T(8,128)(2,1)S(1)} collective-permute-done((bf16[200,200]{1,0:T(8,128)(2,1)S(1)}, bf16[200,200]{1,0:T(8,128)(2,1)S(1)}, u32[]{:S(2)}, u32[]{:S(2)}) %collective-permute-start.12) | collective-permute-done | bytes 80032 | tf_op jit(solution)/shard_map/ppermute | solution.py:442
  63.9 1.1 %base.1 = (f32[200,512]{1,0:T(8,128)S(1)}, f32[200,512]{1,0:T(8,128)S(1)}, bf16[384,512]{1,0:T(8,128)(2,1)S(1)}) custom-call(bf16[200,512]{1,0:T(8,128)(2,1)S(1)} %bitcast.15, bf16[200,512]{1,0:T(8,128)(2,1)S(1)} %collective-permute-done.other_ref, f32[2,200,200]{2,1,0:T(8,128)S(1)} %get-tuple-element.33.total_ref, ...), custom_call_target="tpu_custom_call" | custom-call | flops 655360000 | bytes 819200 | tf_op jit(solution)/shard_map/base/pallas_call | solution.py:348
  65.0 3.4 %update.1 = f32[1,200,512]{2,1,0:T(8,128)} custom-call(bf16[200,512]{1,0:T(8,128)(2,1)S(1)} %bitcast.16, bf16[200,512]{1,0:T(8,128)(2,1)S(1)} %collective-permute-done.other_ref, f32[200,512]{1,0:T(8,128)S(1)} %get-tuple-element.41.base_ref, f32[200,512]{1,0:T(8,128)S(1)} %get-tuple-element.42.base_other_ref, ...), custom_call_target="tpu_custom_call" | custom-call | tf_op jit(solution)/shard_map/update/pallas_call | solution.py:415
  (26 shorter events, 2.6 us)
Async XLA Ops:
  0.0 26.8 %copy-start.2 = (f32[12]{0:T(128)S(1)}, f32[12]{0:T(128)}, u32[]{:S(2)}) copy-start(f32[12]{0:T(128)} %weight_ref.7) | copy-start | bytes 148
  0.0 8.3 %collective-permute-start = (bf16[200,512]{1,0:T(8,128)(2,1)}, bf16[200,512]{1,0:T(8,128)(2,1)S(1)}, u32[]{:S(2)}, u32[]{:S(2)}) collective-permute-start(bf16[200,512]{1,0:T(8,128)(2,1)} %bitcast.11), channel_id=1, source_target_pairs={{0,1},{1,0},{2,3},{3,2},{4,5},{5,4},{6,7},{7,6},{8,9},{9,8},{10,11... | collective-permute-start | bytes 614408 | tf_op jit(solution)/shard_map/ppermute | solution.py:442
  3.0 8.3 %collective-permute-start.10 = (bf16[200,512]{1,0:T(8,128)(2,1)}, bf16[200,512]{1,0:T(8,128)(2,1)S(1)}, u32[]{:S(2)}, u32[]{:S(2)}) collective-permute-start(bf16[200,512]{1,0:T(8,128)(2,1)} %bitcast.12), channel_id=1, source_target_pairs={{6,0},{4,2},{2,4},{0,6},{14,8},{12,10},{10,12},{8,14},{22,16},{20,... | collective-permute-start | bytes 614408 | tf_op jit(solution)/shard_map/ppermute | solution.py:445
  3.6 27.0 %collective-permute-start.5 = (bf16[200,512]{1,0:T(8,128)(2,1)}, bf16[200,512]{1,0:T(8,128)(2,1)S(1)}, u32[]{:S(2)}, u32[]{:S(2)}) collective-permute-start(bf16[200,512]{1,0:T(8,128)(2,1)} %bitcast.13), channel_id=1, source_target_pairs={{26,0},{24,2},{30,4},{28,6},{2,8},{0,10},{6,12},{4,14},{10,16},{8,... | collective-permute-start | bytes 614408 | tf_op jit(solution)/shard_map/ppermute | solution.py:445
  5.8 11.8 %collective-permute-start.1 = (bf16[200,512]{1,0:T(8,128)(2,1)}, bf16[200,512]{1,0:T(8,128)(2,1)S(1)}, u32[]{:S(2)}, u32[]{:S(2)}) collective-permute-start(bf16[200,512]{1,0:T(8,128)(2,1)} %bitcast.14), channel_id=1, source_target_pairs={{10,0},{8,2},{14,4},{12,6},{18,8},{16,10},{22,12},{20,14},{26,16},... | collective-permute-start | bytes 614408 | tf_op jit(solution)/shard_map/ppermute | solution.py:445
  8.3 9.8 %collective-permute-start.11 = (bf16[200,512]{1,0:T(8,128)(2,1)S(1)}, bf16[200,512]{1,0:T(8,128)(2,1)S(1)}, u32[]{:S(2)}, u32[]{:S(2)}) collective-permute-start(bf16[200,512]{1,0:T(8,128)(2,1)S(1)} %collective-permute-done.other_ref), channel_id=1, source_target_pairs={{6,0},{4,2},{2,4},{0,6},{14,8},{12,10},{10,12},{8,14},{22,16},{20,... | collective-permute-start | bytes 614408 | tf_op jit(solution)/shard_map/ppermute | solution.py:445
  8.6 22.7 %collective-permute-start.7 = (bf16[200,512]{1,0:T(8,128)(2,1)S(1)}, bf16[200,512]{1,0:T(8,128)(2,1)S(1)}, u32[]{:S(2)}, u32[]{:S(2)}) collective-permute-start(bf16[200,512]{1,0:T(8,128)(2,1)S(1)} %collective-permute-done.other_ref), channel_id=1, source_target_pairs={{26,0},{24,2},{30,4},{28,6},{2,8},{0,10},{6,12},{4,14},{10,16},{8,... | collective-permute-start | bytes 614408 | tf_op jit(solution)/shard_map/ppermute | solution.py:445
  11.3 15.1 %collective-permute-start.3 = (bf16[200,512]{1,0:T(8,128)(2,1)S(1)}, bf16[200,512]{1,0:T(8,128)(2,1)S(1)}, u32[]{:S(2)}, u32[]{:S(2)}) collective-permute-start(bf16[200,512]{1,0:T(8,128)(2,1)S(1)} %collective-permute-done.other_ref), channel_id=1, source_target_pairs={{10,0},{8,2},{14,4},{12,6},{18,8},{16,10},{22,12},{20,14},{26,16},... | collective-permute-start | bytes 614408 | tf_op jit(solution)/shard_map/ppermute | solution.py:445
  17.6 19.9 %collective-permute-start.9 = (bf16[200,800]{1,0:T(8,128)(2,1)S(1)}, bf16[200,800]{1,0:T(8,128)(2,1)S(1)}, u32[]{:S(2)}, u32[]{:S(2)}) collective-permute-start(bf16[200,800]{1,0:T(8,128)(2,1)S(1)} %dynamic-slice_bitcast_fusion), channel_id=1, source_target_pairs={{0,1},{1,0},{2,3},{3,2},{4,5},{5,4},{6,7},{7,6},{8,9},{9,8},{10,11... | collective-permute-start | bytes 960008 | tf_op jit(solution)/shard_map/ppermute | solution.py:442
  18.1 16.4 %collective-permute-start.2 = (bf16[200,512]{1,0:T(8,128)(2,1)S(1)}, bf16[200,512]{1,0:T(8,128)(2,1)S(1)}, u32[]{:S(2)}, u32[]{:S(2)}) collective-permute-start(bf16[200,512]{1,0:T(8,128)(2,1)S(1)} %collective-permute-done.1.refs_0_), channel_id=1, source_target_pairs={{6,0},{4,2},{2,4},{0,6},{14,8},{12,10},{10,12},{8,14},{22,16},{20,... | collective-permute-start | bytes 614408 | tf_op jit(solution)/shard_map/ppermute | solution.py:445
  26.4 8.9 %collective-permute-start.4 = (bf16[200,512]{1,0:T(8,128)(2,1)S(1)}, bf16[200,512]{1,0:T(8,128)(2,1)S(1)}, u32[]{:S(2)}, u32[]{:S(2)}) collective-permute-start(bf16[200,512]{1,0:T(8,128)(2,1)S(1)} %collective-permute-done.3.refs_1_), channel_id=1, source_target_pairs={{6,0},{4,2},{2,4},{0,6},{14,8},{12,10},{10,12},{8,14},{22,16},{20,... | collective-permute-start | bytes 614408 | tf_op jit(solution)/shard_map/ppermute | solution.py:445
  26.8 2.2 %copy-start = (bf16[1,12,200,800]{3,2,1,0:T(8,128)(2,1)S(1)}, bf16[1,12,200,800]{3,2,1,0:T(8,128)(2,1)}, u32[]{:S(2)}) copy-start(bf16[1,12,200,800]{3,2,1,0:T(8,128)(2,1)} %margins_ref.7) | copy-start | bytes 11520004
  29.0 17.2 %slice-start = ((s8[4300800]{0:T(1024)(128)(4,1)}), s8[4194304]{0:T(1024)(128)(4,1)S(1)}, s32[]{:S(2)}) async-start(s8[4300800]{0:T(1024)(128)(4,1)} %bitcast.9), calls=%async_computation | async-start | bytes 8388608
  30.7 17.2 %collective-permute-start.15 = (bf16[2,200,512]{2,1,0:T(8,128)(2,1)S(1)}, bf16[2,200,512]{2,1,0:T(8,128)(2,1)S(1)}, u32[]{:S(2)}, u32[]{:S(2)}) collective-permute-start(bf16[2,200,512]{2,1,0:T(8,128)(2,1)S(1)} %get-tuple-element.30.refs_1_), channel_id=1, source_target_pairs={{0,1},{1,0},{2,3},{3,2},{4,5},{5,4},{6,7},{7,6},{8,9},{9,8},{10,11... | collective-permute-start | bytes 1228808 | tf_op jit(solution)/shard_map/ppermute | solution.py:442
  31.3 15.0 %slice-start.1 = ((s8[4300800]{0:T(1024)(128)(4,1)}), s8[106496]{0:T(1024)(128)(4,1)S(1)}, s32[]{:S(2)}) async-start(s8[4300800]{0:T(1024)(128)(4,1)} %bitcast.9), calls=%async_computation.1 | async-start | bytes 212992
  32.9 18.9 %collective-permute-start.14 = (bf16[2,200,512]{2,1,0:T(8,128)(2,1)S(1)}, bf16[2,200,512]{2,1,0:T(8,128)(2,1)S(1)}, u32[]{:S(2)}, u32[]{:S(2)}) collective-permute-start(bf16[2,200,512]{2,1,0:T(8,128)(2,1)S(1)} %get-tuple-element.32.refs_3_), channel_id=1, source_target_pairs={{0,1},{1,0},{2,3},{3,2},{4,5},{5,4},{6,7},{7,6},{8,9},{9,8},{10,11... | collective-permute-start | bytes 1228808 | tf_op jit(solution)/shard_map/ppermute | solution.py:442
  34.5 7.3 %collective-permute-start.6 = (bf16[200,512]{1,0:T(8,128)(2,1)S(1)}, bf16[200,512]{1,0:T(8,128)(2,1)S(1)}, u32[]{:S(2)}, u32[]{:S(2)}) collective-permute-start(bf16[200,512]{1,0:T(8,128)(2,1)S(1)} %collective-permute-done.5.refs_2_), channel_id=1, source_target_pairs={{6,0},{4,2},{2,4},{0,6},{14,8},{12,10},{10,12},{8,14},{22,16},{20,... | collective-permute-start | bytes 614408 | tf_op jit(solution)/shard_map/ppermute | solution.py:445
  35.3 11.0 %collective-permute-start.8 = (bf16[200,512]{1,0:T(8,128)(2,1)S(1)}, bf16[200,512]{1,0:T(8,128)(2,1)S(1)}, u32[]{:S(2)}, u32[]{:S(2)}) collective-permute-start(bf16[200,512]{1,0:T(8,128)(2,1)S(1)} %collective-permute-done.7.refs_3_), channel_id=1, source_target_pairs={{6,0},{4,2},{2,4},{0,6},{14,8},{12,10},{10,12},{8,14},{22,16},{20,... | collective-permute-start | bytes 614408 | tf_op jit(solution)/shard_map/ppermute | solution.py:445
  37.5 18.0 %collective-permute-start.13 = (bf16[1,200,512]{2,1,0:T(8,128)(2,1)S(1)}, bf16[1,200,512]{2,1,0:T(8,128)(2,1)S(1)}, u32[]{:S(2)}, u32[]{:S(2)}) collective-permute-start(bf16[1,200,512]{2,1,0:T(8,128)(2,1)S(1)} %get-tuple-element.26.refs_1_), channel_id=1, source_target_pairs={{0,1},{1,0},{2,3},{3,2},{4,5},{5,4},{6,7},{7,6},{8,9},{9,8},{10,11... | collective-permute-start | bytes 614408 | tf_op jit(solution)/shard_map/ppermute | solution.py:442
  47.9 16.0 %copy-start.1 = (bf16[1,200,512]{2,1,0:T(8,128)(2,1)S(1)}, bf16[1,200,512]{2,1,0:T(8,128)(2,1)}, u32[]{:S(2)}) copy-start(bf16[1,200,512]{2,1,0:T(8,128)(2,1)} %param.5) | copy-start | bytes 614404
  56.2 8.8 %collective-permute-start.16 = (bf16[216,384]{1,0:T(8,128)(2,1)S(1)}, bf16[216,384]{1,0:T(8,128)(2,1)S(1)}, u32[]{:S(2)}, u32[]{:S(2)}) collective-permute-start(bf16[216,384]{1,0:T(8,128)(2,1)S(1)} %get-tuple-element.44), channel_id=1, source_target_pairs={{0,1},{1,0},{2,3},{3,2},{4,5},{5,4},{6,7},{7,6},{8,9},{9,8},{10,11... | collective-permute-start | bytes 497672 | tf_op jit(solution)/shard_map/ppermute | solution.py:442
  57.3 6.6 %collective-permute-start.12 = (bf16[200,200]{1,0:T(8,128)(2,1)S(1)}, bf16[200,200]{1,0:T(8,128)(2,1)S(1)}, u32[]{:S(2)}, u32[]{:S(2)}) collective-permute-start(bf16[200,200]{1,0:T(8,128)(2,1)S(1)} %get-tuple-element.34), channel_id=1, source_target_pairs={{0,1},{1,0},{2,3},{3,2},{4,5},{5,4},{6,7},{7,6},{8,9},{9,8},{10,11... | collective-permute-start | bytes 240008 | tf_op jit(solution)/shard_map/ppermute | solution.py:442

commit v10 on v9

--- a/solution.py
+++ b/solution.py
@@ -97,15 +97,18 @@
     stacked_ref[2 * rows :, :] = times_i(whole).astype(BF16)
 
 
+def masked(product, weight, limit):
+    inside = lax.broadcasted_iota(jnp.int32, (product.shape[0], 1), 0) < limit
+    return (product * jnp.where(inside, jnp.sqrt(jnp.full((1, 1), weight, F32)), 0.0)).astype(BF16)
+
+
 def masked_blocks(margins, stacked, weights, limit):
     count, rows, double = margins.shape
-    inside = lax.broadcasted_iota(jnp.int32, (rows, 1), 0) < limit
     products = dot(margins.reshape(count * rows, double), stacked)
-    blocks = []
-    for place, weight in enumerate(weights):
-        factor = jnp.where(inside, jnp.sqrt(jnp.full((1, 1), weight, F32)), 0.0)
-        blocks.append((products[place * rows : (place + 1) * rows] * factor).astype(BF16))
-    return blocks
+    return [
+        masked(products[place * rows : (place + 1) * rows], weight, limit)
+        for place, weight in enumerate(weights)
+    ]
 
 
 def prepare_kernel(out_ref):
@@ -134,9 +137,21 @@
     side = side_ref[0]
     rows = margins_ref.shape[2]
     limits = [window_ref[...] - side * rows, window_ref[...] - (1 - side) * rows]
+    paired = []
     for number, members in enumerate(groups):
         mine, other = halves[2 * number][...], halves[2 * number + 1][...]
         stack_complex(mine, other, side, rows_ref, stacked_ref)
+        if members[0] % 2 == 0 and len(members) % 2 == 0:
+            for pair in range(members[0] // 2, members[-1] // 2 + 1):
+                for out_ref, place in ((keep_ref, side), (other_ref, 1 - side)):
+                    place = first + 2 * pair + place
+                    product = dot(margins_ref[0, place], stacked_ref[...])
+                    out_ref[pair] = masked(product, weight_ref[place], limits[0])
+                paired.append(pair)
+            if not sent:
+                product = dot(shipped_ref[...], stacked_ref[...])
+                got_ref[0] = masked(product, weight_ref[first + side], limits[1])
+            continue
         start, count = first + members[0], len(members)
         blocks = masked_blocks(
             margins_ref[0, start : start + count],
@@ -153,7 +168,7 @@
                     (got_ref[0],) = masked_blocks(
                         shipped_ref[...][None], stacked_ref[...], [weight], limits[1]
                     )
-    for pair in range(keep_ref.shape[0]):
+    for pair in [pair for pair in range(keep_ref.shape[0]) if pair not in paired]:
         keep_ref[pair] = blocks_ref[2 * pair + side]
         other_ref[pair] = blocks_ref[2 * pair + 1 - side]
 
@@ -239,45 +254,43 @@
     return (rows + -(-spare // 16) * 16, 2 * even + LANES)
 
 
-def cross_kernel(terms, count, has_total, last, *refs):
+def tiles_of(plain, turned):
+    even, left, fit, _ = packing(plain.shape[0])
+    pieces = [plain[:even], turned[:even], plain[even:], turned[even : even + fit]]
+    if left + fit < LANES:
+        pieces.append(jnp.zeros((LANES - left - fit, plain.shape[1]), plain.dtype))
+    return jnp.concatenate(pieces, axis=0)
+
+
+def cross_kernel(terms, count, has_total, *refs):
     blocks, refs = refs[:count], refs[count:]
     rows = blocks[0].shape[1]
-    sums = [jnp.zeros((rows, rows), F32) for _ in range(4)]
+    *_, spare = packing(rows)
+    mine_ref, theirs_ref, packed_ref = refs[-3:]
+    real = imag = jnp.zeros((rows, rows), F32)
+    theirs = jnp.zeros((rows, packed_ref.shape[1]), F32)
+    below = jnp.zeros((spare, rows), F32)
     if has_total:
-        mine_before_ref, theirs_before_ref, *refs = refs
-        sums = [mine_before_ref[0], mine_before_ref[1], theirs_before_ref[0], theirs_before_ref[1]]
-    mine_ref, theirs_ref, *refs = refs
+        mine_before_ref, theirs_before_ref = refs[:2]
+        real, imag = mine_before_ref[0], mine_before_ref[1]
+        theirs = theirs_before_ref[:rows, :]
+        if spare:
+            below = theirs_before_ref[rows : rows + spare, :rows]
     for keep_place, keep_index, got_place, got_index in terms:
         keep, got = blocks[keep_place][keep_index], blocks[got_place][got_index]
-        sums[0] += dot(keep, got, NT)
-        sums[1] += dot(times_minus_i(keep), got, NT)
-        sums[2] += dot(got, keep, NT)
-        sums[3] += dot(times_minus_i(got), keep, NT)
-    mine_ref[0], mine_ref[1] = sums[0], sums[1]
-    real, imag = sums[2], sums[3]
-    if not last:
-        theirs_ref[0], theirs_ref[1] = real, imag
-        return
-    (packed_ref,) = refs
-    even, left, fit, spare = packing(rows)
-    packed_ref[:rows, :even] = real[:, :even]
-    packed_ref[:rows, even : 2 * even] = imag[:, :even]
-    packed_ref[:rows, 2 * even :] = jnp.concatenate(
-        [
-            real[:, even:],
-            imag[:, even : even + fit],
-            jnp.zeros((rows, LANES - left - fit), F32),
-        ][: 3 if left + fit < LANES else 2],
-        axis=1,
-    )
+        real += dot(keep, got, NT)
+        imag += dot(times_minus_i(keep), got, NT)
+        plain = keep.astype(F32)
+        turned = times_i(plain)
+        theirs += dot(got, tiles_of(plain, turned).astype(BF16), NT)
+        if spare:
+            below += dot(turned[rows - spare :].astype(BF16), got, NT)
+    mine_ref[0], mine_ref[1] = real, imag
+    packed_ref[:rows, :] = theirs
     if spare:
         packed_ref[rows:, :] = jnp.zeros((packed_ref.shape[0] - rows, packed_ref.shape[1]), F32)
-        row, column = triangle(rows)
-        identity = jnp.where(row == column, 1.0, 0.0).astype(BF16)
-        packed_ref[rows : rows + spare, :rows] = dot(
-            imag[:, rows - spare :].astype(BF16), identity, TN
-        )
-    theirs_ref[...] = packed_ref[...].astype(BF16)
+        packed_ref[rows : rows + spare, :rows] = below
+    theirs_ref[...] = packed_ref[...].astype(theirs_ref.dtype)
 
 
 def cross(blocks, terms, before, last):
@@ -285,14 +298,14 @@
     operands = [*blocks, *(before or ())]
     packed = packed_shape(rows)
     return pl.pallas_call(
-        functools.partial(cross_kernel, terms, len(blocks), before is not None, last),
+        functools.partial(cross_kernel, terms, len(blocks), before is not None),
         in_specs=[VMEM] * len(operands),
         out_specs=[VMEM] * 2,
         out_shape=[
             jax.ShapeDtypeStruct((2, rows, rows), F32),
-            jax.ShapeDtypeStruct(packed, BF16) if last else jax.ShapeDtypeStruct((2, rows, rows), F32),
+            jax.ShapeDtypeStruct(packed, BF16 if last else F32),
         ],
-        scratch_shapes=[pltpu.VMEM(packed, F32)] if last else [],
+        scratch_shapes=[pltpu.VMEM(packed, F32)],
         cost_estimate=pl.CostEstimate(
             flops=8 * len(terms) * rows * rows * width,
             bytes_accessed=4 * len(terms) * rows * width,
@@ -308,7 +321,7 @@
 
 
 def base_kernel(
-    own_ref, other_ref, total_ref, packed_ref, mine_ref, base_ref, base_other_ref, right_ref, stack_ref
+    own_ref, other_ref, total_ref, packed_ref, mine_ref, base_ref, base_other_ref, right_ref
 ):
     own, other = own_ref[...], other_ref[...]
     own_i, other_i = times_i(own.astype(F32)).astype(BF16), times_i(other.astype(F32)).astype(BF16)
@@ -332,15 +345,8 @@
         + dot_exact_right(real, own, TN)
         - dot_exact_right(imag, own_i, TN)
     )
-    even, left, fit, _ = packing(other.shape[0])
-    plain, turned = other.astype(F32), times_i(other.astype(F32))
-    stack_ref[:even, :] = plain[:even]
-    stack_ref[even : 2 * even, :] = turned[:even]
-    stack_ref[2 * even : 2 * even + left, :] = plain[even:]
-    stack_ref[2 * even + left : 2 * even + left + fit, :] = turned[even : even + fit]
-    if left + fit < LANES:
-        stack_ref[2 * even + left + fit :, :] = jnp.zeros((LANES - left - fit, plain.shape[1]), F32)
-    right_ref[...] = stack_ref[...].astype(BF16)
+    plain = other.astype(F32)
+    right_ref[...] = tiles_of(plain, times_i(plain)).astype(BF16)
 
 
 def base(own, other, total, packed, mine):
@@ -354,7 +360,6 @@
             jax.ShapeDtypeStruct((rows, width), F32),
             jax.ShapeDtypeStruct((packed_shape(rows)[1], width), BF16),
         ],
-        scratch_shapes=[pltpu.VMEM((packed_shape(rows)[1], width), F32)],
         cost_estimate=pl.CostEstimate(
             flops=32 * rows * rows * width, bytes_accessed=8 * rows * width, transcendentals=0
         ),
@@ -391,7 +396,7 @@
         jnp.int32, (half, 2 * half), 1
     )
     gram = jnp.concatenate([real, imag], axis=1)
-    squares = jnp.sum(jnp.where(diagonal, gram, 0.0))
+    squares = jnp.sum(rows_ref[...] * rows_ref[...])
     size = jnp.full((1, 1), 2.0 * squares / half + 1e-06, F32)
     scaling = lax.rsqrt(size)
     rest = gram * (scaling * scaling) - jnp.where(diagonal, CENTRE, 0.0)
@@ -478,8 +483,8 @@
     }
     *rest, got_extra = project_part(0, range(SHIPPED, BATCH), margin, False)
     got = {batch: exchange(blocks[batch][1]) for batch in (2, 1, 0)}
-    (total,) = gather_own([*blocks[2], *blocks[1]], None)
-    total, packed = gather_own([*blocks[0], *rest], total)
+    (total,) = gather_own([*blocks[2], *blocks[1], *blocks[0]], None)
+    total, packed = gather_own(rest, total)
     other_packed = exchange(packed)
     whole = ((0, 0, 1, 0), (0, 1, 1, 1))
     crossed = cross([blocks[2][0], got[2]], whole, None, False)

time: 68.5 us -> 68.7 us (level)
  waiting for transfers between devices: 28.7 us -> 25.9 us
  starting transfers between devices: 21.3 us -> 24 us
    ppermute x10, waiting for transfers between devices: 17.1 us -> 13.1 us  [fetch(): return lax.ppermute(value, 'kpt', fetch_pairs(shift, point_count))]
    ppermute x10, starting transfers between devices: 13 us -> 14.6 us  [fetch(): return lax.ppermute(value, 'kpt', fetch_pairs(shift, point_count))]
    ppermute x7, waiting for transfers between devices: 11.6 us -> 12.9 us  [exchange(): return lax.ppermute(value, 'band', swap)]
    ppermute x7, starting transfers between devices: 8.33 us -> 9.46 us  [exchange(): return lax.ppermute(value, 'band', swap)]
    unnamed x10 -> x6, local copies, waits for them, and re-layouts: 2.24 us -> 2.23 us
  transfers between devices with their start and end apart: 17 -> 17, of which waited for: 8 -> 7; matrix products, arithmetic and copies ran while one was open for 1% -> 1% of each run, Pallas kernels for 15% -> 15%
where the time goes in v10:
time: 68.7 us; the launch traced here: 68.1 us
  waiting for transfers between devices  25.9 us (38%)
  starting transfers between devices  24 us (35%)
  Pallas kernels  14.1 us (21%)
  local copies, waits for them, and re-layouts  3.24 us (5%)
  between operations  0.8 us (1%)
    ppermute x10, starting transfers between devices, fetch(): return lax.ppermute(value, 'kpt', fetch_pairs(shift, point_count))  14.6 us
    ppermute x10, waiting for transfers between devices, fetch(): return lax.ppermute(value, 'kpt', fetch_pairs(shift, point_count))  13.1 us
    ppermute x7, waiting for transfers between devices, exchange(): return lax.ppermute(value, 'band', swap)  12.9 us
    ppermute x7, starting transfers between devices, exchange(): return lax.ppermute(value, 'band', swap)  9.46 us
    pallas_call x4, Pallas kernels, project(): pl.pallas_call(functools.partial(project_kernel, groups, first, sent), in...  5.97 us
    pallas_call x1, Pallas kernels, update(): pl.pallas_call(functools.partial(update_kernel, scale), in_specs=[VMEM] *...  3.18 us
    unnamed x6, local copies, waits for them, and re-layouts  2.23 us
    pallas_call x3, Pallas kernels, cross(): pl.pallas_call(functools.partial(cross_kernel, terms, len(blocks), before...  2.23 us
  transfers between devices with their start and end apart: 17, of which 7 were waited for; matrix products, arithmetic and copies ran while one was open for 1% of the time, Pallas kernels for 15%

profile of v10, /device:TPU:0, one launch (start us, length us, event | category | flops | bytes accessed | tf_op | source)
XLA Modules:
  0.0 68.1 jit_solution(16327063440886616009)
XLA Ops:
  0.0 3.0 %collective-permute-start = (bf16[200,512]{1,0:T(8,128)(2,1)}, bf16[200,512]{1,0:T(8,128)(2,1)S(1)}, u32[]{:S(2)}, u32[]{:S(2)}) collective-permute-start(bf16[200,512]{1,0:T(8,128)(2,1)} %bitcast.9), channel_id=1, source_target_pairs={{0,1},{1,0},{2,3},{3,2},{4,5},{5,4},{6,7},{7,6},{8,9},{9,8},{10,11... | collective-permute-start | bytes 614408 | tf_op jit(solution)/shard_map/ppermute | solution.py:447
  3.0 2.8 %collective-permute-start.8 = (bf16[200,512]{1,0:T(8,128)(2,1)}, bf16[200,512]{1,0:T(8,128)(2,1)S(1)}, u32[]{:S(2)}, u32[]{:S(2)}) collective-permute-start(bf16[200,512]{1,0:T(8,128)(2,1)} %bitcast.10), channel_id=1, source_target_pairs={{10,0},{8,2},{14,4},{12,6},{18,8},{16,10},{22,12},{20,14},{26,16},... | collective-permute-start | bytes 614408 | tf_op jit(solution)/shard_map/ppermute | solution.py:450
  5.8 2.1 %collective-permute-start.6 = (bf16[200,512]{1,0:T(8,128)(2,1)}, bf16[200,512]{1,0:T(8,128)(2,1)S(1)}, u32[]{:S(2)}, u32[]{:S(2)}) collective-permute-start(bf16[200,512]{1,0:T(8,128)(2,1)} %bitcast.11), channel_id=1, source_target_pairs={{6,0},{4,2},{2,4},{0,6},{14,8},{12,10},{10,12},{8,14},{22,16},{20,... | collective-permute-start | bytes 614408 | tf_op jit(solution)/shard_map/ppermute | solution.py:450
  7.8 0.5 collective-permute-done.other_ref
  8.3 3.1 %collective-permute-start.9 = (bf16[200,512]{1,0:T(8,128)(2,1)S(1)}, bf16[200,512]{1,0:T(8,128)(2,1)S(1)}, u32[]{:S(2)}, u32[]{:S(2)}) collective-permute-start(bf16[200,512]{1,0:T(8,128)(2,1)S(1)} %collective-permute-done.other_ref), channel_id=1, source_target_pairs={{10,0},{8,2},{14,4},{12,6},{18,8},{16,10},{22,12},{20,14},{26,16},... | collective-permute-start | bytes 614408 | tf_op jit(solution)/shard_map/ppermute | solution.py:450
  11.4 2.0 %collective-permute-start.7 = (bf16[200,512]{1,0:T(8,128)(2,1)S(1)}, bf16[200,512]{1,0:T(8,128)(2,1)S(1)}, u32[]{:S(2)}, u32[]{:S(2)}) collective-permute-start(bf16[200,512]{1,0:T(8,128)(2,1)S(1)} %collective-permute-done.other_ref), channel_id=1, source_target_pairs={{6,0},{4,2},{2,4},{0,6},{14,8},{12,10},{10,12},{8,14},{22,16},{20,... | collective-permute-start | bytes 614408 | tf_op jit(solution)/shard_map/ppermute | solution.py:450
  13.3 1.2 %collective-permute-start.10 = (bf16[200,512]{1,0:T(8,128)(2,1)S(1)}, bf16[200,512]{1,0:T(8,128)(2,1)S(1)}, u32[]{:S(2)}, u32[]{:S(2)}) collective-permute-start(bf16[200,512]{1,0:T(8,128)(2,1)S(1)} %collective-permute-done.8.refs_0_), channel_id=1, source_target_pairs={{6,0},{4,2},{2,4},{0,6},{14,8},{12,10},{10,12},{8,14},{22,16},{20,... | collective-permute-start | bytes 614408 | tf_op jit(solution)/shard_map/ppermute | solution.py:450
  14.6 5.5 %collective-permute-done.9.refs_1_ = bf16[200,512]{1,0:T(8,128)(2,1)S(1)} collective-permute-done((bf16[200,512]{1,0:T(8,128)(2,1)S(1)}, bf16[200,512]{1,0:T(8,128)(2,1)S(1)}, u32[]{:S(2)}, u32[]{:S(2)}) %collective-permute-start.9) | collective-permute-done | bytes 204832 | tf_op jit(solution)/shard_map/ppermute | solution.py:450
  20.0 1.7 %collective-permute-start.11 = (bf16[200,512]{1,0:T(8,128)(2,1)S(1)}, bf16[200,512]{1,0:T(8,128)(2,1)S(1)}, u32[]{:S(2)}, u32[]{:S(2)}) collective-permute-start(bf16[200,512]{1,0:T(8,128)(2,1)S(1)} %collective-permute-done.9.refs_1_), channel_id=1, source_target_pairs={{6,0},{4,2},{2,4},{0,6},{14,8},{12,10},{10,12},{8,14},{22,16},{20,... | collective-permute-start | bytes 614408 | tf_op jit(solution)/shard_map/ppermute | solution.py:450
  21.8 1.0 %dynamic-slice_bitcast_fusion = bf16[200,800]{1,0:T(8,128)(2,1)S(1)} fusion(bf16[1,12,200,800]{3,2,1,0:T(8,128)(2,1)} %margins_ref.7, s32[]{:T(128)S(6)} %select_n.4), kind=kLoop, calls=%fused_computation | loop fusion | bytes 640004 | tf_op jit(solution)/shard_map/jit(dynamic_index_in_dim)/squeeze | solution.py:456
  23.5 1.3 %collective-permute-start.5 = (bf16[200,800]{1,0:T(8,128)(2,1)S(1)}, bf16[200,800]{1,0:T(8,128)(2,1)S(1)}, u32[]{:S(2)}, u32[]{:S(2)}) collective-permute-start(bf16[200,800]{1,0:T(8,128)(2,1)S(1)} %dynamic-slice_bitcast_fusion), channel_id=1, source_target_pairs={{0,1},{1,0},{2,3},{3,2},{4,5},{5,4},{6,7},{7,6},{8,9},{9,8},{10,11... | collective-permute-start | bytes 960008 | tf_op jit(solution)/shard_map/ppermute | solution.py:447
  24.7 2.2 %copy-done = bf16[1,12,200,800]{3,2,1,0:T(8,128)(2,1)S(1)} copy-done((bf16[1,12,200,800]{3,2,1,0:T(8,128)(2,1)S(1)}, bf16[1,12,200,800]{3,2,1,0:T(8,128)(2,1)}, u32[]{:S(2)}) %copy-start) | copy-done | bytes 3840024
  26.9 1.7 %shard_map.47 = (bf16[2,200,512]{2,1,0:T(8,128)(2,1)S(1)}, bf16[2,200,512]{2,1,0:T(8,128)(2,1)S(1)}) custom-call(s32[1]{0:T(128)} %bitcast.1.side_ref, s32[1,1]{1,0:T(1,128)} %bitcast.6.window_ref, f32[12]{0:T(128)S(1)} %copy-done.2, bf16[1,12,200,800]{3,2,1,0:T(8,128)(2,1)S(1)} %copy-done, bf16[200,512]{1,0:T(8,128)(2,1)S(1)} %collective-permute-done.6.refs_0_, ...), custom_call_target="tpu_custom_call" | custom-call | flops 655360000 | bytes 1280000 | tf_op jit(solution)/shard_map/pallas_call | solution.py:181
  28.6 0.9 %collective-permute-start.15 = (bf16[2,200,512]{2,1,0:T(8,128)(2,1)S(1)}, bf16[2,200,512]{2,1,0:T(8,128)(2,1)S(1)}, u32[]{:S(2)}, u32[]{:S(2)}) collective-permute-start(bf16[2,200,512]{2,1,0:T(8,128)(2,1)S(1)} %get-tuple-element.28.refs_1_), channel_id=1, source_target_pairs={{0,1},{1,0},{2,3},{3,2},{4,5},{5,4},{6,7},{7,6},{8,9},{9,8},{10,11... | collective-permute-start | bytes 1228808 | tf_op jit(solution)/shard_map/ppermute | solution.py:447
  29.5 1.7 %shard_map.48 = (bf16[2,200,512]{2,1,0:T(8,128)(2,1)S(1)}, bf16[2,200,512]{2,1,0:T(8,128)(2,1)S(1)}) custom-call(s32[1]{0:T(128)} %bitcast.1.side_ref, s32[1,1]{1,0:T(1,128)} %bitcast.7.window_ref, f32[12]{0:T(128)S(1)} %copy-done.2, bf16[1,12,200,800]{3,2,1,0:T(8,128)(2,1)S(1)} %copy-done, bf16[200,512]{1,0:T(8,128)(2,1)S(1)} %collective-permute-done.8.refs_0_, ...), custom_call_target="tpu_custom_call" | custom-call | flops 655360000 | bytes 1280000 | tf_op jit(solution)/shard_map/pallas_call | solution.py:181
  31.2 1.3 %collective-permute-start.14 = (bf16[2,200,512]{2,1,0:T(8,128)(2,1)S(1)}, bf16[2,200,512]{2,1,0:T(8,128)(2,1)S(1)}, u32[]{:S(2)}, u32[]{:S(2)}) collective-permute-start(bf16[2,200,512]{2,1,0:T(8,128)(2,1)S(1)} %get-tuple-element.30.refs_3_), channel_id=1, source_target_pairs={{0,1},{1,0},{2,3},{3,2},{4,5},{5,4},{6,7},{7,6},{8,9},{9,8},{10,11... | collective-permute-start | bytes 1228808 | tf_op jit(solution)/shard_map/ppermute | solution.py:447
  32.5 1.7 %collective-permute-start.4 = (bf16[200,512]{1,0:T(8,128)(2,1)S(1)}, bf16[200,512]{1,0:T(8,128)(2,1)S(1)}, u32[]{:S(2)}, u32[]{:S(2)}) collective-permute-start(bf16[200,512]{1,0:T(8,128)(2,1)S(1)} %collective-permute-done.3.refs_3_), channel_id=1, source_target_pairs={{6,0},{4,2},{2,4},{0,6},{14,8},{12,10},{10,12},{8,14},{22,16},{20,... | collective-permute-start | bytes 614408 | tf_op jit(solution)/shard_map/ppermute | solution.py:450
  34.2 1.2 %shard_map.49 = (bf16[1,200,512]{2,1,0:T(8,128)(2,1)S(1)}, bf16[1,200,512]{2,1,0:T(8,128)(2,1)S(1)}) custom-call(s32[1]{0:T(128)} %bitcast.1.side_ref, s32[1,1]{1,0:T(1,128)} %bitcast.8.window_ref, f32[12]{0:T(128)S(1)} %copy-done.2, bf16[1,12,200,800]{3,2,1,0:T(8,128)(2,1)S(1)} %copy-done, bf16[200,512]{1,0:T(8,128)(2,1)S(1)} %collective-permute-done.10.refs_0_, ...), custom_call_target="tpu_custom_call" | custom-call | flops 327680000 | bytes 640000 | tf_op jit(solution)/shard_map/pallas_call | solution.py:181
  35.5 0.9 %collective-permute-start.13 = (bf16[1,200,512]{2,1,0:T(8,128)(2,1)S(1)}, bf16[1,200,512]{2,1,0:T(8,128)(2,1)S(1)}, u32[]{:S(2)}, u32[]{:S(2)}) collective-permute-start(bf16[1,200,512]{2,1,0:T(8,128)(2,1)S(1)} %get-tuple-element.32.refs_5_), channel_id=1, source_target_pairs={{0,1},{1,0},{2,3},{3,2},{4,5},{5,4},{6,7},{7,6},{8,9},{9,8},{10,11... | collective-permute-start | bytes 614408 | tf_op jit(solution)/shard_map/ppermute | solution.py:447
  36.3 3.5 %collective-permute-done.2.refs_0_ = bf16[200,512]{1,0:T(8,128)(2,1)S(1)} collective-permute-done((bf16[200,512]{1,0:T(8,128)(2,1)S(1)}, bf16[200,512]{1,0:T(8,128)(2,1)S(1)}, u32[]{:S(2)}, u32[]{:S(2)}) %collective-permute-start.2) | collective-permute-done | bytes 204832 | tf_op jit(solution)/shard_map/ppermute | solution.py:450
  39.9 4.1 %collective-permute-done.4.refs_1_ = bf16[200,512]{1,0:T(8,128)(2,1)S(1)} collective-permute-done((bf16[200,512]{1,0:T(8,128)(2,1)S(1)}, bf16[200,512]{1,0:T(8,128)(2,1)S(1)}, u32[]{:S(2)}, u32[]{:S(2)}) %collective-permute-start.4) | collective-permute-done | bytes 204832 | tf_op jit(solution)/shard_map/ppermute | solution.py:450
  43.9 1.4 %shard_map.46 = (bf16[1,200,512]{2,1,0:T(8,128)(2,1)S(1)}, bf16[1,200,512]{2,1,0:T(8,128)(2,1)S(1)}, bf16[1,200,512]{2,1,0:T(8,128)(2,1)S(1)}) custom-call(s32[1]{0:T(128)} %bitcast.1.side_ref, s32[1,1]{1,0:T(1,128)} %bitcast.5.window_ref, f32[12]{0:T(128)S(1)} %copy-done.2, bf16[1,12,200,800]{3,2,1,0:T(8,128)(2,1)S(1)} %copy-done, ...), custom_call_target="tpu_custom_call" | custom-call | flops 327680000 | bytes 640000 | tf_op jit(solution)/shard_map/pallas_call | solution.py:181
  45.4 1.3 %shard_map.50.refs_2_ = f32[2,200,200]{2,1,0:T(8,128)S(1)} custom-call(bf16[2,200,512]{2,1,0:T(8,128)(2,1)S(1)} %get-tuple-element.27.refs_0_, bf16[2,200,512]{2,1,0:T(8,128)(2,1)S(1)} %get-tuple-element.28.refs_1_, bf16[2,200,512]{2,1,0:T(8,128)(2,1)S(1)} %get-tuple-element.29.refs_2_.refs_0_, bf16[2,200,512]{2,1,0:T(8,128)(2,1)S(1)} %get-tuple-element.30.refs_3_, ...), custom_call_target="tpu_custom_call" | custom-call | flops 983040000 | bytes 2457600 | tf_op jit(solution)/shard_map/pallas_call | solution.py:231
  46.7 0.8 %shard_map.52 = (f32[2,200,200]{2,1,0:T(8,128)S(1)}, f32[216,384]{1,0:T(8,128)S(1)}) custom-call(bf16[2,200,512]{2,1,0:T(8,128)(2,1)S(1)} %get-tuple-element.27.refs_0_, bf16[2,200,512]{2,1,0:T(8,128)(2,1)S(1)} %collective-permute-done.15.refs_1_), custom_call_target="tpu_custom_call" | custom-call | flops 327680000 | bytes 819200 | tf_op jit(solution)/shard_map/pallas_call | solution.py:300
  47.4 4.9 %collective-permute-done.14.refs_1_ = bf16[2,200,512]{2,1,0:T(8,128)(2,1)S(1)} collective-permute-done((bf16[2,200,512]{2,1,0:T(8,128)(2,1)S(1)}, bf16[2,200,512]{2,1,0:T(8,128)(2,1)S(1)}, u32[]{:S(2)}, u32[]{:S(2)}) %collective-permute-start.14) | collective-permute-done | bytes 409632 | tf_op jit(solution)/shard_map/ppermute | solution.py:447
  52.3 1.0 %shard_map.53 = (f32[2,200,200]{2,1,0:T(8,128)S(1)}, f32[216,384]{1,0:T(8,128)S(1)}) custom-call(bf16[2,200,512]{2,1,0:T(8,128)(2,1)S(1)} %get-tuple-element.29.refs_2_.refs_0_, bf16[2,200,512]{2,1,0:T(8,128)(2,1)S(1)} %collective-permute-done.14.refs_1_, bf16[1,200,512]{2,1,0:T(8,128)(2,1)S(1)} %get-tuple-element.25.refs_0_.refs_2_, ...), custom_call_target="tpu_custom_call" | custom-call | flops 491520000 | bytes 1228800 | tf_op jit(solution)/shard_map/pallas_call | solution.py:300
  53.4 2.4 %collective-permute-done.13.refs_1_ = bf16[1,200,512]{2,1,0:T(8,128)(2,1)S(1)} collective-permute-done((bf16[1,200,512]{2,1,0:T(8,128)(2,1)S(1)}, bf16[1,200,512]{2,1,0:T(8,128)(2,1)S(1)}, u32[]{:S(2)}, u32[]{:S(2)}) %collective-permute-start.13) | collective-permute-done | bytes 204832 | tf_op jit(solution)/shard_map/ppermute | solution.py:447
  56.2 1.6 %collective-permute-start.16 = (bf16[216,384]{1,0:T(8,128)(2,1)S(1)}, bf16[216,384]{1,0:T(8,128)(2,1)S(1)}, u32[]{:S(2)}, u32[]{:S(2)}) collective-permute-start(bf16[216,384]{1,0:T(8,128)(2,1)S(1)} %get-tuple-element.44), channel_id=1, source_target_pairs={{0,1},{1,0},{2,3},{3,2},{4,5},{5,4},{6,7},{7,6},{8,9},{9,8},{10,11... | collective-permute-start | bytes 497672 | tf_op jit(solution)/shard_map/ppermute | solution.py:447
  58.2 0.5 collective-permute-start.12
  58.7 5.1 %collective-permute-done.12.packed_ref = bf16[200,200]{1,0:T(8,128)(2,1)S(1)} collective-permute-done((bf16[200,200]{1,0:T(8,128)(2,1)S(1)}, bf16[200,200]{1,0:T(8,128)(2,1)S(1)}, u32[]{:S(2)}, u32[]{:S(2)}) %collective-permute-start.12) | collective-permute-done | bytes 80032 | tf_op jit(solution)/shard_map/ppermute | solution.py:447
  63.9 1.1 %base.1 = (f32[200,512]{1,0:T(8,128)S(1)}, f32[200,512]{1,0:T(8,128)S(1)}, bf16[384,512]{1,0:T(8,128)(2,1)S(1)}) custom-call(bf16[200,512]{1,0:T(8,128)(2,1)S(1)} %bitcast.13, bf16[200,512]{1,0:T(8,128)(2,1)S(1)} %collective-permute-done.other_ref, f32[2,200,200]{2,1,0:T(8,128)S(1)} %get-tuple-element.33.total_ref, ...), custom_call_target="tpu_custom_call" | custom-call | flops 655360000 | bytes 819200 | tf_op jit(solution)/shard_map/base/pallas_call | solution.py:354
  64.9 3.2 %update.1 = f32[1,200,512]{2,1,0:T(8,128)} custom-call(bf16[200,512]{1,0:T(8,128)(2,1)S(1)} %bitcast.14, bf16[200,512]{1,0:T(8,128)(2,1)S(1)} %collective-permute-done.other_ref, f32[200,512]{1,0:T(8,128)S(1)} %get-tuple-element.41.base_ref, f32[200,512]{1,0:T(8,128)S(1)} %get-tuple-element.42.base_other_ref, ...), custom_call_target="tpu_custom_call" | custom-call | tf_op jit(solution)/shard_map/update/pallas_call | solution.py:420
  (21 shorter events, 0.9 us)
Async XLA Ops:
  0.0 24.7 %copy-start.2 = (f32[12]{0:T(128)S(1)}, f32[12]{0:T(128)}, u32[]{:S(2)}) copy-start(f32[12]{0:T(128)} %weight_ref.7) | copy-start | bytes 148
  0.0 8.3 %collective-permute-start = (bf16[200,512]{1,0:T(8,128)(2,1)}, bf16[200,512]{1,0:T(8,128)(2,1)S(1)}, u32[]{:S(2)}, u32[]{:S(2)}) collective-permute-start(bf16[200,512]{1,0:T(8,128)(2,1)} %bitcast.9), channel_id=1, source_target_pairs={{0,1},{1,0},{2,3},{3,2},{4,5},{5,4},{6,7},{7,6},{8,9},{9,8},{10,11... | collective-permute-start | bytes 614408 | tf_op jit(solution)/shard_map/ppermute | solution.py:447
  3.0 10.3 %collective-permute-start.8 = (bf16[200,512]{1,0:T(8,128)(2,1)}, bf16[200,512]{1,0:T(8,128)(2,1)S(1)}, u32[]{:S(2)}, u32[]{:S(2)}) collective-permute-start(bf16[200,512]{1,0:T(8,128)(2,1)} %bitcast.10), channel_id=1, source_target_pairs={{10,0},{8,2},{14,4},{12,6},{18,8},{16,10},{22,12},{20,14},{26,16},... | collective-permute-start | bytes 614408 | tf_op jit(solution)/shard_map/ppermute | solution.py:450
  5.8 7.6 %collective-permute-start.6 = (bf16[200,512]{1,0:T(8,128)(2,1)}, bf16[200,512]{1,0:T(8,128)(2,1)S(1)}, u32[]{:S(2)}, u32[]{:S(2)}) collective-permute-start(bf16[200,512]{1,0:T(8,128)(2,1)} %bitcast.11), channel_id=1, source_target_pairs={{6,0},{4,2},{2,4},{0,6},{14,8},{12,10},{10,12},{8,14},{22,16},{20,... | collective-permute-start | bytes 614408 | tf_op jit(solution)/shard_map/ppermute | solution.py:450
  7.8 20.8 %collective-permute-start.1 = (bf16[200,512]{1,0:T(8,128)(2,1)}, bf16[200,512]{1,0:T(8,128)(2,1)S(1)}, u32[]{:S(2)}, u32[]{:S(2)}) collective-permute-start(bf16[200,512]{1,0:T(8,128)(2,1)} %bitcast.12), channel_id=1, source_target_pairs={{26,0},{24,2},{30,4},{28,6},{2,8},{0,10},{6,12},{4,14},{10,16},{8,... | collective-permute-start | bytes 614408 | tf_op jit(solution)/shard_map/ppermute | solution.py:450
  8.3 11.8 %collective-permute-start.9 = (bf16[200,512]{1,0:T(8,128)(2,1)S(1)}, bf16[200,512]{1,0:T(8,128)(2,1)S(1)}, u32[]{:S(2)}, u32[]{:S(2)}) collective-permute-start(bf16[200,512]{1,0:T(8,128)(2,1)S(1)} %collective-permute-done.other_ref), channel_id=1, source_target_pairs={{10,0},{8,2},{14,4},{12,6},{18,8},{16,10},{22,12},{20,14},{26,16},... | collective-permute-start | bytes 614408 | tf_op jit(solution)/shard_map/ppermute | solution.py:450
  11.4 12.1 %collective-permute-start.7 = (bf16[200,512]{1,0:T(8,128)(2,1)S(1)}, bf16[200,512]{1,0:T(8,128)(2,1)S(1)}, u32[]{:S(2)}, u32[]{:S(2)}) collective-permute-start(bf16[200,512]{1,0:T(8,128)(2,1)S(1)} %collective-permute-done.other_ref), channel_id=1, source_target_pairs={{6,0},{4,2},{2,4},{0,6},{14,8},{12,10},{10,12},{8,14},{22,16},{20,... | collective-permute-start | bytes 614408 | tf_op jit(solution)/shard_map/ppermute | solution.py:450
  13.3 16.2 %collective-permute-start.3 = (bf16[200,512]{1,0:T(8,128)(2,1)S(1)}, bf16[200,512]{1,0:T(8,128)(2,1)S(1)}, u32[]{:S(2)}, u32[]{:S(2)}) collective-permute-start(bf16[200,512]{1,0:T(8,128)(2,1)S(1)} %collective-permute-done.other_ref), channel_id=1, source_target_pairs={{26,0},{24,2},{30,4},{28,6},{2,8},{0,10},{6,12},{4,14},{10,16},{8,... | collective-permute-start | bytes 614408 | tf_op jit(solution)/shard_map/ppermute | solution.py:450
  13.3 19.1 %collective-permute-start.10 = (bf16[200,512]{1,0:T(8,128)(2,1)S(1)}, bf16[200,512]{1,0:T(8,128)(2,1)S(1)}, u32[]{:S(2)}, u32[]{:S(2)}) collective-permute-start(bf16[200,512]{1,0:T(8,128)(2,1)S(1)} %collective-permute-done.8.refs_0_), channel_id=1, source_target_pairs={{6,0},{4,2},{2,4},{0,6},{14,8},{12,10},{10,12},{8,14},{22,16},{20,... | collective-permute-start | bytes 614408 | tf_op jit(solution)/shard_map/ppermute | solution.py:450
  20.0 12.4 %collective-permute-start.11 = (bf16[200,512]{1,0:T(8,128)(2,1)S(1)}, bf16[200,512]{1,0:T(8,128)(2,1)S(1)}, u32[]{:S(2)}, u32[]{:S(2)}) collective-permute-start(bf16[200,512]{1,0:T(8,128)(2,1)S(1)} %collective-permute-done.9.refs_1_), channel_id=1, source_target_pairs={{6,0},{4,2},{2,4},{0,6},{14,8},{12,10},{10,12},{8,14},{22,16},{20,... | collective-permute-start | bytes 614408 | tf_op jit(solution)/shard_map/ppermute | solution.py:450
  23.5 12.0 %collective-permute-start.5 = (bf16[200,800]{1,0:T(8,128)(2,1)S(1)}, bf16[200,800]{1,0:T(8,128)(2,1)S(1)}, u32[]{:S(2)}, u32[]{:S(2)}) collective-permute-start(bf16[200,800]{1,0:T(8,128)(2,1)S(1)} %dynamic-slice_bitcast_fusion), channel_id=1, source_target_pairs={{0,1},{1,0},{2,3},{3,2},{4,5},{5,4},{6,7},{7,6},{8,9},{9,8},{10,11... | collective-permute-start | bytes 960008 | tf_op jit(solution)/shard_map/ppermute | solution.py:447
  24.7 2.2 %copy-start = (bf16[1,12,200,800]{3,2,1,0:T(8,128)(2,1)S(1)}, bf16[1,12,200,800]{3,2,1,0:T(8,128)(2,1)}, u32[]{:S(2)}) copy-start(bf16[1,12,200,800]{3,2,1,0:T(8,128)(2,1)} %margins_ref.7) | copy-start | bytes 11520004
  28.6 18.0 %collective-permute-start.15 = (bf16[2,200,512]{2,1,0:T(8,128)(2,1)S(1)}, bf16[2,200,512]{2,1,0:T(8,128)(2,1)S(1)}, u32[]{:S(2)}, u32[]{:S(2)}) collective-permute-start(bf16[2,200,512]{2,1,0:T(8,128)(2,1)S(1)} %get-tuple-element.28.refs_1_), channel_id=1, source_target_pairs={{0,1},{1,0},{2,3},{3,2},{4,5},{5,4},{6,7},{7,6},{8,9},{9,8},{10,11... | collective-permute-start | bytes 1228808 | tf_op jit(solution)/shard_map/ppermute | solution.py:447
  31.2 21.1 %collective-permute-start.14 = (bf16[2,200,512]{2,1,0:T(8,128)(2,1)S(1)}, bf16[2,200,512]{2,1,0:T(8,128)(2,1)S(1)}, u32[]{:S(2)}, u32[]{:S(2)}) collective-permute-start(bf16[2,200,512]{2,1,0:T(8,128)(2,1)S(1)} %get-tuple-element.30.refs_3_), channel_id=1, source_target_pairs={{0,1},{1,0},{2,3},{3,2},{4,5},{5,4},{6,7},{7,6},{8,9},{9,8},{10,11... | collective-permute-start | bytes 1228808 | tf_op jit(solution)/shard_map/ppermute | solution.py:447
  32.5 7.4 %collective-permute-start.2 = (bf16[200,512]{1,0:T(8,128)(2,1)S(1)}, bf16[200,512]{1,0:T(8,128)(2,1)S(1)}, u32[]{:S(2)}, u32[]{:S(2)}) collective-permute-start(bf16[200,512]{1,0:T(8,128)(2,1)S(1)} %collective-permute-done.1.refs_2_), channel_id=1, source_target_pairs={{6,0},{4,2},{2,4},{0,6},{14,8},{12,10},{10,12},{8,14},{22,16},{20,... | collective-permute-start | bytes 614408 | tf_op jit(solution)/shard_map/ppermute | solution.py:450
  32.5 11.4 %collective-permute-start.4 = (bf16[200,512]{1,0:T(8,128)(2,1)S(1)}, bf16[200,512]{1,0:T(8,128)(2,1)S(1)}, u32[]{:S(2)}, u32[]{:S(2)}) collective-permute-start(bf16[200,512]{1,0:T(8,128)(2,1)S(1)} %collective-permute-done.3.refs_3_), channel_id=1, source_target_pairs={{6,0},{4,2},{2,4},{0,6},{14,8},{12,10},{10,12},{8,14},{22,16},{20,... | collective-permute-start | bytes 614408 | tf_op jit(solution)/shard_map/ppermute | solution.py:450
  35.5 20.3 %collective-permute-start.13 = (bf16[1,200,512]{2,1,0:T(8,128)(2,1)S(1)}, bf16[1,200,512]{2,1,0:T(8,128)(2,1)S(1)}, u32[]{:S(2)}, u32[]{:S(2)}) collective-permute-start(bf16[1,200,512]{2,1,0:T(8,128)(2,1)S(1)} %get-tuple-element.32.refs_5_), channel_id=1, source_target_pairs={{0,1},{1,0},{2,3},{3,2},{4,5},{5,4},{6,7},{7,6},{8,9},{9,8},{10,11... | collective-permute-start | bytes 614408 | tf_op jit(solution)/shard_map/ppermute | solution.py:447
  45.4 18.5 %copy-start.1 = (bf16[1,200,512]{2,1,0:T(8,128)(2,1)S(1)}, bf16[1,200,512]{2,1,0:T(8,128)(2,1)}, u32[]{:S(2)}) copy-start(bf16[1,200,512]{2,1,0:T(8,128)(2,1)} %param.5) | copy-start | bytes 614404
  56.2 8.8 %collective-permute-start.16 = (bf16[216,384]{1,0:T(8,128)(2,1)S(1)}, bf16[216,384]{1,0:T(8,128)(2,1)S(1)}, u32[]{:S(2)}, u32[]{:S(2)}) collective-permute-start(bf16[216,384]{1,0:T(8,128)(2,1)S(1)} %get-tuple-element.44), channel_id=1, source_target_pairs={{0,1},{1,0},{2,3},{3,2},{4,5},{5,4},{6,7},{7,6},{8,9},{9,8},{10,11... | collective-permute-start | bytes 497672 | tf_op jit(solution)/shard_map/ppermute | solution.py:447
  58.2 5.7 %collective-permute-start.12 = (bf16[200,200]{1,0:T(8,128)(2,1)S(1)}, bf16[200,200]{1,0:T(8,128)(2,1)S(1)}, u32[]{:S(2)}, u32[]{:S(2)}) collective-permute-start(bf16[200,200]{1,0:T(8,128)(2,1)S(1)} %get-tuple-element.34), channel_id=1, source_target_pairs={{0,1},{1,0},{2,3},{3,2},{4,5},{5,4},{6,7},{7,6},{8,9},{9,8},{10,11... | collective-permute-start | bytes 240008 | tf_op jit(solution)/shard_map/ppermute | solution.py:447

commit v11 on v10

--- a/solution.py
+++ b/solution.py
@@ -97,18 +97,15 @@
     stacked_ref[2 * rows :, :] = times_i(whole).astype(BF16)
 
 
-def masked(product, weight, limit):
-    inside = lax.broadcasted_iota(jnp.int32, (product.shape[0], 1), 0) < limit
-    return (product * jnp.where(inside, jnp.sqrt(jnp.full((1, 1), weight, F32)), 0.0)).astype(BF16)
-
-
 def masked_blocks(margins, stacked, weights, limit):
     count, rows, double = margins.shape
+    inside = lax.broadcasted_iota(jnp.int32, (rows, 1), 0) < limit
     products = dot(margins.reshape(count * rows, double), stacked)
-    return [
-        masked(products[place * rows : (place + 1) * rows], weight, limit)
-        for place, weight in enumerate(weights)
-    ]
+    blocks = []
+    for place, weight in enumerate(weights):
+        factor = jnp.where(inside, jnp.sqrt(jnp.full((1, 1), weight, F32)), 0.0)
+        blocks.append((products[place * rows : (place + 1) * rows] * factor).astype(BF16))
+    return blocks
 
 
 def prepare_kernel(out_ref):
@@ -137,21 +134,9 @@
     side = side_ref[0]
     rows = margins_ref.shape[2]
     limits = [window_ref[...] - side * rows, window_ref[...] - (1 - side) * rows]
-    paired = []
     for number, members in enumerate(groups):
         mine, other = halves[2 * number][...], halves[2 * number + 1][...]
         stack_complex(mine, other, side, rows_ref, stacked_ref)
-        if members[0] % 2 == 0 and len(members) % 2 == 0:
-            for pair in range(members[0] // 2, members[-1] // 2 + 1):
-                for out_ref, place in ((keep_ref, side), (other_ref, 1 - side)):
-                    place = first + 2 * pair + place
-                    product = dot(margins_ref[0, place], stacked_ref[...])
-                    out_ref[pair] = masked(product, weight_ref[place], limits[0])
-                paired.append(pair)
-            if not sent:
-                product = dot(shipped_ref[...], stacked_ref[...])
-                got_ref[0] = masked(product, weight_ref[first + side], limits[1])
-            continue
         start, count = first + members[0], len(members)
         blocks = masked_blocks(
             margins_ref[0, start : start + count],
@@ -168,7 +153,7 @@
                     (got_ref[0],) = masked_blocks(
                         shipped_ref[...][None], stacked_ref[...], [weight], limits[1]
                     )
-    for pair in [pair for pair in range(keep_ref.shape[0]) if pair not in paired]:
+    for pair in range(keep_ref.shape[0]):
         keep_ref[pair] = blocks_ref[2 * pair + side]
         other_ref[pair] = blocks_ref[2 * pair + 1 - side]
 

time: 68.7 us -> 68.7 us (level)
  transfers between devices with their start and end apart: 17 -> 17, of which waited for: 7 -> 7; matrix products, arithmetic and copies ran while one was open for 1% -> 1% of each run, Pallas kernels for 15% -> 16%
where the time goes in v11:
time: 68.7 us; the launch traced here: 68.1 us
  waiting for transfers between devices  25.7 us (37%)
  starting transfers between devices  24 us (35%)
  Pallas kernels  14.3 us (21%)
  local copies, waits for them, and re-layouts  3.24 us (5%)
  between operations  0.8 us (1%)
    ppermute x10, starting transfers between devices, fetch(): return lax.ppermute(value, 'kpt', fetch_pairs(shift, point_count))  14.6 us
    ppermute x10, waiting for transfers between devices, fetch(): return lax.ppermute(value, 'kpt', fetch_pairs(shift, point_count))  13 us
    ppermute x7, waiting for transfers between devices, exchange(): return lax.ppermute(value, 'band', swap)  12.7 us
    ppermute x7, starting transfers between devices, exchange(): return lax.ppermute(value, 'band', swap)  9.46 us
    pallas_call x4, Pallas kernels, project(): pl.pallas_call(functools.partial(project_kernel, groups, first, sent), in...  6.17 us
    pallas_call x1, Pallas kernels, update(): pl.pallas_call(functools.partial(update_kernel, scale), in_specs=[VMEM] *...  3.18 us
    unnamed x6, local copies, waits for them, and re-layouts  2.23 us
    pallas_call x3, Pallas kernels, cross(): pl.pallas_call(functools.partial(cross_kernel, terms, len(blocks), before...  2.23 us
  transfers between devices with their start and end apart: 17, of which 7 were waited for; matrix products, arithmetic and copies ran while one was open for 1% of the time, Pallas kernels for 16%

profile of v11, /device:TPU:0, one launch (start us, length us, event | category | flops | bytes accessed | tf_op | source)
XLA Modules:
  0.0 68.1 jit_solution(662158615104649034)
XLA Ops:
  0.0 3.0 %collective-permute-start = (bf16[200,512]{1,0:T(8,128)(2,1)}, bf16[200,512]{1,0:T(8,128)(2,1)S(1)}, u32[]{:S(2)}, u32[]{:S(2)}) collective-permute-start(bf16[200,512]{1,0:T(8,128)(2,1)} %bitcast.9), channel_id=1, source_target_pairs={{0,1},{1,0},{2,3},{3,2},{4,5},{5,4},{6,7},{7,6},{8,9},{9,8},{10,11... | collective-permute-start | bytes 614408 | tf_op jit(solution)/shard_map/ppermute | solution.py:432
  3.0 2.8 %collective-permute-start.8 = (bf16[200,512]{1,0:T(8,128)(2,1)}, bf16[200,512]{1,0:T(8,128)(2,1)S(1)}, u32[]{:S(2)}, u32[]{:S(2)}) collective-permute-start(bf16[200,512]{1,0:T(8,128)(2,1)} %bitcast.10), channel_id=1, source_target_pairs={{10,0},{8,2},{14,4},{12,6},{18,8},{16,10},{22,12},{20,14},{26,16},... | collective-permute-start | bytes 614408 | tf_op jit(solution)/shard_map/ppermute | solution.py:435
  5.8 2.1 %collective-permute-start.6 = (bf16[200,512]{1,0:T(8,128)(2,1)}, bf16[200,512]{1,0:T(8,128)(2,1)S(1)}, u32[]{:S(2)}, u32[]{:S(2)}) collective-permute-start(bf16[200,512]{1,0:T(8,128)(2,1)} %bitcast.11), channel_id=1, source_target_pairs={{6,0},{4,2},{2,4},{0,6},{14,8},{12,10},{10,12},{8,14},{22,16},{20,... | collective-permute-start | bytes 614408 | tf_op jit(solution)/shard_map/ppermute | solution.py:435
  7.8 0.5 collective-permute-done.other_ref
  8.3 3.1 %collective-permute-start.9 = (bf16[200,512]{1,0:T(8,128)(2,1)S(1)}, bf16[200,512]{1,0:T(8,128)(2,1)S(1)}, u32[]{:S(2)}, u32[]{:S(2)}) collective-permute-start(bf16[200,512]{1,0:T(8,128)(2,1)S(1)} %collective-permute-done.other_ref), channel_id=1, source_target_pairs={{10,0},{8,2},{14,4},{12,6},{18,8},{16,10},{22,12},{20,14},{26,16},... | collective-permute-start | bytes 614408 | tf_op jit(solution)/shard_map/ppermute | solution.py:435
  11.4 2.0 %collective-permute-start.7 = (bf16[200,512]{1,0:T(8,128)(2,1)S(1)}, bf16[200,512]{1,0:T(8,128)(2,1)S(1)}, u32[]{:S(2)}, u32[]{:S(2)}) collective-permute-start(bf16[200,512]{1,0:T(8,128)(2,1)S(1)} %collective-permute-done.other_ref), channel_id=1, source_target_pairs={{6,0},{4,2},{2,4},{0,6},{14,8},{12,10},{10,12},{8,14},{22,16},{20,... | collective-permute-start | bytes 614408 | tf_op jit(solution)/shard_map/ppermute | solution.py:435
  13.3 1.2 %collective-permute-start.10 = (bf16[200,512]{1,0:T(8,128)(2,1)S(1)}, bf16[200,512]{1,0:T(8,128)(2,1)S(1)}, u32[]{:S(2)}, u32[]{:S(2)}) collective-permute-start(bf16[200,512]{1,0:T(8,128)(2,1)S(1)} %collective-permute-done.8.refs_0_), channel_id=1, source_target_pairs={{6,0},{4,2},{2,4},{0,6},{14,8},{12,10},{10,12},{8,14},{22,16},{20,... | collective-permute-start | bytes 614408 | tf_op jit(solution)/shard_map/ppermute | solution.py:435
  14.6 5.5 %collective-permute-done.9.refs_1_ = bf16[200,512]{1,0:T(8,128)(2,1)S(1)} collective-permute-done((bf16[200,512]{1,0:T(8,128)(2,1)S(1)}, bf16[200,512]{1,0:T(8,128)(2,1)S(1)}, u32[]{:S(2)}, u32[]{:S(2)}) %collective-permute-start.9) | collective-permute-done | bytes 204832 | tf_op jit(solution)/shard_map/ppermute | solution.py:435
  20.0 1.7 %collective-permute-start.11 = (bf16[200,512]{1,0:T(8,128)(2,1)S(1)}, bf16[200,512]{1,0:T(8,128)(2,1)S(1)}, u32[]{:S(2)}, u32[]{:S(2)}) collective-permute-start(bf16[200,512]{1,0:T(8,128)(2,1)S(1)} %collective-permute-done.9.refs_1_), channel_id=1, source_target_pairs={{6,0},{4,2},{2,4},{0,6},{14,8},{12,10},{10,12},{8,14},{22,16},{20,... | collective-permute-start | bytes 614408 | tf_op jit(solution)/shard_map/ppermute | solution.py:435
  21.8 1.0 %dynamic-slice_bitcast_fusion = bf16[200,800]{1,0:T(8,128)(2,1)S(1)} fusion(bf16[1,12,200,800]{3,2,1,0:T(8,128)(2,1)} %margins_ref.7, s32[]{:T(128)S(6)} %select_n.4), kind=kLoop, calls=%fused_computation | loop fusion | bytes 640004 | tf_op jit(solution)/shard_map/jit(dynamic_index_in_dim)/squeeze | solution.py:441
  23.5 1.3 %collective-permute-start.5 = (bf16[200,800]{1,0:T(8,128)(2,1)S(1)}, bf16[200,800]{1,0:T(8,128)(2,1)S(1)}, u32[]{:S(2)}, u32[]{:S(2)}) collective-permute-start(bf16[200,800]{1,0:T(8,128)(2,1)S(1)} %dynamic-slice_bitcast_fusion), channel_id=1, source_target_pairs={{0,1},{1,0},{2,3},{3,2},{4,5},{5,4},{6,7},{7,6},{8,9},{9,8},{10,11... | collective-permute-start | bytes 960008 | tf_op jit(solution)/shard_map/ppermute | solution.py:432
  24.7 2.2 %copy-done = bf16[1,12,200,800]{3,2,1,0:T(8,128)(2,1)S(1)} copy-done((bf16[1,12,200,800]{3,2,1,0:T(8,128)(2,1)S(1)}, bf16[1,12,200,800]{3,2,1,0:T(8,128)(2,1)}, u32[]{:S(2)}) %copy-start) | copy-done | bytes 3840024
  26.9 1.7 %shard_map.47 = (bf16[2,200,512]{2,1,0:T(8,128)(2,1)S(1)}, bf16[2,200,512]{2,1,0:T(8,128)(2,1)S(1)}) custom-call(s32[1]{0:T(128)} %bitcast.1.side_ref, s32[1,1]{1,0:T(1,128)} %bitcast.6.window_ref, f32[12]{0:T(128)S(1)} %copy-done.2, bf16[1,12,200,800]{3,2,1,0:T(8,128)(2,1)S(1)} %copy-done, bf16[200,512]{1,0:T(8,128)(2,1)S(1)} %collective-permute-done.6.refs_0_, ...), custom_call_target="tpu_custom_call" | custom-call | flops 655360000 | bytes 1280000 | tf_op jit(solution)/shard_map/pallas_call | solution.py:166
  28.6 0.9 %collective-permute-start.15 = (bf16[2,200,512]{2,1,0:T(8,128)(2,1)S(1)}, bf16[2,200,512]{2,1,0:T(8,128)(2,1)S(1)}, u32[]{:S(2)}, u32[]{:S(2)}) collective-permute-start(bf16[2,200,512]{2,1,0:T(8,128)(2,1)S(1)} %get-tuple-element.28.refs_1_), channel_id=1, source_target_pairs={{0,1},{1,0},{2,3},{3,2},{4,5},{5,4},{6,7},{7,6},{8,9},{9,8},{10,11... | collective-permute-start | bytes 1228808 | tf_op jit(solution)/shard_map/ppermute | solution.py:432
  29.5 1.7 %shard_map.48 = (bf16[2,200,512]{2,1,0:T(8,128)(2,1)S(1)}, bf16[2,200,512]{2,1,0:T(8,128)(2,1)S(1)}) custom-call(s32[1]{0:T(128)} %bitcast.1.side_ref, s32[1,1]{1,0:T(1,128)} %bitcast.7.window_ref, f32[12]{0:T(128)S(1)} %copy-done.2, bf16[1,12,200,800]{3,2,1,0:T(8,128)(2,1)S(1)} %copy-done, bf16[200,512]{1,0:T(8,128)(2,1)S(1)} %collective-permute-done.8.refs_0_, ...), custom_call_target="tpu_custom_call" | custom-call | flops 655360000 | bytes 1280000 | tf_op jit(solution)/shard_map/pallas_call | solution.py:166
  31.2 1.3 %collective-permute-start.14 = (bf16[2,200,512]{2,1,0:T(8,128)(2,1)S(1)}, bf16[2,200,512]{2,1,0:T(8,128)(2,1)S(1)}, u32[]{:S(2)}, u32[]{:S(2)}) collective-permute-start(bf16[2,200,512]{2,1,0:T(8,128)(2,1)S(1)} %get-tuple-element.30.refs_3_), channel_id=1, source_target_pairs={{0,1},{1,0},{2,3},{3,2},{4,5},{5,4},{6,7},{7,6},{8,9},{9,8},{10,11... | collective-permute-start | bytes 1228808 | tf_op jit(solution)/shard_map/ppermute | solution.py:432
  32.5 1.7 %collective-permute-start.4 = (bf16[200,512]{1,0:T(8,128)(2,1)S(1)}, bf16[200,512]{1,0:T(8,128)(2,1)S(1)}, u32[]{:S(2)}, u32[]{:S(2)}) collective-permute-start(bf16[200,512]{1,0:T(8,128)(2,1)S(1)} %collective-permute-done.3.refs_3_), channel_id=1, source_target_pairs={{6,0},{4,2},{2,4},{0,6},{14,8},{12,10},{10,12},{8,14},{22,16},{20,... | collective-permute-start | bytes 614408 | tf_op jit(solution)/shard_map/ppermute | solution.py:435
  34.2 1.2 %shard_map.49 = (bf16[1,200,512]{2,1,0:T(8,128)(2,1)S(1)}, bf16[1,200,512]{2,1,0:T(8,128)(2,1)S(1)}) custom-call(s32[1]{0:T(128)} %bitcast.1.side_ref, s32[1,1]{1,0:T(1,128)} %bitcast.8.window_ref, f32[12]{0:T(128)S(1)} %copy-done.2, bf16[1,12,200,800]{3,2,1,0:T(8,128)(2,1)S(1)} %copy-done, bf16[200,512]{1,0:T(8,128)(2,1)S(1)} %collective-permute-done.10.refs_0_, ...), custom_call_target="tpu_custom_call" | custom-call | flops 327680000 | bytes 640000 | tf_op jit(solution)/shard_map/pallas_call | solution.py:166
  35.4 0.9 %collective-permute-start.13 = (bf16[1,200,512]{2,1,0:T(8,128)(2,1)S(1)}, bf16[1,200,512]{2,1,0:T(8,128)(2,1)S(1)}, u32[]{:S(2)}, u32[]{:S(2)}) collective-permute-start(bf16[1,200,512]{2,1,0:T(8,128)(2,1)S(1)} %get-tuple-element.32.refs_5_), channel_id=1, source_target_pairs={{0,1},{1,0},{2,3},{3,2},{4,5},{5,4},{6,7},{7,6},{8,9},{9,8},{10,11... | collective-permute-start | bytes 614408 | tf_op jit(solution)/shard_map/ppermute | solution.py:432
  36.3 3.5 %collective-permute-done.2.refs_0_ = bf16[200,512]{1,0:T(8,128)(2,1)S(1)} collective-permute-done((bf16[200,512]{1,0:T(8,128)(2,1)S(1)}, bf16[200,512]{1,0:T(8,128)(2,1)S(1)}, u32[]{:S(2)}, u32[]{:S(2)}) %collective-permute-start.2) | collective-permute-done | bytes 204832 | tf_op jit(solution)/shard_map/ppermute | solution.py:435
  39.8 4.1 %collective-permute-done.4.refs_1_ = bf16[200,512]{1,0:T(8,128)(2,1)S(1)} collective-permute-done((bf16[200,512]{1,0:T(8,128)(2,1)S(1)}, bf16[200,512]{1,0:T(8,128)(2,1)S(1)}, u32[]{:S(2)}, u32[]{:S(2)}) %collective-permute-start.4) | collective-permute-done | bytes 204832 | tf_op jit(solution)/shard_map/ppermute | solution.py:435
  43.9 1.6 %shard_map.46 = (bf16[1,200,512]{2,1,0:T(8,128)(2,1)S(1)}, bf16[1,200,512]{2,1,0:T(8,128)(2,1)S(1)}, bf16[1,200,512]{2,1,0:T(8,128)(2,1)S(1)}) custom-call(s32[1]{0:T(128)} %bitcast.1.side_ref, s32[1,1]{1,0:T(1,128)} %bitcast.5.window_ref, f32[12]{0:T(128)S(1)} %copy-done.2, bf16[1,12,200,800]{3,2,1,0:T(8,128)(2,1)S(1)} %copy-done, ...), custom_call_target="tpu_custom_call" | custom-call | flops 327680000 | bytes 640000 | tf_op jit(solution)/shard_map/pallas_call | solution.py:166
  45.5 1.3 %shard_map.50.refs_2_ = f32[2,200,200]{2,1,0:T(8,128)S(1)} custom-call(bf16[2,200,512]{2,1,0:T(8,128)(2,1)S(1)} %get-tuple-element.27.refs_0_, bf16[2,200,512]{2,1,0:T(8,128)(2,1)S(1)} %get-tuple-element.28.refs_1_, bf16[2,200,512]{2,1,0:T(8,128)(2,1)S(1)} %get-tuple-element.29.refs_2_.refs_0_, bf16[2,200,512]{2,1,0:T(8,128)(2,1)S(1)} %get-tuple-element.30.refs_3_, ...), custom_call_target="tpu_custom_call" | custom-call | flops 983040000 | bytes 2457600 | tf_op jit(solution)/shard_map/pallas_call | solution.py:216
  46.8 0.8 %shard_map.52 = (f32[2,200,200]{2,1,0:T(8,128)S(1)}, f32[216,384]{1,0:T(8,128)S(1)}) custom-call(bf16[2,200,512]{2,1,0:T(8,128)(2,1)S(1)} %get-tuple-element.27.refs_0_, bf16[2,200,512]{2,1,0:T(8,128)(2,1)S(1)} %collective-permute-done.15.refs_1_), custom_call_target="tpu_custom_call" | custom-call | flops 327680000 | bytes 819200 | tf_op jit(solution)/shard_map/pallas_call | solution.py:285
  47.6 4.7 %collective-permute-done.14.refs_1_ = bf16[2,200,512]{2,1,0:T(8,128)(2,1)S(1)} collective-permute-done((bf16[2,200,512]{2,1,0:T(8,128)(2,1)S(1)}, bf16[2,200,512]{2,1,0:T(8,128)(2,1)S(1)}, u32[]{:S(2)}, u32[]{:S(2)}) %collective-permute-start.14) | collective-permute-done | bytes 409632 | tf_op jit(solution)/shard_map/ppermute | solution.py:432
  52.3 1.0 %shard_map.53 = (f32[2,200,200]{2,1,0:T(8,128)S(1)}, f32[216,384]{1,0:T(8,128)S(1)}) custom-call(bf16[2,200,512]{2,1,0:T(8,128)(2,1)S(1)} %get-tuple-element.29.refs_2_.refs_0_, bf16[2,200,512]{2,1,0:T(8,128)(2,1)S(1)} %collective-permute-done.14.refs_1_, bf16[1,200,512]{2,1,0:T(8,128)(2,1)S(1)} %get-tuple-element.25.refs_0_.refs_2_, ...), custom_call_target="tpu_custom_call" | custom-call | flops 491520000 | bytes 1228800 | tf_op jit(solution)/shard_map/pallas_call | solution.py:285
  53.4 2.4 %collective-permute-done.13.refs_1_ = bf16[1,200,512]{2,1,0:T(8,128)(2,1)S(1)} collective-permute-done((bf16[1,200,512]{2,1,0:T(8,128)(2,1)S(1)}, bf16[1,200,512]{2,1,0:T(8,128)(2,1)S(1)}, u32[]{:S(2)}, u32[]{:S(2)}) %collective-permute-start.13) | collective-permute-done | bytes 204832 | tf_op jit(solution)/shard_map/ppermute | solution.py:432
  56.2 1.6 %collective-permute-start.16 = (bf16[216,384]{1,0:T(8,128)(2,1)S(1)}, bf16[216,384]{1,0:T(8,128)(2,1)S(1)}, u32[]{:S(2)}, u32[]{:S(2)}) collective-permute-start(bf16[216,384]{1,0:T(8,128)(2,1)S(1)} %get-tuple-element.44), channel_id=1, source_target_pairs={{0,1},{1,0},{2,3},{3,2},{4,5},{5,4},{6,7},{7,6},{8,9},{9,8},{10,11... | collective-permute-start | bytes 497672 | tf_op jit(solution)/shard_map/ppermute | solution.py:432
  58.2 0.5 collective-permute-start.12
  58.7 5.1 %collective-permute-done.12.packed_ref = bf16[200,200]{1,0:T(8,128)(2,1)S(1)} collective-permute-done((bf16[200,200]{1,0:T(8,128)(2,1)S(1)}, bf16[200,200]{1,0:T(8,128)(2,1)S(1)}, u32[]{:S(2)}, u32[]{:S(2)}) %collective-permute-start.12) | collective-permute-done | bytes 80032 | tf_op jit(solution)/shard_map/ppermute | solution.py:432
  63.9 1.1 %base.1 = (f32[200,512]{1,0:T(8,128)S(1)}, f32[200,512]{1,0:T(8,128)S(1)}, bf16[384,512]{1,0:T(8,128)(2,1)S(1)}) custom-call(bf16[200,512]{1,0:T(8,128)(2,1)S(1)} %bitcast.13, bf16[200,512]{1,0:T(8,128)(2,1)S(1)} %collective-permute-done.other_ref, f32[2,200,200]{2,1,0:T(8,128)S(1)} %get-tuple-element.33.total_ref, ...), custom_call_target="tpu_custom_call" | custom-call | flops 655360000 | bytes 819200 | tf_op jit(solution)/shard_map/base/pallas_call | solution.py:339
  64.9 3.2 %update.1 = f32[1,200,512]{2,1,0:T(8,128)} custom-call(bf16[200,512]{1,0:T(8,128)(2,1)S(1)} %bitcast.14, bf16[200,512]{1,0:T(8,128)(2,1)S(1)} %collective-permute-done.other_ref, f32[200,512]{1,0:T(8,128)S(1)} %get-tuple-element.41.base_ref, f32[200,512]{1,0:T(8,128)S(1)} %get-tuple-element.42.base_other_ref, ...), custom_call_target="tpu_custom_call" | custom-call | tf_op jit(solution)/shard_map/update/pallas_call | solution.py:405
  (21 shorter events, 0.9 us)
Async XLA Ops:
  0.0 24.7 %copy-start.2 = (f32[12]{0:T(128)S(1)}, f32[12]{0:T(128)}, u32[]{:S(2)}) copy-start(f32[12]{0:T(128)} %weight_ref.7) | copy-start | bytes 148
  0.0 8.3 %collective-permute-start = (bf16[200,512]{1,0:T(8,128)(2,1)}, bf16[200,512]{1,0:T(8,128)(2,1)S(1)}, u32[]{:S(2)}, u32[]{:S(2)}) collective-permute-start(bf16[200,512]{1,0:T(8,128)(2,1)} %bitcast.9), channel_id=1, source_target_pairs={{0,1},{1,0},{2,3},{3,2},{4,5},{5,4},{6,7},{7,6},{8,9},{9,8},{10,11... | collective-permute-start | bytes 614408 | tf_op jit(solution)/shard_map/ppermute | solution.py:432
  3.0 10.3 %collective-permute-start.8 = (bf16[200,512]{1,0:T(8,128)(2,1)}, bf16[200,512]{1,0:T(8,128)(2,1)S(1)}, u32[]{:S(2)}, u32[]{:S(2)}) collective-permute-start(bf16[200,512]{1,0:T(8,128)(2,1)} %bitcast.10), channel_id=1, source_target_pairs={{10,0},{8,2},{14,4},{12,6},{18,8},{16,10},{22,12},{20,14},{26,16},... | collective-permute-start | bytes 614408 | tf_op jit(solution)/shard_map/ppermute | solution.py:435
  5.8 7.6 %collective-permute-start.6 = (bf16[200,512]{1,0:T(8,128)(2,1)}, bf16[200,512]{1,0:T(8,128)(2,1)S(1)}, u32[]{:S(2)}, u32[]{:S(2)}) collective-permute-start(bf16[200,512]{1,0:T(8,128)(2,1)} %bitcast.11), channel_id=1, source_target_pairs={{6,0},{4,2},{2,4},{0,6},{14,8},{12,10},{10,12},{8,14},{22,16},{20,... | collective-permute-start | bytes 614408 | tf_op jit(solution)/shard_map/ppermute | solution.py:435
  7.8 20.8 %collective-permute-start.1 = (bf16[200,512]{1,0:T(8,128)(2,1)}, bf16[200,512]{1,0:T(8,128)(2,1)S(1)}, u32[]{:S(2)}, u32[]{:S(2)}) collective-permute-start(bf16[200,512]{1,0:T(8,128)(2,1)} %bitcast.12), channel_id=1, source_target_pairs={{26,0},{24,2},{30,4},{28,6},{2,8},{0,10},{6,12},{4,14},{10,16},{8,... | collective-permute-start | bytes 614408 | tf_op jit(solution)/shard_map/ppermute | solution.py:435
  8.3 11.8 %collective-permute-start.9 = (bf16[200,512]{1,0:T(8,128)(2,1)S(1)}, bf16[200,512]{1,0:T(8,128)(2,1)S(1)}, u32[]{:S(2)}, u32[]{:S(2)}) collective-permute-start(bf16[200,512]{1,0:T(8,128)(2,1)S(1)} %collective-permute-done.other_ref), channel_id=1, source_target_pairs={{10,0},{8,2},{14,4},{12,6},{18,8},{16,10},{22,12},{20,14},{26,16},... | collective-permute-start | bytes 614408 | tf_op jit(solution)/shard_map/ppermute | solution.py:435
  11.4 12.1 %collective-permute-start.7 = (bf16[200,512]{1,0:T(8,128)(2,1)S(1)}, bf16[200,512]{1,0:T(8,128)(2,1)S(1)}, u32[]{:S(2)}, u32[]{:S(2)}) collective-permute-start(bf16[200,512]{1,0:T(8,128)(2,1)S(1)} %collective-permute-done.other_ref), channel_id=1, source_target_pairs={{6,0},{4,2},{2,4},{0,6},{14,8},{12,10},{10,12},{8,14},{22,16},{20,... | collective-permute-start | bytes 614408 | tf_op jit(solution)/shard_map/ppermute | solution.py:435
  13.3 16.2 %collective-permute-start.3 = (bf16[200,512]{1,0:T(8,128)(2,1)S(1)}, bf16[200,512]{1,0:T(8,128)(2,1)S(1)}, u32[]{:S(2)}, u32[]{:S(2)}) collective-permute-start(bf16[200,512]{1,0:T(8,128)(2,1)S(1)} %collective-permute-done.other_ref), channel_id=1, source_target_pairs={{26,0},{24,2},{30,4},{28,6},{2,8},{0,10},{6,12},{4,14},{10,16},{8,... | collective-permute-start | bytes 614408 | tf_op jit(solution)/shard_map/ppermute | solution.py:435
  13.3 19.1 %collective-permute-start.10 = (bf16[200,512]{1,0:T(8,128)(2,1)S(1)}, bf16[200,512]{1,0:T(8,128)(2,1)S(1)}, u32[]{:S(2)}, u32[]{:S(2)}) collective-permute-start(bf16[200,512]{1,0:T(8,128)(2,1)S(1)} %collective-permute-done.8.refs_0_), channel_id=1, source_target_pairs={{6,0},{4,2},{2,4},{0,6},{14,8},{12,10},{10,12},{8,14},{22,16},{20,... | collective-permute-start | bytes 614408 | tf_op jit(solution)/shard_map/ppermute | solution.py:435
  20.0 12.4 %collective-permute-start.11 = (bf16[200,512]{1,0:T(8,128)(2,1)S(1)}, bf16[200,512]{1,0:T(8,128)(2,1)S(1)}, u32[]{:S(2)}, u32[]{:S(2)}) collective-permute-start(bf16[200,512]{1,0:T(8,128)(2,1)S(1)} %collective-permute-done.9.refs_1_), channel_id=1, source_target_pairs={{6,0},{4,2},{2,4},{0,6},{14,8},{12,10},{10,12},{8,14},{22,16},{20,... | collective-permute-start | bytes 614408 | tf_op jit(solution)/shard_map/ppermute | solution.py:435
  23.5 12.0 %collective-permute-start.5 = (bf16[200,800]{1,0:T(8,128)(2,1)S(1)}, bf16[200,800]{1,0:T(8,128)(2,1)S(1)}, u32[]{:S(2)}, u32[]{:S(2)}) collective-permute-start(bf16[200,800]{1,0:T(8,128)(2,1)S(1)} %dynamic-slice_bitcast_fusion), channel_id=1, source_target_pairs={{0,1},{1,0},{2,3},{3,2},{4,5},{5,4},{6,7},{7,6},{8,9},{9,8},{10,11... | collective-permute-start | bytes 960008 | tf_op jit(solution)/shard_map/ppermute | solution.py:432
  24.7 2.2 %copy-start = (bf16[1,12,200,800]{3,2,1,0:T(8,128)(2,1)S(1)}, bf16[1,12,200,800]{3,2,1,0:T(8,128)(2,1)}, u32[]{:S(2)}) copy-start(bf16[1,12,200,800]{3,2,1,0:T(8,128)(2,1)} %margins_ref.7) | copy-start | bytes 11520004
  28.6 18.2 %collective-permute-start.15 = (bf16[2,200,512]{2,1,0:T(8,128)(2,1)S(1)}, bf16[2,200,512]{2,1,0:T(8,128)(2,1)S(1)}, u32[]{:S(2)}, u32[]{:S(2)}) collective-permute-start(bf16[2,200,512]{2,1,0:T(8,128)(2,1)S(1)} %get-tuple-element.28.refs_1_), channel_id=1, source_target_pairs={{0,1},{1,0},{2,3},{3,2},{4,5},{5,4},{6,7},{7,6},{8,9},{9,8},{10,11... | collective-permute-start | bytes 1228808 | tf_op jit(solution)/shard_map/ppermute | solution.py:432
  31.2 21.1 %collective-permute-start.14 = (bf16[2,200,512]{2,1,0:T(8,128)(2,1)S(1)}, bf16[2,200,512]{2,1,0:T(8,128)(2,1)S(1)}, u32[]{:S(2)}, u32[]{:S(2)}) collective-permute-start(bf16[2,200,512]{2,1,0:T(8,128)(2,1)S(1)} %get-tuple-element.30.refs_3_), channel_id=1, source_target_pairs={{0,1},{1,0},{2,3},{3,2},{4,5},{5,4},{6,7},{7,6},{8,9},{9,8},{10,11... | collective-permute-start | bytes 1228808 | tf_op jit(solution)/shard_map/ppermute | solution.py:432
  32.5 7.4 %collective-permute-start.2 = (bf16[200,512]{1,0:T(8,128)(2,1)S(1)}, bf16[200,512]{1,0:T(8,128)(2,1)S(1)}, u32[]{:S(2)}, u32[]{:S(2)}) collective-permute-start(bf16[200,512]{1,0:T(8,128)(2,1)S(1)} %collective-permute-done.1.refs_2_), channel_id=1, source_target_pairs={{6,0},{4,2},{2,4},{0,6},{14,8},{12,10},{10,12},{8,14},{22,16},{20,... | collective-permute-start | bytes 614408 | tf_op jit(solution)/shard_map/ppermute | solution.py:435
  32.5 11.4 %collective-permute-start.4 = (bf16[200,512]{1,0:T(8,128)(2,1)S(1)}, bf16[200,512]{1,0:T(8,128)(2,1)S(1)}, u32[]{:S(2)}, u32[]{:S(2)}) collective-permute-start(bf16[200,512]{1,0:T(8,128)(2,1)S(1)} %collective-permute-done.3.refs_3_), channel_id=1, source_target_pairs={{6,0},{4,2},{2,4},{0,6},{14,8},{12,10},{10,12},{8,14},{22,16},{20,... | collective-permute-start | bytes 614408 | tf_op jit(solution)/shard_map/ppermute | solution.py:435
  35.4 20.3 %collective-permute-start.13 = (bf16[1,200,512]{2,1,0:T(8,128)(2,1)S(1)}, bf16[1,200,512]{2,1,0:T(8,128)(2,1)S(1)}, u32[]{:S(2)}, u32[]{:S(2)}) collective-permute-start(bf16[1,200,512]{2,1,0:T(8,128)(2,1)S(1)} %get-tuple-element.32.refs_5_), channel_id=1, source_target_pairs={{0,1},{1,0},{2,3},{3,2},{4,5},{5,4},{6,7},{7,6},{8,9},{9,8},{10,11... | collective-permute-start | bytes 614408 | tf_op jit(solution)/shard_map/ppermute | solution.py:432
  45.5 18.3 %copy-start.1 = (bf16[1,200,512]{2,1,0:T(8,128)(2,1)S(1)}, bf16[1,200,512]{2,1,0:T(8,128)(2,1)}, u32[]{:S(2)}) copy-start(bf16[1,200,512]{2,1,0:T(8,128)(2,1)} %param.5) | copy-start | bytes 614404
  56.2 8.8 %collective-permute-start.16 = (bf16[216,384]{1,0:T(8,128)(2,1)S(1)}, bf16[216,384]{1,0:T(8,128)(2,1)S(1)}, u32[]{:S(2)}, u32[]{:S(2)}) collective-permute-start(bf16[216,384]{1,0:T(8,128)(2,1)S(1)} %get-tuple-element.44), channel_id=1, source_target_pairs={{0,1},{1,0},{2,3},{3,2},{4,5},{5,4},{6,7},{7,6},{8,9},{9,8},{10,11... | collective-permute-start | bytes 497672 | tf_op jit(solution)/shard_map/ppermute | solution.py:432
  58.2 5.7 %collective-permute-start.12 = (bf16[200,200]{1,0:T(8,128)(2,1)S(1)}, bf16[200,200]{1,0:T(8,128)(2,1)S(1)}, u32[]{:S(2)}, u32[]{:S(2)}) collective-permute-start(bf16[200,200]{1,0:T(8,128)(2,1)S(1)} %get-tuple-element.34), channel_id=1, source_target_pairs={{0,1},{1,0},{2,3},{3,2},{4,5},{5,4},{6,7},{7,6},{8,9},{9,8},{10,11... | collective-permute-start | bytes 240008 | tf_op jit(solution)/shard_map/ppermute | solution.py:432
